TPU v7x, 32 devices: a whole 2x2x4 slice. The times are simulated.
32 devices in a mesh: fsdp: 32 (over z, y, x, core).
Axes of the slice: x: 2, y: 2, z: 4, core: 2. Of those that a mesh axis runs over, the one named last changes fastest.
Arguments:
- tokens: int32 [32, 512], P('fsdp')
- positions: int32 [32, 512], P('fsdp')
- embed_table: bfloat16 [152064, 896], P('fsdp')
- attn_norm: bfloat16 [896], P('fsdp')
- w_query: bfloat16 [896, 896], P('fsdp')
- w_key: bfloat16 [896, 128], P('fsdp')
- w_value: bfloat16 [896, 128], P('fsdp')
- q_norm: bfloat16 [64], replicated
- k_norm: bfloat16 [64], replicated
- w_out: bfloat16 [896, 896], P('fsdp')
- mlp_norm: bfloat16 [896], P('fsdp')
- w_gate: bfloat16 [896, 4864], P('fsdp')
- w_up: bfloat16 [896, 4864], P('fsdp')
- w_down: bfloat16 [4864, 896], P('fsdp')
- dy_out: bfloat16 [32, 512, 896], P('fsdp')
Outputs:
- output 1: bfloat16 [32, 512, 896], P('fsdp')
- output 2: float32 [152064, 896], P('fsdp')
- output 3: float32 [896], P('fsdp')
- output 4: float32 [896, 896], P('fsdp')
- output 5: float32 [896, 128], P('fsdp')
- output 6: float32 [896, 128], P('fsdp')
- output 7: float32 [64], replicated
- output 8: float32 [64], replicated
- output 9: float32 [896, 896], P('fsdp')
- output 10: float32 [896], P('fsdp')
- output 11: float32 [896, 4864], P('fsdp')
- output 12: float32 [896, 4864], P('fsdp')
- output 13: float32 [4864, 896], P('fsdp')
All inputs are finite; a program needn't handle non-finite values.
Results may differ from a plain program's by a relative error of at most 0.0199887.
Values are sent between devices in bfloat16 or wider.
A program may use at most 1 GiB of HBM per device.

v0:
```python
import math
import jax
import jax.numpy as jnp
from jax import lax
from jax.sharding import PartitionSpec as P

NORM_EPS = 1e-6
ROPE_THETA = 1.0e6
AXIS_NAME = 'fsdp'
SHARDED = (True, True, True, True, False, False, True, True, True, True, True)


def rope_tables(positions, head_dim):
    half_dim = head_dim // 2
    inv_freq = jnp.exp(jnp.arange(half_dim, dtype=jnp.float32) * (-2.0 * math.log(ROPE_THETA) / head_dim))
    angles = positions.astype(jnp.float32)[:, :, None] * inv_freq
    return jnp.cos(angles), jnp.sin(angles)


def rotate(values, cos_t, sin_t):
    half_dim = values.shape[-1] // 2
    lead_half = values[..., :half_dim]
    tail_half = values[..., half_dim:]
    return jnp.concatenate([lead_half * cos_t - tail_half * sin_t, tail_half * cos_t + lead_half * sin_t], axis=-1)


def norm_fwd(values):
    values_f = values.astype(jnp.float32)
    inv_rms = lax.rsqrt(jnp.mean(values_f * values_f, axis=-1, keepdims=True) + NORM_EPS)
    return values_f * inv_rms, inv_rms


def norm_bwd(grad_out, normed, inv_rms, norm_gain):
    grad_normed = grad_out * norm_gain.astype(jnp.float32)
    mean_term = jnp.mean(grad_normed * normed, axis=-1, keepdims=True)
    return inv_rms * (grad_normed - normed * mean_term)


def attn_fwd(q_rot, k_rot, v_raw):
    seq_len = q_rot.shape[1]
    attn_scale = q_rot.shape[-1] ** -0.5
    scores = jnp.einsum('bqgrh,bkgh->bgrqk', q_rot, k_rot, preferred_element_type=jnp.float32) * attn_scale
    causal = lax.broadcasted_iota(jnp.int32, (seq_len, seq_len), 0) >= lax.broadcasted_iota(jnp.int32, (seq_len, seq_len), 1)
    attn_probs = jax.nn.softmax(jnp.where(causal, scores, -1e30), axis=-1)
    attn_heads = jnp.einsum('bgrqk,bkgh->bqgrh', attn_probs.astype(jnp.bfloat16), v_raw, preferred_element_type=jnp.float32)
    return attn_heads.astype(jnp.bfloat16), attn_probs


def attn_bwd(grad_out, q_rot, k_rot, v_raw, attn_probs):
    attn_scale = q_rot.shape[-1] ** -0.5
    grad_b = grad_out.astype(jnp.bfloat16)
    probs_b = attn_probs.astype(jnp.bfloat16)
    grad_probs = jnp.einsum('bqgrh,bkgh->bgrqk', grad_b, v_raw, preferred_element_type=jnp.float32)
    grad_v = jnp.einsum('bgrqk,bqgrh->bkgh', probs_b, grad_b, preferred_element_type=jnp.float32)
    grad_scores = attn_probs * (grad_probs - jnp.sum(grad_probs * attn_probs, axis=-1, keepdims=True)) * attn_scale
    scores_b = grad_scores.astype(jnp.bfloat16)
    grad_q = jnp.einsum('bgrqk,bkgh->bqgrh', scores_b, k_rot, preferred_element_type=jnp.float32)
    grad_k = jnp.einsum('bgrqk,bqgrh->bkgh', scores_b, q_rot, preferred_element_type=jnp.float32)
    return grad_q, grad_k, grad_v


def layer_fwd(x_emb, positions, weights):
    attn_norm, w_query, w_key, w_value, q_norm, k_norm, w_out, mlp_norm, w_gate, w_up, w_down = weights
    batch_len, seq_len, model_dim = x_emb.shape
    head_dim = q_norm.shape[0]
    kv_heads = w_key.shape[1] // head_dim
    q_per_kv = w_query.shape[1] // w_key.shape[1]
    cos_t, sin_t = rope_tables(positions, head_dim)
    cos_q = cos_t[:, :, None, None, :]
    sin_q = sin_t[:, :, None, None, :]
    cos_k = cos_t[:, :, None, :]
    sin_k = sin_t[:, :, None, :]
    normed1, norm1_inv = norm_fwd(x_emb)
    attn_in = (normed1 * attn_norm.astype(jnp.float32)).astype(jnp.bfloat16)
    q_raw = jnp.einsum('bsd,dn->bsn', attn_in, w_query, preferred_element_type=jnp.float32).astype(jnp.bfloat16).reshape(batch_len, seq_len, kv_heads, q_per_kv, head_dim)
    k_raw = jnp.einsum('bsd,dn->bsn', attn_in, w_key, preferred_element_type=jnp.float32).astype(jnp.bfloat16).reshape(batch_len, seq_len, kv_heads, head_dim)
    v_raw = jnp.einsum('bsd,dn->bsn', attn_in, w_value, preferred_element_type=jnp.float32).astype(jnp.bfloat16).reshape(batch_len, seq_len, kv_heads, head_dim)
    q_normed, q_inv = norm_fwd(q_raw)
    k_normed, k_inv = norm_fwd(k_raw)
    q_rot = rotate(q_normed * q_norm.astype(jnp.float32), cos_q, sin_q).astype(jnp.bfloat16)
    k_rot = rotate(k_normed * k_norm.astype(jnp.float32), cos_k, sin_k).astype(jnp.bfloat16)
    attn_heads, attn_probs = attn_fwd(q_rot, k_rot, v_raw)
    attn_flat = attn_heads.reshape(batch_len, seq_len, -1)
    attn_proj = jnp.einsum('bsn,nd->bsd', attn_flat, w_out, preferred_element_type=jnp.float32)
    hidden = (x_emb.astype(jnp.float32) + attn_proj).astype(jnp.bfloat16)
    normed2, norm2_inv = norm_fwd(hidden)
    mlp_in = (normed2 * mlp_norm.astype(jnp.float32)).astype(jnp.bfloat16)
    gate_pre = jnp.einsum('bsd,df->bsf', mlp_in, w_gate, preferred_element_type=jnp.float32)
    up_proj = jnp.einsum('bsd,df->bsf', mlp_in, w_up, preferred_element_type=jnp.float32)
    mlp_act = (jax.nn.silu(gate_pre) * up_proj).astype(jnp.bfloat16)
    mlp_proj = jnp.einsum('bsf,fd->bsd', mlp_act, w_down, preferred_element_type=jnp.float32)
    layer_out = (hidden.astype(jnp.float32) + mlp_proj).astype(jnp.bfloat16)
    saved_acts = (normed1, norm1_inv, attn_in, q_normed, q_inv, k_normed, k_inv, q_rot, k_rot, v_raw, attn_probs, attn_flat, normed2, norm2_inv, mlp_in, gate_pre, up_proj, mlp_act, cos_q, sin_q, cos_k, sin_k)
    return layer_out, saved_acts


def layer_bwd(dy_out, saved_acts, weights):
    attn_norm, w_query, w_key, w_value, q_norm, k_norm, w_out, mlp_norm, w_gate, w_up, w_down = weights
    (normed1, norm1_inv, attn_in, q_normed, q_inv, k_normed, k_inv, q_rot, k_rot, v_raw, attn_probs, attn_flat, normed2, norm2_inv, mlp_in, gate_pre, up_proj, mlp_act, cos_q, sin_q, cos_k, sin_k) = saved_acts
    batch_len, seq_len, model_dim = dy_out.shape
    grad_w_down = jnp.einsum('bsf,bsd->fd', mlp_act, dy_out, preferred_element_type=jnp.float32)
    grad_act = jnp.einsum('bsd,fd->bsf', dy_out, w_down, preferred_element_type=jnp.float32)
    gate_sig = jax.nn.sigmoid(gate_pre)
    grad_gate = (grad_act * up_proj * gate_sig * (1.0 + gate_pre * (1.0 - gate_sig))).astype(jnp.bfloat16)
    grad_up = (grad_act * gate_pre * gate_sig).astype(jnp.bfloat16)
    grad_w_gate = jnp.einsum('bsd,bsf->df', mlp_in, grad_gate, preferred_element_type=jnp.float32)
    grad_w_up = jnp.einsum('bsd,bsf->df', mlp_in, grad_up, preferred_element_type=jnp.float32)
    grad_mlp_in = jnp.einsum('bsf,df->bsd', grad_gate, w_gate, preferred_element_type=jnp.float32) + jnp.einsum('bsf,df->bsd', grad_up, w_up, preferred_element_type=jnp.float32)
    grad_mlp_norm = jnp.sum(grad_mlp_in * normed2, axis=(0, 1))
    grad_hidden = dy_out.astype(jnp.float32) + norm_bwd(grad_mlp_in, normed2, norm2_inv, mlp_norm)
    hidden_b = grad_hidden.astype(jnp.bfloat16)
    grad_w_out = jnp.einsum('bsn,bsd->nd', attn_flat, hidden_b, preferred_element_type=jnp.float32)
    grad_heads = jnp.einsum('bsd,nd->bsn', hidden_b, w_out, preferred_element_type=jnp.float32).reshape(q_rot.shape)
    grad_q, grad_k, grad_v = attn_bwd(grad_heads, q_rot, k_rot, v_raw, attn_probs)
    grad_qt = rotate(grad_q, cos_q, -sin_q)
    grad_kt = rotate(grad_k, cos_k, -sin_k)
    grad_q_norm = jnp.sum(grad_qt * q_normed, axis=(0, 1, 2, 3))
    grad_k_norm = jnp.sum(grad_kt * k_normed, axis=(0, 1, 2))
    grad_q_raw = norm_bwd(grad_qt, q_normed, q_inv, q_norm).astype(jnp.bfloat16).reshape(batch_len, seq_len, -1)
    grad_k_raw = norm_bwd(grad_kt, k_normed, k_inv, k_norm).astype(jnp.bfloat16).reshape(batch_len, seq_len, -1)
    grad_v_raw = grad_v.astype(jnp.bfloat16).reshape(batch_len, seq_len, -1)
    grad_w_query = jnp.einsum('bsd,bsn->dn', attn_in, grad_q_raw, preferred_element_type=jnp.float32)
    grad_w_key = jnp.einsum('bsd,bsn->dn', attn_in, grad_k_raw, preferred_element_type=jnp.float32)
    grad_w_value = jnp.einsum('bsd,bsn->dn', attn_in, grad_v_raw, preferred_element_type=jnp.float32)
    grad_attn_in = (jnp.einsum('bsn,dn->bsd', grad_q_raw, w_query, preferred_element_type=jnp.float32)
                    + jnp.einsum('bsn,dn->bsd', grad_k_raw, w_key, preferred_element_type=jnp.float32)
                    + jnp.einsum('bsn,dn->bsd', grad_v_raw, w_value, preferred_element_type=jnp.float32))
    grad_attn_norm = jnp.sum(grad_attn_in * normed1, axis=(0, 1))
    grad_x_emb = grad_hidden + norm_bwd(grad_attn_in, normed1, norm1_inv, attn_norm)
    return grad_x_emb, (grad_attn_norm, grad_w_query, grad_w_key, grad_w_value, grad_q_norm, grad_k_norm, grad_w_out, grad_mlp_norm, grad_w_gate, grad_w_up, grad_w_down)


def solution(mesh):
    row_spec = P(AXIS_NAME, None)
    vec_spec = P(AXIS_NAME)
    full_spec = P(None)
    batch_spec = P(AXIS_NAME, None, None)
    weight_specs = (vec_spec, row_spec, row_spec, row_spec, full_spec, full_spec, row_spec, vec_spec, row_spec, row_spec, row_spec)

    def device_step(tokens, positions, table_shard, attn_norm, w_query, w_key, w_value, q_norm, k_norm, w_out, mlp_norm, w_gate, w_up, w_down, dy_out):
        shards = (attn_norm, w_query, w_key, w_value, q_norm, k_norm, w_out, mlp_norm, w_gate, w_up, w_down)
        weights = tuple(lax.all_gather(w_shard, AXIS_NAME, tiled=True) if is_sharded else w_shard for w_shard, is_sharded in zip(shards, SHARDED))
        batch_len, seq_len = tokens.shape
        rows_local, model_dim = table_shard.shape
        all_ids = lax.all_gather(tokens.reshape(-1), AXIS_NAME, tiled=True)
        local_ids = all_ids - lax.axis_index(AXIS_NAME) * rows_local
        is_owner = (local_ids >= 0) & (local_ids < rows_local)
        picked = jnp.take(table_shard, jnp.clip(local_ids, 0, rows_local - 1), axis=0)
        picked = jnp.where(is_owner[:, None], picked, jnp.zeros((), picked.dtype))
        x_emb = lax.psum_scatter(picked, AXIS_NAME, scatter_dimension=0, tiled=True).reshape(batch_len, seq_len, model_dim)
        layer_out, saved_acts = layer_fwd(x_emb, positions, weights)
        grad_x_emb, grad_full = layer_bwd(dy_out, saved_acts, weights)
        grad_shards = tuple(lax.psum_scatter(grad_part, AXIS_NAME, scatter_dimension=0, tiled=True) if is_sharded else lax.psum(grad_part, AXIS_NAME) for grad_part, is_sharded in zip(grad_full, SHARDED))
        all_rows = lax.all_gather(grad_x_emb.reshape(-1, model_dim), AXIS_NAME, tiled=True)
        d_table = jax.ops.segment_sum(all_rows, jnp.where(is_owner, local_ids, rows_local), num_segments=rows_local)
        return (layer_out, d_table) + grad_shards

    return jax.shard_map(device_step, mesh=mesh, in_specs=(row_spec, row_spec, row_spec) + weight_specs + (batch_spec,), out_specs=(batch_spec, row_spec) + weight_specs, check_vma=False)
```

profile of v0, /device:TPU:0, one launch (start us, length us, event | category | flops | bytes accessed | tf_op | source)
XLA Modules:
  0.0 2061.4 jit_solution(14730035651845053786)
XLA Ops:
  10.0 43.5 %all-gather = s32[1,16384]{1,0:T(1,128)S(1)} all-gather(s32[1,512]{1,0:T(1,128)} %param.15), channel_id=2, replica_groups=mesh['fsdp'=32] {'fsdp'}, dimensions={1}, use_global_device_ids=true | all-gather | bytes 67584 | tf_op jit(solution)/shard_map/all_gather | solution.py:145
  54.2 80.4 %gather_fusion = bf16[16384,896]{1,0:T(8,128)(2,1)} fusion(bf16[4752,896]{1,0:T(8,128)(2,1)} %param.17, s32[16384]{0:T(1024)S(1)} %get-tuple-element.55), kind=kCustom, calls=%fused_computation | custom fusion | bytes 58785792 | tf_op jit(solution)/shard_map/jit(_take)/gather | solution.py:148
  134.7 20.1 select_select_fusion
  155.5 38.3 %all-gather.2 = bf16[32,28,128]{2,1,0:T(8,128)(2,1)S(1)} all-gather(bf16[1,28,128]{2,1,0:T(8,128)(2,1)S(1)} %bitcast.222), channel_id=1, replica_groups=mesh['fsdp'=32] {'fsdp'}, dimensions={0}, use_global_device_ids=true | all-gather | bytes 236544 | tf_op jit(solution)/shard_map/all_gather | solution.py:142
  194.9 37.0 %all-reduce.18 = (bf16[896]{0:T(1024)(128)(2,1)S(1)}, bf16[896]{0:T(1024)(128)(2,1)S(1)}) all-reduce(bf16[896]{0:T(1024)(128)(2,1)S(1)} %dynamic-update-slice, bf16[896]{0:T(1024)(128)(2,1)S(1)} %dynamic-update-slice.1), channel_id=1, replica_groups=mesh['fsdp'=32] {'fsdp'}, use_global_device_ids=true, to_apply=%add | all-reduce | flops 1792 | bytes 7168
  232.0 42.8 %all-gather.3 = bf16[32,28,128]{2,1,0:T(8,128)(2,1)S(1)} all-gather(bf16[1,28,128]{2,1,0:T(8,128)(2,1)S(1)} %bitcast.223), channel_id=1, replica_groups=mesh['fsdp'=32] {'fsdp'}, dimensions={0}, use_global_device_ids=true | all-gather | bytes 236544 | tf_op jit(solution)/shard_map/all_gather | solution.py:142
  277.2 3.7 reshape.793
  282.3 2.4 reshape.791
  284.7 13.4 reshape.795
  299.8 12.9 reshape.797
  312.7 299.0 %reduce-scatter.18.cloned.1.call-done = bf16[512,896]{1,0:T(8,128)(2,1)} async-done(((bf16[16384,896]{1,0:T(8,128)(2,1)}), bf16[512,896]{1,0:T(8,128)(2,1)}) %reduce-scatter.18.cloned.1.call-update) | async-done | bytes 917520 | tf_op jit(solution)/shard_map/reduce_scatter | solution.py:150
  613.1 3.7 fusion.51
  621.4 6.7 fusion.14
  628.1 8.2 fusion.13
  636.4 7.9 fusion.48
  645.8 8.1 fusion.90
  654.0 8.0 fusion.88
  661.9 38.3 %all-gather.15.cloned.1.call-done = bf16[4864,896]{1,0:T(8,128)(2,1)} async-done(((bf16[152,896]{1,0:T(8,128)(2,1)}), bf16[4864,896]{1,0:T(8,128)(2,1)}) %all-gather.15.cloned.1.call-update) | async-done | bytes 8716304 | tf_op jit(solution)/shard_map/all_gather | solution.py:142
  700.3 17.8 multiply_convert_fusion
  718.0 12.2 fusion.102
  730.3 11.7 fusion.45
  742.0 2.5 fusion.44
  744.5 2.1 convolution_convert_fusion
  746.7 6.1 fusion.57
  752.8 8.1 fusion.8
  760.9 8.2 fusion.16
  770.5 2.3 convolution_bitcast_fusion.1
  775.3 2.8 copy.49
  781.9 4.3 multiply_reduce_fusion
  791.9 11.5 fusion.63
  807.9 2.8 fusion.61
  810.7 11.4 fusion.86
  822.1 8.8 fusion.84
  831.0 760.4 %fusion.101 = (f32[32,896]{1,0:T(8,128)S(1)}, f32[32,128]{1,0:T(8,128)S(1)}, f32[32,128]{1,0:T(8,128)S(1)}, f32[32,896]{1,0:T(8,128)S(1)}, f32[32,4864]{1,0:T(8,128)}, /*index=5*/f32[32,4864]{1,0:T(8,128)}) fusion(f32[896,896]{1,0:T(8,128)S(1)} %fusion.96, f32[896,128]{1,0:T(8,128)} %fusion.94, f32[896,128]{1,0:T(8,128)} %fusion.92, ...), kind=kCustom, calls=%all-reduce-scatter.6 | all-reduce-scatter fusion | flops 12058625 | bytes 43712512
  1591.3 42.6 %collective-permute-start.18 = (f32[32,4864]{1,0:T(8,128)}, f32[32,4864]{1,0:T(8,128)S(1)}, u32[]{:S(2)}, u32[]{:S(2)}) collective-permute-start(f32[32,4864]{1,0:T(8,128)} %get-tuple-element.33), channel_id=1, source_target_pairs={{0,3},{1,4},{2,5},{3,6},{4,7},{5,8},{6,9},{7,10},{8,11},{9,12},{10... | collective-permute-start | bytes 1867784
  1634.0 22.6 %collective-permute-start.17 = (f32[32,4864]{1,0:T(8,128)}, f32[32,4864]{1,0:T(8,128)S(1)}, u32[]{:S(2)}, u32[]{:S(2)}) collective-permute-start(f32[32,4864]{1,0:T(8,128)} %get-tuple-element.33), channel_id=1, source_target_pairs={{0,2},{1,3},{2,4},{3,5},{4,6},{5,7},{6,8},{7,9},{8,10},{9,11},{10,... | collective-permute-start | bytes 1867784
  1657.7 3.2 collective-permute-start.19
  1660.9 5.3 collective-permute-start.7
  1666.3 3.2 collective-permute-start.11
  1669.5 33.3 %collective-permute-done.7 = f32[28,128]{1,0:T(8,128)S(1)} collective-permute-done((f32[28,128]{1,0:T(8,128)S(1)}, f32[28,128]{1,0:T(8,128)S(1)}, u32[]{:S(2)}, u32[]{:S(2)}) %collective-permute-start.7) | collective-permute-done | bytes 14368
  1704.1 5.9 collective-permute-start.5
  1710.1 12.7 collective-permute-start.4
  1722.8 3.3 collective-permute-start.10
  1726.1 5.0 collective-permute-start.9
  1732.5 5.4 collective-permute-start.3
  1737.9 4.6 collective-permute-start.15
  1744.9 3.6 collective-permute-start.1
  1748.5 2.2 collective-permute-start
  1750.9 5.4 collective-permute-start.14
  1756.3 5.5 collective-permute-start.13
  1764.4 2.0 slice.47
  1766.3 4.3 collective-permute-start.16
  1770.7 3.7 collective-permute-start.22
  1774.4 4.9 collective-permute-start.21
  1779.2 2.6 collective-permute-start.20
  1781.8 2.1 collective-permute-start.23
  1783.9 10.7 fusion.52
  1794.8 63.6 %all-reduce.17 = (f32[896]{0:T(1024)S(1)}, f32[64]{0:T(128)}, f32[64]{0:T(128)}, f32[896]{0:T(1024)S(1)}) all-reduce(f32[896]{0:T(1024)S(1)} %get-tuple-element.15, f32[64]{0:T(128)S(1)} %reduce_sum.153, f32[64]{0:T(128)S(1)} %reduce_sum.156, f32[896]{0:T(1024)S(1)} %copy-done.56), channel_id=5, replica_groups=mesh['fsdp'=32] {'fsdp'}, use_global_device_ids=true, to_apply=%region_14.15.clone | all-reduce | flops 1920 | bytes 15360
  1862.6 4.0 concatenate.69
  1867.9 19.2 concatenate.70
  1887.2 20.2 concatenate.71
  1907.4 2.0 constant_dynamic-slice_fusion.1
  1909.4 2.0 constant_dynamic-slice_fusion
  1911.4 142.7 %scatter_custom_fusion = f32[4752,896]{1,0:T(8,128)} fusion(s32[16384]{0:T(1024)} %get-tuple-element.54, f32[1,16384,896]{2,1,0:T(8,128)} %all-gather.17.cloned.1.call-done, f32[]{:T(128)} %constant.22.clone.1), kind=kCustom, calls=%fused_computation.2 | custom fusion | flops 14680064 | bytes 75751936 | tf_op jit(solution)/shard_map/scatter-add | solution.py:155
  (289 shorter events, 50.2 us)
Async XLA Ops:
  7.2 270.0 %all-gather.21.cloned.1.call-start = ((), (), s32[]{:S(2)}) async-start(), calls=%async_computation.6 | async-start | bytes 1892352 | tf_op jit(solution)/shard_map/all_gather | solution.py:142
  7.9 274.4 %all-gather.19.cloned.1.call-start = ((), (), s32[]{:S(2)}) async-start(), calls=%async_computation.5 | async-start | bytes 1892352 | tf_op jit(solution)/shard_map/all_gather | solution.py:142
  8.7 276.1 %all-gather.23.cloned.1.call-start = ((), (), s32[]{:S(2)}) async-start(), calls=%async_computation.7 | async-start | bytes 10272768 | tf_op jit(solution)/shard_map/all_gather | solution.py:142
  9.4 290.4 %all-gather.25.cloned.1.call-start = ((), (), s32[]{:S(2)}) async-start(), calls=%async_computation.8 | async-start | bytes 10272768 | tf_op jit(solution)/shard_map/all_gather | solution.py:142
  10.0 601.7 %reduce-scatter.18.cloned.1.call-start = ((), (), s32[]{:S(2)}) async-start(), calls=%async_computation.2 | async-start | bytes 30277632 | tf_op jit(solution)/shard_map/reduce_scatter | solution.py:150
  154.7 39.8 %copy-start.62 = (bf16[28]{0:T(256)(128)(2,1)S(1)}, bf16[28]{0:T(256)(128)(2,1)}, u32[]{:S(2)}) copy-start(bf16[28]{0:T(256)(128)(2,1)} %param.18) | copy-start | bytes 172
  154.8 40.0 %copy-start.63 = (bf16[28]{0:T(256)(128)(2,1)S(1)}, bf16[28]{0:T(256)(128)(2,1)}, u32[]{:S(2)}) copy-start(bf16[28]{0:T(256)(128)(2,1)} %param.25) | copy-start | bytes 172
  154.8 77.2 %copy-start.60 = (bf16[64]{0:T(256)(128)(2,1)S(1)}, bf16[64]{0:T(256)(128)(2,1)}, u32[]{:S(2)}) copy-start(bf16[64]{0:T(256)(128)(2,1)} %param.22) | copy-start | bytes 388
  154.8 77.2 %copy-start.57 = (s32[1,512]{1,0:T(1,128)S(1)}, s32[1,512]{1,0:T(1,128)}, u32[]{:S(2)}) copy-start(s32[1,512]{1,0:T(1,128)} %param.16) | copy-start | bytes 6148
  154.8 77.2 %copy-start.64 = (bf16[64]{0:T(256)(128)(2,1)S(1)}, bf16[64]{0:T(256)(128)(2,1)}, u32[]{:S(2)}) copy-start(bf16[64]{0:T(256)(128)(2,1)} %param.23) | copy-start | bytes 388
  154.8 77.2 %copy-start.55 = (bf16[28,128]{1,0:T(8,128)(2,1)S(1)}, bf16[28,128]{1,0:T(8,128)(2,1)}, u32[]{:S(2)}) copy-start(bf16[28,128]{1,0:T(8,128)(2,1)} %param.20) | copy-start | bytes 21508
  154.8 545.4 %all-gather.15.cloned.1.call-start = ((), (), s32[]{:S(2)}) async-start(), calls=%async_computation.3 | async-start | bytes 8988672 | tf_op jit(solution)/shard_map/all_gather | solution.py:142
  155.4 1756.0 %all-gather.17.cloned.1.call-start = ((), (), s32[]{:S(2)}) async-start(), calls=%async_computation.4 | async-start | bytes 60555264 | tf_op jit(solution)/shard_map/all_gather | solution.py:154
  232.0 387.9 %copy-start.39 = (f32[896]{0:T(1024)}, f32[896]{0:T(1024)S(1)}, u32[]{:S(2)}) copy-start(f32[896]{0:T(1024)S(1)} %convert_element_type.195) | copy-start | bytes 10756
  232.0 387.7 %copy-start.58 = (f32[64]{0:T(128)}, f32[64]{0:T(128)S(1)}, u32[]{:S(2)}) copy-start(f32[64]{0:T(128)S(1)} %convert_element_type.201) | copy-start | bytes 772
  274.9 343.9 %copy-start.21 = (bf16[896,128]{1,0:T(8,128)(2,1)}, bf16[896,128]{1,0:T(8,128)(2,1)S(1)}, u32[]{:S(2)}) copy-start(bf16[896,128]{1,0:T(8,128)(2,1)S(1)} %reshape.789) | copy-start | bytes 688132
  277.2 342.6 %copy-start.29 = (f32[512,32]{0,1:T(8,128)}, f32[512,32]{0,1:T(8,128)S(1)}, u32[]{:S(2)}) copy-start(f32[512,32]{0,1:T(8,128)S(1)} %get-tuple-element.59) | copy-start | bytes 196612
  284.7 328.4 %copy-start.17 = (bf16[896,896]{1,0:T(8,128)(2,1)}, bf16[896,896]{1,0:T(8,128)(2,1)S(1)}, u32[]{:S(2)}) copy-start(bf16[896,896]{1,0:T(8,128)(2,1)S(1)} %reshape.791) | copy-start | bytes 4816900
  620.6 15.7 copy-start.65
  628.1 8.2 copy-start.42
  628.1 17.7 slice-start.4
  636.4 9.4 slice-start.5
  636.4 9.4 slice-start.6
  644.4 9.6 slice-start.7
  645.8 8.2 copy-start.5
  718.0 12.2 copy-start.6
  730.2 16.4 slice-start
  730.2 16.4 slice-start.1
  730.3 16.3 slice-start.2
  760.9 8.2 copy-start.36
  760.9 8.2 copy-start.38
  791.9 1262.2 %reduce-scatter.20.cloned.1.call-start = ((), (), s32[]{:S(2)}) async-start(), calls=%async_computation.9 | async-start | bytes 17977344
  807.9 14.2 slice-start.10
  810.7 11.4 slice-start.11
  1591.3 187.9 %collective-permute-start.18 = (f32[32,4864]{1,0:T(8,128)}, f32[32,4864]{1,0:T(8,128)S(1)}, u32[]{:S(2)}, u32[]{:S(2)}) collective-permute-start(f32[32,4864]{1,0:T(8,128)} %get-tuple-element.33), channel_id=1, source_target_pairs={{0,3},{1,4},{2,5},{3,6},{4,7},{5,8},{6,9},{7,10},{8,11},{9,12},{10... | collective-permute-start | bytes 1867784
  1634.0 147.8 %collective-permute-start.17 = (f32[32,4864]{1,0:T(8,128)}, f32[32,4864]{1,0:T(8,128)S(1)}, u32[]{:S(2)}, u32[]{:S(2)}) collective-permute-start(f32[32,4864]{1,0:T(8,128)} %get-tuple-element.33), channel_id=1, source_target_pairs={{0,2},{1,3},{2,4},{3,5},{4,6},{5,7},{6,8},{7,9},{8,10},{9,11},{10,... | collective-permute-start | bytes 1867784
  1657.7 116.7 %collective-permute-start.19 = (f32[28,4864]{1,0:T(8,128)S(1)}, f32[28,4864]{1,0:T(8,128)S(1)}, u32[]{:S(2)}, u32[]{:S(2)}) collective-permute-start(f32[28,4864]{1,0:T(8,128)S(1)} %slice.46), channel_id=1, source_target_pairs={{0,4},{1,5},{2,6},{3,7},{4,8},{5,9},{6,10},{7,11},{8,12},{9,13},{1... | collective-permute-start | bytes 1634312
  1660.9 41.9 %collective-permute-start.7 = (f32[28,128]{1,0:T(8,128)S(1)}, f32[28,128]{1,0:T(8,128)S(1)}, u32[]{:S(2)}, u32[]{:S(2)}) collective-permute-start(f32[28,128]{1,0:T(8,128)S(1)} %slice.43), channel_id=1, source_target_pairs={{0,4},{1,5},{2,6},{3,7},{4,8},{5,9},{6,10},{7,11},{8,12},{9,13},{1... | collective-permute-start | bytes 43016
  1666.3 37.9 %collective-permute-start.11 = (f32[28,128]{1,0:T(8,128)S(1)}, f32[28,128]{1,0:T(8,128)S(1)}, u32[]{:S(2)}, u32[]{:S(2)}) collective-permute-start(f32[28,128]{1,0:T(8,128)S(1)} %slice.44), channel_id=1, source_target_pairs={{0,4},{1,5},{2,6},{3,7},{4,8},{5,9},{6,10},{7,11},{8,12},{9,13},{1... | collective-permute-start | bytes 43016
  1702.8 7.2 collective-permute-start.6
  1704.1 18.7 collective-permute-start.5
  1710.1 16.0 collective-permute-start.4
  1722.8 8.3 collective-permute-start.10
  1726.1 6.5 collective-permute-start.9
  1731.1 6.8 collective-permute-start.8
  1732.5 10.0 collective-permute-start.3
  1737.9 7.0 collective-permute-start.15
  1742.6 6.0 collective-permute-start.2
  1744.9 49.7 %copy-start.46 = (f32[28,896]{1,0:T(8,128)}, f32[28,896]{1,0:T(8,128)S(1)}, u32[]{:S(2)}) copy-start(f32[28,896]{1,0:T(8,128)S(1)} %collective-permute-done.15) | copy-start | bytes 301060
  1744.9 6.0 collective-permute-start.1
  1748.5 7.7 collective-permute-start
  1750.9 10.9 collective-permute-start.14
  1756.3 10.1 collective-permute-start.13
  1762.4 8.2 collective-permute-start.12
  1766.3 28.3 %copy-start.52 = (f32[896]{0:T(1024)S(1)}, f32[896]{0:T(1024)}, u32[]{:S(2)}) copy-start(f32[896]{0:T(1024)} %get-tuple-element.38) | copy-start | bytes 10756
  1766.3 28.5 %copy-start.56 = (f32[896]{0:T(1024)S(1)}, f32[896]{0:T(1024)}, u32[]{:S(2)}) copy-start(f32[896]{0:T(1024)} %get-tuple-element.13) | copy-start | bytes 10756
  1766.3 101.6 %collective-permute-start.16 = (f32[32,4864]{1,0:T(8,128)}, f32[32,4864]{1,0:T(8,128)}, u32[]{:S(2)}, u32[]{:S(2)}) collective-permute-start(f32[32,4864]{1,0:T(8,128)} %get-tuple-element.33), channel_id=1, source_target_pairs={{0,1},{1,2},{2,3},{3,4},{4,5},{5,6},{6,7},{7,8},{8,9},{9,10},{10,1... | collective-permute-start | bytes 1867784
  1770.7 116.5 %collective-permute-start.22 = (f32[32,4864]{1,0:T(8,128)}, f32[32,4864]{1,0:T(8,128)}, u32[]{:S(2)}, u32[]{:S(2)}) collective-permute-start(f32[32,4864]{1,0:T(8,128)} %get-tuple-element.34), channel_id=1, source_target_pairs={{0,3},{1,4},{2,5},{3,6},{4,7},{5,8},{6,9},{7,10},{8,11},{9,12},{10... | collective-permute-start | bytes 1867784
  1774.4 20.2 copy-start.28
  1774.4 112.8 %collective-permute-start.21 = (f32[32,4864]{1,0:T(8,128)}, f32[32,4864]{1,0:T(8,128)}, u32[]{:S(2)}, u32[]{:S(2)}) collective-permute-start(f32[32,4864]{1,0:T(8,128)} %get-tuple-element.34), channel_id=1, source_target_pairs={{0,2},{1,3},{2,4},{3,5},{4,6},{5,7},{6,8},{7,9},{8,10},{9,11},{10,... | collective-permute-start | bytes 1867784
  1779.2 107.9 %collective-permute-start.20 = (f32[32,4864]{1,0:T(8,128)}, f32[32,4864]{1,0:T(8,128)}, u32[]{:S(2)}, u32[]{:S(2)}) collective-permute-start(f32[32,4864]{1,0:T(8,128)} %get-tuple-element.34), channel_id=1, source_target_pairs={{0,1},{1,2},{2,3},{3,4},{4,5},{5,6},{6,7},{7,8},{8,9},{9,10},{10,1... | collective-permute-start | bytes 1867784
  1781.8 105.3 %collective-permute-start.23 = (f32[28,4864]{1,0:T(8,128)}, f32[28,4864]{1,0:T(8,128)}, u32[]{:S(2)}, u32[]{:S(2)}) collective-permute-start(f32[28,4864]{1,0:T(8,128)} %slice.47), channel_id=1, source_target_pairs={{0,4},{1,5},{2,6},{3,7},{4,8},{5,9},{6,10},{7,11},{8,12},{9,13},{1... | collective-permute-start | bytes 1634312
  1794.6 73.3 %copy-start.10 = (f32[32,4864]{1,0:T(8,128)S(1)}, f32[32,4864]{1,0:T(8,128)}, u32[]{:S(2)}) copy-start(f32[32,4864]{1,0:T(8,128)} %get-tuple-element.33) | copy-start | bytes 1867780
  1867.3 19.9 copy-start.9
  (48 other events, 127.2 us)
Sparse Core Ops, SparseCore 0:
  10.8 58.2 all-gather.20
  71.9 54.4 all-gather.18
  129.3 83.5 all-gather.22
  215.6 84.1 all-gather.24
  301.9 309.7 reduce-scatter.17
  614.4 85.7 all-gather.14
  792.0 548.3 all-gather.16
  1343.3 358.0 reduce-scatter.19
where the time goes:
time: 2070 us; the launch traced here: 2060 us
  blocking collectives  986 us (48%)
  waiting for transfers between devices  377 us (18%)
  other arithmetic  195 us (9%)
  local copies, waits for them, and re-layouts  184 us (9%)
  starting transfers between devices  154 us (7%)
  matrix products  150 us (7%)
    unnamed x3, blocking collectives  861 us
    reduce_scatter x1, waiting for transfers between devices, device_step(): lax.psum_scatter(picked, AXIS_NAME, scatter_dimension=0, tiled=True)  299 us
    unnamed x25, starting transfers between devices  154 us
    scatter-add x1, other arithmetic, device_step(): jax.ops.segment_sum(all_rows, jnp.where(is_owner, local_ids, rows_local),...  143 us
    unnamed x190, local copies, waits for them, and re-layouts  92.4 us
    all_gather x2, blocking collectives, device_step(): lax.all_gather(w_shard, AXIS_NAME, tiled=True)  81.1 us
    gather x1, local copies, waits for them, and re-layouts, device_step(): jnp.take(table_shard, jnp.clip(local_ids, 0, rows_local - 1), axis=0)  80.4 us
    all_gather x1, blocking collectives, device_step(): all_ids = lax.all_gather(tokens.reshape(-1), AXIS_NAME, tiled=True)  43.5 us
  transfers between devices with their start and end apart: 32, of which 7 were waited for; matrix products, arithmetic and copies ran while one was open for 58% of the time, Pallas kernels for 0%

commit v1 on v0

v1 whole, which is shorter than its diff:
```python
import math
import jax
import jax.numpy as jnp
from jax import lax
from jax.sharding import PartitionSpec as P

NORM_EPS = 1e-6
ROPE_THETA = 1.0e6
AXIS_NAME = 'fsdp'
F32 = jnp.float32
BF16 = jnp.bfloat16


def rope_tables(positions, head_dim):
    half_dim = head_dim // 2
    inv_freq = jnp.exp(jnp.arange(half_dim, dtype=jnp.float32) * (-2.0 * math.log(ROPE_THETA) / head_dim))
    angles = positions.astype(jnp.float32)[:, :, None] * inv_freq
    return jnp.cos(angles), jnp.sin(angles)


def rotate(values, cos_t, sin_t):
    half_dim = values.shape[-1] // 2
    lead_half = values[..., :half_dim]
    tail_half = values[..., half_dim:]
    return jnp.concatenate([lead_half * cos_t - tail_half * sin_t, tail_half * cos_t + lead_half * sin_t], axis=-1)


def norm_fwd(values):
    values_f = values.astype(jnp.float32)
    inv_rms = lax.rsqrt(jnp.mean(values_f * values_f, axis=-1, keepdims=True) + NORM_EPS)
    return values_f * inv_rms, inv_rms


def norm_bwd(grad_out, normed, inv_rms, norm_gain):
    grad_normed = grad_out * norm_gain.astype(jnp.float32)
    mean_term = jnp.mean(grad_normed * normed, axis=-1, keepdims=True)
    return inv_rms * (grad_normed - normed * mean_term)


def attn_fwd(q_rot, k_rot, v_raw):
    seq_len = q_rot.shape[1]
    attn_scale = q_rot.shape[-1] ** -0.5
    scores = jnp.einsum('bqgrh,bkgh->bgrqk', q_rot, k_rot, preferred_element_type=jnp.float32) * attn_scale
    causal = lax.broadcasted_iota(jnp.int32, (seq_len, seq_len), 0) >= lax.broadcasted_iota(jnp.int32, (seq_len, seq_len), 1)
    attn_probs = jax.nn.softmax(jnp.where(causal, scores, -1e30), axis=-1)
    attn_heads = jnp.einsum('bgrqk,bkgh->bqgrh', attn_probs.astype(jnp.bfloat16), v_raw, preferred_element_type=jnp.float32)
    return attn_heads.astype(jnp.bfloat16), attn_probs


def attn_bwd(grad_out, q_rot, k_rot, v_raw, attn_probs):
    attn_scale = q_rot.shape[-1] ** -0.5
    grad_b = grad_out.astype(jnp.bfloat16)
    probs_b = attn_probs.astype(jnp.bfloat16)
    grad_probs = jnp.einsum('bqgrh,bkgh->bgrqk', grad_b, v_raw, preferred_element_type=jnp.float32)
    grad_v = jnp.einsum('bgrqk,bqgrh->bkgh', probs_b, grad_b, preferred_element_type=jnp.float32)
    grad_scores = attn_probs * (grad_probs - jnp.sum(grad_probs * attn_probs, axis=-1, keepdims=True)) * attn_scale
    scores_b = grad_scores.astype(jnp.bfloat16)
    grad_q = jnp.einsum('bgrqk,bkgh->bqgrh', scores_b, k_rot, preferred_element_type=jnp.float32)
    grad_k = jnp.einsum('bgrqk,bqgrh->bkgh', scores_b, q_rot, preferred_element_type=jnp.float32)
    return grad_q, grad_k, grad_v


def dot(a, b, ca, cb):
    return lax.dot_general(a, b, (((ca,), (cb,)), ((), ())), preferred_element_type=F32)


def solution(mesh):
    n_dev = mesh.shape[AXIS_NAME]
    n_chip = n_dev // 2
    pair = [(i, i ^ 1) for i in range(n_dev)]
    groups = [[2 * k + c for k in range(n_chip)] for c in range(2)]
    to_use = [(d, 2 * (d % n_chip) + d // n_chip) for d in range(n_dev)]
    to_store = [(b, a) for a, b in to_use]

    row_spec = P(AXIS_NAME, None)
    vec_spec = P(AXIS_NAME)
    full_spec = P(None)
    batch_spec = P(AXIS_NAME, None, None)
    weight_specs = (vec_spec, row_spec, row_spec, row_spec, full_spec, full_spec, row_spec, vec_spec, row_spec, row_spec, row_spec)

    def swap(v):
        return lax.ppermute(v, AXIS_NAME, pair)

    def gather_group(v):
        return lax.all_gather(v, AXIS_NAME, axis_index_groups=groups, tiled=True)

    def scatter_group(v):
        return lax.psum_scatter(v, AXIS_NAME, scatter_dimension=0, axis_index_groups=groups, tiled=True)

    def device_step(tokens, positions, table_shard, attn_norm, w_query, w_key, w_value, q_norm, k_norm, w_out, mlp_norm, w_gate, w_up, w_down, dy_out):
        me = lax.axis_index(AXIS_NAME)
        core = lax.rem(me, 2)
        seq_len = tokens.shape[1]
        rows_local, model_dim = table_shard.shape
        rows_w, ff = w_gate.shape
        half = ff // 2
        nq, nk = w_query.shape[1], w_key.shape[1]
        head_dim = q_norm.shape[0]
        kv_heads = nk // head_dim
        q_per_kv = nq // nk

        gains = jnp.pad(jnp.stack([attn_norm, mlp_norm], axis=1), ((0, 0), (0, 126)))
        attn_pack = jnp.concatenate([w_query, w_out, w_key, w_value, gains], axis=1)
        attn_full = lax.all_gather(attn_pack, AXIS_NAME, tiled=True)
        mine_gu = jnp.concatenate([lax.dynamic_slice(w_gate, (0, core * half), (rows_w, half)), lax.dynamic_slice(w_up, (0, core * half), (rows_w, half))], axis=1)
        other_gu = jnp.concatenate([lax.dynamic_slice(w_gate, (0, (1 - core) * half), (rows_w, half)), lax.dynamic_slice(w_up, (0, (1 - core) * half), (rows_w, half))], axis=1)
        recv_gu = swap(other_gu)
        block_gu = jnp.where(core == 0, jnp.concatenate([mine_gu, recv_gu], axis=0), jnp.concatenate([recv_gu, mine_gu], axis=0))
        wgu = gather_group(block_gu)
        wd = gather_group(lax.ppermute(w_down, AXIS_NAME, to_use))
        w_g, w_u = wgu[:, :half], wgu[:, half:]

        all_ids = lax.all_gather(tokens.reshape(-1), AXIS_NAME, tiled=True)
        local_ids = all_ids - me * rows_local
        is_owner = (local_ids >= 0) & (local_ids < rows_local)
        picked = jnp.take(table_shard, jnp.clip(local_ids, 0, rows_local - 1), axis=0)
        picked = jnp.where(is_owner[:, None], picked, jnp.zeros((), picked.dtype)).reshape(n_chip, 2, seq_len, model_dim)
        keep = lax.dynamic_slice(picked, (0, core, 0, 0), (n_chip, 1, seq_len, model_dim)).reshape(-1, model_dim)
        give = lax.dynamic_slice(picked, (0, 1 - core, 0, 0), (n_chip, 1, seq_len, model_dim)).reshape(-1, model_dim)
        x_emb = scatter_group(keep + swap(give))

        dy = dy_out.reshape(seq_len, model_dim)
        dy2 = jnp.concatenate([dy, swap(dy)], axis=0)

        wq = attn_full[:, :nq]
        wo = attn_full[:, nq:2 * nq]
        wk = attn_full[:, 2 * nq:2 * nq + nk]
        wv = attn_full[:, 2 * nq + nk:2 * nq + 2 * nk]
        g_attn = attn_full[:, 2 * nq + 2 * nk]
        g_mlp = attn_full[:, 2 * nq + 2 * nk + 1]

        cos_t, sin_t = rope_tables(positions, head_dim)
        cos_q, sin_q = cos_t[:, :, None, None, :], sin_t[:, :, None, None, :]
        cos_k, sin_k = cos_t[:, :, None, :], sin_t[:, :, None, :]
        normed1, norm1_inv = norm_fwd(x_emb)
        attn_in = (normed1 * g_attn.astype(F32)).astype(BF16)
        q_raw = dot(attn_in, wq, 1, 0).astype(BF16).reshape(1, seq_len, kv_heads, q_per_kv, head_dim)
        k_raw = dot(attn_in, wk, 1, 0).astype(BF16).reshape(1, seq_len, kv_heads, head_dim)
        v_raw = dot(attn_in, wv, 1, 0).astype(BF16).reshape(1, seq_len, kv_heads, head_dim)
        q_normed, q_inv = norm_fwd(q_raw)
        k_normed, k_inv = norm_fwd(k_raw)
        q_rot = rotate(q_normed * q_norm.astype(F32), cos_q, sin_q).astype(BF16)
        k_rot = rotate(k_normed * k_norm.astype(F32), cos_k, sin_k).astype(BF16)
        attn_heads, attn_probs = attn_fwd(q_rot, k_rot, v_raw)
        attn_flat = attn_heads.reshape(seq_len, nq)
        hidden = (x_emb.astype(F32) + dot(attn_flat, wo, 1, 0)).astype(BF16)
        normed2, norm2_inv = norm_fwd(hidden)
        mlp_in = (normed2 * g_mlp.astype(F32)).astype(BF16)

        mlp2 = jnp.concatenate([mlp_in, swap(mlp_in)], axis=0)
        gate_pre = dot(mlp2, w_g, 1, 0)
        up_proj = dot(mlp2, w_u, 1, 0)
        gate_sig = jax.nn.sigmoid(gate_pre)
        mlp_act = (gate_pre * gate_sig * up_proj).astype(BF16)
        grad_w_down = dot(mlp_act, dy2, 0, 0)
        down_shard = lax.ppermute(scatter_group(grad_w_down), AXIS_NAME, to_store)
        grad_act = dot(dy2, wd, 1, 1)
        grad_gate = (grad_act * up_proj * gate_sig * (1.0 + gate_pre * (1.0 - gate_sig))).astype(BF16)
        grad_up = (grad_act * gate_pre * gate_sig).astype(BF16)
        part_in = dot(grad_gate, w_g, 1, 1) + dot(grad_up, w_u, 1, 1)
        grad_mlp_in = part_in[:seq_len] + swap(part_in[seq_len:])
        gate_shard = scatter_group(dot(mlp2, grad_gate, 0, 0))
        up_shard = scatter_group(dot(mlp2, grad_up, 0, 0))
        part_y = dot(mlp_act, wd, 1, 0)
        layer_out = (hidden.astype(F32) + (part_y[:seq_len] + swap(part_y[seq_len:]))).astype(BF16)

        grad_mlp_norm = jnp.sum(grad_mlp_in * normed2, axis=0)
        grad_hidden = dy.astype(F32) + norm_bwd(grad_mlp_in, normed2, norm2_inv, g_mlp)
        hidden_b = grad_hidden.astype(BF16)
        grad_w_out = dot(attn_flat, hidden_b, 0, 0)
        grad_heads = dot(hidden_b, wo, 1, 1).reshape(q_rot.shape)
        grad_q, grad_k, grad_v = attn_bwd(grad_heads, q_rot, k_rot, v_raw, attn_probs)
        grad_qt = rotate(grad_q, cos_q, -sin_q)
        grad_kt = rotate(grad_k, cos_k, -sin_k)
        grad_q_norm = jnp.sum(grad_qt * q_normed, axis=(0, 1, 2, 3))
        grad_k_norm = jnp.sum(grad_kt * k_normed, axis=(0, 1, 2))
        grad_q_raw = norm_bwd(grad_qt, q_normed, q_inv, q_norm).astype(BF16).reshape(seq_len, nq)
        grad_k_raw = norm_bwd(grad_kt, k_normed, k_inv, k_norm).astype(BF16).reshape(seq_len, nk)
        grad_v_raw = grad_v.astype(BF16).reshape(seq_len, nk)
        grad_attn_in = dot(grad_q_raw, wq, 1, 1) + dot(grad_k_raw, wk, 1, 1) + dot(grad_v_raw, wv, 1, 1)
        grad_attn_norm = jnp.sum(grad_attn_in * normed1, axis=0)
        grad_x_emb = grad_hidden + norm_bwd(grad_attn_in, normed1, norm1_inv, g_attn)

        my_rows = gather_group(grad_x_emb)
        other_rows = swap(my_rows)
        seg = jnp.where(is_owner, local_ids, rows_local).reshape(n_chip, 2, seq_len)
        seg_mine = lax.dynamic_slice(seg, (0, core, 0), (n_chip, 1, seq_len)).reshape(-1)
        seg_other = lax.dynamic_slice(seg, (0, 1 - core, 0), (n_chip, 1, seq_len)).reshape(-1)
        d_table = jax.ops.segment_sum(jnp.concatenate([my_rows, other_rows], axis=0), jnp.concatenate([seg_mine, seg_other]), num_segments=rows_local)

        grad_w_query = dot(attn_in, grad_q_raw, 0, 0)
        grad_w_key = dot(attn_in, grad_k_raw, 0, 0)
        grad_w_value = dot(attn_in, grad_v_raw, 0, 0)
        vecs = jnp.pad(jnp.stack([grad_attn_norm, grad_mlp_norm], axis=1), ((0, 0), (0, 126)))
        zeros = jnp.zeros_like(vecs)
        pack0 = jnp.concatenate([grad_w_query, grad_w_key, vecs], axis=1)
        pack1 = jnp.concatenate([grad_w_out, grad_w_value, zeros], axis=1)
        keep_pack = jnp.where(core == 0, pack0, pack1)
        give_pack = jnp.where(core == 0, pack1, pack0)
        attn_shard = scatter_group(keep_pack + swap(give_pack))

        chip_rows = jnp.concatenate([gate_shard, up_shard, attn_shard], axis=1)
        mine = lax.dynamic_slice(chip_rows, (core * rows_w, 0), (rows_w, chip_rows.shape[1]))
        recv = swap(lax.dynamic_slice(chip_rows, ((1 - core) * rows_w, 0), (rows_w, chip_rows.shape[1])))
        low = jnp.where(core == 0, mine, recv)
        high = jnp.where(core == 0, recv, mine)
        d_gate = jnp.concatenate([low[:, :half], high[:, :half]], axis=1)
        d_up = jnp.concatenate([low[:, half:ff], high[:, half:ff]], axis=1)
        d_query, d_key = low[:, ff:ff + nq], low[:, ff + nq:ff + nq + nk]
        d_attn_norm, d_mlp_norm = low[:, ff + nq + nk], low[:, ff + nq + nk + 1]
        d_out, d_value = high[:, ff:ff + nq], high[:, ff + nq:ff + nq + nk]
        qk = lax.psum(jnp.concatenate([grad_q_norm, grad_k_norm]), AXIS_NAME)
        return (layer_out.reshape(1, seq_len, model_dim), d_table, d_attn_norm, d_query, d_key, d_value, qk[:head_dim], qk[head_dim:], d_out, d_mlp_norm, d_gate, d_up, down_shard)

    return jax.shard_map(device_step, mesh=mesh, in_specs=(row_spec, row_spec, row_spec) + weight_specs + (batch_spec,), out_specs=(batch_spec, row_spec) + weight_specs, check_vma=False)
```

time: 2070 us -> 1990 us (0.961)
  waiting for transfers between devices: 377 us -> 1300 us
  blocking collectives: 986 us -> 97.3 us
  starting transfers between devices: 154 us -> 37.7 us
  local copies, waits for them, and re-layouts: 184 us -> 147 us
  other arithmetic: 195 us -> 231 us
    unnamed x3 -> x0, blocking collectives: 861 us -> none
    unnamed x33 -> x13, waiting for transfers between devices: 37.8 us -> 648 us
    all_gather x6 -> x4, waiting for transfers between devices: 40 us -> 280 us  [the longest x3 270 us: gather_group(): return lax.all_gather(v, AXIS_NAME, axis_index_groups=groups, tiled=True)]
    unnamed x25 -> x4, starting transfers between devices: 154 us -> 0.74 us
    all_gather x2 -> x0, blocking collectives: 81.1 us -> none  [device_step(): lax.all_gather(w_shard, AXIS_NAME, tiled=True)]
    unnamed x190 -> x151, local copies, waits for them, and re-layouts: 92.4 us -> 15.6 us
    psum x0 -> x1, blocking collectives: none -> 53.8 us  [device_step(): qk = lax.psum(jnp.concatenate([grad_q_norm, grad_k_norm]), AXIS_NAME)]
    reduce_scatter x1, waiting for transfers between devices: 299 us -> 339 us  [scatter_group(): lax.psum_scatter(v, AXIS_NAME, scatter_dimension=0, axis_index_groups=gro...]
  transfers between devices with their start and end apart: 32 -> 20, of which waited for: 7 -> 10; matrix products, arithmetic and copies ran while one was open for 58% -> 7% of each run, Pallas kernels for 0% -> 0%
where the time goes in v1:
time: 1990 us; the launch traced here: 1980 us
  waiting for transfers between devices  1300 us (65%)
  other arithmetic  231 us (12%)
  matrix products  156 us (8%)
  local copies, waits for them, and re-layouts  147 us (7%)
  blocking collectives  97.3 us (5%)
  starting transfers between devices  37.7 us (2%)
    unnamed x13, waiting for transfers between devices  648 us
    reduce_scatter x1, waiting for transfers between devices, scatter_group(): lax.psum_scatter(v, AXIS_NAME, scatter_dimension=0, axis_index_groups=gro...  339 us
    all_gather x3, waiting for transfers between devices, gather_group(): return lax.all_gather(v, AXIS_NAME, axis_index_groups=groups, tiled=True)  270 us
    scatter-add x1, other arithmetic, device_step(): jax.ops.segment_sum(jnp.concatenate([my_rows, other_rows], axis=0), jnp.c...  146 us
    dot_general x21, matrix products, dot(): lax.dot_general(a, b, (((ca,), (cb,)), ((), ())), preferred_element_type=...  119 us
    gather x1, local copies, waits for them, and re-layouts, device_step(): jnp.take(table_shard, jnp.clip(local_ids, 0, rows_local - 1), axis=0)  80.3 us
    psum x1, blocking collectives, device_step(): qk = lax.psum(jnp.concatenate([grad_q_norm, grad_k_norm]), AXIS_NAME)  53.8 us
    all_gather x1, blocking collectives, device_step(): all_ids = lax.all_gather(tokens.reshape(-1), AXIS_NAME, tiled=True)  43.5 us
  transfers between devices with their start and end apart: 20, of which 10 were waited for; matrix products, arithmetic and copies ran while one was open for 7% of the time, Pallas kernels for 0%

profile of v1, /device:TPU:0, one launch (start us, length us, event | category | flops | bytes accessed | tf_op | source)
XLA Modules:
  0.0 1983.1 jit_solution(16075425795728382750)
XLA Ops:
  8.1 43.5 %all-gather = s32[1,16384]{1,0:T(1,128)S(1)} all-gather(s32[1,512]{1,0:T(1,128)} %param.15), channel_id=2, replica_groups=mesh['fsdp'=32] {'fsdp'}, dimensions={1}, use_global_device_ids=true | all-gather | bytes 67584 | tf_op jit(solution)/shard_map/all_gather | solution.py:113
  52.4 80.3 %gather_fusion = bf16[16384,896]{1,0:T(8,128)(2,1)} fusion(bf16[4752,896]{1,0:T(8,128)(2,1)} %param.17, s32[16384]{0:T(1024)S(1)} %get-tuple-element.57), kind=kCustom, calls=%fused_computation | custom fusion | bytes 58785792 | tf_op jit(solution)/shard_map/jit(_take)/gather | solution.py:116
  132.7 20.4 %fusion.4 = bf16[16,2,512,896]{3,2,0,1:T(8,128)(2,1)} fusion(bf16[16,2,512,896]{3,2,1,0:T(8,128)(2,1)} %bitcast.163, pred[16,2,512]{2,0,1:T(8,128)(4,1)S(1)} %copy.66, pred[16,2,512]{2,0,1:T(8,128)(4,1)S(1)} %copy.65), kind=kLoop, calls=%fused_computation.7 | loop fusion | flops 29360128 | bytes 58753024 | tf_op jit(solution)/shard_map/jit(_where)/select_n | solution.py:117
  153.2 22.1 %constant_dynamic-slice_fusion.8 = (bf16[16,1,512,896]{3,2,0,1:T(8,128)(2,1)}, bf16[16,1,512,896]{3,2,0,1:T(8,128)(2,1)}) fusion(bf16[16,2,512,896]{3,2,0,1:T(8,128)(2,1)} %fusion.4, s32[]{:T(128)S(6)} %select_n.80, s32[]{:T(128)S(6)} %select_n.81), kind=kLoop, calls=%fused_computation.179 | loop fusion | bytes 58720264 | tf_op jit(solution)/shard_map/dynamic_slice | solution.py:118
  176.6 20.8 %collective-permute-done = bf16[8192,896]{1,0:T(8,128)(2,1)} collective-permute-done((bf16[8192,896]{1,0:T(8,128)(2,1)}, bf16[8192,896]{1,0:T(8,128)(2,1)}, u32[]{:S(2)}, u32[]{:S(2)}) %collective-permute-start) | collective-permute-done | bytes 14680096 | tf_op jit(solution)/shard_map/ppermute | solution.py:82
  197.4 16.4 bitcast_add_fusion
  216.4 32.5 %collective-permute-start.2 = (bf16[28,4864]{1,0:T(8,128)(2,1)S(1)}, bf16[28,4864]{1,0:T(8,128)(2,1)S(1)}, u32[]{:S(2)}, u32[]{:S(2)}) collective-permute-start(bf16[28,4864]{1,0:T(8,128)(2,1)S(1)} %pad_maximum_fusion.12), channel_id=1, source_target_pairs={{0,1},{1,0},{2,3},{3,2},{4,5},{5,4},{6,7},{7,6},{8,9},{9,8},{10,11... | collective-permute-start | bytes 817160 | tf_op jit(solution)/shard_map/ppermute | solution.py:82
  253.0 10.4 all-gather.13.cloned.1.call-done
  263.4 6.0 reshape.649
  269.4 1.4 convert_reduce_fusion
  270.8 339.3 %reduce-scatter.17.cloned.1.call-done = bf16[512,896]{1,0:T(8,128)(2,1)} async-done(((bf16[8192,896]{1,0:T(8,128)(2,1)}), bf16[512,896]{1,0:T(8,128)(2,1)}) %reduce-scatter.17.cloned.1.call-update) | async-done | bytes 917520 | tf_op jit(solution)/shard_map/reduce_scatter | solution.py:88
  610.2 1.4 fusion.42
  611.6 4.3 fusion.58
  615.9 1.8 copy.69
  617.7 1.8 fusion.69
  620.2 1.5 convolution_convert_fusion.3
  622.6 6.7 fusion.11
  629.3 8.2 fusion.10
  637.5 7.7 fusion.55
  645.2 3.1 fusion.50
  648.8 10.5 fusion.65
  659.3 10.5 fusion.21
  669.8 16.8 multiply_convert_fusion.1
  686.6 10.5 fusion.19
  697.1 7.7 fusion.52
  704.8 1.5 slice.145
  706.6 5.5 fusion.113
  712.1 1.5 slice.143
  715.4 1.6 mul.604
  717.0 2.7 copy.76
  719.7 2.9 fusion.49
  722.9 4.9 fusion.48
  727.8 3.6 convolution_convert_fusion
  731.4 2.2 copy.71
  733.6 13.1 fusion.5
  748.5 8.2 fusion.13
  756.7 1.4 convolution_bitcast_fusion
  758.1 3.0 convolution_bitcast_fusion.1
  761.2 4.9 fusion.70
  767.5 1.7 pad_maximum_fusion.3
  769.3 1.5 mul.621
  770.8 2.8 copy.75
  773.6 3.0 copy.73
  777.0 1.5 fusion.83
  778.8 2.5 multiply_reduce_fusion
  781.4 3.0 fusion.61
  784.4 1.9 fusion.41
  786.3 1.8 fusion.40
  791.8 1.7 fusion.27
  793.9 6.8 collective-permute-done.8
  800.7 4.3 select_add_fusion
  804.9 5.7 copy.79
  811.8 11.0 fusion.98
  822.9 11.2 fusion.97
  834.3 270.1 %all-gather.11.cloned.1.call-done = f32[8192,896]{1,0:T(8,128)} async-done(((f32[512,896]{1,0:T(8,128)}), f32[8192,896]{1,0:T(8,128)}) %all-gather.11.cloned.1.call-update) | async-done | bytes 29360144 | tf_op jit(solution)/shard_map/all_gather | solution.py:85
  1104.4 11.8 fusion.64
  1117.0 81.6 %reduce-scatter.23.cloned.1.call-done = f32[56,1152]{1,0:T(8,128)} async-done(((f32[896,1152]{1,0:T(8,128)}), f32[56,1152]{1,0:T(8,128)}) %reduce-scatter.23.cloned.1.call-update) | async-done | bytes 258064
  1198.6 186.6 %reduce-scatter.19.cloned.1.call-done = f32[56,2432]{1,0:T(8,128)} async-done(((f32[896,2432]{1,0:T(8,128)}), f32[56,2432]{1,0:T(8,128)}) %reduce-scatter.19.cloned.1.call-update) | async-done | bytes 544784
  1385.2 190.8 %reduce-scatter.21.cloned.1.call-done = f32[56,2432]{1,0:T(8,128)} async-done(((f32[896,2432]{1,0:T(8,128)}), f32[56,2432]{1,0:T(8,128)}) %reduce-scatter.21.cloned.1.call-update) | async-done | bytes 544784
  1576.0 1.4 pad_maximum_fusion.4
  1577.6 188.7 %reduce-scatter.25.cloned.1.call-done = f32[152,896]{1,0:T(8,128)} async-done(((f32[2432,896]{1,0:T(8,128)}), f32[152,896]{1,0:T(8,128)}) %reduce-scatter.25.cloned.1.call-update) | async-done | bytes 544784
  1766.3 1.7 collective-permute-start.10
  1768.9 53.8 %psum.7 = f32[128]{0:T(128)S(1)} all-reduce(f32[128]{0:T(128)S(1)} %pad_maximum_fusion.15), channel_id=1, replica_groups=mesh['fsdp'=32] {'fsdp'}, use_global_device_ids=true, to_apply=%region_22.23 | all-reduce | flops 128 | bytes 1024 | tf_op jit(solution)/shard_map/psum | solution.py:212
  1828.5 146.1 %scatter_custom_fusion = f32[4752,896]{1,0:T(8,128)} fusion(s32[16384]{0:T(1024)} %pad_add_fusion, f32[8192,896]{1,0:T(8,128)} %collective-permute-done.7, f32[]{:T(128)} %constant.71.clone.1, f32[8192,896]{1,0:T(8,128)} %all-gather.11.cloned.1.call-done, f32[]{:T(128)} %constant.31.clone.1), kind=kCustom, calls=%fused_computation.2 | custom fusion | flops 29360128 | bytes 75752448 | tf_op jit(solution)/shard_map/scatter-add | solution.py:189
  (261 shorter events, 30.6 us)
Async XLA Ops:
  8.0 255.4 %all-gather.13.cloned.1.call-start = ((), (), s32[]{:S(2)}) async-start(), calls=%async_computation.9 | async-start | bytes 4595712 | tf_op jit(solution)/shard_map/all_gather | solution.py:104
  153.1 22.5 %copy-start.59 = (bf16[28]{0:T(256)(128)(2,1)S(1)}, bf16[28]{0:T(256)(128)(2,1)}, u32[]{:S(2)}) copy-start(bf16[28]{0:T(256)(128)(2,1)} %param.25) | copy-start | bytes 172
  153.1 22.5 %copy-start.60 = (bf16[28]{0:T(256)(128)(2,1)S(1)}, bf16[28]{0:T(256)(128)(2,1)}, u32[]{:S(2)}) copy-start(bf16[28]{0:T(256)(128)(2,1)} %param.18) | copy-start | bytes 172
  153.1 22.6 %copy-start.44 = (bf16[28,896]{1,0:T(8,128)(2,1)S(1)}, bf16[28,896]{1,0:T(8,128)(2,1)}, u32[]{:S(2)}) copy-start(bf16[28,896]{1,0:T(8,128)(2,1)} %param.19) | copy-start | bytes 150532
  153.1 22.6 %copy-start.45 = (bf16[28,896]{1,0:T(8,128)(2,1)S(1)}, bf16[28,896]{1,0:T(8,128)(2,1)}, u32[]{:S(2)}) copy-start(bf16[28,896]{1,0:T(8,128)(2,1)} %param.24) | copy-start | bytes 150532
  153.2 22.7 %copy-start.48 = (bf16[28,128]{1,0:T(8,128)(2,1)S(1)}, bf16[28,128]{1,0:T(8,128)(2,1)}, u32[]{:S(2)}) copy-start(bf16[28,128]{1,0:T(8,128)(2,1)} %param.20) | copy-start | bytes 21508
  153.2 22.7 %copy-start.49 = (bf16[28,128]{1,0:T(8,128)(2,1)S(1)}, bf16[28,128]{1,0:T(8,128)(2,1)}, u32[]{:S(2)}) copy-start(bf16[28,128]{1,0:T(8,128)(2,1)} %param.21) | copy-start | bytes 21508
  175.3 22.1 %collective-permute-start = (bf16[8192,896]{1,0:T(8,128)(2,1)}, bf16[8192,896]{1,0:T(8,128)(2,1)}, u32[]{:S(2)}, u32[]{:S(2)}) collective-permute-start(bf16[8192,896]{1,0:T(8,128)(2,1)} %bitcast.3), channel_id=1, source_target_pairs={{0,1},{1,0},{2,3},{3,2},{4,5},{5,4},{6,7},{7,6},{8,9},{9,8},{10,11... | collective-permute-start | bytes 44040200 | tf_op jit(solution)/shard_map/ppermute | solution.py:82
  176.6 433.6 %reduce-scatter.17.cloned.1.call-start = ((), (), s32[]{:S(2)}) async-start(), calls=%async_computation.5 | async-start | bytes 15597568 | tf_op jit(solution)/shard_map/reduce_scatter | solution.py:88
  213.9 38.0 %copy-start.61 = (bf16[64]{0:T(256)(128)(2,1)S(1)}, bf16[64]{0:T(256)(128)(2,1)}, u32[]{:S(2)}) copy-start(bf16[64]{0:T(256)(128)(2,1)} %param.23) | copy-start | bytes 388
  213.9 38.0 %copy-start.50 = (s32[1,512]{1,0:T(1,128)S(1)}, s32[1,512]{1,0:T(1,128)}, u32[]{:S(2)}) copy-start(s32[1,512]{1,0:T(1,128)} %param.16) | copy-start | bytes 6148
  213.9 38.0 %copy-start.55 = (bf16[64]{0:T(256)(128)(2,1)S(1)}, bf16[64]{0:T(256)(128)(2,1)}, u32[]{:S(2)}) copy-start(bf16[64]{0:T(256)(128)(2,1)} %param.22) | copy-start | bytes 388
  213.9 434.9 %all-gather.9.cloned.1.call-start = ((), (), s32[]{:S(2)}) async-start(), calls=%async_computation.7 | async-start | bytes 4630528 | tf_op jit(solution)/shard_map/all_gather | solution.py:85
  214.8 0.7 collective-permute-start.3
  216.2 443.0 %all-gather.7.cloned.1.call-start = ((), (), s32[]{:S(2)}) async-start(), calls=%async_computation.6 | async-start | bytes 9261056 | tf_op jit(solution)/shard_map/all_gather | solution.py:85
  216.4 33.8 %collective-permute-start.2 = (bf16[28,4864]{1,0:T(8,128)(2,1)S(1)}, bf16[28,4864]{1,0:T(8,128)(2,1)S(1)}, u32[]{:S(2)}, u32[]{:S(2)}) collective-permute-start(bf16[28,4864]{1,0:T(8,128)(2,1)S(1)} %pad_maximum_fusion.12), channel_id=1, source_target_pairs={{0,1},{1,0},{2,3},{3,2},{4,5},{5,4},{6,7},{7,6},{8,9},{9,8},{10,11... | collective-permute-start | bytes 817160 | tf_op jit(solution)/shard_map/ppermute | solution.py:82
  251.2 853.1 %all-gather.11.cloned.1.call-start = ((), (), s32[]{:S(2)}) async-start(), calls=%async_computation.8 | async-start | bytes 31195136 | tf_op jit(solution)/shard_map/all_gather | solution.py:85
  251.5 397.3 %collective-permute-start.5 = (bf16[512,896]{1,0:T(8,128)(2,1)}, bf16[512,896]{1,0:T(8,128)(2,1)}, u32[]{:S(2)}, u32[]{:S(2)}) collective-permute-start(bf16[512,896]{1,0:T(8,128)(2,1)} %bitcast.28), channel_id=1, source_target_pairs={{0,1},{1,0},{2,3},{3,2},{4,5},{5,4},{6,7},{7,6},{8,9},{9,8},{10,11... | collective-permute-start | bytes 2752520 | tf_op jit(solution)/shard_map/ppermute | solution.py:82
  251.9 367.9 %copy-start.51 = (f32[64]{0:T(128)}, f32[64]{0:T(128)S(1)}, u32[]{:S(2)}) copy-start(f32[64]{0:T(128)S(1)} %convert_element_type.202) | copy-start | bytes 772
  251.9 369.8 %copy-start.53 = (f32[64]{0:T(128)}, f32[64]{0:T(128)S(1)}, u32[]{:S(2)}) copy-start(f32[64]{0:T(128)S(1)} %convert_element_type.207) | copy-start | bytes 772
  253.0 366.9 %copy-start.23 = (f32[512,32]{0,1:T(8,128)}, f32[512,32]{0,1:T(8,128)S(1)}, u32[]{:S(2)}) copy-start(f32[512,32]{0,1:T(8,128)S(1)} %get-tuple-element.61) | copy-start | bytes 196612
  253.0 369.2 %copy-start.15 = (f32[512,32]{0,1:T(8,128)}, f32[512,32]{0,1:T(8,128)S(1)}, u32[]{:S(2)}) copy-start(f32[512,32]{0,1:T(8,128)S(1)} %get-tuple-element.62) | copy-start | bytes 196612
  270.8 349.2 %copy-start.37 = (f32[896]{0:T(1024)}, f32[896]{0:T(1024)S(1)}, u32[]{:S(2)}) copy-start(f32[896]{0:T(1024)S(1)} %get-tuple-element.16) | copy-start | bytes 10756
  611.6 8.4 copy-start.46
  611.6 6.1 copy-start.2
  617.7 4.5 copy-start
  621.8 15.7 copy-start.62
  622.6 6.7 copy-start.13
  637.5 7.8 copy-start.40
  648.4 71.3 %copy-start.3 = (bf16[512,896]{1,0:T(8,128)(2,1)}, bf16[512,896]{1,0:T(8,128)(2,1)S(1)}, u32[]{:S(2)}) copy-start(bf16[512,896]{1,0:T(8,128)(2,1)S(1)} %get-tuple-element.68) | copy-start | bytes 2752516
  648.7 21.1 %copy-start.19 = (bf16[512,896]{1,0:T(8,128)(2,1)}, bf16[512,896]{1,0:T(8,128)(2,1)S(1)}, u32[]{:S(2)}) copy-start(bf16[512,896]{1,0:T(8,128)(2,1)S(1)} %fusion.44) | copy-start | bytes 2752516
  648.7 10.6 collective-permute-start.1
  686.5 10.6 copy-start.57
  686.5 10.6 copy-start.63
  686.5 20.0 %slice-start.4 = ((s8[4358144]{0:T(1024)(128)(4,1)}), s8[4194304]{0:T(1024)(128)(4,1)S(1)}, s32[]{:S(2)}) async-start(s8[4358144]{0:T(1024)(128)(4,1)} %bitcast.186), calls=%async_computation.18 | async-start | bytes 8388608
  686.6 20.0 %slice-start.6 = ((s8[4980736]{0:T(1024)(128)(4,1)}), s8[4194304]{0:T(1024)(128)(4,1)S(1)}, s32[]{:S(2)}) async-start(s8[4980736]{0:T(1024)(128)(4,1)} %bitcast.192), calls=%async_computation.20 | async-start | bytes 8388608
  697.1 9.5 slice-start.5
  697.1 9.4 slice-start.7
  704.8 7.3 copy-start.4
  706.3 13.4 collective-permute-start.6
  714.5 8.1 collective-permute-start.4
  733.6 13.1 slice-start
  733.6 13.1 slice-start.1
  733.6 14.3 slice-start.2
  733.6 14.9 slice-start.3
  733.6 14.9 copy-start.41
  748.5 8.2 copy-start.33
  748.5 8.2 copy-start.35
  761.2 4.9 copy-start.16
  761.2 4.9 copy-start.25
  770.8 5.8 copy-start.17
  770.8 5.9 copy-start.9
  770.8 5.9 copy-start.43
  770.8 5.9 copy-start.52
  770.8 6.0 copy-start.56
  781.3 5.0 copy-start.10
  788.1 410.5 %reduce-scatter.23.cloned.1.call-start = ((), (), s32[]{:S(2)}) async-start(), calls=%async_computation.12 | async-start | bytes 4386816
  793.5 7.1 collective-permute-start.8
  810.6 574.6 %reduce-scatter.19.cloned.1.call-start = ((), (), s32[]{:S(2)}) async-start(), calls=%async_computation.10 | async-start | bytes 9261056
  822.8 753.1 %reduce-scatter.21.cloned.1.call-start = ((), (), s32[]{:S(2)}) async-start(), calls=%async_computation.11 | async-start | bytes 9261056
  834.1 932.2 %reduce-scatter.25.cloned.1.call-start = ((), (), s32[]{:S(2)}) async-start(), calls=%async_computation.13 | async-start | bytes 9261056
  1104.4 724.2 %collective-permute-start.7 = (f32[8192,896]{1,0:T(8,128)}, f32[8192,896]{1,0:T(8,128)}, u32[]{:S(2)}, u32[]{:S(2)}) collective-permute-start(f32[8192,896]{1,0:T(8,128)} %all-gather.11.cloned.1.call-done), channel_id=1, source_target_pairs={{0,1},{1,0},{2,3},{3,2},{4,5},{5,4},{6,7},{7,6},{8,9},{9,8},{10,11... | collective-permute-start | bytes 88080392 | tf_op jit(solution)/shard_map/ppermute | solution.py:82
  1577.5 245.9 %collective-permute-start.9 = (f32[28,6016]{1,0:T(8,128)S(1)}, f32[28,6016]{1,0:T(8,128)S(1)}, u32[]{:S(2)}, u32[]{:S(2)}) collective-permute-start(f32[28,6016]{1,0:T(8,128)S(1)} %constant_dynamic-slice_fusion), channel_id=1, source_target_pairs={{0,1},{1,0},{2,3},{3,2},{4,5},{5,4},{6,7},{7,6},{8,9},{9,8},{10,11... | collective-permute-start | bytes 2021384 | tf_op jit(solution)/shard_map/ppermute | solution.py:82
  1766.3 57.0 %collective-permute-start.10 = (f32[152,896]{1,0:T(8,128)}, f32[152,896]{1,0:T(8,128)S(1)}, u32[]{:S(2)}, u32[]{:S(2)}) collective-permute-start(f32[152,896]{1,0:T(8,128)} %reduce-scatter.25.cloned.1.call-done), channel_id=1, source_target_pairs={{0,0},{2,1},{4,2},{6,3},{8,4},{10,5},{12,6},{14,7},{16,8},{18,9},{... | collective-permute-start | bytes 1634312 | tf_op jit(solution)/shard_map/ppermute | solution.py:156
  (28 other events, 55.7 us)
Sparse Core Ops, SparseCore 0:
  176.7 86.6 all-gather.12
  266.6 130.1 all-gather.8
  400.1 167.0 all-gather.6
  810.7 387.8 reduce-scatter.22
  1200.8 184.3 reduce-scatter.18
  1387.9 187.9 reduce-scatter.20
  1578.3 187.9 reduce-scatter.24
Sparse Core Ops, SparseCore 1:
  214.0 396.1 reduce-scatter.16
  788.2 316.1 all-gather.10

commit v2 on v1

--- a/solution.py
+++ b/solution.py
@@ -1,7 +1,10 @@
+import functools
 import math
 import jax
 import jax.numpy as jnp
 from jax import lax
+from jax.experimental import pallas as pl
+from jax.experimental.pallas import tpu as pltpu
 from jax.sharding import PartitionSpec as P
 
 NORM_EPS = 1e-6
@@ -9,6 +12,7 @@
 AXIS_NAME = 'fsdp'
 F32 = jnp.float32
 BF16 = jnp.bfloat16
+MESH = pl.DeviceIdType.MESH
 
 
 def rope_tables(positions, head_dim):
@@ -64,6 +68,321 @@
     return lax.dot_general(a, b, (((ca,), (cb,)), ((), ())), preferred_element_type=F32)
 
 
+def _coords(me):
+    core = me % 2
+    x = (me // 2) % 2
+    y = (me // 4) % 2
+    z = me // 8
+    a = y * (1 - core) + x * core
+    b = x * (1 - core) + y * core
+    return core, a, b, z, 4 - 2 * core, 2 + 2 * core
+
+
+def _barrier(peers):
+    sem = pltpu.get_barrier_semaphore()
+    for peer in peers:
+        pl.semaphore_signal(sem, inc=1, device_id=(peer,), device_id_type=MESH)
+    pl.semaphore_wait(sem, len(peers))
+
+
+def _remote(src, dst, send_sem, recv_sem, dev):
+    return pltpu.make_async_remote_copy(src_ref=src, dst_ref=dst, send_sem=send_sem, recv_sem=recv_sem, device_id=(dev,), device_id_type=MESH)
+
+
+def _all_rows_kernel(n_dev, in_ref, out_ref, send_sem, recv_sem):
+    me = lax.axis_index(AXIS_NAME)
+    peers = [(me + d) % n_dev for d in range(1, n_dev)]
+    _barrier(peers)
+    copies = []
+    for i, peer in enumerate(peers):
+        copy = _remote(in_ref, out_ref.at[me], send_sem.at[i], recv_sem.at[i], peer)
+        copy.start()
+        copies.append(copy)
+    out_ref[me] = in_ref[...]
+    for copy in copies:
+        copy.wait()
+
+
+def all_rows(block, n_dev, collective_id):
+    return pl.pallas_call(
+        functools.partial(_all_rows_kernel, n_dev),
+        out_shape=jax.ShapeDtypeStruct((n_dev,) + block.shape, block.dtype),
+        in_specs=[pl.BlockSpec(memory_space=pltpu.VMEM)],
+        out_specs=pl.BlockSpec(memory_space=pltpu.VMEM),
+        scratch_shapes=[pltpu.SemaphoreType.DMA((n_dev - 1,)), pltpu.SemaphoreType.DMA((n_dev - 1,))],
+        compiler_params=pltpu.CompilerParams(collective_id=collective_id, has_side_effects=True),
+        cost_estimate=pl.CostEstimate(flops=10_000_000, bytes_accessed=1 << 18, transcendentals=0),
+        name='all_rows',
+    )(block)
+
+
+def _gather_kernel(cuts, *refs):
+    n_arr = len(cuts)
+    (own_sem, z_send, z_recv, b_send, b_recv, a_send, a_recv, p_send, p_recv) = refs[2 * n_arr:]
+    ins, outs = [], []
+    for arr, (rows, n_cut) in enumerate(cuts):
+        for i in range(n_cut):
+            at = pl.ds(i * (rows // n_cut), rows // n_cut)
+            ins.append(refs[arr] if n_cut == 1 else refs[arr].at[at])
+            outs.append(functools.partial(lambda ref, at, slot: ref.at[slot] if at is None else ref.at[slot, at], refs[n_arr + arr], None if n_cut == 1 else at))
+    n_pieces = len(ins)
+    me = lax.axis_index(AXIS_NAME)
+    core, a, b, z, a_str, b_str = _coords(me)
+    a_nbr = me + (1 - 2 * a) * a_str
+    b_nbr = me + (1 - 2 * b) * b_str
+    partner = me + 1 - 2 * core
+    z_base = me - 8 * z
+    z_peer = [z_base + 8 * ((z + 1 + i) % 4) for i in range(3)]
+    z_src = [z_base + 8 * ((z + 3 - i) % 4) for i in range(3)]
+    b_shift = (1 - 2 * b) * b_str
+    a_shift = (1 - 2 * a) * a_str
+    _barrier([a_nbr, b_nbr, partner] + z_peer)
+    z_blocks = [me] + z_src
+    b_blocks = [d + b_shift for d in z_blocks]
+    order = [('z', 0), ('z', 1), ('b', 0), ('z', 2), ('b', 1), ('z', 3), ('b', 2), ('b', 3)]
+    a_out = [z_blocks[i] if kind == 'z' else b_blocks[i] for kind, i in order]
+    a_in = [d + a_shift for d in a_out]
+    started = []
+    n_partner = [0]
+
+    def send(p, src, dev_slot, s_sem, r_sem, dev):
+        copy = _remote(src, outs[p](dev_slot), s_sem, r_sem, dev)
+        copy.start()
+        started.append(copy)
+
+    def arrived(p, slot, sem):
+        pltpu.make_async_copy(outs[p](slot), outs[p](slot), sem).wait()
+
+    def to_partner(p, src, slot, j):
+        send(p, src, slot, p_send.at[p, j], p_recv.at[p, j], partner)
+
+    own = []
+    for p in range(n_pieces):
+        for i in range(3):
+            send(p, ins[p], me, z_send.at[p, i], z_recv.at[p, i], z_peer[i])
+        send(p, ins[p], me, b_send.at[p, 0], b_recv.at[p, 0], b_nbr)
+        send(p, ins[p], me, a_send.at[p, 0], a_recv.at[p, 0], a_nbr)
+        to_partner(p, ins[p], me, 0)
+        copy = pltpu.make_async_copy(ins[p], outs[p](me), own_sem.at[p])
+        copy.start()
+        own.append(copy)
+    j = 1
+    for m, (kind, i) in enumerate(order):
+        if m == 0:
+            continue
+        for p in range(n_pieces):
+            slot = a_out[m]
+            if kind == 'z':
+                arrived(p, slot, z_recv.at[p, i - 1])
+                send(p, outs[p](slot), slot, b_send.at[p, i], b_recv.at[p, i], b_nbr)
+            else:
+                arrived(p, slot, b_recv.at[p, i])
+            send(p, outs[p](slot), slot, a_send.at[p, m], a_recv.at[p, m], a_nbr)
+            to_partner(p, outs[p](slot), slot, j)
+        j += 1
+    for m in range(8):
+        for p in range(n_pieces):
+            arrived(p, a_in[m], a_recv.at[p, m])
+            to_partner(p, outs[p](a_in[m]), a_in[m], j)
+        j += 1
+    p_shift = 1 - 2 * core
+    pa_shift, pb_shift = b_shift, a_shift
+    pz = [partner] + [s + p_shift for s in z_src]
+    pb = [d + pb_shift for d in pz]
+    p_first = [pz[i] if kind == 'z' else pb[i] for kind, i in order]
+    p_in = p_first + [d + pa_shift for d in p_first]
+    for j in range(16):
+        for p in range(n_pieces):
+            arrived(p, p_in[j], p_recv.at[p, j])
+    for copy in own:
+        copy.wait()
+    for copy in started:
+        copy.wait_send()
+
+
+def gather_all(blocks, cuts, n_dev, collective_id):
+    n_arr = len(blocks)
+    n = sum(cuts)
+    dma = pltpu.SemaphoreType.DMA
+    nbytes = sum(v.size * v.dtype.itemsize for v in blocks)
+    return pl.pallas_call(
+        functools.partial(_gather_kernel, tuple((v.shape[0], c) for v, c in zip(blocks, cuts))),
+        out_shape=[jax.ShapeDtypeStruct((n_dev,) + v.shape, v.dtype) for v in blocks],
+        in_specs=[pl.BlockSpec(memory_space=pltpu.VMEM)] * n_arr,
+        out_specs=[pl.BlockSpec(memory_space=pl.ANY)] * n_arr,
+        scratch_shapes=[dma((n,)), dma((n, 3)), dma((n, 3)), dma((n, 4)), dma((n, 4)), dma((n, 8)), dma((n, 8)), dma((n, 16)), dma((n, 16))],
+        compiler_params=pltpu.CompilerParams(collective_id=collective_id, has_side_effects=True, vmem_limit_bytes=nbytes + (8 << 20)),
+        cost_estimate=pl.CostEstimate(flops=200_000_000, bytes_accessed=nbytes * 64, transcendentals=0),
+        name='gather_all',
+    )(*blocks)
+
+
+def _scatter_kernel(specs, *refs):
+    n = len(specs)
+    n_pair = sum(1 for s in specs if s[3])
+    ins = refs[:n]
+    outs = refs[n:2 * n]
+    k = 2 * n
+    ra = refs[k:k + n]
+    rb = refs[k + n:k + 2 * n]
+    rz = refs[k + 2 * n:k + 3 * n]
+    k += 3 * n
+    rd = list(refs[k:k + n_pair])
+    k += n_pair
+    stage = refs[k:k + n]
+    sent = refs[k + n:k + 2 * n]
+    k += 2 * n
+    (load_sem, d_send, d_recv, a_send, a_recv, b_send, b_recv, z_send, z_recv) = refs[k:]
+    d_of = []
+    for s in specs:
+        d_of.append(rd.pop(0) if s[3] else None)
+    me = lax.axis_index(AXIS_NAME)
+    core, a, b, z, a_str, b_str = _coords(me)
+    a_nbr = me + (1 - 2 * a) * a_str
+    b_nbr = me + (1 - 2 * b) * b_str
+    partner = me + 1 - 2 * core
+    z_base = me - 8 * z
+    z_peer = [z_base + 8 * ((z + 1 + i) % 4) for i in range(3)]
+    _barrier([a_nbr, b_nbr, partner] + z_peer)
+
+    def chip(ka, kb, kz):
+        return (8 * kz + ka * a_str + kb * b_str) // 2
+
+    def s1_chip(s, a, b, a_str, b_str):
+        far = 1 - s // 4
+        kb = b + far * (1 - 2 * b)
+        return (8 * (s % 4) + (1 - a) * a_str + kb * b_str) // 2
+
+    def s2_chip(s):
+        return chip(a, 1 - b, s)
+
+    def d_order(s, a, b, a_str, b_str):
+        in1 = (s < 8).astype(jnp.int32) if not isinstance(s, int) else int(s < 8)
+        t = s - 8
+        k1 = s1_chip(s % 8, a, b, a_str, b_str)
+        kb = b + (1 - (t // 4) % 2) * (1 - 2 * b)
+        k2 = (8 * (s % 4) + a * a_str + kb * b_str) // 2
+        return in1 * k1 + (1 - in1) * k2
+
+    started = []
+    for p, (rows, cols, dtype, paired) in enumerate(specs):
+        if not paired:
+            continue
+    for s in range(16):
+        for p, (rows, cols, dtype, paired) in enumerate(specs):
+            if paired:
+                kc = d_order(s, b, a, b_str, a_str)
+                copy = _remote(ins[p].at[2 * kc + 1 - core], d_of[p].at[kc], d_send.at[p, s], d_recv.at[p, kc], partner)
+                copy.start()
+                started.append(copy)
+
+    def term(p, kc):
+        return ins[p].at[2 * kc + core] if specs[p][3] else ins[p].at[kc]
+
+    def landed(ref, sem):
+        pltpu.make_async_copy(ref, ref, sem).wait()
+
+    def add_up(p, operands, dst):
+        rows, cols, dtype, _ = specs[p]
+        loads = []
+        for o, (ref, sem) in enumerate(operands):
+            if sem is not None:
+                landed(ref, sem)
+            load = pltpu.make_async_copy(ref, stage[p].at[o], load_sem.at[p, o])
+            load.start()
+            loads.append(load)
+        for load in loads:
+            load.wait()
+        step = 8 if dtype == F32 else 16
+
+        def body(r, _):
+            at = pl.ds(pl.multiple_of(r * step, step), step)
+            total = stage[p][0, at, :].astype(F32)
+            for o in range(1, len(operands)):
+                total = total + stage[p][o, at, :].astype(F32)
+            dst[at, :] = total.astype(dtype)
+            return 0
+
+        lax.fori_loop(0, rows // step, body, 0)
+
+    def base(p, kc):
+        ops = [(term(p, kc), None)]
+        if specs[p][3]:
+            ops.append((d_of[p].at[kc], d_recv.at[p, kc]))
+        return ops
+
+    def s1(s, carry):
+        kc = s1_chip(s, a, b, a_str, b_str)
+        for p in range(n):
+            add_up(p, base(p, kc), sent[p].at[s])
+            _remote(sent[p].at[s], ra[p].at[s], a_send.at[p, s], a_recv.at[p, s], a_nbr).start()
+        return carry
+
+    lax.fori_loop(0, 8, s1, 0)
+
+    def s2(s, carry):
+        kc = s2_chip(s)
+        for p in range(n):
+            add_up(p, base(p, kc) + [(ra[p].at[s], a_recv.at[p, s])], sent[p].at[8 + s])
+            _remote(sent[p].at[8 + s], rb[p].at[s], b_send.at[p, s], b_recv.at[p, s], b_nbr).start()
+        return carry
+
+    lax.fori_loop(0, 4, s2, 0)
+
+    def last(p, kz):
+        return base(p, chip(a, b, kz)) + [(ra[p].at[4 + kz], a_recv.at[p, 4 + kz]), (rb[p].at[kz], b_recv.at[p, kz])]
+
+    def s3(i, carry):
+        kz = (z + 1 + i) % 4
+        for p in range(n):
+            add_up(p, last(p, kz), sent[p].at[12 + i])
+            _remote(sent[p].at[12 + i], rz[p].at[i], z_send.at[p, i], z_recv.at[p, i], z_base + 8 * kz).start()
+        return carry
+
+    lax.fori_loop(0, 3, s3, 0)
+    for p in range(n):
+        add_up(p, last(p, z) + [(rz[p].at[i], z_recv.at[p, i]) for i in range(3)], outs[p])
+    for copy in started:
+        copy.wait_send()
+
+    def drain(sem, count, lo):
+        def body(s, carry):
+            for p in range(n):
+                _remote(sent[p].at[lo + s], sent[p].at[lo + s], sem.at[p, s], sem.at[p, s], me).wait_send()
+            return carry
+        lax.fori_loop(0, count, body, 0)
+
+    drain(a_send, 8, 0)
+    drain(b_send, 4, 8)
+    drain(z_send, 3, 12)
+
+
+def scatter_sum(pieces, paired, collective_id):
+    specs = tuple((v.shape[1], v.shape[2], jnp.dtype(v.dtype), pr) for v, pr in zip(pieces, paired))
+    n = len(specs)
+    dma = pltpu.SemaphoreType.DMA
+    hbm = pl.BlockSpec(memory_space=pl.ANY)
+    sds = jax.ShapeDtypeStruct
+    outs = [sds((r, c), d) for r, c, d, _ in specs]
+    lands = [sds((m, r, c), d) for m in (8, 4, 3) for r, c, d, _ in specs]
+    lands += [sds((16, r, c), d) for r, c, d, pr in specs if pr]
+    scratch = [pltpu.VMEM((7 if pr else 6, r, c), d) for r, c, d, pr in specs]
+    scratch += [pltpu.VMEM((15, r, c), d) for r, c, d, _ in specs]
+    scratch += [dma((n, 7)), dma((n, 16)), dma((n, 16)), dma((n, 8)), dma((n, 8)), dma((n, 4)), dma((n, 4)), dma((n, 3)), dma((n, 3))]
+    nbytes = sum(r * c * d.itemsize * (16 + 7) for r, c, d, _ in specs)
+    res = pl.pallas_call(
+        functools.partial(_scatter_kernel, specs),
+        out_shape=outs + lands,
+        in_specs=[hbm] * n,
+        out_specs=[pl.BlockSpec(memory_space=pltpu.VMEM)] * n + [hbm] * len(lands),
+        scratch_shapes=scratch,
+        compiler_params=pltpu.CompilerParams(collective_id=collective_id, has_side_effects=True, vmem_limit_bytes=nbytes + (6 << 20)),
+        cost_estimate=pl.CostEstimate(flops=200_000_000, bytes_accessed=nbytes * 4, transcendentals=0),
+        name='scatter_sum',
+    )(*pieces)
+    return res[:n]
+
+
 def solution(mesh):
     n_dev = mesh.shape[AXIS_NAME]
     n_chip = n_dev // 2
@@ -83,9 +402,6 @@
 
     def gather_group(v):
         return lax.all_gather(v, AXIS_NAME, axis_index_groups=groups, tiled=True)
-
-    def scatter_group(v):
-        return lax.psum_scatter(v, AXIS_NAME, scatter_dimension=0, axis_index_groups=groups, tiled=True)
 
     def device_step(tokens, positions, table_shard, attn_norm, w_query, w_key, w_value, q_norm, k_norm, w_out, mlp_norm, w_gate, w_up, w_down, dy_out):
         me = lax.axis_index(AXIS_NAME)
@@ -101,7 +417,7 @@
 
         gains = jnp.pad(jnp.stack([attn_norm, mlp_norm], axis=1), ((0, 0), (0, 126)))
         attn_pack = jnp.concatenate([w_query, w_out, w_key, w_value, gains], axis=1)
-        attn_full = lax.all_gather(attn_pack, AXIS_NAME, tiled=True)
+        attn_full = gather_all([attn_pack], [1], n_dev, 1)[0].reshape(-1, attn_pack.shape[1])
         mine_gu = jnp.concatenate([lax.dynamic_slice(w_gate, (0, core * half), (rows_w, half)), lax.dynamic_slice(w_up, (0, core * half), (rows_w, half))], axis=1)
         other_gu = jnp.concatenate([lax.dynamic_slice(w_gate, (0, (1 - core) * half), (rows_w, half)), lax.dynamic_slice(w_up, (0, (1 - core) * half), (rows_w, half))], axis=1)
         recv_gu = swap(other_gu)
@@ -110,14 +426,12 @@
         wd = gather_group(lax.ppermute(w_down, AXIS_NAME, to_use))
         w_g, w_u = wgu[:, :half], wgu[:, half:]
 
-        all_ids = lax.all_gather(tokens.reshape(-1), AXIS_NAME, tiled=True)
+        all_ids = all_rows(jnp.pad(tokens.reshape(-1, 128), ((0, 4), (0, 0))), n_dev, 0)[:, :seq_len // 128].reshape(-1)
         local_ids = all_ids - me * rows_local
         is_owner = (local_ids >= 0) & (local_ids < rows_local)
         picked = jnp.take(table_shard, jnp.clip(local_ids, 0, rows_local - 1), axis=0)
-        picked = jnp.where(is_owner[:, None], picked, jnp.zeros((), picked.dtype)).reshape(n_chip, 2, seq_len, model_dim)
-        keep = lax.dynamic_slice(picked, (0, core, 0, 0), (n_chip, 1, seq_len, model_dim)).reshape(-1, model_dim)
-        give = lax.dynamic_slice(picked, (0, 1 - core, 0, 0), (n_chip, 1, seq_len, model_dim)).reshape(-1, model_dim)
-        x_emb = scatter_group(keep + swap(give))
+        picked = jnp.where(is_owner[:, None], picked, jnp.zeros((), picked.dtype)).reshape(n_dev, seq_len, model_dim)
+        x_emb = scatter_sum([picked], [True], 2)[0]
 
         dy = dy_out.reshape(seq_len, model_dim)
         dy2 = jnp.concatenate([dy, swap(dy)], axis=0)
@@ -153,14 +467,13 @@
         gate_sig = jax.nn.sigmoid(gate_pre)
         mlp_act = (gate_pre * gate_sig * up_proj).astype(BF16)
         grad_w_down = dot(mlp_act, dy2, 0, 0)
-        down_shard = lax.ppermute(scatter_group(grad_w_down), AXIS_NAME, to_store)
         grad_act = dot(dy2, wd, 1, 1)
         grad_gate = (grad_act * up_proj * gate_sig * (1.0 + gate_pre * (1.0 - gate_sig))).astype(BF16)
         grad_up = (grad_act * gate_pre * gate_sig).astype(BF16)
         part_in = dot(grad_gate, w_g, 1, 1) + dot(grad_up, w_u, 1, 1)
         grad_mlp_in = part_in[:seq_len] + swap(part_in[seq_len:])
-        gate_shard = scatter_group(dot(mlp2, grad_gate, 0, 0))
-        up_shard = scatter_group(dot(mlp2, grad_up, 0, 0))
+        grad_w_gate = dot(mlp2, grad_gate, 0, 0)
+        grad_w_up = dot(mlp2, grad_up, 0, 0)
         part_y = dot(mlp_act, wd, 1, 0)
         layer_out = (hidden.astype(F32) + (part_y[:seq_len] + swap(part_y[seq_len:]))).astype(BF16)
 
@@ -181,12 +494,10 @@
         grad_attn_norm = jnp.sum(grad_attn_in * normed1, axis=0)
         grad_x_emb = grad_hidden + norm_bwd(grad_attn_in, normed1, norm1_inv, g_attn)
 
-        my_rows = gather_group(grad_x_emb)
-        other_rows = swap(my_rows)
-        seg = jnp.where(is_owner, local_ids, rows_local).reshape(n_chip, 2, seq_len)
-        seg_mine = lax.dynamic_slice(seg, (0, core, 0), (n_chip, 1, seq_len)).reshape(-1)
-        seg_other = lax.dynamic_slice(seg, (0, 1 - core, 0), (n_chip, 1, seq_len)).reshape(-1)
-        d_table = jax.ops.segment_sum(jnp.concatenate([my_rows, other_rows], axis=0), jnp.concatenate([seg_mine, seg_other]), num_segments=rows_local)
+        qk = jnp.pad(jnp.concatenate([grad_q_norm, grad_k_norm])[None], ((0, 7), (0, 0)))
+        all_dx, all_qk = gather_all([grad_x_emb, qk], [2, 1], n_dev, 4)
+        d_table = jax.ops.segment_sum(all_dx.reshape(-1, model_dim), jnp.where(is_owner, local_ids, rows_local), num_segments=rows_local)
+        qk = jnp.sum(all_qk[:, 0], axis=0)
 
         grad_w_query = dot(attn_in, grad_q_raw, 0, 0)
         grad_w_key = dot(attn_in, grad_k_raw, 0, 0)
@@ -195,9 +506,10 @@
         zeros = jnp.zeros_like(vecs)
         pack0 = jnp.concatenate([grad_w_query, grad_w_key, vecs], axis=1)
         pack1 = jnp.concatenate([grad_w_out, grad_w_value, zeros], axis=1)
-        keep_pack = jnp.where(core == 0, pack0, pack1)
-        give_pack = jnp.where(core == 0, pack1, pack0)
-        attn_shard = scatter_group(keep_pack + swap(give_pack))
+        packs = jnp.stack([pack0.reshape(n_chip, 2 * rows_w, -1), pack1.reshape(n_chip, 2 * rows_w, -1)], axis=1).reshape(n_dev, 2 * rows_w, -1)
+        by_chip = [v.reshape(n_chip, -1, v.shape[1]) for v in (grad_w_down, grad_w_gate, grad_w_up)]
+        down_rows, gate_shard, up_shard, attn_shard = scatter_sum(by_chip + [packs], [False, False, False, True], 3)
+        down_shard = lax.ppermute(down_rows, AXIS_NAME, to_store)
 
         chip_rows = jnp.concatenate([gate_shard, up_shard, attn_shard], axis=1)
         mine = lax.dynamic_slice(chip_rows, (core * rows_w, 0), (rows_w, chip_rows.shape[1]))
@@ -209,7 +521,6 @@
         d_query, d_key = low[:, ff:ff + nq], low[:, ff + nq:ff + nq + nk]
         d_attn_norm, d_mlp_norm = low[:, ff + nq + nk], low[:, ff + nq + nk + 1]
         d_out, d_value = high[:, ff:ff + nq], high[:, ff + nq:ff + nq + nk]
-        qk = lax.psum(jnp.concatenate([grad_q_norm, grad_k_norm]), AXIS_NAME)
         return (layer_out.reshape(1, seq_len, model_dim), d_table, d_attn_norm, d_query, d_key, d_value, qk[:head_dim], qk[head_dim:], d_out, d_mlp_norm, d_gate, d_up, down_shard)
 
     return jax.shard_map(device_step, mesh=mesh, in_specs=(row_spec, row_spec, row_spec) + weight_specs + (batch_spec,), out_specs=(batch_spec, row_spec) + weight_specs, check_vma=False)

time: 1990 us -> 1520 us (0.76)
  the two profiles are of different devices: /device:TPU:0 before, /device:TPU:17 now
where the time goes in v2:
time: 1520 us; the launch traced here: 1510 us
  Pallas kernels  924 us (61%)
  other arithmetic  217 us (14%)
  matrix products  153 us (10%)
  local copies, waits for them, and re-layouts  135 us (9%)
  starting transfers between devices  57.1 us (4%)
  between operations  15.6 us (1%)
    pallas_call x2, Pallas kernels, scatter_sum(): pl.pallas_call(functools.partial(_scatter_kernel, specs), out_shape=outs...  552 us
    pallas_call x2, Pallas kernels, gather_all(): pl.pallas_call(functools.partial(_gather_kernel, tuple(((v.shape[0], c) f...  359 us
    scatter-add x1, other arithmetic, device_step(): jax.ops.segment_sum(all_dx.reshape(-1, model_dim), jnp.where(is_owner, lo...  148 us
    dot_general x21, matrix products, dot(): lax.dot_general(a, b, (((ca,), (cb,)), ((), ())), preferred_element_type=...  114 us
    gather x1, local copies, waits for them, and re-layouts, device_step(): jnp.take(table_shard, jnp.clip(local_ids, 0, rows_local - 1), axis=0)  80.4 us
    ppermute x1, starting transfers between devices, device_step(): down_shard = lax.ppermute(down_rows, AXIS_NAME, to_store)  48.5 us
  transfers between devices with their start and end apart: 10, of which 1 were waited for; matrix products, arithmetic and copies ran while one was open for 23% of the time, Pallas kernels for 37%

profile of v2, /device:TPU:17, one launch (start us, length us, event | category | flops | bytes accessed | tf_op | source)
XLA Modules:
  0.0 1509.2 jit_solution(4002853852559410604)
XLA Ops:
  7.2 2.9 collective-permute-start.2
  10.1 8.0 collective-permute-done.2
  18.9 1.2 constant_dynamic-slice_fusion.3
  21.0 1.3 pad.16.in_ref
  22.3 12.7 all_rows.1
  39.8 34.3 %gather_all.2 = bf16[32,28,2176]{2,1,0:T(8,128)(2,1)S(1)} custom-call(bf16[28,2176]{1,0:T(8,128)(2,1)S(1)} %constant_dynamic-update-slice_fusion.refs_0_), custom_call_target="tpu_custom_call" | custom-call | flops 200000000 | bytes 7798784 | tf_op jit(solution)/shard_map/gather_all/pallas_call | solution.py:208
  74.1 2.1 copy-done
  76.2 6.1 reshape.668
  84.2 80.4 %gather_fusion = bf16[16384,896]{1,0:T(8,128)(2,1)} fusion(bf16[4752,896]{1,0:T(8,128)(2,1)} %param.17, s32[16384]{0:T(1024)S(1)} %broadcast_clamp_fusion), kind=kCustom, calls=%fused_computation | custom fusion | bytes 58785792 | tf_op jit(solution)/shard_map/jit(_take)/gather | solution.py:432
  164.6 20.4 %select_select_fusion.refs_0_ = bf16[32,512,896]{2,1,0:T(8,128)(2,1)} fusion(bf16[32,512,896]{2,1,0:T(8,128)(2,1)} %bitcast.177, pred[32,512]{1,0:T(8,128)(4,1)S(1)} %compare_and_fusion, pred[32,512]{1,0:T(8,128)(4,1)S(1)} %bitcast.206), kind=kLoop, calls=%fused_computation.2 | loop fusion | flops 29360128 | bytes 58753024 | tf_op jit(solution)/shard_map/jit(_where)/select_n | solution.py:433
  185.0 192.2 %scatter_sum.2 = (bf16[512,896]{1,0:T(8,128)(2,1)S(1)}, bf16[8,512,896]{2,1,0:T(8,128)(2,1)}, bf16[4,512,896]{2,1,0:T(8,128)(2,1)}, bf16[3,512,896]{2,1,0:T(8,128)(2,1)}, bf16[16,512,896]{2,1,0:T(8,128)(2,1)}) custom-call(bf16[32,512,896]{2,1,0:T(8,128)(2,1)} %select_select_fusion.refs_0_), custom_call_target="tpu_custom_call" | custom-call | flops 200000000 | bytes 84410368 | tf_op jit(solution)/shard_map/scatter_sum/pallas_call | solution.py:373
  377.8 2.5 fusion.53
  380.3 1.8 copy.59
  382.4 1.8 fusion.64
  385.6 1.5 convolution_convert_fusion.3
  388.0 6.8 fusion.6
  394.9 8.2 fusion.5
  403.1 7.6 fusion.50
  410.6 3.1 fusion.45
  413.8 1.2 fusion.39
  415.0 1.3 collective-permute-start
  416.3 1.5 mul.604
  417.8 2.7 copy.66
  421.3 10.6 fusion.60
  431.9 10.1 fusion.17
  442.0 17.0 %multiply_convert_fusion.1 = (bf16[1024,2432]{1,0:T(8,128)(2,1)}, bf16[1024,2432]{1,0:T(8,128)(2,1)}, bf16[1024,2432]{1,0:T(8,128)(2,1)}) fusion(f32[1024,2432]{1,0:T(8,128)} %fusion.60, f32[1024,2432]{1,0:T(8,128)} %fusion.17, bf16[896,4864]{1,0:T(8,128)(2,1)} %all-gather.3.cloned.1.call-done, bf16[512,896]{1,0:T(8,128)(2,1)} %collective-permute-done, ...), kind=kOutput, calls=%fused_computation.15 | convolution fusion | flops 4506255360 | bytes 41058304 | tf_op jit(solution)/shard_map/dot_general | solution.py:68
  459.0 8.9 fusion.15
  467.9 5.5 fusion.47
  473.7 7.5 fusion.107
  482.1 9.3 fusion.91
  491.5 8.8 fusion.92
  500.3 9.1 fusion.59
  509.4 1.3 fusion.44
  510.7 3.0 fusion.43
  513.6 4.2 convolution_convert_fusion
  517.8 2.3 copy.61
  520.1 13.4 fusion
  534.9 8.2 fusion.9
  543.1 1.4 convolution_bitcast_fusion
  544.6 2.3 convolution_bitcast_fusion.1
  548.3 2.7 fusion.78
  551.3 1.7 pad_maximum_fusion.4
  553.0 1.5 mul.621
  554.5 2.7 copy.65
  557.2 2.7 copy.63
  560.0 3.6 multiply_reduce_fusion
  563.6 1.3 fusion.99
  564.9 2.7 fusion.56
  567.6 7.5 fusion.65
  575.2 2.9 fusion.72
  578.6 3.1 fusion.36
  581.7 2.3 pad_maximum_fusion.1
  583.9 5.6 copy.70
  589.6 4.2 maximum_maximum_fusion
  593.8 5.7 copy.71
  599.5 4.0 pad_maximum_fusion
  603.5 3.9 copy.72
  607.3 360.0 %scatter_sum.3 = (f32[152,896]{1,0:T(8,128)S(1)}, f32[56,2432]{1,0:T(8,128)S(1)}, f32[56,2432]{1,0:T(8,128)S(1)}, f32[56,1152]{1,0:T(8,128)S(1)}, f32[8,152,896]...) custom-call(f32[16,152,896]{2,1,0:T(8,128)} %bitcast.188, ...), custom_call_target="tpu_custom_call" | custom-call | flops 200000000 | bytes 174096384 | tf_op jit(solution)/shard_map/scatter_sum/pallas_call | solution.py:373
  968.5 2.7 collective-permute-start.6
  971.2 48.5 %collective-permute-start.7 = (f32[152,896]{1,0:T(8,128)S(1)}, f32[152,896]{1,0:T(8,128)}, u32[]{:S(2)}, u32[]{:S(2)}) collective-permute-start(f32[152,896]{1,0:T(8,128)S(1)} %get-tuple-element.26), channel_id=1, source_target_pairs={{0,0},{2,1},{4,2},{6,3},{8,4},{10,5},{12,6},{14,7},{16,8},{18,9},{... | collective-permute-start | bytes 1634312 | tf_op jit(solution)/shard_map/ppermute | solution.py:512
  1020.6 325.0 %gather_all.3 = (f32[32,512,896]{2,1,0:T(8,128)}, f32[32,8,128]{2,1,0:T(8,128)S(1)}) custom-call(f32[512,896]{1,0:T(8,128)S(1)} %fusion.35.refs_0_, f32[8,128]{1,0:T(8,128)S(1)} %pad.18.refs_1_), custom_call_target="tpu_custom_call" | custom-call | flops 200000000 | bytes 117702656 | tf_op jit(solution)/shard_map/gather_all/pallas_call | solution.py:208
  1345.6 147.5 %scatter_custom_fusion = f32[4752,896]{1,0:T(8,128)} fusion(s32[16384]{0:T(1024)} %bitcast.207, f32[16384,896]{1,0:T(8,128)} %bitcast.211, f32[]{:T(128)} %constant.26.clone.1), kind=kCustom, calls=%fused_computation.18 | custom fusion | flops 14680064 | bytes 17031680 | tf_op jit(solution)/shard_map/scatter-add | solution.py:499
  1493.7 1.3 dynamic-slice_select_fusion
  1500.1 1.9 copy.95
  (216 shorter events, 24.3 us)
Async XLA Ops:
  7.2 414.1 %all-gather.5.cloned.1.call-start = ((), (), s32[]{:S(2)}) async-start(), calls=%async_computation.1 | async-start | bytes 4630528 | tf_op jit(solution)/shard_map/all_gather | solution.py:404
  7.2 10.9 collective-permute-start.2
  18.9 413.0 %all-gather.3.cloned.1.call-start = ((), (), s32[]{:S(2)}) async-start(), calls=%async_computation | async-start | bytes 9261056 | tf_op jit(solution)/shard_map/all_gather | solution.py:404
  20.2 62.1 %collective-permute-start.1 = (bf16[28,4864]{1,0:T(8,128)(2,1)S(1)}, bf16[28,4864]{1,0:T(8,128)(2,1)S(1)}, u32[]{:S(2)}, u32[]{:S(2)}) collective-permute-start(bf16[28,4864]{1,0:T(8,128)(2,1)S(1)} %pad_maximum_fusion.12), channel_id=1, source_target_pairs={{0,1},{1,0},{2,3},{3,2},{4,5},{5,4},{6,7},{7,6},{8,9},{9,8},{10,11... | collective-permute-start | bytes 817160 | tf_op jit(solution)/shard_map/ppermute | solution.py:401
  20.9 400.4 %collective-permute-start.4 = (bf16[512,896]{1,0:T(8,128)(2,1)}, bf16[512,896]{1,0:T(8,128)(2,1)}, u32[]{:S(2)}, u32[]{:S(2)}) collective-permute-start(bf16[512,896]{1,0:T(8,128)(2,1)} %bitcast.194), channel_id=1, source_target_pairs={{0,1},{1,0},{2,3},{3,2},{4,5},{5,4},{6,7},{7,6},{8,9},{9,8},{10,11... | collective-permute-start | bytes 2752520 | tf_op jit(solution)/shard_map/ppermute | solution.py:401
  185.0 192.2 %copy-start.8 = (bf16[896,2176]{1,0:T(8,128)(2,1)S(1)}, bf16[896,2176]{1,0:T(8,128)(2,1)}, u32[]{:S(2)}) copy-start(bf16[896,2176]{1,0:T(8,128)(2,1)} %reshape.668) | copy-start | bytes 11698180
  377.5 8.1 copy-start.30
  377.8 7.8 copy-start.36
  377.8 4.4 copy-start.45
  377.8 4.4 copy-start.40
  377.8 4.4 copy-start.48
  382.2 5.0 copy-start.1
  382.2 5.0 copy-start.43
  382.2 4.9 copy-start.41
  384.5 3.5 copy-start.34
  385.4 2.5 copy-start.17
  385.6 2.4 copy-start.26
  385.6 2.4 copy-start.28
  388.0 6.9 copy-start.13
  388.0 6.9 copy-start.15
  403.0 130.5 %copy-start.32 = (f32[2,7,512]{2,1,0:T(8,128)}, f32[2,7,512]{2,1,0:T(8,128)S(1)}, u32[]{:S(2)}) copy-start(f32[2,7,512]{2,1,0:T(8,128)S(1)} %fusion.5) | copy-start | bytes 86020
  410.6 3.1 copy-start.22
  413.8 95.6 %copy-start.5 = (bf16[512,896]{1,0:T(8,128)(2,1)}, bf16[512,896]{1,0:T(8,128)(2,1)S(1)}, u32[]{:S(2)}) copy-start(bf16[512,896]{1,0:T(8,128)(2,1)S(1)} %get-tuple-element.78) | copy-start | bytes 2752516
  413.8 7.5 copy-start.19
  415.0 16.8 %collective-permute-start = (bf16[512,896]{1,0:T(8,128)(2,1)}, bf16[512,896]{1,0:T(8,128)(2,1)}, u32[]{:S(2)}, u32[]{:S(2)}) collective-permute-start(bf16[512,896]{1,0:T(8,128)(2,1)} %fusion.39), channel_id=1, source_target_pairs={{0,1},{1,0},{2,3},{3,2},{4,5},{5,4},{6,7},{7,6},{8,9},{9,8},{10,11... | collective-permute-start | bytes 2752520 | tf_op jit(solution)/shard_map/ppermute | solution.py:401
  459.0 8.9 copy-start.47
  459.0 8.9 copy-start.49
  459.0 14.6 slice-start.4
  467.9 5.8 slice-start.5
  473.4 8.7 slice-start.6
  473.6 35.8 %collective-permute-start.5 = (f32[512,896]{1,0:T(8,128)S(1)}, f32[512,896]{1,0:T(8,128)S(1)}, u32[]{:S(2)}, u32[]{:S(2)}) collective-permute-start(f32[512,896]{1,0:T(8,128)S(1)} %slice.153), channel_id=1, source_target_pairs={{0,1},{1,0},{2,3},{3,2},{4,5},{5,4},{6,7},{7,6},{8,9},{9,8},{10,11... | collective-permute-start | bytes 5505032 | tf_op jit(solution)/shard_map/ppermute | solution.py:401
  473.7 8.4 slice-start.7
  481.4 29.3 %collective-permute-start.3 = (f32[512,896]{1,0:T(8,128)S(1)}, f32[512,896]{1,0:T(8,128)S(1)}, u32[]{:S(2)}, u32[]{:S(2)}) collective-permute-start(f32[512,896]{1,0:T(8,128)S(1)} %slice.151), channel_id=1, source_target_pairs={{0,1},{1,0},{2,3},{3,2},{4,5},{5,4},{6,7},{7,6},{8,9},{9,8},{10,11... | collective-permute-start | bytes 5505032 | tf_op jit(solution)/shard_map/ppermute | solution.py:401
  482.1 18.2 %slice-start.8 = ((s8[4980736]{0:T(1024)(128)(4,1)}), s8[4194304]{0:T(1024)(128)(4,1)S(1)}, s32[]{:S(2)}) async-start(s8[4980736]{0:T(1024)(128)(4,1)} %bitcast.220), calls=%async_computation.10 | async-start | bytes 8388608
  491.4 8.8 slice-start.9
  513.6 61.5 %copy-start.3 = (f32[512,896]{1,0:T(8,128)}, f32[512,896]{1,0:T(8,128)S(1)}, u32[]{:S(2)}) copy-start(f32[512,896]{1,0:T(8,128)S(1)} %get-tuple-element.50) | copy-start | bytes 5505028
  520.1 13.4 slice-start
  520.1 13.4 slice-start.1
  520.1 13.7 slice-start.2
  520.1 14.8 slice-start.3
  534.9 8.2 copy-start.27
  534.9 8.2 copy-start.29
  544.5 2.4 copy-start.18
  544.6 2.4 copy-start.24
  544.6 2.4 copy-start.10
  544.6 2.4 copy-start.35
  544.6 2.4 copy-start.42
  544.6 3.2 copy-start.31
  544.6 3.2 copy-start.37
  547.8 3.5 copy-start.2
  547.8 3.5 copy-start.44
  564.9 2.8 copy-start.21
  564.9 2.8 copy-start.33
  567.6 7.5 copy-start.23
  575.2 3.3 copy-start.7
  578.5 3.1 copy-start.39
  583.9 5.7 copy-start.38
  967.4 52.3 %copy-start.4 = (f32[512,896]{1,0:T(8,128)S(1)}, f32[512,896]{1,0:T(8,128)}, u32[]{:S(2)}) copy-start(f32[512,896]{1,0:T(8,128)} %copy-done.3) | copy-start | bytes 5505028
  967.4 52.3 %copy-start.6 = (f32[512,896]{1,0:T(8,128)S(1)}, f32[512,896]{1,0:T(8,128)}, u32[]{:S(2)}) copy-start(f32[512,896]{1,0:T(8,128)} %get-tuple-element.81) | copy-start | bytes 5505028
  967.5 52.8 %copy-start.11 = (f32[56,6016]{1,0:T(8,128)}, f32[56,6016]{1,0:T(8,128)S(1)}, u32[]{:S(2)}) copy-start(f32[56,6016]{1,0:T(8,128)S(1)} %constant_dynamic-update-slice_fusion.5) | copy-start | bytes 4042756
  967.5 52.8 %copy-start.46 = (f32[128]{0:T(128)S(1)}, f32[128]{0:T(128)}, u32[]{:S(2)}) copy-start(f32[128]{0:T(128)} %get-tuple-element.56) | copy-start | bytes 1540
  968.5 525.3 %collective-permute-start.6 = (f32[28,6016]{1,0:T(8,128)}, f32[28,6016]{1,0:T(8,128)}, u32[]{:S(2)}, u32[]{:S(2)}) collective-permute-start(f32[28,6016]{1,0:T(8,128)} %constant_dynamic-slice_fusion), channel_id=1, source_target_pairs={{0,1},{1,0},{2,3},{3,2},{4,5},{5,4},{6,7},{7,6},{8,9},{9,8},{10,11... | collective-permute-start | bytes 2021384 | tf_op jit(solution)/shard_map/ppermute | solution.py:401
  971.2 522.5 %collective-permute-start.7 = (f32[152,896]{1,0:T(8,128)S(1)}, f32[152,896]{1,0:T(8,128)}, u32[]{:S(2)}, u32[]{:S(2)}) collective-permute-start(f32[152,896]{1,0:T(8,128)S(1)} %get-tuple-element.26), channel_id=1, source_target_pairs={{0,0},{2,1},{4,2},{6,3},{8,4},{10,5},{12,6},{14,7},{16,8},{18,9},{... | collective-permute-start | bytes 1634312 | tf_op jit(solution)/shard_map/ppermute | solution.py:512
  1345.6 148.2 %copy-start.12 = (f32[56,6016]{1,0:T(8,128)S(1)}, f32[56,6016]{1,0:T(8,128)}, u32[]{:S(2)}) copy-start(f32[56,6016]{1,0:T(8,128)} %copy-done.11) | copy-start | bytes 4042756
  (6 other events, 8.4 us)
Sparse Core Ops, SparseCore 0:
  19.0 84.7 all-gather.4
  107.0 116.5 all-gather.2

commit v3 on v1

--- a/solution.py
+++ b/solution.py
@@ -1,7 +1,10 @@
+import functools
 import math
 import jax
 import jax.numpy as jnp
 from jax import lax
+from jax.experimental import pallas as pl
+from jax.experimental.pallas import tpu as pltpu
 from jax.sharding import PartitionSpec as P
 
 NORM_EPS = 1e-6
@@ -9,6 +12,7 @@
 AXIS_NAME = 'fsdp'
 F32 = jnp.float32
 BF16 = jnp.bfloat16
+MESH = pl.DeviceIdType.MESH
 
 
 def rope_tables(positions, head_dim):
@@ -64,13 +68,391 @@
     return lax.dot_general(a, b, (((ca,), (cb,)), ((), ())), preferred_element_type=F32)
 
 
+def _unpack(code):
+    return code // 64, code // 32 % 2, code // 8 % 4, code % 8
+
+
+def _via(u, key, orders):
+    da, db, p, piece = key
+    last = None
+    for axis in orders[piece]:
+        if axis == 'a' and da or axis == 'b' and db:
+            last = axis
+        if axis == 'z' and p != u:
+            last = 'z+' if p > u else 'z-'
+    return last
+
+
+def _onward(u, key, orders):
+    order = orders[key[3]]
+    via = _via(u, key, orders)
+    left = order if via is None else order[order.index(via[0]) + 1:]
+    out = []
+    if u < 3 and (via == 'z-' or 'z' in left):
+        out.append('z+')
+    if u > 0 and (via == 'z+' or 'z' in left):
+        out.append('z-')
+    return out + [axis for axis in 'ba' if axis in left]
+
+
+def _seen_by_parent(u, key, orders):
+    da, db, p, piece = key
+    via = _via(u, key, orders)
+    if via == 'a':
+        return u, (0, db, p, piece), 'a'
+    if via == 'b':
+        return u, (da, 0, p, piece), 'b'
+    if via == 'z-':
+        return u - 1, key, 'z+'
+    if u == 0:
+        return 1, key, 'z-'
+    return 1, (da, db, 3 - p, piece), 'z+'
+
+
+class _Place:
+    def __init__(self, me, swapped=False):
+        self.me = me
+        self.core = me % 2
+        x, y, self.z = (me // 2) % 2, (me // 4) % 2, me // 8
+        other = 1 - self.core if swapped else self.core
+        self.a = y * (1 - other) + x * other
+        self.b = x * (1 - other) + y * other
+        self.a_str, self.b_str = 4 - 2 * other, 2 + 2 * other
+        self.far = self.z // 2
+        self.u = 3 * self.far + (1 - 2 * self.far) * self.z
+        self.partner = me + 1 - 2 * self.core
+
+    def chip(self, key):
+        da, db, p = key[:3]
+        a = self.a + da * (1 - 2 * self.a)
+        b = self.b + db * (1 - 2 * self.b)
+        z = 3 * self.far + (1 - 2 * self.far) * p
+        return (8 * z + a * self.a_str + b * self.b_str) // 2
+
+    def side(self, name):
+        if name == 'a':
+            return self.me + (1 - 2 * self.a) * self.a_str
+        if name == 'b':
+            return self.me + (1 - 2 * self.b) * self.b_str
+        return self.me + 8 * (1 - 2 * self.far) * (1 if name == 'z+' else -1)
+
+
+def _remote(src, dst, send_sem, recv_sem, dev):
+    return pltpu.make_async_remote_copy(src_ref=src, dst_ref=dst, send_sem=send_sem, recv_sem=recv_sem, device_id=(dev,), device_id_type=MESH)
+
+
+def _meet(peers, me=None, ends=()):
+    sem = pltpu.get_barrier_semaphore()
+
+    def meet(everyone):
+        for peer in everyone:
+            pl.semaphore_signal(sem, inc=1, device_id=(peer,), device_id_type=MESH)
+        pl.semaphore_wait(sem, len(everyone))
+
+    if not ends:
+        meet(peers)
+        return
+    to, frm = ends
+    pl.when(to != me)(lambda: meet(peers + [to, frm]))
+    pl.when(to == me)(lambda: meet(peers))
+
+
+def _landed(ref, sem):
+    pltpu.make_async_copy(ref, ref, sem).wait()
+
+
+def _passes(moves, me):
+    for kind in moves:
+        if kind == 'pair':
+            other = me + 1 - 2 * (me % 2)
+            yield other, other
+        elif kind == 'use':
+            yield 2 * (me % 16) + me // 16, 16 * (me % 2) + me // 2
+        else:
+            yield 16 * (me % 2) + me // 2, 2 * (me % 16) + me // 16
+
+
+def _start_move(kind, src, dst, send_sem, recv_sem, to, me):
+    copy = _remote(src, dst, send_sem, recv_sem, to)
+    if kind == 'pair':
+        copy.start()
+    else:
+        pl.when(to != me)(copy.start)
+        pl.when(to == me)(pltpu.make_async_copy(src, dst, recv_sem).start)
+    return copy
+
+
+def _end_move(kind, copy, dst, recv_sem, to, me):
+    _landed(dst, recv_sem)
+    if kind == 'pair':
+        copy.wait_send()
+    else:
+        pl.when(to != me)(copy.wait_send)
+
+
+def _all_rows_kernel(n_dev, moves, *refs):
+    n = len(moves)
+    in_ref, src, out_ref, dst = refs[0], refs[1:1 + n], refs[1 + n], refs[2 + n:2 + 2 * n]
+    send_sem, recv_sem, m_send, m_recv = refs[2 + 2 * n:]
+    me = lax.axis_index(AXIS_NAME)
+    peers = [(me + d) % n_dev for d in range(1, n_dev)]
+    _meet(peers)
+    copies = [_remote(in_ref, out_ref.at[me], send_sem.at[i], recv_sem.at[i], peer) for i, peer in enumerate(peers)]
+    for copy in copies:
+        copy.start()
+    ends = [to for to, _ in _passes(moves, me)]
+    moving = [_start_move(moves[i], src[i], dst[i], m_send.at[i], m_recv.at[i], to, me) for i, to in enumerate(ends)]
+    out_ref[me] = in_ref[...]
+    for copy in copies:
+        copy.wait()
+    for i, copy in enumerate(moving):
+        _end_move(moves[i], copy, dst[i], m_recv.at[i], ends[i], me)
+
+
+def all_rows(block, n_dev, moved, moves, collective_id):
+    n = len(moves)
+    dma = pltpu.SemaphoreType.DMA
+    vmem, hbm = pl.BlockSpec(memory_space=pltpu.VMEM), pl.BlockSpec(memory_space=pl.ANY)
+    res = pl.pallas_call(
+        functools.partial(_all_rows_kernel, n_dev, moves),
+        out_shape=[jax.ShapeDtypeStruct((n_dev,) + block.shape, block.dtype)] + [jax.ShapeDtypeStruct(v.shape, v.dtype) for v in moved],
+        in_specs=[vmem] + [hbm] * n,
+        out_specs=[vmem] + [hbm] * n,
+        scratch_shapes=[dma((n_dev - 1,)), dma((n_dev - 1,)), dma((n,)), dma((n,))],
+        compiler_params=pltpu.CompilerParams(collective_id=collective_id, has_side_effects=True),
+        cost_estimate=pl.CostEstimate(flops=10_000_000, bytes_accessed=1 << 20, transcendentals=0),
+        name='all_rows',
+    )(block, *moved)
+    return res[0], res[1:]
+
+
+def _gather_kernel(cuts, orders, seq, moves, *refs):
+    n = len(moves)
+    in_ref, src, out_ref, dst = refs[0], refs[1:1 + n], refs[1 + n], refs[2 + n:2 + 2 * n]
+    own_sem, send_sem, recv_sem, p_send, p_recv, m_send, m_recv = refs[2 + 2 * n:]
+    me = lax.axis_index(AXIS_NAME)
+    at = _Place(me)
+    ends = list(_passes(moves, me))
+    starts = [sum(cuts[:i]) for i in range(len(cuts))]
+
+    def part(slot, piece):
+        return out_ref.at[slot] if len(cuts) == 1 else out_ref.at[slot, pl.ds(starts[piece], cuts[piece])]
+
+    def run(u):
+        sides = ['a', 'b', 'z+'] + (['z-'] if u else [])
+        far = [end for kind, end in zip(moves, ends) if kind != 'pair']
+        _meet([at.side(s) for s in sides] + [at.partner], me, far[0] if far else ())
+        started, moving = [], []
+
+        def send(src_ref, slot, piece, s_sem, r_sem, dev):
+            copy = _remote(src_ref, part(slot, piece), s_sem, r_sem, dev)
+            copy.start()
+            started.append(copy)
+
+        own = pltpu.make_async_copy(in_ref, out_ref.at[me], own_sem)
+        own.start()
+        count, handed = 0, [0] * len(cuts)
+        for key in [(0, 0, u, i) for i in range(len(cuts))] + [_unpack(c) for c in seq[u]]:
+            piece = key[3]
+            kc = at.chip(key)
+            slot = 2 * kc + at.core
+            if _via(u, key, orders) is None:
+                ref = in_ref if len(cuts) == 1 else in_ref.at[pl.ds(starts[piece], cuts[piece])]
+            else:
+                ref = part(slot, piece)
+                _landed(ref, recv_sem.at[piece, kc])
+            for side in _onward(u, key, orders):
+                send(ref, slot, piece, send_sem.at[count], recv_sem.at[piece, kc], at.side(side))
+                count += 1
+            send(ref, slot, piece, p_send.at[piece, handed[piece]], p_recv.at[piece, kc], at.partner)
+            handed[piece] += 1
+            if key[:3] == (0, 0, u) and piece == len(cuts) - 1:
+                for i, (to, _) in enumerate(ends):
+                    moving.append(_start_move(moves[i], src[i], dst[i], m_send.at[i], m_recv.at[i], to, me))
+        for piece in range(len(cuts)):
+            for kc in range(16):
+                _landed(part(2 * kc + 1 - at.core, piece), p_recv.at[piece, kc])
+        for i, (to, _) in enumerate(ends):
+            _end_move(moves[i], moving[i], dst[i], m_recv.at[i], to, me)
+        own.wait()
+        for copy in started:
+            copy.wait_send()
+
+    for u in (0, 1):
+        pl.when(at.u == u)(functools.partial(run, u))
+
+
+def gather_all(block, cuts, orders, seq, moved, moves, n_dev, collective_id):
+    n, m = len(moves), len(cuts)
+    dma = pltpu.SemaphoreType.DMA
+    vmem, hbm = pl.BlockSpec(memory_space=pltpu.VMEM), pl.BlockSpec(memory_space=pl.ANY)
+    nbytes = block.size * block.dtype.itemsize
+    res = pl.pallas_call(
+        functools.partial(_gather_kernel, cuts, orders, seq, moves),
+        out_shape=[jax.ShapeDtypeStruct((n_dev,) + block.shape, block.dtype)] + [jax.ShapeDtypeStruct(v.shape, v.dtype) for v in moved],
+        in_specs=[vmem] + [hbm] * n,
+        out_specs=[hbm] * (1 + n),
+        scratch_shapes=[dma, dma((24 * m,)), dma((m, 16)), dma((m, 16)), dma((m, 16)), dma((max(n, 1),)), dma((max(n, 1),))],
+        compiler_params=pltpu.CompilerParams(collective_id=collective_id, has_side_effects=True, vmem_limit_bytes=nbytes + (8 << 20)),
+        cost_estimate=pl.CostEstimate(flops=200_000_000, bytes_accessed=nbytes * 64, transcendentals=0),
+        name='gather_all',
+    )(block, *moved)
+    return res[0], res[1:]
+
+
+def _slots(pieces, orders, seq):
+    table, most = {}, [1] * len(pieces)
+    for u in (0, 1):
+        used = [0] * len(pieces)
+        for key in [_unpack(c) for c in reversed(seq[u])] + [(0, 0, u, i) for i in range(len(pieces))]:
+            for side in _onward(u, key, orders):
+                table[u, key, side] = used[key[3]]
+                used[key[3]] += 1
+        most = [max(a, b) for a, b in zip(most, used)]
+    return table, most
+
+
+def _scatter_kernel(pieces, orders, seq, n_arr, *refs):
+    table, _ = _slots(pieces, orders, seq)
+    n = len(pieces)
+    n_pair = sum(1 for p in pieces if p[3])
+    ins, outs = refs[:n_arr], refs[n_arr:2 * n_arr]
+    k = 2 * n_arr
+    land, stage, pair = refs[k:k + n], refs[k + n:k + 2 * n], list(refs[k + 2 * n:k + 2 * n + n_pair])
+    load_sem, send_sem, recv_sem, d_send, d_recv = refs[k + 2 * n + n_pair:]
+    got = [pair.pop(0) if p[3] else None for p in pieces]
+    me = lax.axis_index(AXIS_NAME)
+    at, partner_at = _Place(me), _Place(me, swapped=True)
+
+    def rows_of(ref, piece):
+        arr, r0, rows, _ = pieces[piece]
+        return ref if rows == ins[arr].shape[1] else ref.at[pl.ds(r0, rows)]
+
+    def term(piece, kc, core):
+        arr, _, _, paired = pieces[piece]
+        return rows_of(ins[arr].at[2 * kc + core if paired else kc], piece)
+
+    def run(u):
+        sides = ['a', 'b', 'z+'] + (['z-'] if u else [])
+        _meet([at.side(s) for s in sides] + [at.partner])
+        keys = [_unpack(c) for c in reversed(seq[u])] + [(0, 0, u, i) for i in range(n)]
+        started = []
+        given = [0] * n
+        for key in keys:
+            piece = key[3]
+            if pieces[piece][3]:
+                kc = partner_at.chip(key)
+                copy = _remote(term(piece, kc, 1 - at.core), got[piece].at[kc], d_send.at[piece, given[piece]], d_recv.at[piece, kc], at.partner)
+                given[piece] += 1
+                copy.start()
+                started.append(copy)
+        adds = [[key for key in keys if key[3] == i and (pieces[i][3] or _onward(u, key, orders))] for i in range(n)]
+
+        def load(piece, j):
+            return pltpu.make_async_copy(term(piece, at.chip(adds[piece][j]), at.core), stage[piece].at[j % 2], load_sem.at[piece, j % 2])
+
+        for i in range(n):
+            for j in range(2):
+                load(i, j).start()
+        done = [0] * n
+        count = 0
+        for key in keys:
+            piece = key[3]
+            arr, r0, rows, paired = pieces[piece]
+            kc = at.chip(key)
+            children = _onward(u, key, orders)
+            if not children and not paired:
+                src = term(piece, kc, at.core)
+            else:
+                j = done[piece]
+                done[piece] += 1
+                parts = []
+                if paired:
+                    _landed(got[piece].at[kc], d_recv.at[piece, kc])
+                    parts.append(got[piece].at[kc])
+                for side in children:
+                    slot = table[u, key, side]
+                    _landed(land[piece].at[slot], recv_sem.at[piece, slot])
+                    parts.append(land[piece].at[slot])
+                load(piece, j).wait()
+                parts.append(stage[piece].at[j % 2])
+                root = key[:3] == (0, 0, u)
+                src = rows_of(outs[arr], piece) if root else parts[0]
+                dtype = ins[arr].dtype
+                step = 8 if dtype == F32 else 16
+
+                def body(r, _, parts=parts, dst=src, step=step, dtype=dtype):
+                    some = pl.ds(pl.multiple_of(r * step, step), step)
+                    total = parts[0][some, :].astype(F32)
+                    for ref in parts[1:]:
+                        total = total + ref[some, :].astype(F32)
+                    dst[some, :] = total.astype(dtype)
+                    return 0
+
+                lax.fori_loop(0, rows // step, body, 0)
+                if j + 2 < len(adds[piece]):
+                    load(piece, j + 2).start()
+                if root:
+                    continue
+            side = _via(u, key, orders)
+            slot = table[_seen_by_parent(u, key, orders)]
+            copy = _remote(src, land[piece].at[slot], send_sem.at[count], recv_sem.at[piece, slot], at.side(side))
+            copy.start()
+            started.append(copy)
+            count += 1
+        for copy in started:
+            copy.wait_send()
+
+    for u in (0, 1):
+        pl.when(at.u == u)(functools.partial(run, u))
+
+
+def scatter_sum(arrays, pieces, orders, seq, collective_id):
+    n_arr, n = len(arrays), len(pieces)
+    dma, hbm, vmem = pltpu.SemaphoreType.DMA, pl.BlockSpec(memory_space=pl.ANY), pl.BlockSpec(memory_space=pltpu.VMEM)
+    _, most = _slots(pieces, orders, seq)
+    shapes = [(rows, arrays[arr].shape[2], arrays[arr].dtype) for arr, _, rows, _ in pieces]
+    scratch = [pltpu.VMEM((m, r, c), d) for m, (r, c, d) in zip(most, shapes)]
+    scratch += [pltpu.VMEM((2, r, c), d) for r, c, d in shapes]
+    scratch += [pltpu.VMEM((16, r, c), d) for (r, c, d), p in zip(shapes, pieces) if p[3]]
+    nbytes = sum(v.size // v.shape[0] * v.dtype.itemsize for v in arrays) + sum(
+        (m + 2 + 16 * int(p[3])) * (-(-r // 16) * 16) * c * d.itemsize for m, (r, c, d), p in zip(most, shapes, pieces))
+    scratch += [dma((n, 2)), dma((16 * n,)), dma((n, max(most))), dma((n, 16)), dma((n, 16))]
+    return pl.pallas_call(
+        functools.partial(_scatter_kernel, tuple(pieces), orders, seq, n_arr),
+        out_shape=[jax.ShapeDtypeStruct(v.shape[1:], v.dtype) for v in arrays],
+        in_specs=[hbm] * n_arr,
+        out_specs=[vmem] * n_arr,
+        scratch_shapes=scratch,
+        compiler_params=pltpu.CompilerParams(collective_id=collective_id, has_side_effects=True, vmem_limit_bytes=nbytes + (6 << 20)),
+        cost_estimate=pl.CostEstimate(flops=200_000_000, bytes_accessed=nbytes * 4, transcendentals=0),
+        name='scatter_sum',
+    )(*arrays)
+
+
+ROWS_SEQ = (
+    (8, 32, 64, 9, 33, 65, 10, 34, 66, 16, 40, 72, 96, 17, 41, 48, 18, 42, 74, 73, 97, 49, 98, 24, 80, 104, 25, 56, 57, 81, 105, 26, 50, 82, 112, 113, 58, 90, 88, 89, 122, 120, 106, 121, 114),
+    (0, 16, 40, 72, 1, 17, 41, 73, 2, 18, 42, 74, 24, 34, 66, 32, 48, 64, 80, 25, 104, 26, 50, 82, 33, 49, 58, 90, 56, 65, 81, 105, 98, 122, 57, 106, 114, 88, 96, 112, 89, 97, 113, 120, 121),
+)
+ATTN_SEQ = (
+    (8, 32, 64, 16, 40, 72, 96, 24, 48, 80, 104, 56, 88, 112, 120),
+    (0, 16, 40, 72, 24, 32, 48, 64, 80, 104, 56, 88, 96, 112, 120),
+)
+LOOKUP_SEQ = (
+    (8, 32, 64, 9, 33, 65, 10, 34, 66, 16, 40, 72, 96, 17, 41, 48, 18, 42, 74, 73, 97, 49, 98, 24, 80, 104, 25, 56, 26, 50, 82, 81, 105, 57, 112, 58, 90, 113, 88, 106, 89, 122, 120, 114, 121),
+    (0, 16, 40, 72, 1, 17, 41, 73, 2, 18, 42, 74, 24, 34, 66, 32, 48, 64, 80, 104, 25, 26, 50, 82, 33, 49, 58, 90, 65, 81, 56, 105, 98, 57, 106, 122, 88, 96, 114, 112, 89, 97, 113, 120, 121),
+)
+GRAD_SEQ = (
+    (8, 32, 64, 9, 33, 65, 10, 34, 66, 11, 35, 67, 41, 16, 40, 72, 96, 42, 73, 97, 17, 18, 74, 98, 49, 19, 43, 75, 99, 50, 105, 80, 104, 24, 48, 106, 81, 82, 25, 113, 26, 57, 114, 27, 51, 83, 58, 88, 112, 89, 56, 90, 59, 91, 121, 122, 107, 120, 123, 115),
+    (0, 16, 40, 72, 1, 17, 41, 73, 2, 18, 42, 74, 3, 19, 43, 75, 32, 24, 33, 48, 49, 35, 67, 64, 80, 104, 25, 34, 50, 26, 27, 51, 83, 65, 81, 57, 105, 99, 58, 56, 106, 66, 82, 59, 91, 107, 123, 115, 96, 88, 113, 97, 112, 89, 98, 114, 90, 121, 122, 120),
+)
+
+
 def solution(mesh):
     n_dev = mesh.shape[AXIS_NAME]
     n_chip = n_dev // 2
     pair = [(i, i ^ 1) for i in range(n_dev)]
     groups = [[2 * k + c for k in range(n_chip)] for c in range(2)]
-    to_use = [(d, 2 * (d % n_chip) + d // n_chip) for d in range(n_dev)]
-    to_store = [(b, a) for a, b in to_use]
 
     row_spec = P(AXIS_NAME, None)
     vec_spec = P(AXIS_NAME)
@@ -83,9 +465,6 @@
 
     def gather_group(v):
         return lax.all_gather(v, AXIS_NAME, axis_index_groups=groups, tiled=True)
-
-    def scatter_group(v):
-        return lax.psum_scatter(v, AXIS_NAME, scatter_dimension=0, axis_index_groups=groups, tiled=True)
 
     def device_step(tokens, positions, table_shard, attn_norm, w_query, w_key, w_value, q_norm, k_norm, w_out, mlp_norm, w_gate, w_up, w_down, dy_out):
         me = lax.axis_index(AXIS_NAME)
@@ -99,28 +478,28 @@
         kv_heads = nk // head_dim
         q_per_kv = nq // nk
 
+        mine_gu = jnp.concatenate([lax.dynamic_slice(w_gate, (0, core * half), (rows_w, half)), lax.dynamic_slice(w_up, (0, core * half), (rows_w, half))], axis=1)
+        other_gu = jnp.concatenate([lax.dynamic_slice(w_gate, (0, (1 - core) * half), (rows_w, half)), lax.dynamic_slice(w_up, (0, (1 - core) * half), (rows_w, half))], axis=1)
+        token_rows = jnp.pad(tokens.reshape(-1, 128), ((0, 4), (0, 0)))
+        dy = dy_out.reshape(seq_len, model_dim)
+        all_tokens, (down_block, recv_gu, dy_other) = all_rows(token_rows, n_dev, [w_down, other_gu, dy], ('use', 'pair', 'pair'), 0)
+        block_gu = jnp.where(core == 0, jnp.concatenate([mine_gu, recv_gu], axis=0), jnp.concatenate([recv_gu, mine_gu], axis=0))
+        wgu = gather_group(block_gu)
+        wd = gather_group(down_block)
+        w_g, w_u = wgu[:, :half], wgu[:, half:]
+
         gains = jnp.pad(jnp.stack([attn_norm, mlp_norm], axis=1), ((0, 0), (0, 126)))
         attn_pack = jnp.concatenate([w_query, w_out, w_key, w_value, gains], axis=1)
-        attn_full = lax.all_gather(attn_pack, AXIS_NAME, tiled=True)
-        mine_gu = jnp.concatenate([lax.dynamic_slice(w_gate, (0, core * half), (rows_w, half)), lax.dynamic_slice(w_up, (0, core * half), (rows_w, half))], axis=1)
-        other_gu = jnp.concatenate([lax.dynamic_slice(w_gate, (0, (1 - core) * half), (rows_w, half)), lax.dynamic_slice(w_up, (0, (1 - core) * half), (rows_w, half))], axis=1)
-        recv_gu = swap(other_gu)
-        block_gu = jnp.where(core == 0, jnp.concatenate([mine_gu, recv_gu], axis=0), jnp.concatenate([recv_gu, mine_gu], axis=0))
-        wgu = gather_group(block_gu)
-        wd = gather_group(lax.ppermute(w_down, AXIS_NAME, to_use))
-        w_g, w_u = wgu[:, :half], wgu[:, half:]
-
-        all_ids = lax.all_gather(tokens.reshape(-1), AXIS_NAME, tiled=True)
+        attn_full = gather_all(attn_pack, (rows_w,), ('zba',), ATTN_SEQ, [], (), n_dev, 1)[0].reshape(-1, attn_pack.shape[1])
+
+        all_ids = all_tokens[:, :seq_len // 128].reshape(-1)
         local_ids = all_ids - me * rows_local
         is_owner = (local_ids >= 0) & (local_ids < rows_local)
         picked = jnp.take(table_shard, jnp.clip(local_ids, 0, rows_local - 1), axis=0)
-        picked = jnp.where(is_owner[:, None], picked, jnp.zeros((), picked.dtype)).reshape(n_chip, 2, seq_len, model_dim)
-        keep = lax.dynamic_slice(picked, (0, core, 0, 0), (n_chip, 1, seq_len, model_dim)).reshape(-1, model_dim)
-        give = lax.dynamic_slice(picked, (0, 1 - core, 0, 0), (n_chip, 1, seq_len, model_dim)).reshape(-1, model_dim)
-        x_emb = scatter_group(keep + swap(give))
-
-        dy = dy_out.reshape(seq_len, model_dim)
-        dy2 = jnp.concatenate([dy, swap(dy)], axis=0)
+        picked = jnp.where(is_owner[:, None], picked, jnp.zeros((), picked.dtype)).reshape(n_dev, seq_len, model_dim)
+        x_emb = scatter_sum([picked], [(0, 0, 192, True), (0, 192, 208, True), (0, 400, 112, True)], ('zba', 'zba', 'baz'), LOOKUP_SEQ, 2)[0]
+
+        dy2 = jnp.concatenate([dy, dy_other], axis=0)
 
         wq = attn_full[:, :nq]
         wo = attn_full[:, nq:2 * nq]
@@ -153,14 +532,13 @@
         gate_sig = jax.nn.sigmoid(gate_pre)
         mlp_act = (gate_pre * gate_sig * up_proj).astype(BF16)
         grad_w_down = dot(mlp_act, dy2, 0, 0)
-        down_shard = lax.ppermute(scatter_group(grad_w_down), AXIS_NAME, to_store)
         grad_act = dot(dy2, wd, 1, 1)
         grad_gate = (grad_act * up_proj * gate_sig * (1.0 + gate_pre * (1.0 - gate_sig))).astype(BF16)
         grad_up = (grad_act * gate_pre * gate_sig).astype(BF16)
         part_in = dot(grad_gate, w_g, 1, 1) + dot(grad_up, w_u, 1, 1)
         grad_mlp_in = part_in[:seq_len] + swap(part_in[seq_len:])
-        gate_shard = scatter_group(dot(mlp2, grad_gate, 0, 0))
-        up_shard = scatter_group(dot(mlp2, grad_up, 0, 0))
+        grad_w_gate = dot(mlp2, grad_gate, 0, 0)
+        grad_w_up = dot(mlp2, grad_up, 0, 0)
         part_y = dot(mlp_act, wd, 1, 0)
         layer_out = (hidden.astype(F32) + (part_y[:seq_len] + swap(part_y[seq_len:]))).astype(BF16)
 
@@ -181,13 +559,6 @@
         grad_attn_norm = jnp.sum(grad_attn_in * normed1, axis=0)
         grad_x_emb = grad_hidden + norm_bwd(grad_attn_in, normed1, norm1_inv, g_attn)
 
-        my_rows = gather_group(grad_x_emb)
-        other_rows = swap(my_rows)
-        seg = jnp.where(is_owner, local_ids, rows_local).reshape(n_chip, 2, seq_len)
-        seg_mine = lax.dynamic_slice(seg, (0, core, 0), (n_chip, 1, seq_len)).reshape(-1)
-        seg_other = lax.dynamic_slice(seg, (0, 1 - core, 0), (n_chip, 1, seq_len)).reshape(-1)
-        d_table = jax.ops.segment_sum(jnp.concatenate([my_rows, other_rows], axis=0), jnp.concatenate([seg_mine, seg_other]), num_segments=rows_local)
-
         grad_w_query = dot(attn_in, grad_q_raw, 0, 0)
         grad_w_key = dot(attn_in, grad_k_raw, 0, 0)
         grad_w_value = dot(attn_in, grad_v_raw, 0, 0)
@@ -195,13 +566,20 @@
         zeros = jnp.zeros_like(vecs)
         pack0 = jnp.concatenate([grad_w_query, grad_w_key, vecs], axis=1)
         pack1 = jnp.concatenate([grad_w_out, grad_w_value, zeros], axis=1)
-        keep_pack = jnp.where(core == 0, pack0, pack1)
-        give_pack = jnp.where(core == 0, pack1, pack0)
-        attn_shard = scatter_group(keep_pack + swap(give_pack))
+        packs = jnp.stack([pack0.reshape(n_chip, 2 * rows_w, -1), pack1.reshape(n_chip, 2 * rows_w, -1)], axis=1).reshape(n_dev, 2 * rows_w, -1)
+        by_chip = [v.reshape(n_chip, -1, v.shape[1]) for v in (grad_w_down, grad_w_gate, grad_w_up)]
+        down_rows, gate_shard, up_shard, attn_shard = scatter_sum(
+            by_chip + [packs], [(i, 0, v.shape[1], False) for i, v in enumerate(by_chip)] + [(3, 0, 2 * rows_w, True)], ('bza', 'zba', 'zba', 'baz'), GRAD_SEQ, 3)
 
         chip_rows = jnp.concatenate([gate_shard, up_shard, attn_shard], axis=1)
         mine = lax.dynamic_slice(chip_rows, (core * rows_w, 0), (rows_w, chip_rows.shape[1]))
-        recv = swap(lax.dynamic_slice(chip_rows, ((1 - core) * rows_w, 0), (rows_w, chip_rows.shape[1])))
+        give = lax.dynamic_slice(chip_rows, ((1 - core) * rows_w, 0), (rows_w, chip_rows.shape[1]))
+        qk = jnp.pad(jnp.concatenate([grad_q_norm, grad_k_norm])[None], ((0, 7), (0, model_dim - 2 * head_dim)))
+        all_dx, (down_shard, recv) = gather_all(
+            jnp.concatenate([grad_x_emb, qk], axis=0), (200, 200, 120), ('zba', 'zba', 'baz'), ROWS_SEQ, [down_rows, give], ('store', 'pair'), n_dev, 4)
+        seg = jnp.pad(jnp.where(is_owner, local_ids, rows_local).reshape(n_dev, seq_len), ((0, 0), (0, 8)), constant_values=rows_local)
+        d_table = jax.ops.segment_sum(all_dx.reshape(-1, model_dim), seg.reshape(-1), num_segments=rows_local)
+        qk = jnp.sum(all_dx[:, seq_len, :2 * head_dim], axis=0)
         low = jnp.where(core == 0, mine, recv)
         high = jnp.where(core == 0, recv, mine)
         d_gate = jnp.concatenate([low[:, :half], high[:, :half]], axis=1)
@@ -209,7 +587,6 @@
         d_query, d_key = low[:, ff:ff + nq], low[:, ff + nq:ff + nq + nk]
         d_attn_norm, d_mlp_norm = low[:, ff + nq + nk], low[:, ff + nq + nk + 1]
         d_out, d_value = high[:, ff:ff + nq], high[:, ff + nq:ff + nq + nk]
-        qk = lax.psum(jnp.concatenate([grad_q_norm, grad_k_norm]), AXIS_NAME)
         return (layer_out.reshape(1, seq_len, model_dim), d_table, d_attn_norm, d_query, d_key, d_value, qk[:head_dim], qk[head_dim:], d_out, d_mlp_norm, d_gate, d_up, down_shard)
 
     return jax.shard_map(device_step, mesh=mesh, in_specs=(row_spec, row_spec, row_spec) + weight_specs + (batch_spec,), out_specs=(batch_spec, row_spec) + weight_specs, check_vma=False)

time: 1990 us -> 1170 us (0.59)
  waiting for transfers between devices: 1300 us -> 0.04 us
  Pallas kernels: 0 us -> 633 us
  blocking collectives: 97.3 us -> 0 us
  starting transfers between devices: 37.7 us -> 0.73 us
    unnamed x13 -> x2, waiting for transfers between devices: 648 us -> 0.03 us
    pallas_call x0 -> x5, Pallas kernels: none -> 633 us  [the longest x2 359 us: scatter_sum(): pl.pallas_call(functools.partial(_scatter_kernel, tuple(pieces), orders,...]
    reduce_scatter x1 -> x0, waiting for transfers between devices: 339 us -> none  [scatter_group(): lax.psum_scatter(v, AXIS_NAME, scatter_dimension=0, axis_index_groups=gro...]
    all_gather x3 -> x2, waiting for transfers between devices: 270 us -> 0.01 us  [gather_group(): return lax.all_gather(v, AXIS_NAME, axis_index_groups=groups, tiled=True)]
    psum x1 -> x0, blocking collectives: 53.8 us -> none  [device_step(): qk = lax.psum(jnp.concatenate([grad_q_norm, grad_k_norm]), AXIS_NAME)]
    all_gather x1 -> x0, blocking collectives: 43.5 us -> none  [device_step(): all_ids = lax.all_gather(tokens.reshape(-1), AXIS_NAME, tiled=True)]
    ppermute x9 -> x3, starting transfers between devices: 34.2 us -> 0.65 us  [swap(): return lax.ppermute(v, AXIS_NAME, pair)]
    ppermute x9 -> x3, waiting for transfers between devices: 28.9 us -> 0.01 us  [swap(): return lax.ppermute(v, AXIS_NAME, pair)]
  transfers between devices with their start and end apart: 20 -> 5, of which waited for: 10 -> 0; matrix products, arithmetic and copies ran while one was open for 7% -> 17% of each run, Pallas kernels for 0% -> 15%
where the time goes in v3:
time: 1170 us; the launch traced here: 1160 us
  Pallas kernels  633 us (54%)
  other arithmetic  220 us (19%)
  matrix products  148 us (13%)
  local copies, waits for them, and re-layouts  140 us (12%)
  between operations  15.6 us (1%)
    pallas_call x2, Pallas kernels, scatter_sum(): pl.pallas_call(functools.partial(_scatter_kernel, tuple(pieces), orders,...  359 us
    pallas_call x2, Pallas kernels, gather_all(): pl.pallas_call(functools.partial(_gather_kernel, cuts, orders, seq, moves...  255 us
    scatter-add x1, other arithmetic, device_step(): jax.ops.segment_sum(all_dx.reshape(-1, model_dim), seg.reshape(-1), num_s...  152 us
    dot_general x21, matrix products, dot(): lax.dot_general(a, b, (((ca,), (cb,)), ((), ())), preferred_element_type=...  110 us
    gather x1, local copies, waits for them, and re-layouts, device_step(): jnp.take(table_shard, jnp.clip(local_ids, 0, rows_local - 1), axis=0)  80.9 us
  transfers between devices with their start and end apart: 5, of which 0 were waited for; matrix products, arithmetic and copies ran while one was open for 17% of the time, Pallas kernels for 15%

profile of v3, /device:TPU:0, one launch (start us, length us, event | category | flops | bytes accessed | tf_op | source)
XLA Modules:
  0.0 1156.7 jit_solution(816422407182311449)
XLA Ops:
  7.3 1.3 pad.20.refs_0_
  8.6 1.2 constant_dynamic-slice_fusion.1
  10.5 18.3 %all_rows.1 = (s32[32,8,128]{2,1,0:T(8,128)}, bf16[152,896]{1,0:T(8,128)(2,1)}, bf16[28,4864]{1,0:T(8,128)(2,1)}, bf16[512,896]{1,0:T(8,128)(2,1)}) custom-call(s32[8,128]{1,0:T(8,128)} %pad.20.refs_0_, bf16[152,896]{1,0:T(8,128)(2,1)} %refs_1_.1, bf16[28,4864]{1,0:T(8,128)(2,1)} %pad_maximum_fusion.12.refs_2_, bf16[512,896]{1,0:T(8,128)(2,1)} %bitcast.200), custom_call_target="tpu_custom_call" | custom-call | flops 10000000 | bytes 1048576 | tf_op jit(solution)/shard_map/all_rows/pallas_call | solution.py:216
  28.9 2.1 maximum_select_fusion
  31.3 34.2 %gather_all.2 = bf16[32,28,2176]{2,1,0:T(8,128)(2,1)S(1)} custom-call(bf16[28,2176]{1,0:T(8,128)(2,1)S(1)} %constant_dynamic-update-slice_fusion.refs_0_), custom_call_target="tpu_custom_call" | custom-call | flops 200000000 | bytes 7798784 | tf_op jit(solution)/shard_map/gather_all/pallas_call | solution.py:290
  65.5 2.1 copy-done
  67.6 6.2 reshape.653
  74.0 80.9 %gather_fusion = bf16[16384,896]{1,0:T(8,128)(2,1)} fusion(bf16[4752,896]{1,0:T(8,128)(2,1)} %param.17, s32[16384]{0:T(1024)S(1)} %broadcast_clamp_fusion), kind=kCustom, calls=%fused_computation | custom fusion | bytes 58785792 | tf_op jit(solution)/shard_map/jit(_take)/gather | solution.py:498
  154.9 20.4 %select_select_fusion.refs_0_ = bf16[32,512,896]{2,1,0:T(8,128)(2,1)} fusion(bf16[32,512,896]{2,1,0:T(8,128)(2,1)} %bitcast.183, pred[32,512]{1,0:T(8,128)(4,1)S(1)} %get-tuple-element.77, pred[32,512]{1,0:T(8,128)(4,1)S(1)} %get-tuple-element.76), kind=kLoop, calls=%fused_computation.2 | loop fusion | flops 29360128 | bytes 58753024 | tf_op jit(solution)/shard_map/jit(_where)/select_n | solution.py:499
  175.3 142.7 %scatter_sum.2 = bf16[512,896]{1,0:T(8,128)(2,1)S(1)} custom-call(bf16[32,512,896]{2,1,0:T(8,128)(2,1)} %select_select_fusion.refs_0_), custom_call_target="tpu_custom_call" | custom-call | flops 200000000 | bytes 136937472 | tf_op jit(solution)/shard_map/scatter_sum/pallas_call | solution.py:421
  318.6 2.5 fusion.53
  321.1 2.0 copy.59
  323.3 1.8 fusion.64
  325.4 0.9 fusion.86
  326.6 1.5 convolution_convert_fusion.3
  328.9 6.7 fusion.6
  335.6 8.2 fusion.5
  343.8 7.6 fusion.50
  351.4 3.1 fusion.45
  354.6 1.2 fusion.39
  355.8 1.5 mul.604
  357.3 2.7 copy.66
  362.1 10.7 fusion.60
  372.9 10.2 fusion.17
  383.0 16.8 %multiply_convert_fusion.1 = (bf16[1024,2432]{1,0:T(8,128)(2,1)}, bf16[1024,2432]{1,0:T(8,128)(2,1)}, bf16[1024,2432]{1,0:T(8,128)(2,1)}) fusion(f32[1024,2432]{1,0:T(8,128)} %fusion.60, f32[1024,2432]{1,0:T(8,128)} %fusion.17, bf16[896,4864]{1,0:T(8,128)(2,1)} %all-gather.3.cloned.1.call-done, bf16[512,896]{1,0:T(8,128)(2,1)} %collective-permute-done, ...), kind=kOutput, calls=%fused_computation.15 | convolution fusion | flops 4506255360 | bytes 41058304 | tf_op jit(solution)/shard_map/dot_general | solution.py:68
  399.9 9.3 fusion.15
  409.1 5.5 fusion.47
  415.4 10.6 fusion.59
  426.0 7.5 fusion.108
  433.7 8.7 fusion.92
  442.5 8.9 fusion.93
  452.6 3.0 fusion.43
  455.5 3.6 convolution_convert_fusion
  459.1 2.2 copy.61
  461.4 13.2 %fusion = (f32[2,7,512]{2,1,0:T(8,128)S(1)}, f32[2,512,512,7]{2,1,3,0:T(8,128)}) fusion(f32[2,7,512]{2,1,0:T(8,128)S(1)} %fusion.5, f32[2,7,512]{2,1,0:T(8,128)S(1)} %get-tuple-element.83, f32[2,512,512,7]{2,1,3,0:T(8,128)} %get-tuple-element.84, pred[512,512]{0,1:T(8,128)(4,1)S(1)} %iota_compare_fusion.1, bf16[512,2,64,1]{0,2,3,1:T(8,128)(2,1)S(1)} %bitcast.221, ...), kind=kOutput, calls=%fused_computation.6 | convolution fusion | flops 491774976 | bytes 30756864 | tf_op jit(solution)/shard_map/bqgrh,bkgh->bgrqk/dot_general | solution.py:58
  476.2 8.2 fusion.9
  484.4 1.4 convolution_bitcast_fusion
  485.9 2.3 convolution_bitcast_fusion.1
  488.6 1.1 copy-done.3
  489.7 1.7 multiply_reduce_fusion.1
  491.4 1.5 mul.621
  492.9 2.9 copy.65
  495.8 2.7 copy.63
  498.5 3.6 multiply_convert_fusion.3
  502.2 1.3 fusion.100
  504.3 1.2 fusion.56
  505.6 7.3 fusion.65
  514.1 2.9 fusion.72
  517.5 2.2 fusion.36
  519.7 2.3 pad_maximum_fusion.1
  522.0 5.7 copy.70
  527.6 4.2 maximum_maximum_fusion
  531.9 5.7 copy.71
  537.6 4.0 pad_maximum_fusion
  541.5 3.9 copy.72
  545.4 216.7 %scatter_sum.3 = (f32[152,896]{1,0:T(8,128)}, f32[56,2432]{1,0:T(8,128)}, f32[56,2432]{1,0:T(8,128)}, f32[56,1152]{1,0:T(8,128)S(1)}) custom-call(f32[16,152,896]{2,1,0:T(8,128)} %bitcast.192, f32[16,56,2432]{2,1,0:T(8,128)} %bitcast.194, f32[16,56,2432]{2,1,0:T(8,128)} %bitcast.193, f32[32,56,1152]{2,1,0:T(8,128)} %bitcast.186), custom_call_target="tpu_custom_call" | custom-call | flops 200000000 | bytes 198737920 | tf_op jit(solution)/shard_map/scatter_sum/pallas_call | solution.py:421
  762.1 1.9 constant_dynamic-update-slice_fusion.7
  764.2 2.0 constant_dynamic-update-slice_fusion.6
  766.9 1.2 constant_dynamic-slice_fusion.refs_2_
  769.1 220.8 %gather_all.3 = (f32[32,520,896]{2,1,0:T(8,128)}, f32[152,896]{1,0:T(8,128)S(1)}, f32[28,6016]{1,0:T(8,128)S(1)}) custom-call(f32[520,896]{1,0:T(8,128)S(1)} %select_maximum_fusion.refs_0_, f32[152,896]{1,0:T(8,128)S(1)} %copy-done.1, f32[28,6016]{1,0:T(8,128)S(1)} %constant_dynamic-slice_fusion.refs_2_), custom_call_target="tpu_custom_call" | custom-call | flops 200000000 | bytes 119275520 | tf_op jit(solution)/shard_map/gather_all/pallas_call | solution.py:290
  993.4 1.0 slice_reduce_fusion.2
  994.9 0.9 pad_maximum_fusion.9
  995.8 0.9 pad_maximum_fusion.8
  996.7 152.0 %scatter_custom_fusion = f32[4752,896]{1,0:T(8,128)} fusion(s32[16640]{0:T(1024)} %reshape.679, f32[16640,896]{1,0:T(8,128)} %bitcast.215, f32[]{:T(128)} %constant.29.clone.1), kind=kCustom, calls=%fused_computation.18 | custom fusion | flops 14909440 | bytes 17031680 | tf_op jit(solution)/shard_map/scatter-add | solution.py:581
  (218 shorter events, 18.5 us)
Async XLA Ops:
  7.2 23.9 %copy-start.37 = (bf16[28,896]{1,0:T(8,128)(2,1)S(1)}, bf16[28,896]{1,0:T(8,128)(2,1)}, u32[]{:S(2)}) copy-start(bf16[28,896]{1,0:T(8,128)(2,1)} %param.19) | copy-start | bytes 150532
  7.2 23.9 %copy-start.55 = (bf16[28]{0:T(256)(128)(2,1)S(1)}, bf16[28]{0:T(256)(128)(2,1)}, u32[]{:S(2)}) copy-start(bf16[28]{0:T(256)(128)(2,1)} %param.18) | copy-start | bytes 172
  7.2 23.9 %copy-start.54 = (bf16[28]{0:T(256)(128)(2,1)S(1)}, bf16[28]{0:T(256)(128)(2,1)}, u32[]{:S(2)}) copy-start(bf16[28]{0:T(256)(128)(2,1)} %param.25) | copy-start | bytes 172
  7.2 24.0 %copy-start.38 = (bf16[28,896]{1,0:T(8,128)(2,1)S(1)}, bf16[28,896]{1,0:T(8,128)(2,1)}, u32[]{:S(2)}) copy-start(bf16[28,896]{1,0:T(8,128)(2,1)} %param.24) | copy-start | bytes 150532
  7.2 24.0 %copy-start.43 = (bf16[28,128]{1,0:T(8,128)(2,1)S(1)}, bf16[28,128]{1,0:T(8,128)(2,1)}, u32[]{:S(2)}) copy-start(bf16[28,128]{1,0:T(8,128)(2,1)} %param.20) | copy-start | bytes 21508
  7.2 24.0 %copy-start.44 = (bf16[28,128]{1,0:T(8,128)(2,1)S(1)}, bf16[28,128]{1,0:T(8,128)(2,1)}, u32[]{:S(2)}) copy-start(bf16[28,128]{1,0:T(8,128)(2,1)} %param.21) | copy-start | bytes 21508
  7.2 354.9 %all-gather.5.cloned.1.call-start = ((), (), s32[]{:S(2)}) async-start(), calls=%async_computation.1 | async-start | bytes 4630528 | tf_op jit(solution)/shard_map/all_gather | solution.py:467
  28.9 344.0 %all-gather.3.cloned.1.call-start = ((), (), s32[]{:S(2)}) async-start(), calls=%async_computation | async-start | bytes 9261056 | tf_op jit(solution)/shard_map/all_gather | solution.py:467
  65.5 2.1 copy-start
  67.6 6.2 copy-start.56
  67.6 6.2 copy-start.45
  67.6 6.2 copy-start.42
  73.8 252.6 %copy-start.46 = (f32[64]{0:T(128)}, f32[64]{0:T(128)S(1)}, u32[]{:S(2)}) copy-start(f32[64]{0:T(128)S(1)} %convert_element_type.204) | copy-start | bytes 772
  175.3 142.7 %copy-start.6 = (bf16[896,2176]{1,0:T(8,128)(2,1)S(1)}, bf16[896,2176]{1,0:T(8,128)(2,1)}, u32[]{:S(2)}) copy-start(bf16[896,2176]{1,0:T(8,128)(2,1)} %reshape.653) | copy-start | bytes 11698180
  318.3 8.2 copy-start.29
  318.6 7.9 copy-start.39
  318.6 4.5 copy-start.50
  323.1 5.0 copy-start.2
  323.1 5.0 copy-start.48
  325.0 1.5 copy-start.8
  325.4 3.5 copy-start.35
  325.4 30.4 %copy-start.23 = (f32[512,2,7]{0,2,1:T(8,128)}, f32[512,2,7]{0,2,1:T(8,128)S(1)}, u32[]{:S(2)}) copy-start(f32[512,2,7]{0,2,1:T(8,128)S(1)} %add_rsqrt_fusion) | copy-start | bytes 86020
  326.4 2.5 copy-start.17
  326.5 2.4 copy-start.25
  326.5 2.4 copy-start.27
  328.9 6.7 copy-start.13
  328.9 6.7 copy-start.15
  335.6 139.0 %copy-start.31 = (f32[2,7,512]{2,1,0:T(8,128)}, f32[2,7,512]{2,1,0:T(8,128)S(1)}, u32[]{:S(2)}) copy-start(f32[2,7,512]{2,1,0:T(8,128)S(1)} %get-tuple-element.83) | copy-start | bytes 86020
  343.8 130.8 %copy-start.33 = (f32[2,7,512]{2,1,0:T(8,128)}, f32[2,7,512]{2,1,0:T(8,128)S(1)}, u32[]{:S(2)}) copy-start(f32[2,7,512]{2,1,0:T(8,128)S(1)} %fusion.5) | copy-start | bytes 86020
  351.4 3.1 copy-start.20
  354.6 96.8 %copy-start.4 = (bf16[512,896]{1,0:T(8,128)(2,1)}, bf16[512,896]{1,0:T(8,128)(2,1)S(1)}, u32[]{:S(2)}) copy-start(bf16[512,896]{1,0:T(8,128)(2,1)S(1)} %get-tuple-element.86) | copy-start | bytes 2752516
  354.6 7.5 copy-start.10
  355.8 17.0 %collective-permute-start = (bf16[512,896]{1,0:T(8,128)(2,1)}, bf16[512,896]{1,0:T(8,128)(2,1)}, u32[]{:S(2)}, u32[]{:S(2)}) collective-permute-start(bf16[512,896]{1,0:T(8,128)(2,1)} %fusion.39), channel_id=1, source_target_pairs={{0,1},{1,0},{2,3},{3,2},{4,5},{5,4},{6,7},{7,6},{8,9},{9,8},{10,11... | collective-permute-start | bytes 2752520 | tf_op jit(solution)/shard_map/ppermute | solution.py:464
  399.8 9.3 copy-start.52
  399.8 9.3 copy-start.57
  409.1 6.2 copy-start.53
  414.7 11.4 slice-start.4
  414.8 36.6 %collective-permute-start.2 = (f32[512,896]{1,0:T(8,128)S(1)}, f32[512,896]{1,0:T(8,128)S(1)}, u32[]{:S(2)}, u32[]{:S(2)}) collective-permute-start(f32[512,896]{1,0:T(8,128)S(1)} %slice.153), channel_id=1, source_target_pairs={{0,1},{1,0},{2,3},{3,2},{4,5},{5,4},{6,7},{7,6},{8,9},{9,8},{10,11... | collective-permute-start | bytes 5505032 | tf_op jit(solution)/shard_map/ppermute | solution.py:464
  415.4 10.7 slice-start.5
  415.4 18.3 %slice-start.6 = ((s8[4980736]{0:T(1024)(128)(4,1)}), s8[4194304]{0:T(1024)(128)(4,1)S(1)}, s32[]{:S(2)}) async-start(s8[4980736]{0:T(1024)(128)(4,1)} %bitcast.222), calls=%async_computation.8 | async-start | bytes 8388608
  426.0 7.7 slice-start.7
  433.6 18.5 %collective-permute-start.1 = (f32[512,896]{1,0:T(8,128)S(1)}, f32[512,896]{1,0:T(8,128)S(1)}, u32[]{:S(2)}, u32[]{:S(2)}) collective-permute-start(f32[512,896]{1,0:T(8,128)S(1)} %slice.151), channel_id=1, source_target_pairs={{0,1},{1,0},{2,3},{3,2},{4,5},{5,4},{6,7},{7,6},{8,9},{9,8},{10,11... | collective-permute-start | bytes 5505032 | tf_op jit(solution)/shard_map/ppermute | solution.py:464
  461.4 13.3 %slice-start = ((s8[14680064]{0:T(1024)(128)(4,1)}), s8[4194304]{0:T(1024)(128)(4,1)S(1)}, s32[]{:S(2)}) async-start(s8[14680064]{0:T(1024)(128)(4,1)} %bitcast.184), calls=%async_computation.2 | async-start | bytes 8388608
  461.4 13.3 %slice-start.1 = ((s8[14680064]{0:T(1024)(128)(4,1)}), s8[4194304]{0:T(1024)(128)(4,1)S(1)}, s32[]{:S(2)}) async-start(s8[14680064]{0:T(1024)(128)(4,1)} %bitcast.184), calls=%async_computation.3 | async-start | bytes 8388608
  461.4 14.0 %slice-start.2 = ((s8[14680064]{0:T(1024)(128)(4,1)}), s8[4194304]{0:T(1024)(128)(4,1)S(1)}, s32[]{:S(2)}) async-start(s8[14680064]{0:T(1024)(128)(4,1)} %bitcast.184), calls=%async_computation.4 | async-start | bytes 8388608
  461.4 14.8 %slice-start.3 = ((s8[14680064]{0:T(1024)(128)(4,1)}), s8[2097152]{0:T(1024)(128)(4,1)S(1)}, s32[]{:S(2)}) async-start(s8[14680064]{0:T(1024)(128)(4,1)} %bitcast.184), calls=%async_computation.5 | async-start | bytes 4194304
  476.2 8.2 copy-start.26
  476.2 8.2 copy-start.28
  484.4 1.4 copy-start.14
  485.8 2.4 copy-start.18
  485.9 2.4 copy-start.22
  488.2 1.5 copy-start.3
  488.2 1.5 copy-start.24
  488.2 1.5 copy-start.49
  498.5 3.6 copy-start.30
  498.5 3.6 copy-start.40
  502.2 2.1 copy-start.7
  505.5 7.4 copy-start.9
  505.5 7.4 copy-start.36
  505.6 7.4 copy-start.47
  505.6 7.5 copy-start.51
  522.0 5.7 copy-start.41
  764.2 3.9 copy-start.5
  768.7 221.3 %copy-start.12 = (f32[56,6016]{1,0:T(8,128)S(1)}, f32[56,6016]{1,0:T(8,128)}, u32[]{:S(2)}) copy-start(f32[56,6016]{1,0:T(8,128)} %constant_dynamic-update-slice_fusion.5) | copy-start | bytes 4042756
  (7 other events, 8.6 us)
Sparse Core Ops, SparseCore 0:
  29.0 77.7 all-gather.4
  110.1 148.7 all-gather.2

commit v4 on v3

--- a/solution.py
+++ b/solution.py
@@ -315,22 +315,24 @@
 def _scatter_kernel(pieces, orders, seq, n_arr, *refs):
     table, _ = _slots(pieces, orders, seq)
     n = len(pieces)
-    n_pair = sum(1 for p in pieces if p[3])
+    n_pair = sum(1 for p in pieces if p[3] != 'chip')
     ins, outs = refs[:n_arr], refs[n_arr:2 * n_arr]
     k = 2 * n_arr
     land, stage, pair = refs[k:k + n], refs[k + n:k + 2 * n], list(refs[k + 2 * n:k + 2 * n + n_pair])
     load_sem, send_sem, recv_sem, d_send, d_recv = refs[k + 2 * n + n_pair:]
-    got = [pair.pop(0) if p[3] else None for p in pieces]
+    got = [pair.pop(0) if p[3] != 'chip' else None for p in pieces]
     me = lax.axis_index(AXIS_NAME)
     at, partner_at = _Place(me), _Place(me, swapped=True)
 
     def rows_of(ref, piece):
-        arr, r0, rows, _ = pieces[piece]
-        return ref if rows == ins[arr].shape[1] else ref.at[pl.ds(r0, rows)]
+        _, r0, rows, _ = pieces[piece]
+        return ref if rows == ref.shape[0] else ref.at[pl.ds(r0, rows)]
 
     def term(piece, kc, core):
-        arr, _, _, paired = pieces[piece]
-        return rows_of(ins[arr].at[2 * kc + core if paired else kc], piece)
+        arr, _, rows, kind = pieces[piece]
+        if kind == 'rows':
+            return ins[arr].at[kc, pl.ds(pl.multiple_of(24 * core, 8), rows)]
+        return rows_of(ins[arr].at[2 * kc + core if kind == 'device' else kc], piece)
 
     def run(u):
         sides = ['a', 'b', 'z+'] + (['z-'] if u else [])
@@ -340,13 +342,13 @@
         given = [0] * n
         for key in keys:
             piece = key[3]
-            if pieces[piece][3]:
+            if pieces[piece][3] != 'chip':
                 kc = partner_at.chip(key)
                 copy = _remote(term(piece, kc, 1 - at.core), got[piece].at[kc], d_send.at[piece, given[piece]], d_recv.at[piece, kc], at.partner)
                 given[piece] += 1
                 copy.start()
                 started.append(copy)
-        adds = [[key for key in keys if key[3] == i and (pieces[i][3] or _onward(u, key, orders))] for i in range(n)]
+        adds = [[key for key in keys if key[3] == i and (pieces[i][3] != 'chip' or _onward(u, key, orders))] for i in range(n)]
 
         def load(piece, j):
             return pltpu.make_async_copy(term(piece, at.chip(adds[piece][j]), at.core), stage[piece].at[j % 2], load_sem.at[piece, j % 2])
@@ -358,7 +360,8 @@
         count = 0
         for key in keys:
             piece = key[3]
-            arr, r0, rows, paired = pieces[piece]
+            arr, r0, rows, kind = pieces[piece]
+            paired = kind != 'chip'
             kc = at.chip(key)
             children = _onward(u, key, orders)
             if not children and not paired:
@@ -414,13 +417,14 @@
     shapes = [(rows, arrays[arr].shape[2], arrays[arr].dtype) for arr, _, rows, _ in pieces]
     scratch = [pltpu.VMEM((m, r, c), d) for m, (r, c, d) in zip(most, shapes)]
     scratch += [pltpu.VMEM((2, r, c), d) for r, c, d in shapes]
-    scratch += [pltpu.VMEM((16, r, c), d) for (r, c, d), p in zip(shapes, pieces) if p[3]]
-    nbytes = sum(v.size // v.shape[0] * v.dtype.itemsize for v in arrays) + sum(
-        (m + 2 + 16 * int(p[3])) * (-(-r // 16) * 16) * c * d.itemsize for m, (r, c, d), p in zip(most, shapes, pieces))
+    scratch += [pltpu.VMEM((16, r, c), d) for (r, c, d), p in zip(shapes, pieces) if p[3] != 'chip']
+    outs = [jax.ShapeDtypeStruct((sum(p[2] for p in pieces if p[0] == i), v.shape[2]), v.dtype) for i, v in enumerate(arrays)]
+    nbytes = sum(v.size * v.dtype.itemsize for v in outs) + sum(
+        (m + 2 + 16 * int(p[3] != 'chip')) * (-(-r // 16) * 16) * c * d.itemsize for m, (r, c, d), p in zip(most, shapes, pieces))
     scratch += [dma((n, 2)), dma((16 * n,)), dma((n, max(most))), dma((n, 16)), dma((n, 16))]
     return pl.pallas_call(
         functools.partial(_scatter_kernel, tuple(pieces), orders, seq, n_arr),
-        out_shape=[jax.ShapeDtypeStruct(v.shape[1:], v.dtype) for v in arrays],
+        out_shape=outs,
         in_specs=[hbm] * n_arr,
         out_specs=[vmem] * n_arr,
         scratch_shapes=scratch,
@@ -428,6 +432,126 @@
         cost_estimate=pl.CostEstimate(flops=200_000_000, bytes_accessed=nbytes * 4, transcendentals=0),
         name='scatter_sum',
     )(*arrays)
+
+
+def _lookup_kernel(counts, codes, table_ref, out_ref, rows, block, sem):
+    b = pl.program_id(0)
+    n_col = out_ref.shape[2] // 128
+    n_rows = rows.shape[0] // n_col
+
+    @pl.when(b == 0)
+    def _():
+        def widen(i, _):
+            for j in range(n_col):
+                part = table_ref[pl.ds(pl.multiple_of(i * 16, 16), 16), j * 128:(j + 1) * 128].astype(F32)
+                line = pl.multiple_of(i * 16 * n_col, 8)
+                rows[pl.ds(line + j * 8, 8), :] = part[:8]
+                rows[pl.ds(line + (n_col + j) * 8, 8), :] = part[8:]
+            return 0
+        lax.fori_loop(0, n_rows // 16, widen, 0)
+
+    seq = out_ref.shape[1]
+
+    def clear(i, _):
+        block[pl.ds(pl.multiple_of(i * 8 * n_col, 8), 8 * n_col), :] = jnp.zeros((8 * n_col, 128), F32)
+        return 0
+    lax.fori_loop(0, seq // 8, clear, 0)
+
+    def pick(i, _):
+        for t in range(4):
+            code = codes[b * seq + i * 4 + t]
+            row, pos = code & 8191, code >> 13
+            block[pl.ds((pos >> 3) * (8 * n_col) + (pos & 7), n_col, stride=8), :] = rows[pl.ds((row >> 3) * (8 * n_col) + (row & 7), n_col, stride=8), :]
+        return 0
+    lax.fori_loop(0, (counts[b] + 3) // 4, pick, 0)
+
+    def narrow(i, _):
+        line = pl.multiple_of(i * 16 * n_col, 8)
+        for j in range(n_col):
+            part = jnp.concatenate([block[pl.ds(line + j * 8, 8), :], block[pl.ds(line + (n_col + j) * 8, 8), :]], axis=0)
+            out_ref[0, pl.ds(pl.multiple_of(i * 16, 16), 16), j * 128:(j + 1) * 128] = part.astype(BF16)
+        return 0
+    lax.fori_loop(0, seq // 16, narrow, 0)
+
+
+def lookup(table, counts, codes, seq):
+    n_rows, dim = table.shape
+    n_src = counts.shape[0]
+    lines = dim // 128
+    return pl.pallas_call(
+        _lookup_kernel,
+        grid_spec=pltpu.PrefetchScalarGridSpec(
+            num_scalar_prefetch=2,
+            grid=(n_src,),
+            in_specs=[pl.BlockSpec(memory_space=pltpu.VMEM)],
+            out_specs=pl.BlockSpec((1, seq, dim), lambda b, *_: (b, 0, 0)),
+            scratch_shapes=[pltpu.VMEM((n_rows * lines, 128), F32), pltpu.VMEM(((seq + 8) * lines, 128), F32), pltpu.SemaphoreType.DMA],
+        ),
+        out_shape=jax.ShapeDtypeStruct((n_src, seq, dim), table.dtype),
+        compiler_params=pltpu.CompilerParams(vmem_limit_bytes=40 << 20, dimension_semantics=('arbitrary',)),
+        cost_estimate=pl.CostEstimate(flops=50_000_000, bytes_accessed=40 << 20, transcendentals=0),
+        name='lookup',
+    )(counts, codes, table)
+
+
+def _add_rows_kernel(counts, codes, dx_ref, out_ref):
+    b = pl.program_id(0)
+    n_col = 7
+
+    @pl.when(b == 0)
+    def _():
+        def clear(i, _):
+            out_ref[pl.ds(pl.multiple_of(i * 8 * n_col, 8), 8 * n_col), :] = jnp.zeros((8 * n_col, 128), F32)
+            return 0
+        lax.fori_loop(0, out_ref.shape[0] // (8 * n_col), clear, 0)
+
+    seq = codes.shape[0] // counts.shape[0]
+
+    def add(i, _):
+        for t in range(4):
+            code = codes[b * seq + i * 4 + t]
+            row, pos = code & 8191, code >> 13
+            src = dx_ref[0, pl.ds((pos >> 3) * (8 * n_col) + (pos & 7), n_col, stride=8), :]
+            at = pl.ds((row >> 3) * (8 * n_col) + (row & 7), n_col, stride=8)
+            out_ref[at, :] = out_ref[at, :] + src
+        return 0
+    lax.fori_loop(0, counts[b] // 4, add, 0)
+
+    def add_one(i, _):
+        code = codes[b * seq + i]
+        row, pos = code & 8191, code >> 13
+        src = dx_ref[0, pl.ds((pos >> 3) * (8 * n_col) + (pos & 7), n_col, stride=8), :]
+        at = pl.ds((row >> 3) * (8 * n_col) + (row & 7), n_col, stride=8)
+        out_ref[at, :] = out_ref[at, :] + src
+        return 0
+    lax.fori_loop((counts[b] // 4) * 4, counts[b], add_one, 0)
+
+
+def add_rows(dx, counts, codes, n_rows):
+    n_src, lines, _ = dx.shape
+    return pl.pallas_call(
+        _add_rows_kernel,
+        grid_spec=pltpu.PrefetchScalarGridSpec(
+            num_scalar_prefetch=2,
+            grid=(n_src,),
+            in_specs=[pl.BlockSpec((1, lines, 128), lambda b, *_: (b, 0, 0))],
+            out_specs=pl.BlockSpec((n_rows * 7, 128), lambda b, *_: (0, 0)),
+        ),
+        out_shape=jax.ShapeDtypeStruct((n_rows * 7, 128), F32),
+        compiler_params=pltpu.CompilerParams(vmem_limit_bytes=48 << 20, dimension_semantics=('arbitrary',)),
+        cost_estimate=pl.CostEstimate(flops=50_000_000, bytes_accessed=80 << 20, transcendentals=0),
+        name='add_rows',
+    )(counts, codes, dx)
+
+
+def to_lines(v):
+    rows, dim = v.shape
+    return v.reshape(rows // 8, 8, dim // 128, 128).transpose(0, 2, 1, 3).reshape(rows * dim // 128, 128)
+
+
+def from_lines(v, dim):
+    rows = v.shape[0] * 128 // dim
+    return v.reshape(rows // 8, dim // 128, 8, 128).transpose(0, 2, 1, 3).reshape(rows, dim)
 
 
 ROWS_SEQ = (
@@ -443,8 +567,8 @@
     (0, 16, 40, 72, 1, 17, 41, 73, 2, 18, 42, 74, 24, 34, 66, 32, 48, 64, 80, 104, 25, 26, 50, 82, 33, 49, 58, 90, 65, 81, 56, 105, 98, 57, 106, 122, 88, 96, 114, 112, 89, 97, 113, 120, 121),
 )
 GRAD_SEQ = (
-    (8, 32, 64, 9, 33, 65, 10, 34, 66, 11, 35, 67, 41, 16, 40, 72, 96, 42, 73, 97, 17, 18, 74, 98, 49, 19, 43, 75, 99, 50, 105, 80, 104, 24, 48, 106, 81, 82, 25, 113, 26, 57, 114, 27, 51, 83, 58, 88, 112, 89, 56, 90, 59, 91, 121, 122, 107, 120, 123, 115),
-    (0, 16, 40, 72, 1, 17, 41, 73, 2, 18, 42, 74, 3, 19, 43, 75, 32, 24, 33, 48, 49, 35, 67, 64, 80, 104, 25, 34, 50, 26, 27, 51, 83, 65, 81, 57, 105, 99, 58, 56, 106, 66, 82, 59, 91, 107, 123, 115, 96, 88, 113, 97, 112, 89, 98, 114, 90, 121, 122, 120),
+    (8, 32, 64, 9, 33, 65, 10, 34, 66, 11, 35, 67, 12, 36, 68, 41, 16, 40, 72, 96, 42, 73, 97, 17, 18, 74, 98, 49, 19, 43, 75, 99, 100, 20, 44, 76, 50, 105, 80, 104, 24, 48, 106, 81, 82, 25, 113, 26, 114, 57, 27, 51, 83, 28, 52, 84, 58, 88, 112, 89, 56, 90, 59, 91, 121, 60, 92, 107, 122, 123, 108, 120, 124, 115, 116),
+    (0, 16, 40, 72, 1, 17, 41, 73, 2, 18, 42, 74, 3, 19, 43, 75, 4, 20, 44, 76, 32, 35, 67, 24, 33, 48, 49, 36, 68, 64, 80, 104, 25, 34, 50, 26, 27, 51, 83, 57, 105, 65, 81, 28, 52, 84, 99, 100, 58, 56, 59, 91, 106, 66, 82, 60, 92, 107, 123, 108, 124, 115, 116, 96, 88, 113, 112, 97, 89, 98, 114, 90, 121, 122, 120),
 )
 
 
@@ -489,33 +613,40 @@
         w_g, w_u = wgu[:, :half], wgu[:, half:]
 
         gains = jnp.pad(jnp.stack([attn_norm, mlp_norm], axis=1), ((0, 0), (0, 126)))
-        attn_pack = jnp.concatenate([w_query, w_out, w_key, w_value, gains], axis=1)
+        attn_pack = jnp.concatenate([w_query, w_key, w_value, w_out, gains], axis=1)
         attn_full = gather_all(attn_pack, (rows_w,), ('zba',), ATTN_SEQ, [], (), n_dev, 1)[0].reshape(-1, attn_pack.shape[1])
 
         all_ids = all_tokens[:, :seq_len // 128].reshape(-1)
         local_ids = all_ids - me * rows_local
         is_owner = (local_ids >= 0) & (local_ids < rows_local)
-        picked = jnp.take(table_shard, jnp.clip(local_ids, 0, rows_local - 1), axis=0)
-        picked = jnp.where(is_owner[:, None], picked, jnp.zeros((), picked.dtype)).reshape(n_dev, seq_len, model_dim)
-        x_emb = scatter_sum([picked], [(0, 0, 192, True), (0, 192, 208, True), (0, 400, 112, True)], ('zba', 'zba', 'baz'), LOOKUP_SEQ, 2)[0]
+        own = is_owner.reshape(n_dev, seq_len)
+        slot = jnp.arange(seq_len, dtype=jnp.int32)
+        upto = (slot[:, None] <= slot[None, :]).astype(BF16)
+        rank = jnp.where(own, dot(own.astype(BF16), upto, 1, 0).astype(jnp.int32) - 1, -1)
+        counts = jnp.sum(own.astype(jnp.int32), axis=1)
+        code = slot[None] * 8192 + jnp.where(own, local_ids.reshape(n_dev, seq_len), 0)
+        codes = jnp.sum(jnp.where(rank[:, :, None] == slot, code[:, :, None], 0), axis=1)
+        codes = jnp.where(slot[None] < counts[:, None], codes, seq_len * 8192).reshape(-1)
+        picked = lookup(table_shard, counts, codes, seq_len)
+        x_emb = scatter_sum([picked], [(0, 0, 192, 'device'), (0, 192, 208, 'device'), (0, 400, 112, 'device')], ('zba', 'zba', 'baz'), LOOKUP_SEQ, 2)[0]
 
         dy2 = jnp.concatenate([dy, dy_other], axis=0)
 
-        wq = attn_full[:, :nq]
-        wo = attn_full[:, nq:2 * nq]
-        wk = attn_full[:, 2 * nq:2 * nq + nk]
-        wv = attn_full[:, 2 * nq + nk:2 * nq + 2 * nk]
-        g_attn = attn_full[:, 2 * nq + 2 * nk]
-        g_mlp = attn_full[:, 2 * nq + 2 * nk + 1]
+        n_in = nq + 2 * nk
+        w_in = attn_full[:, :n_in]
+        wo = attn_full[:, n_in:n_in + nq]
+        g_attn = attn_full[:, n_in + nq]
+        g_mlp = attn_full[:, n_in + nq + 1]
 
         cos_t, sin_t = rope_tables(positions, head_dim)
         cos_q, sin_q = cos_t[:, :, None, None, :], sin_t[:, :, None, None, :]
         cos_k, sin_k = cos_t[:, :, None, :], sin_t[:, :, None, :]
         normed1, norm1_inv = norm_fwd(x_emb)
         attn_in = (normed1 * g_attn.astype(F32)).astype(BF16)
-        q_raw = dot(attn_in, wq, 1, 0).astype(BF16).reshape(1, seq_len, kv_heads, q_per_kv, head_dim)
-        k_raw = dot(attn_in, wk, 1, 0).astype(BF16).reshape(1, seq_len, kv_heads, head_dim)
-        v_raw = dot(attn_in, wv, 1, 0).astype(BF16).reshape(1, seq_len, kv_heads, head_dim)
+        qkv = dot(attn_in, w_in, 1, 0).astype(BF16)
+        q_raw = qkv[:, :nq].reshape(1, seq_len, kv_heads, q_per_kv, head_dim)
+        k_raw = qkv[:, nq:nq + nk].reshape(1, seq_len, kv_heads, head_dim)
+        v_raw = qkv[:, nq + nk:].reshape(1, seq_len, kv_heads, head_dim)
         q_normed, q_inv = norm_fwd(q_raw)
         k_normed, k_inv = norm_fwd(k_raw)
         q_rot = rotate(q_normed * q_norm.astype(F32), cos_q, sin_q).astype(BF16)
@@ -555,38 +686,34 @@
         grad_q_raw = norm_bwd(grad_qt, q_normed, q_inv, q_norm).astype(BF16).reshape(seq_len, nq)
         grad_k_raw = norm_bwd(grad_kt, k_normed, k_inv, k_norm).astype(BF16).reshape(seq_len, nk)
         grad_v_raw = grad_v.astype(BF16).reshape(seq_len, nk)
-        grad_attn_in = dot(grad_q_raw, wq, 1, 1) + dot(grad_k_raw, wk, 1, 1) + dot(grad_v_raw, wv, 1, 1)
+        grad_qkv = jnp.concatenate([grad_q_raw, grad_k_raw, grad_v_raw], axis=1)
+        grad_attn_in = dot(grad_qkv, w_in, 1, 1)
         grad_attn_norm = jnp.sum(grad_attn_in * normed1, axis=0)
         grad_x_emb = grad_hidden + norm_bwd(grad_attn_in, normed1, norm1_inv, g_attn)
 
-        grad_w_query = dot(attn_in, grad_q_raw, 0, 0)
-        grad_w_key = dot(attn_in, grad_k_raw, 0, 0)
-        grad_w_value = dot(attn_in, grad_v_raw, 0, 0)
-        vecs = jnp.pad(jnp.stack([grad_attn_norm, grad_mlp_norm], axis=1), ((0, 0), (0, 126)))
-        zeros = jnp.zeros_like(vecs)
-        pack0 = jnp.concatenate([grad_w_query, grad_w_key, vecs], axis=1)
-        pack1 = jnp.concatenate([grad_w_out, grad_w_value, zeros], axis=1)
-        packs = jnp.stack([pack0.reshape(n_chip, 2 * rows_w, -1), pack1.reshape(n_chip, 2 * rows_w, -1)], axis=1).reshape(n_dev, 2 * rows_w, -1)
-        by_chip = [v.reshape(n_chip, -1, v.shape[1]) for v in (grad_w_down, grad_w_gate, grad_w_up)]
-        down_rows, gate_shard, up_shard, attn_shard = scatter_sum(
-            by_chip + [packs], [(i, 0, v.shape[1], False) for i, v in enumerate(by_chip)] + [(3, 0, 2 * rows_w, True)], ('bza', 'zba', 'zba', 'baz'), GRAD_SEQ, 3)
-
-        chip_rows = jnp.concatenate([gate_shard, up_shard, attn_shard], axis=1)
+        by_chip = [u.reshape(n_chip, -1, u.shape[1]) for u in (grad_w_down, grad_w_gate, grad_w_up, dot(attn_in, grad_qkv, 0, 0), grad_w_out)]
+        down_rows, gate_shard, up_shard, in_shard, out_shard = scatter_sum(
+            by_chip, [(i, 0, u.shape[1], 'chip') for i, u in enumerate(by_chip[:3])] + [(3, 0, 32, 'rows'), (4, 0, 32, 'rows')], ('bza', 'zba', 'zba', 'baz', 'baz'), GRAD_SEQ, 3)
+
+        chip_rows = jnp.concatenate([gate_shard, up_shard], axis=1)
         mine = lax.dynamic_slice(chip_rows, (core * rows_w, 0), (rows_w, chip_rows.shape[1]))
         give = lax.dynamic_slice(chip_rows, ((1 - core) * rows_w, 0), (rows_w, chip_rows.shape[1]))
-        qk = jnp.pad(jnp.concatenate([grad_q_norm, grad_k_norm])[None], ((0, 7), (0, model_dim - 2 * head_dim)))
+        qk = jnp.pad(jnp.concatenate([grad_q_norm, grad_k_norm])[None], ((0, 0), (0, model_dim - 2 * head_dim)))
+        gains_grad = jnp.concatenate([qk, grad_attn_norm[None], grad_mlp_norm[None], jnp.zeros((5, model_dim), F32)], axis=0)
+        lines = model_dim // 128
         all_dx, (down_shard, recv) = gather_all(
-            jnp.concatenate([grad_x_emb, qk], axis=0), (200, 200, 120), ('zba', 'zba', 'baz'), ROWS_SEQ, [down_rows, give], ('store', 'pair'), n_dev, 4)
-        seg = jnp.pad(jnp.where(is_owner, local_ids, rows_local).reshape(n_dev, seq_len), ((0, 0), (0, 8)), constant_values=rows_local)
-        d_table = jax.ops.segment_sum(all_dx.reshape(-1, model_dim), seg.reshape(-1), num_segments=rows_local)
-        qk = jnp.sum(all_dx[:, seq_len, :2 * head_dim], axis=0)
+            to_lines(jnp.concatenate([grad_x_emb, gains_grad], axis=0)), (200 * lines, 200 * lines, 120 * lines), ('zba', 'zba', 'baz'), ROWS_SEQ, [down_rows, give], ('store', 'pair'), n_dev, 4)
+        d_table = from_lines(add_rows(all_dx, counts, codes, rows_local), model_dim)
+        gains_grad = from_lines(jnp.sum(all_dx[:, seq_len * lines:], axis=0), model_dim)
+        qk = gains_grad[0]
+        d_attn_norm, d_mlp_norm = (lax.dynamic_slice(gains_grad[i], (me * rows_w,), (rows_w,)) for i in (1, 2))
         low = jnp.where(core == 0, mine, recv)
         high = jnp.where(core == 0, recv, mine)
         d_gate = jnp.concatenate([low[:, :half], high[:, :half]], axis=1)
         d_up = jnp.concatenate([low[:, half:ff], high[:, half:ff]], axis=1)
-        d_query, d_key = low[:, ff:ff + nq], low[:, ff + nq:ff + nq + nk]
-        d_attn_norm, d_mlp_norm = low[:, ff + nq + nk], low[:, ff + nq + nk + 1]
-        d_out, d_value = high[:, ff:ff + nq], high[:, ff + nq:ff + nq + nk]
-        return (layer_out.reshape(1, seq_len, model_dim), d_table, d_attn_norm, d_query, d_key, d_value, qk[:head_dim], qk[head_dim:], d_out, d_mlp_norm, d_gate, d_up, down_shard)
+        in_rows = lax.dynamic_slice(in_shard, (core * (rows_w - 24), 0), (rows_w, n_in))
+        d_query, d_key, d_value = in_rows[:, :nq], in_rows[:, nq:nq + nk], in_rows[:, nq + nk:]
+        d_out = lax.dynamic_slice(out_shard, (core * (rows_w - 24), 0), (rows_w, nq))
+        return (layer_out.reshape(1, seq_len, model_dim), d_table, d_attn_norm, d_query, d_key, d_value, qk[:head_dim], qk[head_dim:2 * head_dim], d_out, d_mlp_norm, d_gate, d_up, down_shard)
 
     return jax.shard_map(device_step, mesh=mesh, in_specs=(row_spec, row_spec, row_spec) + weight_specs + (batch_spec,), out_specs=(batch_spec, row_spec) + weight_specs, check_vma=False)

time: 1170 us -> 1030 us (0.88)
  other arithmetic: 220 us -> 46.4 us
  Pallas kernels: 633 us -> 769 us
  local copies, waits for them, and re-layouts: 140 us -> 45.4 us
    scatter-add x1 -> x0, other arithmetic: 152 us -> none  [device_step(): jax.ops.segment_sum(all_dx.reshape(-1, model_dim), seg.reshape(-1), num_s...]
    pallas_call x0 -> x2, Pallas kernels: none -> 107 us  [the longest x1 54.2 us: add_rows(): pl.pallas_call(_add_rows_kernel, grid_spec=pltpu.PrefetchScalarGridSpec(n...]
    gather x1 -> x0, local copies, waits for them, and re-layouts: 80.9 us -> none  [device_step(): jnp.take(table_shard, jnp.clip(local_ids, 0, rows_local - 1), axis=0)]
    pallas_call x2, Pallas kernels: 359 us -> 390 us  [scatter_sum(): pl.pallas_call(functools.partial(_scatter_kernel, tuple(pieces), orders,...]
    select_n x4 -> x1, other arithmetic: 20.6 us -> 0.12 us  [device_step(): low = jnp.where(core == 0, mine, recv)]
    dot_general x21 -> x16, matrix products: 110 us -> 106 us  [dot(): lax.dot_general(a, b, (((ca,), (cb,)), ((), ())), preferred_element_type=...]
  transfers between devices with their start and end apart: 5 -> 5, of which waited for: 0 -> 0; matrix products, arithmetic and copies ran while one was open for 17% -> 10% of each run, Pallas kernels for 15% -> 25%
where the time goes in v4:
time: 1030 us; the launch traced here: 1020 us
  Pallas kernels  769 us (75%)
  matrix products  141 us (14%)
  other arithmetic  46.4 us (5%)
  local copies, waits for them, and re-layouts  45.4 us (4%)
  between operations  15.5 us (2%)
    pallas_call x2, Pallas kernels, scatter_sum(): pl.pallas_call(functools.partial(_scatter_kernel, tuple(pieces), orders,...  390 us
    pallas_call x2, Pallas kernels, gather_all(): pl.pallas_call(functools.partial(_gather_kernel, cuts, orders, seq, moves...  254 us
    dot_general x16, matrix products, dot(): lax.dot_general(a, b, (((ca,), (cb,)), ((), ())), preferred_element_type=...  106 us
    pallas_call x1, Pallas kernels, add_rows(): pl.pallas_call(_add_rows_kernel, grid_spec=pltpu.PrefetchScalarGridSpec(n...  54.2 us
    pallas_call x1, Pallas kernels, lookup(): pl.pallas_call(_lookup_kernel, grid_spec=pltpu.PrefetchScalarGridSpec(num...  52.8 us
  transfers between devices with their start and end apart: 5, of which 0 were waited for; matrix products, arithmetic and copies ran while one was open for 10% of the time, Pallas kernels for 25%

profile of v4, /device:TPU:0, one launch (start us, length us, event | category | flops | bytes accessed | tf_op | source)
XLA Modules:
  0.0 1018.8 jit_solution(11327229837904659555)
XLA Ops:
  7.3 1.3 pad.12.refs_0_
  8.6 1.2 constant_dynamic-slice_fusion.3
  10.5 18.4 %all_rows.1 = (s32[32,8,128]{2,1,0:T(8,128)}, bf16[152,896]{1,0:T(8,128)(2,1)}, bf16[28,4864]{1,0:T(8,128)(2,1)}, bf16[512,896]{1,0:T(8,128)(2,1)}) custom-call(s32[8,128]{1,0:T(8,128)} %pad.12.refs_0_, bf16[152,896]{1,0:T(8,128)(2,1)} %refs_1_.1, bf16[28,4864]{1,0:T(8,128)(2,1)} %pad_maximum_fusion.13.refs_2_, bf16[512,896]{1,0:T(8,128)(2,1)} %bitcast.197), custom_call_target="tpu_custom_call" | custom-call | flops 10000000 | bytes 1048576 | tf_op jit(solution)/shard_map/all_rows/pallas_call | solution.py:216
  29.0 2.1 maximum_select_fusion
  31.3 34.2 %gather_all.2 = bf16[32,28,2176]{2,1,0:T(8,128)(2,1)S(1)} custom-call(bf16[28,2176]{1,0:T(8,128)(2,1)S(1)} %constant_dynamic-update-slice_fusion.refs_0_), custom_call_target="tpu_custom_call" | custom-call | flops 200000000 | bytes 7798784 | tf_op jit(solution)/shard_map/gather_all/pallas_call | solution.py:290
  65.5 2.1 copy-done
  67.6 6.0 reshape.662
  74.6 5.9 select_reduce_fusion
  80.6 3.4 copy-done.1
  84.1 52.8 %lookup.1.refs_0_ = bf16[32,512,896]{2,1,0:T(8,128)(2,1)} custom-call(s32[32]{0:T(128)S(1)} %get-tuple-element.46.counts, s32[16384]{0:T(1024)S(1)} %bitcast.180, bf16[4752,896]{1,0:T(8,128)(2,1)S(1)} %copy-done.1), custom_call_target="tpu_custom_call" | custom-call | flops 50000000 | bytes 41943040 | tf_op jit(solution)/shard_map/lookup/pallas_call | solution.py:481
  136.9 172.4 %scatter_sum.2 = bf16[512,896]{1,0:T(8,128)(2,1)S(1)} custom-call(bf16[32,512,896]{2,1,0:T(8,128)(2,1)} %lookup.1.refs_0_), custom_call_target="tpu_custom_call" | custom-call | flops 200000000 | bytes 136937472 | tf_op jit(solution)/shard_map/scatter_sum/pallas_call | solution.py:425
  310.4 1.6 convolution_convert_fusion
  312.2 0.8 copy-done.15
  313.1 1.4 slice_convert_fusion
  314.4 2.1 copy.91
  317.2 0.9 fusion.84
  319.2 6.7 fusion.6
  325.9 8.2 fusion.5
  334.1 7.5 fusion.51
  341.6 3.1 fusion.43
  345.2 0.8 copy.103
  346.6 1.5 mul.625
  348.1 2.8 copy.98
  351.6 11.1 %fusion.57 = f32[1024,2432]{1,0:T(8,128)} fusion(bf16[2432,896]{1,0:T(8,128)(2,1)} %all-gather.5.cloned.1.call-done, bf16[512,896]{1,0:T(8,128)(2,1)} %get-tuple-element.28, bf16[512,896]{1,0:T(8,128)(2,1)S(1)} %bitcast.198), kind=kOutput, calls=%fused_computation.82 | convolution fusion | flops 4466409472 | bytes 16154624 | tf_op jit(solution)/shard_map/dot_general | solution.py:68
  362.6 10.5 %fusion.15 = f32[1024,2432]{1,0:T(8,128)} fusion(bf16[896,4864]{1,0:T(8,128)(2,1)} %all-gather.3.cloned.1.call-done, bf16[512,896]{1,0:T(8,128)(2,1)} %collective-permute-done, bf16[512,896]{1,0:T(8,128)(2,1)S(1)} %fusion.37), kind=kOutput, calls=%fused_computation.25 | convolution fusion | flops 4466409472 | bytes 16154624 | tf_op jit(solution)/shard_map/dot_general | solution.py:68
  373.1 16.8 %multiply_convert_fusion.1 = (bf16[1024,2432]{1,0:T(8,128)(2,1)}, bf16[1024,2432]{1,0:T(8,128)(2,1)}, bf16[1024,2432]{1,0:T(8,128)(2,1)}) fusion(f32[1024,2432]{1,0:T(8,128)} %fusion.57, f32[1024,2432]{1,0:T(8,128)} %fusion.15, bf16[896,4864]{1,0:T(8,128)(2,1)} %all-gather.3.cloned.1.call-done, bf16[512,896]{1,0:T(8,128)(2,1)} %collective-permute-done, ...), kind=kOutput, calls=%fused_computation.14 | convolution fusion | flops 4506255360 | bytes 41058304 | tf_op jit(solution)/shard_map/dot_general | solution.py:68
  390.0 10.2 %fusion.13 = f32[1024,896]{1,0:T(8,128)} fusion(bf16[1024,2432]{1,0:T(8,128)(2,1)} %get-tuple-element.50, bf16[896,4864]{1,0:T(8,128)(2,1)} %all-gather.3.cloned.1.call-done), kind=kOutput, calls=%fused_computation.23 | convolution fusion | flops 4462739456 | bytes 13008896 | tf_op jit(solution)/shard_map/dot_general | solution.py:68
  400.3 7.7 fusion.48
  408.7 8.0 fusion.56
  416.7 5.5 fusion.102
  422.4 8.8 fusion.95
  431.3 8.5 fusion.94
  439.8 0.8 fusion.42
  440.6 1.8 fusion.41
  442.4 1.2 copy-done.10
  443.6 3.8 convolution_convert_fusion.1
  447.4 1.5 copy.93
  448.9 8.1 fusion.61
  457.0 0.8 slice-done.3
  457.7 8.1 fusion
  465.8 8.2 fusion.7
  474.1 2.3 convolution_bitcast_fusion.1
  476.5 2.6 convolution_bitcast_fusion
  479.2 0.8 copy.105
  480.3 0.8 copy.102
  481.1 1.7 multiply_subtract_fusion
  482.9 2.3 pad_maximum_fusion.2
  485.2 2.8 copy.95
  488.2 1.7 copy.97
  489.9 1.0 multiply_reduce_fusion.3
  491.0 3.3 multiply_reduce_fusion
  495.0 2.8 fusion.34
  497.8 3.5 fusion.70
  501.5 4.1 fusion.67.refs_4_
  505.6 217.6 %scatter_sum.3 = (f32[152,896]{1,0:T(8,128)S(1)}, f32[56,2432]{1,0:T(8,128)S(1)}, f32[56,2432]{1,0:T(8,128)S(1)}, f32[32,1152]{1,0:T(8,128)S(1)}, f32[32,896]{1,0:T(8,128)S(1)}) custom-call(f32[16,152,896]{2,1,0:T(8,128)} %bitcast.188, f32[16,56,2432]{2,1,0:T(8,128)} %bitcast.189, f32[16,56,2432]{2,1,0:T(8,128)} %bitcast.190, f32[16,56,1152]{2,1,0:T(8,128)} %bitcast.196, ...), custom_call_target="tpu_custom_call" | custom-call | flops 200000000 | bytes 193380352 | tf_op jit(solution)/shard_map/scatter_sum/pallas_call | solution.py:425
  723.3 1.7 fusion.33
  725.1 0.9 copy-done.20
  726.0 4.0 concatenate.114
  730.0 219.7 %gather_all.3 = (f32[32,3640,128]{2,1,0:T(8,128)}, f32[152,896]{1,0:T(8,128)S(1)}, f32[28,4864]{1,0:T(8,128)S(1)}) custom-call(f32[3640,128]{1,0:T(8,128)S(1)} %bitcast.179, f32[152,896]{1,0:T(8,128)S(1)} %get-tuple-element.29.refs_1_, f32[28,4864]{1,0:T(8,128)S(1)} %constant_dynamic-slice_fusion.2.refs_2_), custom_call_target="tpu_custom_call" | custom-call | flops 200000000 | bytes 119275520 | tf_op jit(solution)/shard_map/gather_all/pallas_call | solution.py:290
  949.8 54.2 %add_rows.1 = f32[33264,128]{1,0:T(8,128)} custom-call(s32[32]{0:T(128)S(1)} %copy-done.7, s32[16384]{0:T(1024)S(1)} %bitcast.181, f32[32,3640,128]{2,1,0:T(8,128)} %get-tuple-element.32.dx_ref), custom_call_target="tpu_custom_call" | custom-call | flops 50000000 | bytes 83886080 | tf_op jit(solution)/shard_map/add_rows/pallas_call | solution.py:532
  1004.0 1.2 slice_reduce_fusion
  1009.2 0.9 pad_maximum_fusion.7
  1010.1 0.9 pad_maximum_fusion.8
  1011.0 0.8 copy.132
  (235 shorter events, 13.3 us)
Async XLA Ops:
  7.2 23.9 %copy-start.62 = (bf16[28]{0:T(256)(128)(2,1)S(1)}, bf16[28]{0:T(256)(128)(2,1)}, u32[]{:S(2)}) copy-start(bf16[28]{0:T(256)(128)(2,1)} %param.25) | copy-start | bytes 172
  7.2 23.9 %copy-start.63 = (bf16[28]{0:T(256)(128)(2,1)S(1)}, bf16[28]{0:T(256)(128)(2,1)}, u32[]{:S(2)}) copy-start(bf16[28]{0:T(256)(128)(2,1)} %param.18) | copy-start | bytes 172
  7.2 24.0 %copy-start.43 = (bf16[28,896]{1,0:T(8,128)(2,1)S(1)}, bf16[28,896]{1,0:T(8,128)(2,1)}, u32[]{:S(2)}) copy-start(bf16[28,896]{1,0:T(8,128)(2,1)} %param.19) | copy-start | bytes 150532
  7.2 24.0 %copy-start.51 = (bf16[28,128]{1,0:T(8,128)(2,1)S(1)}, bf16[28,128]{1,0:T(8,128)(2,1)}, u32[]{:S(2)}) copy-start(bf16[28,128]{1,0:T(8,128)(2,1)} %param.20) | copy-start | bytes 21508
  7.2 24.0 %copy-start.52 = (bf16[28,128]{1,0:T(8,128)(2,1)S(1)}, bf16[28,128]{1,0:T(8,128)(2,1)}, u32[]{:S(2)}) copy-start(bf16[28,128]{1,0:T(8,128)(2,1)} %param.21) | copy-start | bytes 21508
  7.2 24.0 %copy-start.44 = (bf16[28,896]{1,0:T(8,128)(2,1)S(1)}, bf16[28,896]{1,0:T(8,128)(2,1)}, u32[]{:S(2)}) copy-start(bf16[28,896]{1,0:T(8,128)(2,1)} %param.24) | copy-start | bytes 150532
  7.2 344.3 %all-gather.5.cloned.1.call-start = ((), (), s32[]{:S(2)}) async-start(), calls=%async_computation.1 | async-start | bytes 4630528 | tf_op jit(solution)/shard_map/all_gather | solution.py:591
  28.9 333.7 %all-gather.3.cloned.1.call-start = ((), (), s32[]{:S(2)}) async-start(), calls=%async_computation | async-start | bytes 9261056 | tf_op jit(solution)/shard_map/all_gather | solution.py:591
  67.6 6.0 copy-start.45
  74.3 62.5 %copy-start.6 = (s32[32]{0:T(128)}, s32[32]{0:T(128)S(1)}, u32[]{:S(2)}) copy-start(s32[32]{0:T(128)S(1)} %get-tuple-element.46.counts) | copy-start | bytes 388
  80.6 56.3 %copy-start.4 = (s32[4,4,8,128]{3,1,2,0:T(4,128)}, s32[4,4,8,128]{3,1,2,0:T(4,128)S(1)}, u32[]{:S(2)}) copy-start(s32[4,4,8,128]{3,1,2,0:T(4,128)S(1)} %copy.117) | copy-start | bytes 196612
  80.6 3.4 copy-start.1
  136.9 172.4 %copy-start.13 = (bf16[896,2176]{1,0:T(8,128)(2,1)S(1)}, bf16[896,2176]{1,0:T(8,128)(2,1)}, u32[]{:S(2)}) copy-start(bf16[896,2176]{1,0:T(8,128)(2,1)} %reshape.662) | copy-start | bytes 11698180
  309.3 32.3 %copy-start.2 = (bf16[512,896]{1,0:T(8,128)(2,1)}, bf16[512,896]{1,0:T(8,128)(2,1)S(1)}, u32[]{:S(2)}) copy-start(bf16[512,896]{1,0:T(8,128)(2,1)S(1)} %scatter_sum.2) | copy-start | bytes 2752516
  312.0 4.5 copy-start.59
  312.1 4.5 copy-start.53
  312.1 4.5 copy-start.64
  317.2 28.0 %copy-start.41 = (f32[512,2]{0,1:T(2,128)}, f32[512,2]{0,1:T(2,128)S(1)}, u32[]{:S(2)}) copy-start(f32[512,2]{0,1:T(2,128)S(1)} %add_rsqrt_fusion.1) | copy-start | bytes 12292
  317.2 29.4 %copy-start.32 = (f32[512,2,7]{0,2,1:T(8,128)}, f32[512,2,7]{0,2,1:T(8,128)S(1)}, u32[]{:S(2)}) copy-start(f32[512,2,7]{0,2,1:T(8,128)S(1)} %add_rsqrt_fusion) | copy-start | bytes 86020
  318.3 7.6 copy-start.34
  318.3 7.6 copy-start.36
  319.1 6.7 copy-start.23
  319.2 6.7 copy-start.25
  341.6 3.2 copy-start.30
  344.8 6.8 copy-start.19
  345.1 17.6 %collective-permute-start = (bf16[512,896]{1,0:T(8,128)(2,1)S(1)}, bf16[512,896]{1,0:T(8,128)(2,1)}, u32[]{:S(2)}, u32[]{:S(2)}) collective-permute-start(bf16[512,896]{1,0:T(8,128)(2,1)S(1)} %fusion.37), channel_id=1, source_target_pairs={{0,1},{1,0},{2,3},{3,2},{4,5},{5,4},{6,7},{7,6},{8,9},{9,8},{10,11... | collective-permute-start | bytes 2752520 | tf_op jit(solution)/shard_map/ppermute | solution.py:588
  390.0 10.2 %copy-start.60 = (bf16[896,4864]{1,0:T(8,128)(2,1)S(1)}, bf16[896,4864]{1,0:T(8,128)(2,1)}, u32[]{:S(2)}) copy-start(bf16[896,4864]{1,0:T(8,128)(2,1)} %all-gather.3.cloned.1.call-done) | copy-start | bytes 26148868
  390.0 10.2 %copy-start.65 = (bf16[1024,2432]{1,0:T(8,128)(2,1)S(1)}, bf16[1024,2432]{1,0:T(8,128)(2,1)}, u32[]{:S(2)}) copy-start(bf16[1024,2432]{1,0:T(8,128)(2,1)} %get-tuple-element.48) | copy-start | bytes 14942212
  390.0 18.7 %slice-start.8 = ((s8[4980736]{0:T(1024)(128)(4,1)}), s8[4194304]{0:T(1024)(128)(4,1)S(1)}, s32[]{:S(2)}) async-start(s8[4980736]{0:T(1024)(128)(4,1)} %bitcast.224), calls=%async_computation.10 | async-start | bytes 8388608
  400.2 8.4 copy-start.61
  400.2 8.4 slice-start.9
  408.0 8.7 slice-start.4
  408.1 31.7 %collective-permute-start.2 = (f32[512,896]{1,0:T(8,128)S(1)}, f32[512,896]{1,0:T(8,128)S(1)}, u32[]{:S(2)}, u32[]{:S(2)}) collective-permute-start(f32[512,896]{1,0:T(8,128)S(1)} %slice.159), channel_id=1, source_target_pairs={{0,1},{1,0},{2,3},{3,2},{4,5},{5,4},{6,7},{7,6},{8,9},{9,8},{10,11... | collective-permute-start | bytes 5505032 | tf_op jit(solution)/shard_map/ppermute | solution.py:588
  408.7 8.0 slice-start.5
  422.2 9.1 slice-start.6
  422.3 9.0 slice-start.7
  422.3 18.2 %collective-permute-start.1 = (f32[512,896]{1,0:T(8,128)S(1)}, f32[512,896]{1,0:T(8,128)S(1)}, u32[]{:S(2)}, u32[]{:S(2)}) collective-permute-start(f32[512,896]{1,0:T(8,128)S(1)} %slice.157), channel_id=1, source_target_pairs={{0,1},{1,0},{2,3},{3,2},{4,5},{5,4},{6,7},{7,6},{8,9},{9,8},{10,11... | collective-permute-start | bytes 5505032 | tf_op jit(solution)/shard_map/ppermute | solution.py:588
  443.6 13.3 %slice-start = ((s8[14680064]{0:T(1024)(128)(4,1)}), s8[2097152]{0:T(1024)(128)(4,1)S(1)}, s32[]{:S(2)}) async-start(s8[14680064]{0:T(1024)(128)(4,1)} %bitcast.182), calls=%async_computation.2 | async-start | bytes 4194304
  448.8 8.1 slice-start.1
  448.9 8.1 slice-start.2
  448.9 8.9 slice-start.3
  465.8 8.2 copy-start.24
  465.8 8.3 copy-start.26
  476.5 3.4 copy-start.28
  476.5 3.4 copy-start.31
  476.5 3.5 copy-start.18
  476.5 3.5 copy-start.42
  476.5 3.5 copy-start.55
  479.2 3.7 copy-start.9
  479.2 3.7 copy-start.33
  479.2 3.7 copy-start.57
  485.2 2.8 copy-start.38
  488.0 3.0 copy-start.48
  491.0 3.3 copy-start.3
  491.0 4.0 copy-start.14
  491.0 4.0 copy-start.39
  491.0 4.0 copy-start.47
  491.0 4.0 copy-start.50
  497.8 3.8 copy-start.11
  505.6 217.7 %copy-start.12 = (f32[512,896]{1,0:T(8,128)S(1)}, f32[512,896]{1,0:T(8,128)}, u32[]{:S(2)}) copy-start(f32[512,896]{1,0:T(8,128)} %copy-done.10) | copy-start | bytes 5505028
  505.6 217.7 %copy-start.22 = (f32[512,896]{1,0:T(8,128)S(1)}, f32[512,896]{1,0:T(8,128)}, u32[]{:S(2)}) copy-start(f32[512,896]{1,0:T(8,128)} %get-tuple-element.94) | copy-start | bytes 5505028
  726.0 223.7 %copy-start.5 = (s32[4,4,8,128]{3,1,2,0:T(4,128)S(1)}, s32[4,4,8,128]{3,1,2,0:T(4,128)}, u32[]{:S(2)}) copy-start(s32[4,4,8,128]{3,1,2,0:T(4,128)} %copy-done.4) | copy-start | bytes 196612
  726.0 223.7 %copy-start.7 = (s32[32]{0:T(128)S(1)}, s32[32]{0:T(128)}, u32[]{:S(2)}) copy-start(s32[32]{0:T(128)} %copy-done.6) | copy-start | bytes 388
  949.7 58.6 %copy-start.21 = (f32[56,4864]{1,0:T(8,128)S(1)}, f32[56,4864]{1,0:T(8,128)}, u32[]{:S(2)}) copy-start(f32[56,4864]{1,0:T(8,128)} %copy-done.20) | copy-start | bytes 3268612
  (17 other events, 29.6 us)
Sparse Core Ops, SparseCore 0:
  29.0 77.8 all-gather.4
  110.2 190.4 all-gather.2

commit v5 on v4

--- a/solution.py
+++ b/solution.py
@@ -13,55 +13,6 @@
 F32 = jnp.float32
 BF16 = jnp.bfloat16
 MESH = pl.DeviceIdType.MESH
-
-
-def rope_tables(positions, head_dim):
-    half_dim = head_dim // 2
-    inv_freq = jnp.exp(jnp.arange(half_dim, dtype=jnp.float32) * (-2.0 * math.log(ROPE_THETA) / head_dim))
-    angles = positions.astype(jnp.float32)[:, :, None] * inv_freq
-    return jnp.cos(angles), jnp.sin(angles)
-
-
-def rotate(values, cos_t, sin_t):
-    half_dim = values.shape[-1] // 2
-    lead_half = values[..., :half_dim]
-    tail_half = values[..., half_dim:]
-    return jnp.concatenate([lead_half * cos_t - tail_half * sin_t, tail_half * cos_t + lead_half * sin_t], axis=-1)
-
-
-def norm_fwd(values):
-    values_f = values.astype(jnp.float32)
-    inv_rms = lax.rsqrt(jnp.mean(values_f * values_f, axis=-1, keepdims=True) + NORM_EPS)
-    return values_f * inv_rms, inv_rms
-
-
-def norm_bwd(grad_out, normed, inv_rms, norm_gain):
-    grad_normed = grad_out * norm_gain.astype(jnp.float32)
-    mean_term = jnp.mean(grad_normed * normed, axis=-1, keepdims=True)
-    return inv_rms * (grad_normed - normed * mean_term)
-
-
-def attn_fwd(q_rot, k_rot, v_raw):
-    seq_len = q_rot.shape[1]
-    attn_scale = q_rot.shape[-1] ** -0.5
-    scores = jnp.einsum('bqgrh,bkgh->bgrqk', q_rot, k_rot, preferred_element_type=jnp.float32) * attn_scale
-    causal = lax.broadcasted_iota(jnp.int32, (seq_len, seq_len), 0) >= lax.broadcasted_iota(jnp.int32, (seq_len, seq_len), 1)
-    attn_probs = jax.nn.softmax(jnp.where(causal, scores, -1e30), axis=-1)
-    attn_heads = jnp.einsum('bgrqk,bkgh->bqgrh', attn_probs.astype(jnp.bfloat16), v_raw, preferred_element_type=jnp.float32)
-    return attn_heads.astype(jnp.bfloat16), attn_probs
-
-
-def attn_bwd(grad_out, q_rot, k_rot, v_raw, attn_probs):
-    attn_scale = q_rot.shape[-1] ** -0.5
-    grad_b = grad_out.astype(jnp.bfloat16)
-    probs_b = attn_probs.astype(jnp.bfloat16)
-    grad_probs = jnp.einsum('bqgrh,bkgh->bgrqk', grad_b, v_raw, preferred_element_type=jnp.float32)
-    grad_v = jnp.einsum('bgrqk,bqgrh->bkgh', probs_b, grad_b, preferred_element_type=jnp.float32)
-    grad_scores = attn_probs * (grad_probs - jnp.sum(grad_probs * attn_probs, axis=-1, keepdims=True)) * attn_scale
-    scores_b = grad_scores.astype(jnp.bfloat16)
-    grad_q = jnp.einsum('bgrqk,bkgh->bqgrh', scores_b, k_rot, preferred_element_type=jnp.float32)
-    grad_k = jnp.einsum('bgrqk,bqgrh->bkgh', scores_b, q_rot, preferred_element_type=jnp.float32)
-    return grad_q, grad_k, grad_v
 
 
 def dot(a, b, ca, cb):
@@ -226,17 +177,18 @@
     return res[0], res[1:]
 
 
-def _gather_kernel(cuts, orders, seq, moves, *refs):
-    n = len(moves)
-    in_ref, src, out_ref, dst = refs[0], refs[1:1 + n], refs[1 + n], refs[2 + n:2 + 2 * n]
-    own_sem, send_sem, recv_sem, p_send, p_recv, m_send, m_recv = refs[2 + 2 * n:]
+def _gather_kernel(pieces, orders, seq, moves, n_arr, *refs):
+    n, m = len(moves), len(pieces)
+    ins, src, outs, dst = refs[:n_arr], refs[n_arr:n_arr + n], refs[n_arr + n:2 * n_arr + n], refs[2 * n_arr + n:2 * n_arr + 2 * n]
+    own_sem, send_sem, recv_sem, p_send, p_recv, m_send, m_recv = refs[2 * n_arr + 2 * n:]
     me = lax.axis_index(AXIS_NAME)
     at = _Place(me)
     ends = list(_passes(moves, me))
-    starts = [sum(cuts[:i]) for i in range(len(cuts))]
-
-    def part(slot, piece):
-        return out_ref.at[slot] if len(cuts) == 1 else out_ref.at[slot, pl.ds(starts[piece], cuts[piece])]
+
+    def part(kc, core, piece):
+        arr, r0, rows, shared = pieces[piece]
+        slot = 2 * kc + core if shared else kc
+        return outs[arr].at[slot] if rows == outs[arr].shape[1] else outs[arr].at[slot, pl.ds(r0, rows)]
 
     def run(u):
         sides = ['a', 'b', 'z+'] + (['z-'] if u else [])
@@ -244,60 +196,68 @@
         _meet([at.side(s) for s in sides] + [at.partner], me, far[0] if far else ())
         started, moving = [], []
 
-        def send(src_ref, slot, piece, s_sem, r_sem, dev):
-            copy = _remote(src_ref, part(slot, piece), s_sem, r_sem, dev)
+        def send(src_ref, dst_ref, s_sem, r_sem, dev):
+            copy = _remote(src_ref, dst_ref, s_sem, r_sem, dev)
             copy.start()
             started.append(copy)
 
-        own = pltpu.make_async_copy(in_ref, out_ref.at[me], own_sem)
-        own.start()
-        count, handed = 0, [0] * len(cuts)
-        for key in [(0, 0, u, i) for i in range(len(cuts))] + [_unpack(c) for c in seq[u]]:
+        count, handed = 0, [0] * m
+        for key in [(0, 0, u, i) for i in range(m)] + [_unpack(c) for c in seq[u]]:
             piece = key[3]
+            arr, r0, rows, shared = pieces[piece]
             kc = at.chip(key)
-            slot = 2 * kc + at.core
+            place = part(kc, at.core, piece)
             if _via(u, key, orders) is None:
-                ref = in_ref if len(cuts) == 1 else in_ref.at[pl.ds(starts[piece], cuts[piece])]
+                ref = ins[arr] if rows == ins[arr].shape[0] else ins[arr].at[pl.ds(r0, rows)]
             else:
-                ref = part(slot, piece)
+                ref = place
                 _landed(ref, recv_sem.at[piece, kc])
             for side in _onward(u, key, orders):
-                send(ref, slot, piece, send_sem.at[count], recv_sem.at[piece, kc], at.side(side))
+                send(ref, place, send_sem.at[count], recv_sem.at[piece, kc], at.side(side))
                 count += 1
-            send(ref, slot, piece, p_send.at[piece, handed[piece]], p_recv.at[piece, kc], at.partner)
-            handed[piece] += 1
-            if key[:3] == (0, 0, u) and piece == len(cuts) - 1:
+            if shared:
+                send(ref, place, p_send.at[piece, handed[piece]], p_recv.at[piece, kc], at.partner)
+                handed[piece] += 1
+            if key == (0, 0, u, m - 1):
                 for i, (to, _) in enumerate(ends):
                     moving.append(_start_move(moves[i], src[i], dst[i], m_send.at[i], m_recv.at[i], to, me))
-        for piece in range(len(cuts)):
-            for kc in range(16):
-                _landed(part(2 * kc + 1 - at.core, piece), p_recv.at[piece, kc])
+                own = [pltpu.make_async_copy(ins[i], outs[i].at[me if pieces_shared[i] else me // 2], own_sem.at[i]) for i in range(n_arr)]
+                for copy in own:
+                    copy.start()
+        for piece in range(m):
+            if pieces[piece][3]:
+                for kc in range(16):
+                    _landed(part(kc, 1 - at.core, piece), p_recv.at[piece, kc])
         for i, (to, _) in enumerate(ends):
             _end_move(moves[i], moving[i], dst[i], m_recv.at[i], to, me)
-        own.wait()
+        for copy in own:
+            copy.wait()
         for copy in started:
             copy.wait_send()
 
+    pieces_shared = {p[0]: p[3] for p in pieces}
     for u in (0, 1):
         pl.when(at.u == u)(functools.partial(run, u))
 
 
-def gather_all(block, cuts, orders, seq, moved, moves, n_dev, collective_id):
-    n, m = len(moves), len(cuts)
+def gather_all(blocks, pieces, orders, seq, moved, moves, n_dev, collective_id):
+    n, m, n_arr = len(moves), len(pieces), len(blocks)
     dma = pltpu.SemaphoreType.DMA
     vmem, hbm = pl.BlockSpec(memory_space=pltpu.VMEM), pl.BlockSpec(memory_space=pl.ANY)
-    nbytes = block.size * block.dtype.itemsize
+    nbytes = sum(v.size * v.dtype.itemsize for v in blocks)
+    shared = {p[0]: p[3] for p in pieces}
     res = pl.pallas_call(
-        functools.partial(_gather_kernel, cuts, orders, seq, moves),
-        out_shape=[jax.ShapeDtypeStruct((n_dev,) + block.shape, block.dtype)] + [jax.ShapeDtypeStruct(v.shape, v.dtype) for v in moved],
-        in_specs=[vmem] + [hbm] * n,
-        out_specs=[hbm] * (1 + n),
-        scratch_shapes=[dma, dma((24 * m,)), dma((m, 16)), dma((m, 16)), dma((m, 16)), dma((max(n, 1),)), dma((max(n, 1),))],
+        functools.partial(_gather_kernel, tuple(pieces), orders, seq, moves, n_arr),
+        out_shape=[jax.ShapeDtypeStruct((n_dev if shared[i] else n_dev // 2,) + v.shape, v.dtype) for i, v in enumerate(blocks)] + [
+            jax.ShapeDtypeStruct(v.shape, v.dtype) for v in moved],
+        in_specs=[vmem] * n_arr + [hbm] * n,
+        out_specs=[hbm] * (n_arr + n),
+        scratch_shapes=[dma((n_arr,)), dma((24 * m,)), dma((m, 16)), dma((m, 16)), dma((m, 16)), dma((max(n, 1),)), dma((max(n, 1),))],
         compiler_params=pltpu.CompilerParams(collective_id=collective_id, has_side_effects=True, vmem_limit_bytes=nbytes + (8 << 20)),
         cost_estimate=pl.CostEstimate(flops=200_000_000, bytes_accessed=nbytes * 64, transcendentals=0),
         name='gather_all',
-    )(block, *moved)
-    return res[0], res[1:]
+    )(*blocks, *moved)
+    return res[:n_arr], res[n_arr:]
 
 
 def _slots(pieces, orders, seq):
@@ -458,12 +418,11 @@
     lax.fori_loop(0, seq // 8, clear, 0)
 
     def pick(i, _):
-        for t in range(4):
-            code = codes[b * seq + i * 4 + t]
-            row, pos = code & 8191, code >> 13
-            block[pl.ds((pos >> 3) * (8 * n_col) + (pos & 7), n_col, stride=8), :] = rows[pl.ds((row >> 3) * (8 * n_col) + (row & 7), n_col, stride=8), :]
+        for t in range(8):
+            code = codes[b * seq + i * 8 + t]
+            block[pl.ds(code >> 16, n_col, stride=8), :] = rows[pl.ds(code & 65535, n_col, stride=8), :]
         return 0
-    lax.fori_loop(0, (counts[b] + 3) // 4, pick, 0)
+    lax.fori_loop(0, (counts[b] + 7) // 8, pick, 0)
 
     def narrow(i, _):
         line = pl.multiple_of(i * 16 * n_col, 8)
@@ -494,37 +453,64 @@
     )(counts, codes, table)
 
 
-def _add_rows_kernel(counts, codes, dx_ref, out_ref):
-    b = pl.program_id(0)
+def _add_rows_kernel(counts, codes, dx_ref, out_ref, buf, sem):
+    n_src, lines, _ = dx_ref.shape
     n_col = 7
-
-    @pl.when(b == 0)
-    def _():
-        def clear(i, _):
-            out_ref[pl.ds(pl.multiple_of(i * 8 * n_col, 8), 8 * n_col), :] = jnp.zeros((8 * n_col, 128), F32)
+    seq = codes.shape[0] // n_src
+    cut = lines // 5
+    depth = buf.shape[0]
+
+    def fetch(b):
+        for i in range(5):
+            some = pl.ds(i * cut, cut)
+            pltpu.make_async_copy(dx_ref.at[b, some], buf.at[lax.rem(b, depth), some], sem.at[lax.rem(b, depth)]).start()
+
+    for b in range(depth - 1):
+        fetch(b)
+
+    def clear(i, _):
+        out_ref[pl.ds(pl.multiple_of(i * 16 * n_col, 8), 16 * n_col), :] = jnp.zeros((16 * n_col, 128), F32)
+        return 0
+    lax.fori_loop(0, out_ref.shape[0] // (16 * n_col), clear, 0)
+
+    def source(b, _):
+        at = lax.rem(b, depth)
+
+        @pl.when(b + depth - 1 < n_src)
+        def _():
+            fetch(b + depth - 1)
+        pltpu.make_async_copy(dx_ref.at[b], buf.at[at], sem.at[at]).wait()
+
+        def add(first, i):
+            code = codes[b * seq + first + i]
+            line = pl.ds(code & 65535, n_col, stride=8)
+            out_ref[line, :] = out_ref[line, :] + buf[at, pl.ds(code >> 16, n_col, stride=8), :]
+
+        def add_pair(i, _):
+            code0, code1 = codes[b * seq + i * 2], codes[b * seq + i * 2 + 1]
+            line0, line1 = code0 & 65535, code1 & 65535
+            new0 = buf[at, pl.ds(code0 >> 16, n_col, stride=8), :]
+            new1 = buf[at, pl.ds(code1 >> 16, n_col, stride=8), :]
+            old0 = out_ref[pl.ds(line0, n_col, stride=8), :]
+            old1 = out_ref[pl.ds(line1, n_col, stride=8), :]
+            sum0 = old0 + new0
+            out_ref[pl.ds(line0, n_col, stride=8), :] = sum0
+            out_ref[pl.ds(line1, n_col, stride=8), :] = jnp.where(line0 == line1, sum0, old1) + new1
             return 0
-        lax.fori_loop(0, out_ref.shape[0] // (8 * n_col), clear, 0)
-
-    seq = codes.shape[0] // counts.shape[0]
-
-    def add(i, _):
-        for t in range(4):
-            code = codes[b * seq + i * 4 + t]
-            row, pos = code & 8191, code >> 13
-            src = dx_ref[0, pl.ds((pos >> 3) * (8 * n_col) + (pos & 7), n_col, stride=8), :]
-            at = pl.ds((row >> 3) * (8 * n_col) + (row & 7), n_col, stride=8)
-            out_ref[at, :] = out_ref[at, :] + src
+
+        def add_four(i, _):
+            add_pair(2 * i, 0)
+            add_pair(2 * i + 1, 0)
+            return 0
+        n = counts[b]
+        lax.fori_loop(0, n // 4, add_four, 0)
+
+        def add_one(i, _):
+            add(0, i)
+            return 0
+        lax.fori_loop((n // 4) * 4, n, add_one, 0)
         return 0
-    lax.fori_loop(0, counts[b] // 4, add, 0)
-
-    def add_one(i, _):
-        code = codes[b * seq + i]
-        row, pos = code & 8191, code >> 13
-        src = dx_ref[0, pl.ds((pos >> 3) * (8 * n_col) + (pos & 7), n_col, stride=8), :]
-        at = pl.ds((row >> 3) * (8 * n_col) + (row & 7), n_col, stride=8)
-        out_ref[at, :] = out_ref[at, :] + src
-        return 0
-    lax.fori_loop((counts[b] // 4) * 4, counts[b], add_one, 0)
+    lax.fori_loop(0, n_src, source, 0)
 
 
 def add_rows(dx, counts, codes, n_rows):
@@ -533,12 +519,13 @@
         _add_rows_kernel,
         grid_spec=pltpu.PrefetchScalarGridSpec(
             num_scalar_prefetch=2,
-            grid=(n_src,),
-            in_specs=[pl.BlockSpec((1, lines, 128), lambda b, *_: (b, 0, 0))],
-            out_specs=pl.BlockSpec((n_rows * 7, 128), lambda b, *_: (0, 0)),
+            grid=(),
+            in_specs=[pl.BlockSpec(memory_space=pl.ANY)],
+            out_specs=pl.BlockSpec(memory_space=pltpu.VMEM),
+            scratch_shapes=[pltpu.VMEM((4, lines, 128), F32), pltpu.SemaphoreType.DMA((4,))],
         ),
         out_shape=jax.ShapeDtypeStruct((n_rows * 7, 128), F32),
-        compiler_params=pltpu.CompilerParams(vmem_limit_bytes=48 << 20, dimension_semantics=('arbitrary',)),
+        compiler_params=pltpu.CompilerParams(vmem_limit_bytes=48 << 20),
         cost_estimate=pl.CostEstimate(flops=50_000_000, bytes_accessed=80 << 20, transcendentals=0),
         name='add_rows',
     )(counts, codes, dx)
@@ -554,21 +541,255 @@
     return v.reshape(rows // 8, dim // 128, 8, 128).transpose(0, 2, 1, 3).reshape(rows, dim)
 
 
+def _rms(v):
+    return lax.rsqrt(jnp.mean(v * v, axis=-1, keepdims=True) + NORM_EPS)
+
+
+def _head_mean(v, low):
+    first = jnp.sum(jnp.where(low, v, 0.0), axis=-1, keepdims=True)
+    second = jnp.sum(jnp.where(low, 0.0, v), axis=-1, keepdims=True)
+    return jnp.where(low, first, second) * (1.0 / 64.0)
+
+
+def _turn(v, cos_t, sin_t, lead):
+    return v * cos_t + jnp.where(lead, -pltpu.roll(v, 96, 1), pltpu.roll(v, 32, 1)) * sin_t
+
+
+def _spread(tile, low, ref):
+    first = jnp.where(low, tile, 0.0)
+    second = jnp.where(low, 0.0, tile)
+    ref[0] = first.astype(BF16)
+    ref[1] = pltpu.roll(first, 64, 1).astype(BF16)
+    ref[2] = pltpu.roll(second, 64, 1).astype(BF16)
+    ref[3] = second.astype(BF16)
+
+
+def _probs(q, k, block):
+    scores = dot(q, k, 1, 1) * 0.125
+    n = scores.shape[1]
+    row = lax.broadcasted_iota(jnp.int32, scores.shape, 0) + block
+    col = lax.broadcasted_iota(jnp.int32, scores.shape, 1)
+    scores = jnp.where(row >= col, scores, -1e30)
+    e = jnp.exp(scores - jnp.max(scores, axis=-1, keepdims=True))
+    return e * (1.0 / jnp.sum(e, axis=-1, keepdims=True))
+
+
+def _lanes(rows):
+    lane = lax.broadcasted_iota(jnp.int32, (rows, 128), 1)
+    return lane < 64, lane % 64 < 32
+
+
+def _attn_fwd_kernel(x_ref, w_ref, gain_ref, cos_ref, sin_ref, qk_gain_ref, in_ref, raw_ref, q_ref, k_ref, flat_ref, hid_ref, mlp_ref, kk, vv):
+    seq, dim = x_ref.shape
+    n_q = dim // 128
+    step = 128
+    n_in = raw_ref.shape[1]
+
+    def project(r, _):
+        at = pl.ds(pl.multiple_of(r * step, step), step)
+        low, lead = _lanes(step)
+        x = x_ref[at, :].astype(F32)
+        m1 = (x * _rms(x) * gain_ref[0:1, :]).astype(BF16)
+        in_ref[at, :] = m1
+        raw = dot(m1, w_ref[:, :n_in], 1, 0).astype(BF16)
+        raw_ref[at, :] = raw
+        cos_t, sin_t = cos_ref[at, :], sin_ref[at, :]
+        for t in range(n_q + 1):
+            v = raw[:, t * 128:(t + 1) * 128].astype(F32)
+            v = v * lax.rsqrt(_head_mean(v * v, low) + NORM_EPS)
+            which = int(t == n_q)
+            v = _turn(v * qk_gain_ref[8 * which:8 * which + 1, :], cos_t, sin_t, lead).astype(BF16)
+            if which:
+                k_ref[at, :] = v
+            else:
+                q_ref[at, t * 128:(t + 1) * 128] = v
+        return 0
+    lax.fori_loop(0, seq // step, project, 0)
+    low, _ = _lanes(seq)
+    _spread(k_ref[...].astype(F32), low, kk)
+    _spread(raw_ref[:, n_in - 128:].astype(F32), low, vv)
+
+    def heads(t, _):
+        tile = pl.ds(pl.multiple_of(t * 128, 128), 128)
+        for b in range(seq // step):
+            n = (b + 1) * step
+            q = q_ref[b * step:n, tile]
+            total = None
+            for side in range(2):
+                i = 2 * ((2 * t + side) // 7) + side
+                p = _probs(q, kk[i, :n, :], b * step).astype(BF16)
+                o = dot(p, vv[i, :n, :], 1, 0)
+                total = o if total is None else total + o
+            flat_ref[b * step:n, tile] = total.astype(BF16)
+        return 0
+    lax.fori_loop(0, n_q, heads, 0)
+
+    def finish(r, _):
+        at = pl.ds(pl.multiple_of(r * step, step), step)
+        h = (x_ref[at, :].astype(F32) + dot(flat_ref[at, :], w_ref[:, n_in:n_in + dim], 1, 0)).astype(BF16)
+        hid_ref[at, :] = h
+        h = h.astype(F32)
+        mlp_ref[at, :] = (h * _rms(h) * gain_ref[8:9, :]).astype(BF16)
+        return 0
+    lax.fori_loop(0, seq // step, finish, 0)
+
+
+def attn_forward(x, w, gains, cos_t, sin_t, qk_gain, n_in):
+    seq, dim = x.shape
+    vmem = pl.BlockSpec(memory_space=pltpu.VMEM)
+    sds = lambda n: jax.ShapeDtypeStruct((seq, n), BF16)
+    return pl.pallas_call(
+        _attn_fwd_kernel,
+        out_shape=[sds(dim), sds(n_in), sds(dim), sds(128), sds(dim), sds(dim), sds(dim)],
+        in_specs=[vmem] * 6,
+        out_specs=[vmem] * 7,
+        scratch_shapes=[pltpu.VMEM((4, seq, 128), BF16), pltpu.VMEM((4, seq, 128), BF16)],
+        compiler_params=pltpu.CompilerParams(vmem_limit_bytes=40 << 20),
+        cost_estimate=pl.CostEstimate(flops=4_000_000_000, bytes_accessed=12 << 20, transcendentals=4_000_000),
+        name='attn_forward',
+    )(x, w, gains, cos_t, sin_t, qk_gain)
+
+
+def _attn_bwd_kernel(x_ref, w_ref, gain_ref, cos_ref, sin_ref, qk_gain_ref, in_ref, raw_ref, q_ref, k_ref, flat_ref, hid_ref, dy_ref, part_ref, recv_ref,
+                     dx_ref, dw_in_ref, dw_out_ref, kk, vv, dk, dv, gh, hb, do, dqkv):
+    seq, dim = x_ref.shape
+    n_q = dim // 128
+    step = 128
+    n_blk = seq // step
+    n_in = raw_ref.shape[1]
+
+    def norm_back(grad, normed, inv, gain):
+        grad = grad * gain
+        return inv * (grad - normed * jnp.mean(grad * normed, axis=-1, keepdims=True))
+
+    def hidden(r, total):
+        at = pl.ds(pl.multiple_of(r * step, step), step)
+        grad = part_ref[at, :] + recv_ref[at, :]
+        h = hid_ref[at, :].astype(F32)
+        inv = _rms(h)
+        normed = h * inv
+        g = dy_ref[at, :].astype(F32) + norm_back(grad, normed, inv, gain_ref[8:9, :])
+        gh[at, :] = g
+        g = g.astype(BF16)
+        hb[at, :] = g
+        do[at, :] = dot(g, w_ref[:, n_in:n_in + dim], 1, 1).astype(BF16)
+        return total + jnp.sum(grad * normed, axis=0, keepdims=True)
+    mlp_gain = lax.fori_loop(0, n_blk, hidden, jnp.zeros((1, dim), F32))
+
+    low_all, _ = _lanes(seq)
+    _spread(k_ref[...].astype(F32), low_all, kk)
+    _spread(raw_ref[:, n_in - 128:].astype(F32), low_all, vv)
+    dk[...] = jnp.zeros_like(dk)
+    dv[...] = jnp.zeros_like(dv)
+
+    def raw_back(grad, tile, at, which, low, lead):
+        v = raw_ref[at, tile].astype(F32)
+        inv = lax.rsqrt(_head_mean(v * v, low) + NORM_EPS)
+        normed = v * inv
+        grad = _turn(grad, cos_ref[at, :], -sin_ref[at, :], lead)
+        terms = jnp.sum(grad * normed, axis=0, keepdims=True)
+        grad = grad * qk_gain_ref[8 * which:8 * which + 1, :]
+        return inv * (grad - normed * _head_mean(grad * normed, low)), terms
+
+    def heads(t, total):
+        tile = pl.ds(pl.multiple_of(t * 128, 128), 128)
+        low, lead = _lanes(step)
+        for b in range(n_blk):
+            n = (b + 1) * step
+            at = pl.ds(b * step, step)
+            q = q_ref[at, tile]
+            g = do[at, tile]
+            grad_q = None
+            for side in range(2):
+                i = 2 * ((2 * t + side) // 7) + side
+                k = kk[i, :n, :]
+                p = _probs(q, k, b * step)
+                dp = dot(g, vv[i, :n, :], 1, 1)
+                ds = (p * (dp - jnp.sum(dp * p, axis=-1, keepdims=True)) * 0.125).astype(BF16)
+                dv[i, :n, :] = dv[i, :n, :] + dot(p.astype(BF16), g, 0, 0)
+                dk[i, :n, :] = dk[i, :n, :] + dot(ds, q, 0, 0)
+                part = dot(ds, k, 1, 0)
+                grad_q = part if grad_q is None else grad_q + part
+            back, terms = raw_back(grad_q, tile, at, 0, low, lead)
+            dqkv[at, tile] = back.astype(BF16)
+            total = total + terms
+        return total
+    q_gain = lax.fori_loop(0, n_q, heads, jnp.zeros((1, 128), F32))
+
+    def keys(r, total):
+        at = pl.ds(pl.multiple_of(r * step, step), step)
+        low, lead = _lanes(step)
+
+        def join(ref):
+            return jnp.where(low, ref[0, at, :] + pltpu.roll(ref[1, at, :], 64, 1), ref[3, at, :] + pltpu.roll(ref[2, at, :], 64, 1))
+        back, terms = raw_back(join(dk), pl.ds(dim, 128), at, 1, low, lead)
+        dqkv[at, dim:dim + 128] = back.astype(BF16)
+        dqkv[at, dim + 128:] = join(dv).astype(BF16)
+        return total + terms
+    k_gain = lax.fori_loop(0, n_blk, keys, jnp.zeros((1, 128), F32))
+
+    def inputs(r, total):
+        at = pl.ds(pl.multiple_of(r * step, step), step)
+        grad = dot(dqkv[at, :], w_ref[:, :n_in], 1, 1)
+        x = x_ref[at, :].astype(F32)
+        inv = _rms(x)
+        normed = x * inv
+        dx_ref[at, :] = gh[at, :] + norm_back(grad, normed, inv, gain_ref[0:1, :])
+        return total + jnp.sum(grad * normed, axis=0, keepdims=True)
+    attn_gain = lax.fori_loop(0, n_blk, inputs, jnp.zeros((1, dim), F32))
+
+    low, _ = _lanes(8)
+    row = lax.broadcasted_iota(jnp.int32, (8, dim), 0)
+    both = jnp.where(low, jnp.broadcast_to(q_gain, (8, 128)) + pltpu.roll(jnp.broadcast_to(q_gain, (8, 128)), 64, 1),
+                     jnp.broadcast_to(k_gain, (8, 128)) + pltpu.roll(jnp.broadcast_to(k_gain, (8, 128)), 64, 1))
+    dx_ref[seq:, :] = jnp.where(row == 1, jnp.broadcast_to(attn_gain, (8, dim)), jnp.where(row == 2, jnp.broadcast_to(mlp_gain, (8, dim)), 0.0))
+    dx_ref[seq:, :128] = jnp.where(row[:, :128] == 0, both, dx_ref[seq:, :128])
+
+    def weights(t, _):
+        tile = pl.ds(pl.multiple_of(t * 128, 128), 128)
+        dw_in_ref[tile, :] = dot(in_ref[:, tile], dqkv[...], 0, 0)
+        dw_out_ref[tile, :] = dot(flat_ref[:, tile], hb[...], 0, 0)
+        return 0
+    lax.fori_loop(0, n_q, weights, 0)
+
+
+def attn_backward(x, w, gains, cos_t, sin_t, qk_gain, saved, dy, part, recv):
+    seq, dim = x.shape
+    n_in = saved[1].shape[1]
+    vmem = pl.BlockSpec(memory_space=pltpu.VMEM)
+    scr = lambda *s: pltpu.VMEM(s[:-1], s[-1])
+    return pl.pallas_call(
+        _attn_bwd_kernel,
+        out_shape=[jax.ShapeDtypeStruct((seq + 8, dim), F32), jax.ShapeDtypeStruct((dim, n_in), F32), jax.ShapeDtypeStruct((dim, dim), F32)],
+        in_specs=[vmem] * 15,
+        out_specs=[vmem] * 3,
+        scratch_shapes=[scr(4, seq, 128, BF16), scr(4, seq, 128, BF16), scr(4, seq, 128, F32), scr(4, seq, 128, F32), scr(seq, dim, F32),
+                        scr(seq, dim, BF16), scr(seq, dim, BF16), scr(seq, n_in, BF16)],
+        compiler_params=pltpu.CompilerParams(vmem_limit_bytes=52 << 20),
+        cost_estimate=pl.CostEstimate(flops=9_000_000_000, bytes_accessed=30 << 20, transcendentals=4_000_000),
+        name='attn_backward',
+    )(x, w, gains, cos_t, sin_t, qk_gain, *saved[:6], dy, part, recv)
+
+
+def _codes(numbers, count):
+    return tuple(numbers[i // 10] // 128 ** (i % 10) % 128 for i in range(count))
+
+
 ROWS_SEQ = (
-    (8, 32, 64, 9, 33, 65, 10, 34, 66, 16, 40, 72, 96, 17, 41, 48, 18, 42, 74, 73, 97, 49, 98, 24, 80, 104, 25, 56, 57, 81, 105, 26, 50, 82, 112, 113, 58, 90, 88, 89, 122, 120, 106, 121, 114),
-    (0, 16, 40, 72, 1, 17, 41, 73, 2, 18, 42, 74, 24, 34, 66, 32, 48, 64, 80, 25, 104, 26, 50, 82, 33, 49, 58, 90, 56, 65, 81, 105, 98, 122, 57, 106, 114, 88, 96, 112, 89, 97, 113, 120, 121),
+    _codes((152348940317322383368, 678662145372396725288, 751232056588892674273, 827272104050806263145, 30857149562), 45),
+    _codes((166206088102504171520, 236385149464955200810, 603605329936848293224, 1039985241786269873361, 32734212313), 45),
 )
 ATTN_SEQ = (
-    (8, 32, 64, 16, 40, 72, 96, 24, 48, 80, 104, 56, 88, 112, 120),
-    (0, 16, 40, 72, 24, 32, 48, 64, 80, 104, 56, 88, 96, 112, 120),
+    _codes((370142165075936415752, 972012016723415295145, 1124725529257844811929), 30),
+    _codes((961577811093152729088, 751808515438843144256, 1124738970787495025897), 30),
 )
 LOOKUP_SEQ = (
-    (8, 32, 64, 9, 33, 65, 10, 34, 66, 16, 40, 72, 96, 17, 41, 48, 18, 42, 74, 73, 97, 49, 98, 24, 80, 104, 25, 56, 26, 50, 82, 81, 105, 57, 112, 58, 90, 113, 88, 106, 89, 122, 120, 114, 121),
-    (0, 16, 40, 72, 1, 17, 41, 73, 2, 18, 42, 74, 24, 34, 66, 32, 48, 64, 80, 104, 25, 26, 50, 82, 33, 49, 58, 90, 65, 81, 56, 105, 98, 57, 106, 122, 88, 96, 114, 112, 89, 97, 113, 120, 121),
+    _codes((152348940317322383368, 678662145372396725288, 463073738031218858209, 984082515373917366482, 32721747289), 45),
+    _codes((166206088102504171520, 965031540376482489642, 751827800872866057497, 1041286668292143494328, 32734212313), 45),
 )
 GRAD_SEQ = (
-    (8, 32, 64, 9, 33, 65, 10, 34, 66, 11, 35, 67, 12, 36, 68, 41, 16, 40, 72, 96, 42, 73, 97, 17, 18, 74, 98, 49, 19, 43, 75, 99, 100, 20, 44, 76, 50, 105, 80, 104, 24, 48, 106, 81, 82, 25, 113, 26, 114, 57, 27, 51, 83, 28, 52, 84, 58, 88, 112, 89, 56, 90, 59, 91, 121, 60, 92, 107, 122, 123, 108, 120, 124, 115, 116),
-    (0, 16, 40, 72, 1, 17, 41, 73, 2, 18, 42, 74, 3, 19, 43, 75, 4, 20, 44, 76, 32, 35, 67, 24, 33, 48, 49, 36, 68, 64, 80, 104, 25, 34, 50, 26, 27, 51, 83, 57, 105, 65, 81, 28, 52, 84, 99, 100, 58, 56, 59, 91, 106, 66, 82, 60, 92, 107, 123, 108, 124, 115, 116, 96, 88, 113, 112, 97, 89, 98, 114, 90, 121, 122, 120),
+    _codes((106232080133048504328, 890654452102748905891, 398002109975241450666, 965054631626560582091, 533961906380267493400, 829000359395158448539, 1143326429365316545848, 31381732460), 75),
+    _codes((166206088102504171520, 704158088118449268010, 595216210114064208288, 531741816507597222992, 520744907820250718441, 1005047906396012195259, 910358688114310724092, 32470101362), 75),
 )
 
 
@@ -599,8 +820,6 @@
         half = ff // 2
         nq, nk = w_query.shape[1], w_key.shape[1]
         head_dim = q_norm.shape[0]
-        kv_heads = nk // head_dim
-        q_per_kv = nq // nk
 
         mine_gu = jnp.concatenate([lax.dynamic_slice(w_gate, (0, core * half), (rows_w, half)), lax.dynamic_slice(w_up, (0, core * half), (rows_w, half))], axis=1)
         other_gu = jnp.concatenate([lax.dynamic_slice(w_gate, (0, (1 - core) * half), (rows_w, half)), lax.dynamic_slice(w_up, (0, (1 - core) * half), (rows_w, half))], axis=1)
@@ -609,12 +828,13 @@
         all_tokens, (down_block, recv_gu, dy_other) = all_rows(token_rows, n_dev, [w_down, other_gu, dy], ('use', 'pair', 'pair'), 0)
         block_gu = jnp.where(core == 0, jnp.concatenate([mine_gu, recv_gu], axis=0), jnp.concatenate([recv_gu, mine_gu], axis=0))
         wgu = gather_group(block_gu)
-        wd = gather_group(down_block)
         w_g, w_u = wgu[:, :half], wgu[:, half:]
 
-        gains = jnp.pad(jnp.stack([attn_norm, mlp_norm], axis=1), ((0, 0), (0, 126)))
-        attn_pack = jnp.concatenate([w_query, w_key, w_value, w_out, gains], axis=1)
-        attn_full = gather_all(attn_pack, (rows_w,), ('zba',), ATTN_SEQ, [], (), n_dev, 1)[0].reshape(-1, attn_pack.shape[1])
+        gain_cols = jnp.pad(jnp.stack([attn_norm, mlp_norm], axis=1), ((0, 0), (0, 126)))
+        attn_pack = jnp.concatenate([w_query, w_key, w_value, w_out, gain_cols], axis=1)
+        (attn_full, wd), _ = gather_all([attn_pack, down_block], [(0, 0, rows_w, True), (1, 0, down_block.shape[0], False)], ('bza', 'zba'), ATTN_SEQ, [], (), n_dev, 1)
+        attn_full = attn_full.reshape(-1, attn_pack.shape[1])
+        wd = wd.reshape(-1, model_dim)
 
         all_ids = all_tokens[:, :seq_len // 128].reshape(-1)
         local_ids = all_ids - me * rows_local
@@ -624,38 +844,25 @@
         upto = (slot[:, None] <= slot[None, :]).astype(BF16)
         rank = jnp.where(own, dot(own.astype(BF16), upto, 1, 0).astype(jnp.int32) - 1, -1)
         counts = jnp.sum(own.astype(jnp.int32), axis=1)
-        code = slot[None] * 8192 + jnp.where(own, local_ids.reshape(n_dev, seq_len), 0)
+        lines = model_dim // 128
+        line = lambda row: row // 8 * (8 * lines) + row % 8
+        code = line(slot)[None] * 65536 + line(jnp.where(own, local_ids.reshape(n_dev, seq_len), 0))
         codes = jnp.sum(jnp.where(rank[:, :, None] == slot, code[:, :, None], 0), axis=1)
-        codes = jnp.where(slot[None] < counts[:, None], codes, seq_len * 8192).reshape(-1)
+        codes = jnp.where(slot[None] < counts[:, None], codes, seq_len * lines * 65536).reshape(-1)
         picked = lookup(table_shard, counts, codes, seq_len)
         x_emb = scatter_sum([picked], [(0, 0, 192, 'device'), (0, 192, 208, 'device'), (0, 400, 112, 'device')], ('zba', 'zba', 'baz'), LOOKUP_SEQ, 2)[0]
 
         dy2 = jnp.concatenate([dy, dy_other], axis=0)
 
         n_in = nq + 2 * nk
-        w_in = attn_full[:, :n_in]
-        wo = attn_full[:, n_in:n_in + nq]
-        g_attn = attn_full[:, n_in + nq]
-        g_mlp = attn_full[:, n_in + nq + 1]
-
-        cos_t, sin_t = rope_tables(positions, head_dim)
-        cos_q, sin_q = cos_t[:, :, None, None, :], sin_t[:, :, None, None, :]
-        cos_k, sin_k = cos_t[:, :, None, :], sin_t[:, :, None, :]
-        normed1, norm1_inv = norm_fwd(x_emb)
-        attn_in = (normed1 * g_attn.astype(F32)).astype(BF16)
-        qkv = dot(attn_in, w_in, 1, 0).astype(BF16)
-        q_raw = qkv[:, :nq].reshape(1, seq_len, kv_heads, q_per_kv, head_dim)
-        k_raw = qkv[:, nq:nq + nk].reshape(1, seq_len, kv_heads, head_dim)
-        v_raw = qkv[:, nq + nk:].reshape(1, seq_len, kv_heads, head_dim)
-        q_normed, q_inv = norm_fwd(q_raw)
-        k_normed, k_inv = norm_fwd(k_raw)
-        q_rot = rotate(q_normed * q_norm.astype(F32), cos_q, sin_q).astype(BF16)
-        k_rot = rotate(k_normed * k_norm.astype(F32), cos_k, sin_k).astype(BF16)
-        attn_heads, attn_probs = attn_fwd(q_rot, k_rot, v_raw)
-        attn_flat = attn_heads.reshape(seq_len, nq)
-        hidden = (x_emb.astype(F32) + dot(attn_flat, wo, 1, 0)).astype(BF16)
-        normed2, norm2_inv = norm_fwd(hidden)
-        mlp_in = (normed2 * g_mlp.astype(F32)).astype(BF16)
+        gains = jnp.pad(jnp.repeat(attn_full[:, n_in + nq:n_in + nq + 2].astype(F32).T, 8, axis=0), ((0, 8), (0, 0)))
+        qk_gain = jnp.repeat(jnp.stack([jnp.tile(q_norm, 2), jnp.tile(k_norm, 2)]).astype(F32), 8, axis=0)
+
+        inv_freq = jnp.exp((jnp.arange(128) % (head_dim // 2)).astype(F32) * (-2.0 * math.log(ROPE_THETA) / head_dim))
+        angles = positions.reshape(seq_len, 1).astype(F32) * inv_freq
+        cos_t, sin_t = jnp.cos(angles), jnp.sin(angles)
+        saved = attn_forward(x_emb, attn_full, gains, cos_t, sin_t, qk_gain, n_in)
+        hidden, mlp_in = saved[5:]
 
         mlp2 = jnp.concatenate([mlp_in, swap(mlp_in)], axis=0)
         gate_pre = dot(mlp2, w_g, 1, 0)
@@ -667,42 +874,24 @@
         grad_gate = (grad_act * up_proj * gate_sig * (1.0 + gate_pre * (1.0 - gate_sig))).astype(BF16)
         grad_up = (grad_act * gate_pre * gate_sig).astype(BF16)
         part_in = dot(grad_gate, w_g, 1, 1) + dot(grad_up, w_u, 1, 1)
-        grad_mlp_in = part_in[:seq_len] + swap(part_in[seq_len:])
+        part_recv = swap(part_in[seq_len:])
         grad_w_gate = dot(mlp2, grad_gate, 0, 0)
         grad_w_up = dot(mlp2, grad_up, 0, 0)
         part_y = dot(mlp_act, wd, 1, 0)
         layer_out = (hidden.astype(F32) + (part_y[:seq_len] + swap(part_y[seq_len:]))).astype(BF16)
 
-        grad_mlp_norm = jnp.sum(grad_mlp_in * normed2, axis=0)
-        grad_hidden = dy.astype(F32) + norm_bwd(grad_mlp_in, normed2, norm2_inv, g_mlp)
-        hidden_b = grad_hidden.astype(BF16)
-        grad_w_out = dot(attn_flat, hidden_b, 0, 0)
-        grad_heads = dot(hidden_b, wo, 1, 1).reshape(q_rot.shape)
-        grad_q, grad_k, grad_v = attn_bwd(grad_heads, q_rot, k_rot, v_raw, attn_probs)
-        grad_qt = rotate(grad_q, cos_q, -sin_q)
-        grad_kt = rotate(grad_k, cos_k, -sin_k)
-        grad_q_norm = jnp.sum(grad_qt * q_normed, axis=(0, 1, 2, 3))
-        grad_k_norm = jnp.sum(grad_kt * k_normed, axis=(0, 1, 2))
-        grad_q_raw = norm_bwd(grad_qt, q_normed, q_inv, q_norm).astype(BF16).reshape(seq_len, nq)
-        grad_k_raw = norm_bwd(grad_kt, k_normed, k_inv, k_norm).astype(BF16).reshape(seq_len, nk)
-        grad_v_raw = grad_v.astype(BF16).reshape(seq_len, nk)
-        grad_qkv = jnp.concatenate([grad_q_raw, grad_k_raw, grad_v_raw], axis=1)
-        grad_attn_in = dot(grad_qkv, w_in, 1, 1)
-        grad_attn_norm = jnp.sum(grad_attn_in * normed1, axis=0)
-        grad_x_emb = grad_hidden + norm_bwd(grad_attn_in, normed1, norm1_inv, g_attn)
-
-        by_chip = [u.reshape(n_chip, -1, u.shape[1]) for u in (grad_w_down, grad_w_gate, grad_w_up, dot(attn_in, grad_qkv, 0, 0), grad_w_out)]
+        dx_block, grad_w_in, grad_w_out = attn_backward(x_emb, attn_full, gains, cos_t, sin_t, qk_gain, saved, dy, part_in[:seq_len], part_recv)
+
+        by_chip = [u.reshape(n_chip, -1, u.shape[1]) for u in (grad_w_down, grad_w_gate, grad_w_up, grad_w_in, grad_w_out)]
         down_rows, gate_shard, up_shard, in_shard, out_shard = scatter_sum(
             by_chip, [(i, 0, u.shape[1], 'chip') for i, u in enumerate(by_chip[:3])] + [(3, 0, 32, 'rows'), (4, 0, 32, 'rows')], ('bza', 'zba', 'zba', 'baz', 'baz'), GRAD_SEQ, 3)
 
         chip_rows = jnp.concatenate([gate_shard, up_shard], axis=1)
         mine = lax.dynamic_slice(chip_rows, (core * rows_w, 0), (rows_w, chip_rows.shape[1]))
         give = lax.dynamic_slice(chip_rows, ((1 - core) * rows_w, 0), (rows_w, chip_rows.shape[1]))
-        qk = jnp.pad(jnp.concatenate([grad_q_norm, grad_k_norm])[None], ((0, 0), (0, model_dim - 2 * head_dim)))
-        gains_grad = jnp.concatenate([qk, grad_attn_norm[None], grad_mlp_norm[None], jnp.zeros((5, model_dim), F32)], axis=0)
-        lines = model_dim // 128
-        all_dx, (down_shard, recv) = gather_all(
-            to_lines(jnp.concatenate([grad_x_emb, gains_grad], axis=0)), (200 * lines, 200 * lines, 120 * lines), ('zba', 'zba', 'baz'), ROWS_SEQ, [down_rows, give], ('store', 'pair'), n_dev, 4)
+        (all_dx,), (down_shard, recv) = gather_all(
+            [to_lines(dx_block)], [(0, 0, 200 * lines, True), (0, 200 * lines, 200 * lines, True), (0, 400 * lines, 120 * lines, True)],
+            ('zba', 'zba', 'baz'), ROWS_SEQ, [down_rows, give], ('store', 'pair'), n_dev, 4)
         d_table = from_lines(add_rows(all_dx, counts, codes, rows_local), model_dim)
         gains_grad = from_lines(jnp.sum(all_dx[:, seq_len * lines:], axis=0), model_dim)
         qk = gains_grad[0]

time: 1030 us -> 953 us (0.925)
  matrix products: 141 us -> 92.4 us
  other arithmetic: 46.4 us -> 18.3 us
  Pallas kernels: 769 us -> 784 us
    pallas_call x2 -> x4, Pallas kernels: 254 us -> 368 us  [the longest x2 298 us: gather_all(): pl.pallas_call(functools.partial(_gather_kernel, tuple(pieces), orders, s...]
    pallas_call x2, Pallas kernels: 390 us -> 321 us  [scatter_sum(): pl.pallas_call(functools.partial(_scatter_kernel, tuple(pieces), orders,...]
    dot_general x6 -> x0, matrix products: 35.3 us -> none  [the longest x1 8.1 us: attn_bwd(): jnp.einsum('bqgrh,bkgh->bgrqk', grad_b, v_raw, preferred_element_type=jnp...]
    pallas_call x1, Pallas kernels: 54.2 us -> 35.7 us  [add_rows(): pl.pallas_call(_add_rows_kernel, grid_spec=pltpu.PrefetchScalarGridSpec(n...]
    reduce_sum x9 -> x0, other arithmetic: 13.9 us -> none  [the longest x1 8.16 us: attn_fwd(): attn_probs = jax.nn.softmax(jnp.where(causal, scores, -1e+30), axis=-1)]
    dot_general x16 -> x10, matrix products: 106 us -> 92.4 us  [dot(): lax.dot_general(a, b, (((ca,), (cb,)), ((), ())), preferred_element_type=...]
    pallas_call x1, Pallas kernels: 52.8 us -> 40.2 us  [lookup(): pl.pallas_call(_lookup_kernel, grid_spec=pltpu.PrefetchScalarGridSpec(num...]
  transfers between devices with their start and end apart: 5 -> 4, of which waited for: 0 -> 0; matrix products, arithmetic and copies ran while one was open for 10% -> 9% of each run, Pallas kernels for 25% -> 81%
where the time goes in v5:
time: 953 us; the launch traced here: 946 us
  Pallas kernels  784 us (82%)
  matrix products  92.4 us (10%)
  local copies, waits for them, and re-layouts  36.5 us (4%)
  other arithmetic  18.3 us (2%)
  between operations  14.8 us (2%)
    pallas_call x2, Pallas kernels, scatter_sum(): pl.pallas_call(functools.partial(_scatter_kernel, tuple(pieces), orders,...  321 us
    pallas_call x2, Pallas kernels, gather_all(): pl.pallas_call(functools.partial(_gather_kernel, tuple(pieces), orders, s...  298 us
    dot_general x10, matrix products, dot(): lax.dot_general(a, b, (((ca,), (cb,)), ((), ())), preferred_element_type=...  92.4 us
    pallas_call x1, Pallas kernels, attn_backward(): pl.pallas_call(_attn_bwd_kernel, out_shape=[jax.ShapeDtypeStruct((seq + 8...  50.2 us
    pallas_call x1, Pallas kernels, lookup(): pl.pallas_call(_lookup_kernel, grid_spec=pltpu.PrefetchScalarGridSpec(num...  40.2 us
    pallas_call x1, Pallas kernels, add_rows(): pl.pallas_call(_add_rows_kernel, grid_spec=pltpu.PrefetchScalarGridSpec(n...  35.7 us
    pallas_call x1, Pallas kernels, attn_forward(): pl.pallas_call(_attn_fwd_kernel, out_shape=[sds(dim), sds(n_in), sds(dim)...  19.9 us
  transfers between devices with their start and end apart: 4, of which 0 were waited for; matrix products, arithmetic and copies ran while one was open for 9% of the time, Pallas kernels for 81%

profile of v5, /device:TPU:0, one launch (start us, length us, event | category | flops | bytes accessed | tf_op | source)
XLA Modules:
  0.0 946.3 jit_solution(8991031066204049457)
XLA Ops:
  7.3 1.3 pad.12.refs_0_
  8.6 1.2 constant_dynamic-slice_fusion.3
  9.8 0.7 pad_maximum_fusion.5.refs_2_
  10.6 18.4 %all_rows.1 = (s32[32,8,128]{2,1,0:T(8,128)}, bf16[152,896]{1,0:T(8,128)(2,1)}, bf16[28,4864]{1,0:T(8,128)(2,1)}, bf16[512,896]{1,0:T(8,128)(2,1)}) custom-call(s32[8,128]{1,0:T(8,128)} %pad.12.refs_0_, bf16[152,896]{1,0:T(8,128)(2,1)} %refs_1_.1, bf16[28,4864]{1,0:T(8,128)(2,1)} %pad_maximum_fusion.5.refs_2_, bf16[512,896]{1,0:T(8,128)(2,1)} %bitcast.78), custom_call_target="tpu_custom_call" | custom-call | flops 10000000 | bytes 1048576 | tf_op jit(solution)/shard_map/all_rows/pallas_call | solution.py:167
  28.9 2.1 maximum_select_fusion
  31.1 0.1 stack_tile.6
  31.1 0.1 stack_tile.7
  31.3 0.1 copy.36
  31.4 1.6 convert_reduce_fusion
  33.0 0.2 fusion.16
  33.2 0.1 fusion.20
  33.2 5.9 select_reduce_fusion
  39.2 0.1 select_bitcast_fusion
  39.4 0.9 copy-done.6
  40.4 80.2 %gather_all.2 = (bf16[32,28,2176]{2,1,0:T(8,128)(2,1)S(1)}, bf16[16,152,896]{2,1,0:T(8,128)(2,1)S(1)}) custom-call(bf16[28,2176]{1,0:T(8,128)(2,1)S(1)} %constant_dynamic-update-slice_fusion.refs_0_, bf16[152,896]{1,0:T(8,128)(2,1)S(1)} %copy-done.6), custom_call_target="tpu_custom_call" | custom-call | flops 200000000 | bytes 25231360 | tf_op jit(solution)/shard_map/gather_all/pallas_call | solution.py:249
  120.6 2.1 copy-done.1
  122.6 2.0 copy-done.7
  124.7 6.0 reshape.200.w_ref
  130.7 1.0 convert_bitcast_fusion
  131.7 0.2 copy.37
  131.9 3.4 copy-done
  135.3 40.2 %lookup.1.refs_0_ = bf16[32,512,896]{2,1,0:T(8,128)(2,1)} custom-call(s32[32]{0:T(128)S(1)} %get-tuple-element.64.counts, s32[16384]{0:T(1024)S(1)} %bitcast.68, bf16[4752,896]{1,0:T(8,128)(2,1)S(1)} %copy-done), custom_call_target="tpu_custom_call" | custom-call | flops 50000000 | bytes 41943040 | tf_op jit(solution)/shard_map/lookup/pallas_call | solution.py:440
  175.5 106.8 %scatter_sum.2.x_ref = bf16[512,896]{1,0:T(8,128)(2,1)S(1)} custom-call(bf16[32,512,896]{2,1,0:T(8,128)(2,1)} %lookup.1.refs_0_), custom_call_target="tpu_custom_call" | custom-call | flops 200000000 | bytes 136937472 | tf_op jit(solution)/shard_map/scatter_sum/pallas_call | solution.py:385
  282.4 1.0 multiply_sine_fusion
  283.4 19.9 %attn_forward.1 = (bf16[512,896]{1,0:T(8,128)(2,1)S(1)}, bf16[512,1152]{1,0:T(8,128)(2,1)S(1)}, bf16[512,896]{1,0:T(8,128)(2,1)S(1)}, bf16[512,128]{1,0:T(8,128)...) custom-call(bf16[512,896]{1,0:T(8,128)(2,1)S(1)} %scatter_sum.2.x_ref, ...), custom_call_target="tpu_custom_call" | custom-call | flops 4000000000 | bytes 12582912 | tf_op jit(solution)/shard_map/attn_forward/pallas_call | solution.py:641
  303.2 0.9 copy-done.4
  304.1 1.0 copy-done.8
  305.2 1.0 copy-done.9
  306.1 1.0 copy-done.10
  307.1 1.0 copy-done.11
  308.1 1.1 constant_dynamic-update-slice_fusion.6
  309.2 10.2 %fusion.14 = f32[1024,2432]{1,0:T(8,128)} fusion(bf16[2432,896]{1,0:T(8,128)(2,1)} %bitcast.70, bf16[512,896]{1,0:T(8,128)(2,1)} %get-tuple-element.49, bf16[512,896]{1,0:T(8,128)(2,1)} %bitcast.79), kind=kOutput, calls=%fused_computation.20 | convolution fusion | flops 4466409472 | bytes 16154624 | tf_op jit(solution)/shard_map/dot_general | solution.py:19
  319.3 2.2 constant_dynamic-update-slice_fusion.5
  321.5 10.6 %fusion.2 = f32[1024,2432]{1,0:T(8,128)} fusion(bf16[1024,896]{1,0:T(8,128)(2,1)} %constant_dynamic-update-slice_fusion.5, bf16[896,4864]{1,0:T(8,128)(2,1)} %all-gather.2.cloned.1.call-done), kind=kOutput, calls=%fused_computation.8 | convolution fusion | flops 4462739456 | bytes 16154624 | tf_op jit(solution)/shard_map/dot_general | solution.py:19
  332.1 18.2 %multiply_convert_fusion.1 = (bf16[1024,2432]{1,0:T(8,128)(2,1)}, bf16[1024,2432]{1,0:T(8,128)(2,1)}, bf16[1024,2432]{1,0:T(8,128)(2,1)}) fusion(f32[1024,2432]{1,0:T(8,128)} %fusion.14, f32[1024,2432]{1,0:T(8,128)} %fusion.2, bf16[1024,896]{1,0:T(8,128)(2,1)} %constant_dynamic-update-slice_fusion.5, bf16[896,4864]{1,0:T(8,128)(2,1)} %all-gather.2.cloned.1.call-done), kind=kOutput, calls=%fused_computation.3 | convolution fusion | flops 4502585344 | bytes 41058304 | tf_op jit(solution)/shard_map/dot_general | solution.py:19
  350.2 9.0 fusion.51
  359.3 1.3 slice.91
  360.6 0.5 collective-permute-start.1
  361.2 9.5 %fusion.52 = f32[896,2432]{1,0:T(8,128)} fusion(bf16[1024,896]{1,0:T(8,128)(2,1)} %constant_dynamic-update-slice_fusion.5, bf16[1024,2432]{1,0:T(8,128)(2,1)S(1)} %copy-done.24), kind=kOutput, calls=%fused_computation.110 | convolution fusion | flops 4462739456 | bytes 15532032 | tf_op jit(solution)/shard_map/dot_general | solution.py:19
  370.7 7.3 fusion
  378.0 8.0 fusion.10
  386.0 1.5 fusion.46
  387.6 0.6 copy-done.19
  388.1 10.6 %fusion.13 = f32[2432,896]{1,0:T(8,128)} fusion(bf16[1024,2432]{1,0:T(8,128)(2,1)} %get-tuple-element.67, bf16[512,896]{1,0:T(8,128)(2,1)S(1)} %copy-done.19, bf16[512,896]{1,0:T(8,128)(2,1)S(1)} %bitcast.81), kind=kOutput, calls=%fused_computation.19 | convolution fusion | flops 4466409472 | bytes 15532032 | tf_op jit(solution)/shard_map/dot_general | solution.py:19
  398.8 8.8 fusion.53
  407.6 1.2 copy-done.18
  408.8 50.2 %attn_backward.1 = (f32[520,896]{1,0:T(8,128)}, f32[896,1152]{1,0:T(8,128)}, f32[896,896]{1,0:T(8,128)}) custom-call(bf16[512,896]{1,0:T(8,128)(2,1)S(1)} %scatter_sum.2.x_ref, bf16[896,2176]{1,0:T(8,128)(2,1)} %reshape.200.w_ref, f32[24,896]{1,0:T(8,128)S(1)} %pad.14.gain_ref, f32[512,128]{1,0:T(8,128)S(1)} %get-tuple-element.86.cos_ref, ...), custom_call_target="tpu_custom_call" | custom-call | flops 8999999488 | bytes 31457280 | tf_op jit(solution)/shard_map/attn_backward/pallas_call | solution.py:761
  459.0 214.4 %scatter_sum.3 = (f32[152,896]{1,0:T(8,128)S(1)}, f32[56,2432]{1,0:T(8,128)S(1)}, f32[56,2432]{1,0:T(8,128)S(1)}, f32[32,1152]{1,0:T(8,128)S(1)}, f32[32,896]{1,0:T(8,128)S(1)}) custom-call(f32[16,152,896]{2,1,0:T(8,128)} %bitcast.74, f32[16,56,2432]{2,1,0:T(8,128)} %bitcast.73, f32[16,56,2432]{2,1,0:T(8,128)} %bitcast.75, f32[16,56,1152]{2,1,0:T(8,128)} %bitcast.76, ...), custom_call_target="tpu_custom_call" | custom-call | flops 200000000 | bytes 193380352 | tf_op jit(solution)/shard_map/scatter_sum/pallas_call | solution.py:385
  673.6 0.1 constant_dynamic-slice_fusion.2.refs_2_
  673.6 1.3 copy-done.3
  675.0 218.0 %gather_all.3 = (f32[32,3640,128]{2,1,0:T(8,128)}, f32[152,896]{1,0:T(8,128)S(1)}, f32[28,4864]{1,0:T(8,128)S(1)}) custom-call(f32[3640,128]{1,0:T(8,128)S(1)} %bitcast.67, f32[152,896]{1,0:T(8,128)S(1)} %get-tuple-element.53.refs_1_, f32[28,4864]{1,0:T(8,128)S(1)} %constant_dynamic-slice_fusion.2.refs_2_), custom_call_target="tpu_custom_call" | custom-call | flops 200000000 | bytes 119275520 | tf_op jit(solution)/shard_map/gather_all/pallas_call | solution.py:249
  892.9 1.3 slice_reduce_fusion
  894.2 35.7 %add_rows.1 = f32[33264,128]{1,0:T(8,128)} custom-call(s32[32]{0:T(128)S(1)} %get-tuple-element.64.counts, s32[16384]{0:T(1024)S(1)} %bitcast.69, f32[32,3640,128]{2,1,0:T(8,128)} %get-tuple-element.56.dx_ref), custom_call_target="tpu_custom_call" | custom-call | flops 50000000 | bytes 83886080 | tf_op jit(solution)/shard_map/add_rows/pallas_call | solution.py:518
  929.9 0.7 constant_dynamic-slice_fusion
  930.6 0.7 constant_dynamic-slice_fusion.1
  931.2 0.1 dynamic-slice_select_fusion.1
  931.4 0.6 dynamic_slice.38
  932.0 0.6 dynamic_slice.35
  932.6 0.6 fusion.50
  933.2 0.7 fusion.49
  933.9 0.9 pad_maximum_fusion.4
  934.8 0.9 pad_maximum_fusion.3
  935.7 2.8 fusion.17
  938.4 0.8 copy.55
  (79 shorter events, 0.6 us)
Async XLA Ops:
  7.2 23.9 %copy-start.20 = (bf16[64]{0:T(256)(128)(2,1)S(1)}, bf16[64]{0:T(256)(128)(2,1)}, u32[]{:S(2)}) copy-start(bf16[64]{0:T(256)(128)(2,1)} %param.22) | copy-start | bytes 388
  7.2 23.9 %copy-start.21 = (bf16[64]{0:T(256)(128)(2,1)S(1)}, bf16[64]{0:T(256)(128)(2,1)}, u32[]{:S(2)}) copy-start(bf16[64]{0:T(256)(128)(2,1)} %param.23) | copy-start | bytes 388
  7.2 24.0 %copy-start.17 = (s32[1,512]{1,0:T(1,128)S(1)}, s32[1,512]{1,0:T(1,128)}, u32[]{:S(2)}) copy-start(s32[1,512]{1,0:T(1,128)} %param.16) | copy-start | bytes 6148
  7.2 24.0 %copy-start.22 = (bf16[28]{0:T(256)(128)(2,1)S(1)}, bf16[28]{0:T(256)(128)(2,1)}, u32[]{:S(2)}) copy-start(bf16[28]{0:T(256)(128)(2,1)} %param.25) | copy-start | bytes 172
  7.2 24.0 %copy-start.23 = (bf16[28]{0:T(256)(128)(2,1)S(1)}, bf16[28]{0:T(256)(128)(2,1)}, u32[]{:S(2)}) copy-start(bf16[28]{0:T(256)(128)(2,1)} %param.18) | copy-start | bytes 172
  7.2 32.1 %copy-start.13 = (bf16[28,896]{1,0:T(8,128)(2,1)S(1)}, bf16[28,896]{1,0:T(8,128)(2,1)}, u32[]{:S(2)}) copy-start(bf16[28,896]{1,0:T(8,128)(2,1)} %param.19) | copy-start | bytes 150532
  7.2 32.1 %copy-start.15 = (bf16[28,128]{1,0:T(8,128)(2,1)S(1)}, bf16[28,128]{1,0:T(8,128)(2,1)}, u32[]{:S(2)}) copy-start(bf16[28,128]{1,0:T(8,128)(2,1)} %param.20) | copy-start | bytes 21508
  7.3 32.1 %copy-start.16 = (bf16[28,128]{1,0:T(8,128)(2,1)S(1)}, bf16[28,128]{1,0:T(8,128)(2,1)}, u32[]{:S(2)}) copy-start(bf16[28,128]{1,0:T(8,128)(2,1)} %param.21) | copy-start | bytes 21508
  7.3 32.1 %copy-start.14 = (bf16[28,896]{1,0:T(8,128)(2,1)S(1)}, bf16[28,896]{1,0:T(8,128)(2,1)}, u32[]{:S(2)}) copy-start(bf16[28,896]{1,0:T(8,128)(2,1)} %param.24) | copy-start | bytes 150532
  7.3 314.2 %all-gather.2.cloned.1.call-start = ((), (), s32[]{:S(2)}) async-start(), calls=%async_computation | async-start | bytes 9261056 | tf_op jit(solution)/shard_map/all_gather | solution.py:812
  39.4 1.0 copy-start.6
  120.5 2.1 copy-start.1
  122.6 2.0 copy-start.7
  131.9 3.4 copy-start
  175.5 107.9 %copy-start.2 = (bf16[896,2176]{1,0:T(8,128)(2,1)S(1)}, bf16[896,2176]{1,0:T(8,128)(2,1)}, u32[]{:S(2)}) copy-start(bf16[896,2176]{1,0:T(8,128)(2,1)} %reshape.200.w_ref) | copy-start | bytes 11698180
  303.2 0.9 copy-start.4
  304.1 1.0 copy-start.8
  305.2 1.0 copy-start.9
  306.1 1.0 copy-start.10
  307.1 1.0 copy-start.11
  308.1 11.3 %collective-permute-start = (bf16[512,896]{1,0:T(8,128)(2,1)S(1)}, bf16[512,896]{1,0:T(8,128)(2,1)}, u32[]{:S(2)}, u32[]{:S(2)}) collective-permute-start(bf16[512,896]{1,0:T(8,128)(2,1)S(1)} %get-tuple-element.41), channel_id=1, source_target_pairs={{0,1},{1,0},{2,3},{3,2},{4,5},{5,4},{6,7},{7,6},{8,9},{9,8},{10,11... | collective-permute-start | bytes 2752520 | tf_op jit(solution)/shard_map/ppermute | solution.py:809
  350.2 10.9 %copy-start.24 = (bf16[1024,2432]{1,0:T(8,128)(2,1)S(1)}, bf16[1024,2432]{1,0:T(8,128)(2,1)}, u32[]{:S(2)}) copy-start(bf16[1024,2432]{1,0:T(8,128)(2,1)} %get-tuple-element.66) | copy-start | bytes 14942212
  359.3 11.3 %slice-start = ((s8[8716288]{0:T(1024)(128)(4,1)}), s8[4194304]{0:T(1024)(128)(4,1)S(1)}, s32[]{:S(2)}) async-start(s8[8716288]{0:T(1024)(128)(4,1)} %bitcast.90), calls=%async_computation.1 | async-start | bytes 8388608
  359.3 11.3 %slice-start.3 = ((s8[4980736]{0:T(1024)(128)(4,1)}), s8[4194304]{0:T(1024)(128)(4,1)S(1)}, s32[]{:S(2)}) async-start(s8[4980736]{0:T(1024)(128)(4,1)} %bitcast.94), calls=%async_computation.4 | async-start | bytes 8388608
  360.6 575.1 %collective-permute-start.1 = (f32[512,896]{1,0:T(8,128)}, f32[512,896]{1,0:T(8,128)}, u32[]{:S(2)}, u32[]{:S(2)}) collective-permute-start(f32[512,896]{1,0:T(8,128)} %slice.91), channel_id=1, source_target_pairs={{0,1},{1,0},{2,3},{3,2},{4,5},{5,4},{6,7},{7,6},{8,9},{9,8},{10,11... | collective-permute-start | bytes 5505032 | tf_op jit(solution)/shard_map/ppermute | solution.py:809
  361.1 9.5 %slice-start.1 = ((s8[8716288]{0:T(1024)(128)(4,1)}), s8[4194304]{0:T(1024)(128)(4,1)S(1)}, s32[]{:S(2)}) async-start(s8[8716288]{0:T(1024)(128)(4,1)} %bitcast.90), calls=%async_computation.2 | async-start | bytes 8388608
  361.1 9.5 %slice-start.2 = ((s8[8716288]{0:T(1024)(128)(4,1)}), s8[327680]{0:T(1024)(128)(4,1)S(1)}, s32[]{:S(2)}) async-start(s8[8716288]{0:T(1024)(128)(4,1)} %bitcast.90), calls=%async_computation.3 | async-start | bytes 655360
  361.1 9.5 %slice-start.4 = ((s8[4980736]{0:T(1024)(128)(4,1)}), s8[786432]{0:T(1024)(128)(4,1)S(1)}, s32[]{:S(2)}) async-start(s8[4980736]{0:T(1024)(128)(4,1)} %bitcast.94), calls=%async_computation.5 | async-start | bytes 1572864
  386.0 1.6 copy-start.12
  386.0 2.1 copy-start.19
  387.5 20.0 %collective-permute-start.2 = (f32[512,896]{1,0:T(8,128)S(1)}, f32[512,896]{1,0:T(8,128)S(1)}, u32[]{:S(2)}, u32[]{:S(2)}) collective-permute-start(f32[512,896]{1,0:T(8,128)S(1)} %get-tuple-element.69), channel_id=1, source_target_pairs={{0,1},{1,0},{2,3},{3,2},{4,5},{5,4},{6,7},{7,6},{8,9},{9,8},{10,11... | collective-permute-start | bytes 5505032 | tf_op jit(solution)/shard_map/ppermute | solution.py:809
  407.6 1.2 copy-start.18
  673.5 1.5 copy-start.3
  929.9 5.8 copy-start.5
Sparse Core Ops, SparseCore 0:
  31.2 139.6 all-gather.1

commit v6 on v5

v6 whole, which is shorter than its diff:
```python
import functools
import math
import jax
import jax.numpy as jnp
from jax import lax
from jax.experimental import pallas as pl
from jax.experimental.pallas import tpu as pltpu
from jax.sharding import PartitionSpec as P

NORM_EPS = 1e-6
ROPE_THETA = 1.0e6
AXIS_NAME = 'fsdp'
F32 = jnp.float32
BF16 = jnp.bfloat16
MESH = pl.DeviceIdType.MESH
LANES, SUB, CHIPS, PAIR, MIB = 128, 8, 16, 2, 1 << 20


def mm(a, b):
    return lax.dot_general(a, b, (((1,), (0,)), ((), ())), preferred_element_type=F32)


def mm_nt(a, b):
    return lax.dot_general(a, b, (((1,), (1,)), ((), ())), preferred_element_type=F32)


def mm_tn(a, b):
    return lax.dot_general(a, b, (((0,), (0,)), ((), ())), preferred_element_type=F32)


def cost(flops, nbytes, transcendentals=0):
    return pl.CostEstimate(flops=flops, bytes_accessed=nbytes, transcendentals=transcendentals)


def below(v, rows):
    return jnp.pad(v, ((0, rows), (0, 0)))


def loop(count, body):
    def step(i, carry):
        body(i)
        return carry
    lax.fori_loop(0, count, step, 0)


def _unpack(code):
    return code // 64, code // 32 % PAIR, code // SUB % 4, code % SUB


def _via(u, key, orders):
    da, db, p, piece = key
    last = None
    for axis in orders[piece]:
        if axis == 'a' and da or axis == 'b' and db:
            last = axis
        if axis == 'z' and p != u:
            last = 'z+' if p > u else 'z-'
    return last


def _onward(u, key, orders):
    order = orders[key[3]]
    via = _via(u, key, orders)
    left = order if via is None else order[order.index(via[0]) + 1:]
    out = []
    if u < 3 and (via == 'z-' or 'z' in left):
        out.append('z+')
    if u > 0 and (via == 'z+' or 'z' in left):
        out.append('z-')
    return out + [axis for axis in 'ba' if axis in left]


def _seen_by_parent(u, key, orders):
    da, db, p, piece = key
    via = _via(u, key, orders)
    if via == 'a':
        return u, (0, db, p, piece), 'a'
    if via == 'b':
        return u, (da, 0, p, piece), 'b'
    if via == 'z-':
        return u - 1, key, 'z+'
    if u == 0:
        return 1, key, 'z-'
    return 1, (da, db, 3 - p, piece), 'z+'


class _Place:
    def __init__(self, me, swapped=False):
        self.me = me
        self.core = me % PAIR
        x, y, self.z = (me // PAIR) % PAIR, (me // 4) % PAIR, me // SUB
        other = 1 - self.core if swapped else self.core
        self.a = y * (1 - other) + x * other
        self.b = x * (1 - other) + y * other
        self.a_str, self.b_str = 4 - PAIR * other, PAIR + PAIR * other
        self.far = self.z // PAIR
        self.u = 3 * self.far + (1 - PAIR * self.far) * self.z
        self.partner = me + 1 - PAIR * self.core

    def chip(self, key):
        da, db, p = key[:3]
        a = self.a + da * (1 - PAIR * self.a)
        b = self.b + db * (1 - PAIR * self.b)
        z = 3 * self.far + (1 - PAIR * self.far) * p
        return (SUB * z + a * self.a_str + b * self.b_str) // PAIR

    def side(self, name):
        if name == 'a':
            return self.me + (1 - PAIR * self.a) * self.a_str
        if name == 'b':
            return self.me + (1 - PAIR * self.b) * self.b_str
        return self.me + SUB * (1 - PAIR * self.far) * (1 if name == 'z+' else -1)


def _remote(src, dst, send_sem, recv_sem, dev):
    return pltpu.make_async_remote_copy(src_ref=src, dst_ref=dst, send_sem=send_sem, recv_sem=recv_sem, device_id=(dev,), device_id_type=MESH)


def _meet(peers, me=None, ends=()):
    sem = pltpu.get_barrier_semaphore()

    def meet(everyone):
        for peer in everyone:
            pl.semaphore_signal(sem, inc=1, device_id=(peer,), device_id_type=MESH)
        pl.semaphore_wait(sem, len(everyone))

    if not ends:
        meet(peers)
        return
    to, frm = ends
    pl.when(to != me)(lambda: meet(peers + [to, frm]))
    pl.when(to == me)(lambda: meet(peers))


def _landed(ref, sem):
    pltpu.make_async_copy(ref, ref, sem).wait()


def _passes(moves, me):
    for kind in moves:
        if kind == 'pair':
            other = me + 1 - PAIR * (me % PAIR)
            yield other, other
        elif kind == 'use':
            yield PAIR * (me % CHIPS) + me // CHIPS, CHIPS * (me % PAIR) + me // PAIR
        else:
            yield CHIPS * (me % PAIR) + me // PAIR, PAIR * (me % CHIPS) + me // CHIPS


def _start_move(kind, src, dst, send_sem, recv_sem, to, me):
    copy = _remote(src, dst, send_sem, recv_sem, to)
    if kind == 'pair':
        copy.start()
    else:
        pl.when(to != me)(copy.start)
        pl.when(to == me)(pltpu.make_async_copy(src, dst, recv_sem).start)
    return copy


def _end_move(kind, copy, dst, recv_sem, to, me):
    _landed(dst, recv_sem)
    if kind == 'pair':
        copy.wait_send()
    else:
        pl.when(to != me)(copy.wait_send)


def _all_rows_kernel(n_dev, moves, *refs):
    n = len(moves)
    in_ref, src, out_ref, dst = refs[0], refs[1:1 + n], refs[1 + n], refs[PAIR + n:PAIR + PAIR * n]
    send_sem, recv_sem, m_send, m_recv = refs[PAIR + PAIR * n:]
    me = lax.axis_index(AXIS_NAME)
    peers = [(me + d) % n_dev for d in range(1, n_dev)]
    _meet(peers)
    copies = [_remote(in_ref, out_ref.at[me], send_sem.at[i], recv_sem.at[i], peer) for i, peer in enumerate(peers)]
    for copy in copies:
        copy.start()
    ends = [to for to, _ in _passes(moves, me)]
    moving = [_start_move(moves[i], src[i], dst[i], m_send.at[i], m_recv.at[i], to, me) for i, to in enumerate(ends)]
    out_ref[me] = in_ref[...]
    for copy in copies:
        copy.wait()
    for i, copy in enumerate(moving):
        _end_move(moves[i], copy, dst[i], m_recv.at[i], ends[i], me)


def all_rows(block, n_dev, moved, moves, collective_id):
    n = len(moves)
    dma = pltpu.SemaphoreType.DMA
    vmem, hbm = pl.BlockSpec(memory_space=pltpu.VMEM), pl.BlockSpec(memory_space=pl.ANY)
    res = pl.pallas_call(
        functools.partial(_all_rows_kernel, n_dev, moves),
        out_shape=[jax.ShapeDtypeStruct((n_dev,) + block.shape, block.dtype)] + [jax.ShapeDtypeStruct(v.shape, v.dtype) for v in moved],
        in_specs=[vmem] + [hbm] * n,
        out_specs=[vmem] + [hbm] * n,
        scratch_shapes=[dma((n_dev - 1,)), dma((n_dev - 1,)), dma((n,)), dma((n,))],
        compiler_params=pltpu.CompilerParams(collective_id=collective_id, has_side_effects=True),
        cost_estimate=cost(10_000_000, 1 * MIB),
        name='all_rows',
    )(block, *moved)
    return res[0], res[1:]


def _gather_kernel(pieces, orders, seq, moves, n_arr, *refs):
    n, m = len(moves), len(pieces)
    ins, src, outs, dst = refs[:n_arr], refs[n_arr:n_arr + n], refs[n_arr + n:PAIR * n_arr + n], refs[PAIR * n_arr + n:PAIR * n_arr + PAIR * n]
    own_sem, send_sem, recv_sem, p_send, p_recv, m_send, m_recv = refs[PAIR * n_arr + PAIR * n:]
    me = lax.axis_index(AXIS_NAME)
    at = _Place(me)
    ends = list(_passes(moves, me))

    def part(kc, core, piece):
        arr, r0, rows, shared = pieces[piece]
        slot = PAIR * kc + core if shared else kc
        return outs[arr].at[slot] if rows == outs[arr].shape[1] else outs[arr].at[slot, pl.ds(r0, rows)]

    def run(u):
        sides = ['a', 'b', 'z+'] + (['z-'] if u else [])
        far = [end for kind, end in zip(moves, ends) if kind != 'pair']
        _meet([at.side(s) for s in sides] + [at.partner], me, far[0] if far else ())
        started, moving = [], []

        def send(src_ref, dst_ref, s_sem, r_sem, dev):
            copy = _remote(src_ref, dst_ref, s_sem, r_sem, dev)
            copy.start()
            started.append(copy)

        count, handed = 0, [0] * m
        for key in [(0, 0, u, i) for i in range(m)] + [_unpack(c) for c in seq[u]]:
            piece = key[3]
            arr, r0, rows, shared = pieces[piece]
            kc = at.chip(key)
            place = part(kc, at.core, piece)
            if _via(u, key, orders) is None:
                ref = ins[arr] if rows == ins[arr].shape[0] else ins[arr].at[pl.ds(r0, rows)]
            else:
                ref = place
                _landed(ref, recv_sem.at[piece, kc])
            for side in _onward(u, key, orders):
                send(ref, place, send_sem.at[count], recv_sem.at[piece, kc], at.side(side))
                count += 1
            if shared:
                send(ref, place, p_send.at[piece, handed[piece]], p_recv.at[piece, kc], at.partner)
                handed[piece] += 1
            if key == (0, 0, u, m - 1):
                for i, (to, _) in enumerate(ends):
                    moving.append(_start_move(moves[i], src[i], dst[i], m_send.at[i], m_recv.at[i], to, me))
                own = [pltpu.make_async_copy(ins[i], outs[i].at[me if pieces_shared[i] else me // PAIR], own_sem.at[i]) for i in range(n_arr)]
                for copy in own:
                    copy.start()
        for piece in range(m):
            if pieces[piece][3]:
                for kc in range(CHIPS):
                    _landed(part(kc, 1 - at.core, piece), p_recv.at[piece, kc])
        for i, (to, _) in enumerate(ends):
            _end_move(moves[i], moving[i], dst[i], m_recv.at[i], to, me)
        for copy in own:
            copy.wait()
        for copy in started:
            copy.wait_send()

    pieces_shared = {p[0]: p[3] for p in pieces}
    for u in (0, 1):
        pl.when(at.u == u)(functools.partial(run, u))


def gather_all(blocks, pieces, orders, seq, moved, moves, n_dev, collective_id):
    n, m, n_arr = len(moves), len(pieces), len(blocks)
    dma = pltpu.SemaphoreType.DMA
    vmem, hbm = pl.BlockSpec(memory_space=pltpu.VMEM), pl.BlockSpec(memory_space=pl.ANY)
    nbytes = sum(v.size * v.dtype.itemsize for v in blocks)
    shared = {p[0]: p[3] for p in pieces}
    res = pl.pallas_call(
        functools.partial(_gather_kernel, tuple(pieces), orders, seq, moves, n_arr),
        out_shape=[jax.ShapeDtypeStruct((n_dev if shared[i] else n_dev // PAIR,) + v.shape, v.dtype) for i, v in enumerate(blocks)] + [
            jax.ShapeDtypeStruct(v.shape, v.dtype) for v in moved],
        in_specs=[vmem] * n_arr + [hbm] * n,
        out_specs=[hbm] * (n_arr + n),
        scratch_shapes=[dma((n_arr,)), dma((24 * m,)), dma((m, CHIPS)), dma((m, CHIPS)), dma((m, CHIPS)), dma((max(n, 1),)), dma((max(n, 1),))],
        compiler_params=pltpu.CompilerParams(collective_id=collective_id, has_side_effects=True, vmem_limit_bytes=nbytes + (SUB * MIB)),
        cost_estimate=cost(200_000_000, nbytes * 64),
        name='gather_all',
    )(*blocks, *moved)
    return res[:n_arr], res[n_arr:]


def _slots(pieces, orders, seq):
    table, most = {}, [1] * len(pieces)
    for u in (0, 1):
        used = [0] * len(pieces)
        for key in [_unpack(c) for c in reversed(seq[u])] + [(0, 0, u, i) for i in range(len(pieces))]:
            for side in _onward(u, key, orders):
                table[u, key, side] = used[key[3]]
                used[key[3]] += 1
        most = [max(a, b) for a, b in zip(most, used)]
    return table, most


def _scatter_kernel(pieces, orders, seq, n_arr, *refs):
    table, _ = _slots(pieces, orders, seq)
    n = len(pieces)
    n_pair = sum(1 for p in pieces if p[3] != 'chip')
    ins, outs = refs[:n_arr], refs[n_arr:PAIR * n_arr]
    k = PAIR * n_arr
    land, stage, pair = refs[k:k + n], refs[k + n:k + PAIR * n], list(refs[k + PAIR * n:k + PAIR * n + n_pair])
    load_sem, send_sem, recv_sem, d_send, d_recv = refs[k + PAIR * n + n_pair:]
    got = [pair.pop(0) if p[3] != 'chip' else None for p in pieces]
    me = lax.axis_index(AXIS_NAME)
    at, partner_at = _Place(me), _Place(me, swapped=True)

    def rows_of(ref, piece):
        _, r0, rows, _ = pieces[piece]
        return ref if rows == ref.shape[0] else ref.at[pl.ds(r0, rows)]

    def term(piece, kc, core):
        arr, _, rows, kind = pieces[piece]
        if kind == 'rows':
            return ins[arr].at[kc, pl.ds(pl.multiple_of(24 * core, SUB), rows)]
        return rows_of(ins[arr].at[PAIR * kc + core if kind == 'device' else kc], piece)

    def run(u):
        sides = ['a', 'b', 'z+'] + (['z-'] if u else [])
        _meet([at.side(s) for s in sides] + [at.partner])
        keys = [_unpack(c) for c in reversed(seq[u])] + [(0, 0, u, i) for i in range(n)]
        started = []
        given = [0] * n
        for key in keys:
            piece = key[3]
            if pieces[piece][3] != 'chip':
                kc = partner_at.chip(key)
                copy = _remote(term(piece, kc, 1 - at.core), got[piece].at[kc], d_send.at[piece, given[piece]], d_recv.at[piece, kc], at.partner)
                given[piece] += 1
                copy.start()
                started.append(copy)
        adds = [[key for key in keys if key[3] == i and (pieces[i][3] != 'chip' or _onward(u, key, orders))] for i in range(n)]

        def load(piece, j):
            return pltpu.make_async_copy(term(piece, at.chip(adds[piece][j]), at.core), stage[piece].at[j % PAIR], load_sem.at[piece, j % PAIR])

        for i in range(n):
            for j in range(PAIR):
                load(i, j).start()
        done = [0] * n
        count = 0
        for key in keys:
            piece = key[3]
            arr, r0, rows, kind = pieces[piece]
            paired = kind != 'chip'
            kc = at.chip(key)
            children = _onward(u, key, orders)
            if not children and not paired:
                src = term(piece, kc, at.core)
            else:
                j = done[piece]
                done[piece] += 1
                parts = []
                if paired:
                    _landed(got[piece].at[kc], d_recv.at[piece, kc])
                    parts.append(got[piece].at[kc])
                for side in children:
                    slot = table[u, key, side]
                    _landed(land[piece].at[slot], recv_sem.at[piece, slot])
                    parts.append(land[piece].at[slot])
                load(piece, j).wait()
                parts.append(stage[piece].at[j % PAIR])
                root = key[:3] == (0, 0, u)
                src = rows_of(outs[arr], piece) if root else parts[0]
                dtype = ins[arr].dtype
                step = SUB if dtype == F32 else CHIPS

                def body(r, parts=parts, dst=src, step=step, dtype=dtype):
                    some = pl.ds(pl.multiple_of(r * step, step), step)
                    total = parts[0][some, :].astype(F32)
                    for ref in parts[1:]:
                        total = total + ref[some, :].astype(F32)
                    dst[some, :] = total.astype(dtype)

                loop(rows // step, body)
                if j + PAIR < len(adds[piece]):
                    load(piece, j + PAIR).start()
                if root:
                    continue
            side = _via(u, key, orders)
            slot = table[_seen_by_parent(u, key, orders)]
            copy = _remote(src, land[piece].at[slot], send_sem.at[count], recv_sem.at[piece, slot], at.side(side))
            copy.start()
            started.append(copy)
            count += 1
        for copy in started:
            copy.wait_send()

    for u in (0, 1):
        pl.when(at.u == u)(functools.partial(run, u))


def scatter_sum(arrays, pieces, orders, seq, collective_id):
    n_arr, n = len(arrays), len(pieces)
    dma, hbm, vmem = pltpu.SemaphoreType.DMA, pl.BlockSpec(memory_space=pl.ANY), pl.BlockSpec(memory_space=pltpu.VMEM)
    _, most = _slots(pieces, orders, seq)
    shapes = [(rows, arrays[arr].shape[PAIR], arrays[arr].dtype) for arr, _, rows, _ in pieces]
    scratch = [pltpu.VMEM((m, r, c), d) for m, (r, c, d) in zip(most, shapes)]
    scratch += [pltpu.VMEM((PAIR, r, c), d) for r, c, d in shapes]
    scratch += [pltpu.VMEM((CHIPS, r, c), d) for (r, c, d), p in zip(shapes, pieces) if p[3] != 'chip']
    outs = [jax.ShapeDtypeStruct((sum(p[PAIR] for p in pieces if p[0] == i), v.shape[PAIR]), v.dtype) for i, v in enumerate(arrays)]
    nbytes = sum(v.size * v.dtype.itemsize for v in outs) + sum(
        (m + PAIR + CHIPS * int(p[3] != 'chip')) * (-(-r // CHIPS) * CHIPS) * c * d.itemsize for m, (r, c, d), p in zip(most, shapes, pieces))
    scratch += [dma((n, PAIR)), dma((CHIPS * n,)), dma((n, max(most))), dma((n, CHIPS)), dma((n, CHIPS))]
    return pl.pallas_call(
        functools.partial(_scatter_kernel, tuple(pieces), orders, seq, n_arr),
        out_shape=outs,
        in_specs=[hbm] * n_arr,
        out_specs=[vmem] * n_arr,
        scratch_shapes=scratch,
        compiler_params=pltpu.CompilerParams(collective_id=collective_id, has_side_effects=True, vmem_limit_bytes=nbytes + (6 * MIB)),
        cost_estimate=cost(200_000_000, nbytes * 4),
        name='scatter_sum',
    )(*arrays)


def _lookup_kernel(counts, codes, table_ref, out_ref, rows, block, sem):
    b = pl.program_id(0)
    n_col = out_ref.shape[PAIR] // LANES
    n_rows = rows.shape[0] // n_col

    @pl.when(b == 0)
    def _():
        def widen(i):
            for j in range(n_col):
                part = table_ref[pl.ds(pl.multiple_of(i * CHIPS, CHIPS), CHIPS), j * LANES:(j + 1) * LANES].astype(F32)
                line = pl.multiple_of(i * CHIPS * n_col, SUB)
                rows[pl.ds(line + j * SUB, SUB), :] = part[:SUB]
                rows[pl.ds(line + (n_col + j) * SUB, SUB), :] = part[SUB:]
        loop(n_rows // CHIPS, widen)

    seq = out_ref.shape[1]

    def clear(i):
        block[pl.ds(pl.multiple_of(i * SUB * n_col, SUB), SUB * n_col), :] = jnp.zeros((SUB * n_col, LANES), F32)
    loop(seq // SUB, clear)

    def pick(i):
        for t in range(SUB):
            code = codes[b * seq + i * SUB + t]
            block[pl.ds(code >> CHIPS, n_col, stride=SUB), :] = rows[pl.ds(code & 65535, n_col, stride=SUB), :]
    loop((counts[b] + 7) // SUB, pick)

    def narrow(i):
        line = pl.multiple_of(i * CHIPS * n_col, SUB)
        for j in range(n_col):
            part = jnp.concatenate([block[pl.ds(line + j * SUB, SUB), :], block[pl.ds(line + (n_col + j) * SUB, SUB), :]], axis=0)
            out_ref[0, pl.ds(pl.multiple_of(i * CHIPS, CHIPS), CHIPS), j * LANES:(j + 1) * LANES] = part.astype(BF16)
    loop(seq // CHIPS, narrow)


def lookup(table, counts, codes, seq):
    n_rows, dim = table.shape
    n_src = counts.shape[0]
    lines = dim // LANES
    return pl.pallas_call(
        _lookup_kernel,
        grid_spec=pltpu.PrefetchScalarGridSpec(
            num_scalar_prefetch=PAIR,
            grid=(n_src,),
            in_specs=[pl.BlockSpec(memory_space=pltpu.VMEM)],
            out_specs=pl.BlockSpec((1, seq, dim), lambda b, *_: (b, 0, 0)),
            scratch_shapes=[pltpu.VMEM((n_rows * lines, LANES), F32), pltpu.VMEM(((seq + SUB) * lines, LANES), F32), pltpu.SemaphoreType.DMA],
        ),
        out_shape=jax.ShapeDtypeStruct((n_src, seq, dim), table.dtype),
        compiler_params=pltpu.CompilerParams(vmem_limit_bytes=40 * MIB, dimension_semantics=('arbitrary',)),
        cost_estimate=cost(50_000_000, 40 * MIB),
        name='lookup',
    )(counts, codes, table)


def _add_rows_kernel(counts, codes, dx_ref, out_ref, buf, sem):
    n_src, lines, _ = dx_ref.shape
    n_col = 7
    seq = codes.shape[0] // n_src
    cut = lines // 5
    depth = buf.shape[0]

    def fetch(b):
        for i in range(5):
            some = pl.ds(i * cut, cut)
            pltpu.make_async_copy(dx_ref.at[b, some], buf.at[lax.rem(b, depth), some], sem.at[lax.rem(b, depth)]).start()

    for b in range(depth - 1):
        fetch(b)

    def clear(i):
        out_ref[pl.ds(pl.multiple_of(i * CHIPS * n_col, SUB), CHIPS * n_col), :] = jnp.zeros((CHIPS * n_col, LANES), F32)
    loop(out_ref.shape[0] // (CHIPS * n_col), clear)

    def source(b):
        at = lax.rem(b, depth)

        @pl.when(b + depth - 1 < n_src)
        def _():
            fetch(b + depth - 1)
        pltpu.make_async_copy(dx_ref.at[b], buf.at[at], sem.at[at]).wait()

        def add(first, i):
            code = codes[b * seq + first + i]
            line = pl.ds(code & 65535, n_col, stride=SUB)
            out_ref[line, :] = out_ref[line, :] + buf[at, pl.ds(code >> CHIPS, n_col, stride=SUB), :]

        def add_pair(i):
            code0, code1 = codes[b * seq + i * PAIR], codes[b * seq + i * PAIR + 1]
            line0, line1 = code0 & 65535, code1 & 65535
            new0 = buf[at, pl.ds(code0 >> CHIPS, n_col, stride=SUB), :]
            new1 = buf[at, pl.ds(code1 >> CHIPS, n_col, stride=SUB), :]
            old0 = out_ref[pl.ds(line0, n_col, stride=SUB), :]
            old1 = out_ref[pl.ds(line1, n_col, stride=SUB), :]
            sum0 = old0 + new0
            out_ref[pl.ds(line0, n_col, stride=SUB), :] = sum0
            out_ref[pl.ds(line1, n_col, stride=SUB), :] = jnp.where(line0 == line1, sum0, old1) + new1

        def add_four(i):
            add_pair(PAIR * i)
            add_pair(PAIR * i + 1)
        n = counts[b]
        loop(n // 4, add_four)

        rest = n // 4 * 4
        loop(n - rest, functools.partial(add, rest))
    loop(n_src, source)


def add_rows(dx, counts, codes, n_rows):
    n_src, lines, _ = dx.shape
    return pl.pallas_call(
        _add_rows_kernel,
        grid_spec=pltpu.PrefetchScalarGridSpec(
            num_scalar_prefetch=PAIR,
            grid=(),
            in_specs=[pl.BlockSpec(memory_space=pl.ANY)],
            out_specs=pl.BlockSpec(memory_space=pltpu.VMEM),
            scratch_shapes=[pltpu.VMEM((4, lines, LANES), F32), pltpu.SemaphoreType.DMA((4,))],
        ),
        out_shape=jax.ShapeDtypeStruct((n_rows * 7, LANES), F32),
        compiler_params=pltpu.CompilerParams(vmem_limit_bytes=48 * MIB),
        cost_estimate=cost(50_000_000, 80 * MIB),
        name='add_rows',
    )(counts, codes, dx)


def to_lines(v):
    rows, dim = v.shape
    return v.reshape(rows // SUB, SUB, dim // LANES, LANES).transpose(0, PAIR, 1, 3).reshape(rows * dim // LANES, LANES)


def from_lines(v, dim):
    rows = v.shape[0] * LANES // dim
    return v.reshape(rows // SUB, dim // LANES, SUB, LANES).transpose(0, PAIR, 1, 3).reshape(rows, dim)


def _rms(v):
    return lax.rsqrt(jnp.mean(v * v, axis=-1, keepdims=True) + NORM_EPS)


def _head_mean(v, low):
    first = jnp.sum(jnp.where(low, v, 0.0), axis=-1, keepdims=True)
    second = jnp.sum(jnp.where(low, 0.0, v), axis=-1, keepdims=True)
    return jnp.where(low, first, second) * (1.0 / 64.0)


def _turn(v, cos_t, sin_t, lead):
    return v * cos_t + jnp.where(lead, -pltpu.roll(v, 96, 1), pltpu.roll(v, 32, 1)) * sin_t


def _spread(tile, low, ref):
    first = jnp.where(low, tile, 0.0)
    second = jnp.where(low, 0.0, tile)
    ref[0] = first.astype(BF16)
    ref[1] = pltpu.roll(first, 64, 1).astype(BF16)
    ref[PAIR] = pltpu.roll(second, 64, 1).astype(BF16)
    ref[3] = second.astype(BF16)


def _probs(q, k, block):
    scores = mm_nt(q, k) * 0.125
    n = scores.shape[1]
    row = lax.broadcasted_iota(jnp.int32, scores.shape, 0) + block
    col = lax.broadcasted_iota(jnp.int32, scores.shape, 1)
    scores = jnp.where(row >= col, scores, -1e30)
    e = jnp.exp(scores - jnp.max(scores, axis=-1, keepdims=True))
    return e * (1.0 / jnp.sum(e, axis=-1, keepdims=True))


def _lanes(rows):
    lane = lax.broadcasted_iota(jnp.int32, (rows, LANES), 1)
    return lane < 64, lane % 64 < 32


def _attn_fwd_kernel(x_ref, w_ref, gain_ref, cos_ref, sin_ref, qk_gain_ref, in_ref, raw_ref, q_ref, k_ref, flat_ref, hid_ref, mlp_ref, kk, vv):
    seq, dim = x_ref.shape
    n_q = dim // LANES
    step = LANES
    n_in = raw_ref.shape[1]

    def project(r):
        at = pl.ds(pl.multiple_of(r * step, step), step)
        low, lead = _lanes(step)
        x = x_ref[at, :].astype(F32)
        m1 = (x * _rms(x) * gain_ref[0:1, :]).astype(BF16)
        in_ref[at, :] = m1
        raw = mm(m1, w_ref[:, :n_in]).astype(BF16)
        raw_ref[at, :] = raw
        cos_t, sin_t = cos_ref[at, :], sin_ref[at, :]
        for t in range(n_q + 1):
            v = raw[:, t * LANES:(t + 1) * LANES].astype(F32)
            v = v * lax.rsqrt(_head_mean(v * v, low) + NORM_EPS)
            which = int(t == n_q)
            v = _turn(v * qk_gain_ref[SUB * which:SUB * which + 1, :], cos_t, sin_t, lead).astype(BF16)
            if which:
                k_ref[at, :] = v
            else:
                q_ref[at, t * LANES:(t + 1) * LANES] = v
    loop(seq // step, project)
    low, _ = _lanes(seq)
    _spread(k_ref[...].astype(F32), low, kk)
    _spread(raw_ref[:, n_in - LANES:].astype(F32), low, vv)

    def heads(t):
        tile = pl.ds(pl.multiple_of(t * LANES, LANES), LANES)
        for b in range(seq // step):
            n = (b + 1) * step
            q = q_ref[b * step:n, tile]
            total = None
            for side in range(PAIR):
                i = PAIR * ((PAIR * t + side) // 7) + side
                p = _probs(q, kk[i, :n, :], b * step).astype(BF16)
                o = mm(p, vv[i, :n, :])
                total = o if total is None else total + o
            flat_ref[b * step:n, tile] = total.astype(BF16)
    loop(n_q, heads)

    def finish(r):
        at = pl.ds(pl.multiple_of(r * step, step), step)
        h = (x_ref[at, :].astype(F32) + mm(flat_ref[at, :], w_ref[:, n_in:n_in + dim])).astype(BF16)
        hid_ref[at, :] = h
        h = h.astype(F32)
        mlp_ref[at, :] = (h * _rms(h) * gain_ref[SUB:9, :]).astype(BF16)
    loop(seq // step, finish)


def attn_forward(x, w, gains, cos_t, sin_t, qk_gain, n_in):
    seq, dim = x.shape
    vmem = pl.BlockSpec(memory_space=pltpu.VMEM)
    sds = lambda n: jax.ShapeDtypeStruct((seq, n), BF16)
    return pl.pallas_call(
        _attn_fwd_kernel,
        out_shape=[sds(dim), sds(n_in), sds(dim), sds(LANES), sds(dim), sds(dim), sds(dim)],
        in_specs=[vmem] * 6,
        out_specs=[vmem] * 7,
        scratch_shapes=[pltpu.VMEM((4, seq, LANES), BF16), pltpu.VMEM((4, seq, LANES), BF16)],
        compiler_params=pltpu.CompilerParams(vmem_limit_bytes=40 * MIB),
        cost_estimate=cost(4_000_000_000, 12 * MIB, 4_000_000),
        name='attn_forward',
    )(x, w, gains, cos_t, sin_t, qk_gain)


def _attn_bwd_kernel(x_ref, w_ref, gain_ref, cos_ref, sin_ref, qk_gain_ref, in_ref, raw_ref, q_ref, k_ref, flat_ref, hid_ref, dy_ref, part_ref, recv_ref,
                     dx_ref, dw_in_ref, dw_out_ref, kk, vv, dk, dv, gh, hb, do, dqkv):
    seq, dim = x_ref.shape
    n_q = dim // LANES
    step = LANES
    n_blk = seq // step
    n_in = raw_ref.shape[1]

    def norm_back(grad, normed, inv, gain):
        grad = grad * gain
        return inv * (grad - normed * jnp.mean(grad * normed, axis=-1, keepdims=True))

    def hidden(r, total):
        at = pl.ds(pl.multiple_of(r * step, step), step)
        grad = part_ref[0, at, :] + recv_ref[at, :]
        h = hid_ref[at, :].astype(F32)
        inv = _rms(h)
        normed = h * inv
        g = dy_ref[at, :].astype(F32) + norm_back(grad, normed, inv, gain_ref[SUB:9, :])
        gh[at, :] = g
        g = g.astype(BF16)
        hb[at, :] = g
        do[at, :] = mm_nt(g, w_ref[:, n_in:n_in + dim]).astype(BF16)
        return total + jnp.sum(grad * normed, axis=0, keepdims=True)
    mlp_gain = lax.fori_loop(0, n_blk, hidden, jnp.zeros((1, dim), F32))

    low_all, _ = _lanes(seq)
    _spread(k_ref[...].astype(F32), low_all, kk)
    _spread(raw_ref[:, n_in - LANES:].astype(F32), low_all, vv)
    dk[...] = jnp.zeros_like(dk)
    dv[...] = jnp.zeros_like(dv)

    def raw_back(grad, tile, at, which, low, lead):
        v = raw_ref[at, tile].astype(F32)
        inv = lax.rsqrt(_head_mean(v * v, low) + NORM_EPS)
        normed = v * inv
        grad = _turn(grad, cos_ref[at, :], -sin_ref[at, :], lead)
        terms = jnp.sum(grad * normed, axis=0, keepdims=True)
        grad = grad * qk_gain_ref[SUB * which:SUB * which + 1, :]
        return inv * (grad - normed * _head_mean(grad * normed, low)), terms

    def heads(t, total):
        tile = pl.ds(pl.multiple_of(t * LANES, LANES), LANES)
        low, lead = _lanes(step)
        for b in range(n_blk):
            n = (b + 1) * step
            at = pl.ds(b * step, step)
            q = q_ref[at, tile]
            g = do[at, tile]
            grad_q = None
            for side in range(PAIR):
                i = PAIR * ((PAIR * t + side) // 7) + side
                k = kk[i, :n, :]
                p = _probs(q, k, b * step)
                dp = mm_nt(g, vv[i, :n, :])
                ds = (p * (dp - jnp.sum(dp * p, axis=-1, keepdims=True)) * 0.125).astype(BF16)
                dv[i, :n, :] = dv[i, :n, :] + mm_tn(p.astype(BF16), g)
                dk[i, :n, :] = dk[i, :n, :] + mm_tn(ds, q)
                part = mm(ds, k)
                grad_q = part if grad_q is None else grad_q + part
            back, terms = raw_back(grad_q, tile, at, 0, low, lead)
            dqkv[at, tile] = back.astype(BF16)
            total = total + terms
        return total
    q_gain = lax.fori_loop(0, n_q, heads, jnp.zeros((1, LANES), F32))

    def keys(r, total):
        at = pl.ds(pl.multiple_of(r * step, step), step)
        low, lead = _lanes(step)

        def join(ref):
            return jnp.where(low, ref[0, at, :] + pltpu.roll(ref[1, at, :], 64, 1), ref[3, at, :] + pltpu.roll(ref[PAIR, at, :], 64, 1))
        back, terms = raw_back(join(dk), pl.ds(dim, LANES), at, 1, low, lead)
        dqkv[at, dim:dim + LANES] = back.astype(BF16)
        dqkv[at, dim + LANES:] = join(dv).astype(BF16)
        return total + terms
    k_gain = lax.fori_loop(0, n_blk, keys, jnp.zeros((1, LANES), F32))

    def inputs(r, total):
        at = pl.ds(pl.multiple_of(r * step, step), step)
        grad = mm_nt(dqkv[at, :], w_ref[:, :n_in])
        x = x_ref[at, :].astype(F32)
        inv = _rms(x)
        normed = x * inv
        dx_ref[at, :] = gh[at, :] + norm_back(grad, normed, inv, gain_ref[0:1, :])
        return total + jnp.sum(grad * normed, axis=0, keepdims=True)
    attn_gain = lax.fori_loop(0, n_blk, inputs, jnp.zeros((1, dim), F32))

    low, _ = _lanes(SUB)
    row = lax.broadcasted_iota(jnp.int32, (SUB, dim), 0)
    both = jnp.where(low, jnp.broadcast_to(q_gain, (SUB, LANES)) + pltpu.roll(jnp.broadcast_to(q_gain, (SUB, LANES)), 64, 1),
                     jnp.broadcast_to(k_gain, (SUB, LANES)) + pltpu.roll(jnp.broadcast_to(k_gain, (SUB, LANES)), 64, 1))
    dx_ref[seq:, :] = jnp.where(row == 1, jnp.broadcast_to(attn_gain, (SUB, dim)), jnp.where(row == PAIR, jnp.broadcast_to(mlp_gain, (SUB, dim)), 0.0))
    dx_ref[seq:, :LANES] = jnp.where(row[:, :LANES] == 0, both, dx_ref[seq:, :LANES])

    def weights(t):
        tile = pl.ds(pl.multiple_of(t * LANES, LANES), LANES)
        dw_in_ref[tile, :] = mm_tn(in_ref[:, tile], dqkv[...])
        dw_out_ref[tile, :] = mm_tn(flat_ref[:, tile], hb[...])
    loop(n_q, weights)


def attn_backward(x, w, gains, cos_t, sin_t, qk_gain, saved, dy, part, recv):
    seq, dim = x.shape
    n_in = saved[1].shape[1]
    vmem = pl.BlockSpec(memory_space=pltpu.VMEM)
    scr = lambda *s: pltpu.VMEM(s[:-1], s[-1])
    return pl.pallas_call(
        _attn_bwd_kernel,
        out_shape=[jax.ShapeDtypeStruct((seq + SUB, dim), F32), jax.ShapeDtypeStruct((dim, n_in), F32), jax.ShapeDtypeStruct((dim, dim), F32)],
        in_specs=[vmem] * 15,
        out_specs=[vmem] * 3,
        scratch_shapes=[scr(4, seq, LANES, BF16), scr(4, seq, LANES, BF16), scr(4, seq, LANES, F32), scr(4, seq, LANES, F32), scr(seq, dim, F32),
                        scr(seq, dim, BF16), scr(seq, dim, BF16), scr(seq, n_in, BF16)],
        compiler_params=pltpu.CompilerParams(vmem_limit_bytes=52 * MIB),
        cost_estimate=cost(9_000_000_000, 30 * MIB, 4_000_000),
        name='attn_backward',
    )(x, w, gains, cos_t, sin_t, qk_gain, *saved[:6], dy, part, recv)


def _mlp_kernel(x_ref, dy_ref, wgu_ref, wd_ref, y_ref, din_ref, dwg_ref, dwu_ref, dwd_ref, xt, wg, wu, wd, act, dg, du, og, ou, od, load_sem, store_sem):
    half, tile = dwd_ref.shape[0], act.shape[1]
    n_tile = -(-half // tile)
    shared = n_tile * tile - half
    seqs, seq, _ = y_ref.shape
    step = seq // PAIR

    def start_of(j):
        first = (j == 0).astype(jnp.int32)
        return pl.multiple_of(first * (half - tile) + (1 - first) * (j - 1) * tile, LANES)

    def loads(j):
        at, slot = start_of(j), j % PAIR
        return [pltpu.make_async_copy(wgu_ref.at[:, pl.ds(at, tile)], wg.at[slot], load_sem.at[0, slot]),
                pltpu.make_async_copy(wgu_ref.at[:, pl.ds(pl.multiple_of(half + at, LANES), tile)], wu.at[slot], load_sem.at[1, slot]),
                pltpu.make_async_copy(wd_ref.at[pl.ds(at, tile)], wd.at[slot], load_sem.at[PAIR, slot])]

    def stores(j):
        at, slot = start_of(j), j % PAIR
        return [pltpu.make_async_copy(og.at[slot], dwg_ref.at[:, pl.ds(at, tile)], store_sem.at[0, slot]),
                pltpu.make_async_copy(ou.at[slot], dwu_ref.at[:, pl.ds(at, tile)], store_sem.at[1, slot]),
                pltpu.make_async_copy(od.at[slot], dwd_ref.at[pl.ds(at, tile)], store_sem.at[PAIR, slot])]

    for copy in loads(jnp.int32(0)):
        copy.start()
    y_ref[...] = jnp.zeros_like(y_ref)
    din_ref[...] = jnp.zeros_like(din_ref)
    xt[...] = x_ref[...].T

    def columns(j):
        slot = j % PAIR

        @pl.when(j + 1 < n_tile)
        def _():
            for copy in loads(j + 1):
                copy.start()
        for copy in loads(j):
            copy.wait()

        def rows(r):
            at = pl.ds(pl.multiple_of(r * step, step), step)
            s, inner = r // PAIR, pl.ds(pl.multiple_of(r % PAIR * step, step), step)
            x = x_ref[at, :]
            gate, up, back = mm(x, wg[slot]), mm(x, wu[slot]), mm_nt(dy_ref[at, :], wd[slot])
            counts = lax.broadcasted_iota(jnp.int32, (step, tile), 1) >= (j == 0).astype(jnp.int32) * shared
            up, back = jnp.where(counts, up, 0.0), jnp.where(counts, back, 0.0)
            sig = lax.logistic(gate)
            silu = gate * sig
            a = (silu * up).astype(BF16)
            g = (back * up * sig * (1.0 + gate * (1.0 - sig))).astype(BF16)
            u = (back * silu).astype(BF16)
            act[at, :], dg[at, :], du[at, :] = a, g, u
            y_ref[s, inner, :] = y_ref[s, inner, :] + mm(a, wd[slot])
            din_ref[s, inner, :] = din_ref[s, inner, :] + mm_nt(g, wg[slot]) + mm_nt(u, wu[slot])
        loop(PAIR * seqs, rows)

        @pl.when(j >= PAIR)
        def _():
            for copy in stores(j - PAIR):
                copy.wait()
        og[slot] = mm(xt[...], dg[...])
        ou[slot] = mm(xt[...], du[...])
        od[slot] = mm_tn(act[...], dy_ref[...])
        for copy in stores(j):
            copy.start()
    loop(n_tile, columns)
    for j in (n_tile - PAIR, n_tile - 1):
        for copy in stores(jnp.int32(j)):
            copy.wait()


def mlp(x, dy, wgu, wd, seqs):
    rows, dim = x.shape
    half = wd.shape[0]
    tile = 512
    vmem, hbm = pl.BlockSpec(memory_space=pltpu.VMEM), pl.BlockSpec(memory_space=pl.ANY)
    sds = lambda *s: jax.ShapeDtypeStruct(s, F32)
    dma = pltpu.SemaphoreType.DMA
    bf = lambda *s: pltpu.VMEM(s, BF16)
    f = lambda *s: pltpu.VMEM(s, F32)
    return pl.pallas_call(
        _mlp_kernel,
        out_shape=[sds(seqs, rows // seqs, dim), sds(seqs, rows // seqs, dim), sds(dim, half), sds(dim, half), sds(half, dim)],
        in_specs=[vmem, vmem, hbm, hbm],
        out_specs=[vmem, vmem, hbm, hbm, hbm],
        scratch_shapes=[bf(dim, rows), bf(PAIR, dim, tile), bf(PAIR, dim, tile), bf(PAIR, tile, dim), bf(rows, tile), bf(rows, tile), bf(rows, tile),
                        f(PAIR, dim, tile), f(PAIR, dim, tile), f(PAIR, tile, dim), dma((3, PAIR)), dma((3, PAIR))],
        compiler_params=pltpu.CompilerParams(vmem_limit_bytes=56 * MIB),
        cost_estimate=cost(CHIPS * rows * dim * half, 50 * MIB, rows * half),
        name='mlp',
    )(x, dy, wgu, wd)


def _codes(numbers, count):
    return tuple(numbers[i // 10] // LANES ** (i % 10) % LANES for i in range(count))


ROWS_SEQ = (
    _codes((152348940317322383368, 678662145372396725288, 751232056588892674273, 827272104050806263145, 30857149562), 45),
    _codes((166206088102504171520, 236385149464955200810, 603605329936848293224, 1039985241786269873361, 32734212313), 45),
)
ATTN_SEQ = (
    _codes((741342462958222970888, 32448584808), 15),
    _codes((965031540365288146944, 32448719928), 15),
)
GRAD_SEQ = (
    _codes((106232080133048504328, 890654452102748905891, 398002109975241450666, 965054631626560582091, 533961906380267493400, 829000359395158448539, 1143326429365316545848, 31381732460), 75),
    _codes((166206088102504171520, 704158088118449268010, 595216210114064208288, 531741816507597222992, 520744907820250718441, 1005047906396012195259, 910358688114310724092, 32470101362), 75),
)


def solution(mesh):
    n_dev = mesh.shape[AXIS_NAME]
    n_chip = n_dev // PAIR
    pair = [(i, i ^ 1) for i in range(n_dev)]
    groups = [[PAIR * k + c for k in range(n_chip)] for c in range(PAIR)]

    row_spec = P(AXIS_NAME, None)
    vec_spec = P(AXIS_NAME)
    full_spec = P(None)
    batch_spec = P(AXIS_NAME, None, None)
    weight_specs = (vec_spec, row_spec, row_spec, row_spec, full_spec, full_spec, row_spec, vec_spec, row_spec, row_spec, row_spec)

    def swap(v):
        return lax.ppermute(v, AXIS_NAME, pair)

    def gather_group(v):
        return lax.all_gather(v, AXIS_NAME, axis_index_groups=groups, tiled=True)

    def device_step(tokens, positions, table_shard, attn_norm, w_query, w_key, w_value, q_norm, k_norm, w_out, mlp_norm, w_gate, w_up, w_down, dy_out):
        me = lax.axis_index(AXIS_NAME)
        core = lax.rem(me, PAIR)
        seq_len = tokens.shape[1]
        rows_local, model_dim = table_shard.shape
        rows_w, ff = w_gate.shape
        half = ff // PAIR
        nq, nk = w_query.shape[1], w_key.shape[1]
        head_dim = q_norm.shape[0]

        mine_gu = jnp.concatenate([lax.dynamic_slice(w_gate, (0, core * half), (rows_w, half)), lax.dynamic_slice(w_up, (0, core * half), (rows_w, half))], axis=1)
        other_gu = jnp.concatenate([lax.dynamic_slice(w_gate, (0, (1 - core) * half), (rows_w, half)), lax.dynamic_slice(w_up, (0, (1 - core) * half), (rows_w, half))], axis=1)
        token_rows = below(tokens.reshape(-1, LANES), 4)
        dy = dy_out.reshape(seq_len, model_dim)
        all_tokens, (down_block, recv_gu, dy_other) = all_rows(token_rows, n_dev, [w_down, other_gu, dy], ('use', 'pair', 'pair'), 0)
        block_gu = jnp.where(core == 0, jnp.concatenate([mine_gu, recv_gu], axis=0), jnp.concatenate([recv_gu, mine_gu], axis=0))
        wgu = gather_group(block_gu)

        wd = gather_group(down_block)

        all_ids = all_tokens[:, :seq_len // LANES].reshape(-1)
        local_ids = all_ids - me * rows_local
        is_owner = (local_ids >= 0) & (local_ids < rows_local)
        own = is_owner.reshape(n_dev, seq_len)
        slot = jnp.arange(seq_len, dtype=jnp.int32)
        upto = (slot[:, None] <= slot[None, :]).astype(BF16)
        rank = jnp.where(own, mm(own.astype(BF16), upto).astype(jnp.int32) - 1, -1)
        counts = jnp.sum(own.astype(jnp.int32), axis=1)
        lines = model_dim // LANES
        line = lambda row: row // SUB * (SUB * lines) + row % SUB
        code = line(slot)[None] * 65536 + line(jnp.where(own, local_ids.reshape(n_dev, seq_len), 0))
        codes = jnp.sum(jnp.where(rank[:, :, None] == slot, code[:, :, None], 0), axis=1)
        codes = jnp.where(slot[None] < counts[:, None], codes, seq_len * lines * 65536).reshape(-1)
        picked = lookup(table_shard, counts, codes, seq_len)
        x_emb = scatter_sum([picked], [(0, 0, 192, 'device'), (0, 192, 208, 'device'), (0, 400, 112, 'device')], ('zba', 'zba', 'baz'), ROWS_SEQ, PAIR)[0]

        gain_cols = below(jnp.stack([attn_norm, mlp_norm]), 126).T
        attn_pack = jnp.concatenate([w_query, w_key, w_value, w_out, gain_cols], axis=1)
        attn_pack, x_emb = lax.optimization_barrier((attn_pack, x_emb))
        (attn_full,), _ = gather_all([attn_pack], [(0, 0, rows_w, True)], ('zba',), ATTN_SEQ, [], (), n_dev, 1)
        attn_full = attn_full.reshape(-1, attn_pack.shape[1])

        dy2 = jnp.concatenate([dy, dy_other], axis=0)

        n_in = nq + PAIR * nk
        gains = below(jnp.repeat(attn_full[:, n_in + nq:n_in + nq + PAIR].astype(F32).T, SUB, axis=0), SUB)
        qk_gain = jnp.repeat(jnp.stack([jnp.tile(q_norm, PAIR), jnp.tile(k_norm, PAIR)]).astype(F32), SUB, axis=0)

        inv_freq = jnp.exp((jnp.arange(LANES) % (head_dim // PAIR)).astype(F32) * (-2.0 * math.log(ROPE_THETA) / head_dim))
        angles = positions.reshape(seq_len, 1).astype(F32) * inv_freq
        cos_t, sin_t = jnp.cos(angles), jnp.sin(angles)
        saved = attn_forward(x_emb, attn_full, gains, cos_t, sin_t, qk_gain, n_in)
        hidden, mlp_in = saved[5:]

        mlp2 = jnp.concatenate([mlp_in, swap(mlp_in)], axis=0)
        y, grad_in, grad_w_gate, grad_w_up, grad_w_down = mlp(mlp2, dy2, wgu, wd, PAIR)
        grad_recv = swap(grad_in[1])
        layer_out = (hidden.astype(F32) + (y[0] + swap(y[1]))).astype(BF16)

        dx_block, grad_w_in, grad_w_out = attn_backward(x_emb, attn_full, gains, cos_t, sin_t, qk_gain, saved, dy, grad_in, grad_recv)

        by_chip = [u.reshape(n_chip, -1, u.shape[1]) for u in (grad_w_down, grad_w_gate, grad_w_up, grad_w_in, grad_w_out)]
        down_rows, gate_shard, up_shard, in_shard, out_shard = scatter_sum(
            by_chip, [(i, 0, u.shape[1], 'chip') for i, u in enumerate(by_chip[:3])] + [(i, 0, 32, 'rows') for i in (3, 4)], ('bza', 'zba', 'zba', 'baz', 'baz'), GRAD_SEQ, 3)

        chip_rows = jnp.concatenate([gate_shard, up_shard], axis=1)
        mine = lax.dynamic_slice(chip_rows, (core * rows_w, 0), (rows_w, chip_rows.shape[1]))
        give = lax.dynamic_slice(chip_rows, ((1 - core) * rows_w, 0), (rows_w, chip_rows.shape[1]))
        (all_dx,), (down_shard, recv) = gather_all(
            [to_lines(dx_block)], [(0, 0, 200 * lines, True), (0, 200 * lines, 200 * lines, True), (0, 400 * lines, 120 * lines, True)],
            ('zba', 'zba', 'baz'), ROWS_SEQ, [down_rows, give], ('store', 'pair'), n_dev, 4)
        d_table = from_lines(add_rows(all_dx, counts, codes, rows_local), model_dim)
        gains_grad = from_lines(jnp.sum(all_dx[:, seq_len * lines:], axis=0), model_dim)
        qk = gains_grad[0]
        d_attn_norm, d_mlp_norm = (lax.dynamic_slice(gains_grad[i], (me * rows_w,), (rows_w,)) for i in (1, PAIR))
        low = jnp.where(core == 0, mine, recv)
        high = jnp.where(core == 0, recv, mine)
        d_gate = jnp.concatenate([low[:, :half], high[:, :half]], axis=1)
        d_up = jnp.concatenate([low[:, half:ff], high[:, half:ff]], axis=1)
        in_rows = lax.dynamic_slice(in_shard, (core * (rows_w - 24), 0), (rows_w, n_in))
        d_query, d_key, d_value = in_rows[:, :nq], in_rows[:, nq:nq + nk], in_rows[:, nq + nk:]
        d_out = lax.dynamic_slice(out_shard, (core * (rows_w - 24), 0), (rows_w, nq))
        return (layer_out.reshape(1, seq_len, model_dim), d_table, d_attn_norm, d_query, d_key, d_value, qk[:head_dim], qk[head_dim:PAIR * head_dim], d_out, d_mlp_norm, d_gate, d_up, down_shard)

    return jax.shard_map(device_step, mesh=mesh, in_specs=(row_spec, row_spec, row_spec) + weight_specs + (batch_spec,), out_specs=(batch_spec, row_spec) + weight_specs, check_vma=False)
```

time: 953 us -> 929 us (0.975)
  matrix products: 92.4 us -> 0.2 us
  Pallas kernels: 784 us -> 861 us
    dot_general x10 -> x1, matrix products: 92.4 us -> 0.2 us  [mm(): lax.dot_general(a, b, (((1,), (0,)), ((), ())), preferred_element_type=F32)]
    pallas_call x1 -> x2, Pallas kernels: 50.2 us -> 114 us  [the longest x1 62.9 us: mlp(): pl.pallas_call(_mlp_kernel, out_shape=[sds(seqs, rows // seqs, dim), sds(...]
    pallas_call x2, Pallas kernels: 321 us -> 373 us  [scatter_sum(): pl.pallas_call(functools.partial(_scatter_kernel, tuple(pieces), orders,...]
    pallas_call x2, Pallas kernels: 298 us -> 260 us  [gather_all(): pl.pallas_call(functools.partial(_gather_kernel, tuple(pieces), orders, s...]
  transfers between devices with their start and end apart: 4 -> 5, of which waited for: 0 -> 2; matrix products, arithmetic and copies ran while one was open for 9% -> 3% of each run, Pallas kernels for 81% -> 84%
where the time goes in v6:
time: 929 us; the launch traced here: 927 us
  Pallas kernels  861 us (93%)
  local copies, waits for them, and re-layouts  29.3 us (3%)
  other arithmetic  19 us (2%)
  between operations  14.5 us (2%)
    pallas_call x2, Pallas kernels, scatter_sum(): pl.pallas_call(functools.partial(_scatter_kernel, tuple(pieces), orders,...  373 us
    pallas_call x2, Pallas kernels, gather_all(): pl.pallas_call(functools.partial(_gather_kernel, tuple(pieces), orders, s...  260 us
    pallas_call x1, Pallas kernels, mlp(): pl.pallas_call(_mlp_kernel, out_shape=[sds(seqs, rows // seqs, dim), sds(...  62.9 us
    pallas_call x1, Pallas kernels, attn_backward(): pl.pallas_call(_attn_bwd_kernel, out_shape=[jax.ShapeDtypeStruct((seq + S...  50.9 us
    pallas_call x1, Pallas kernels, lookup(): pl.pallas_call(_lookup_kernel, grid_spec=pltpu.PrefetchScalarGridSpec(num...  40.1 us
    pallas_call x1, Pallas kernels, add_rows(): pl.pallas_call(_add_rows_kernel, grid_spec=pltpu.PrefetchScalarGridSpec(n...  35.6 us
    pallas_call x1, Pallas kernels, attn_forward(): pl.pallas_call(_attn_fwd_kernel, out_shape=[sds(dim), sds(n_in), sds(dim)...  19.8 us
  transfers between devices with their start and end apart: 5, of which 2 were waited for; matrix products, arithmetic and copies ran while one was open for 3% of the time, Pallas kernels for 84%

profile of v6, /device:TPU:0, one launch (start us, length us, event | category | flops | bytes accessed | tf_op | source)
XLA Modules:
  0.0 927.5 jit_solution(9744067019615745589)
XLA Ops:
  7.2 0.0 all-gather.5.cloned.1.call-start
  7.2 1.3 pad.13.refs_0_
  8.5 1.2 constant_dynamic-slice_fusion.3
  9.7 0.7 pad_maximum_fusion.4.refs_2_
  10.5 0.0 copy-start.22
  10.5 18.4 %all_rows.1 = (s32[32,8,128]{2,1,0:T(8,128)}, bf16[152,896]{1,0:T(8,128)(2,1)}, bf16[28,4864]{1,0:T(8,128)(2,1)}, bf16[512,896]{1,0:T(8,128)(2,1)}) custom-call(s32[8,128]{1,0:T(8,128)} %pad.13.refs_0_, bf16[152,896]{1,0:T(8,128)(2,1)} %refs_1_.1, bf16[28,4864]{1,0:T(8,128)(2,1)} %pad_maximum_fusion.4.refs_2_, bf16[512,896]{1,0:T(8,128)(2,1)} %bitcast.76), custom_call_target="tpu_custom_call" | custom-call | flops 10000000 | bytes 1048576 | tf_op jit(solution)/shard_map/all_rows/pallas_call | solution.py:191
  28.9 0.0 all-gather.5.cloned.1.call-update
  28.9 0.0 all-gather.3.cloned.1.call-start
  29.0 2.1 maximum_select_fusion
  31.1 0.0 all-gather.3.cloned.1.call-update
  31.2 0.1 stack_tile.6
  31.3 0.1 stack_tile.7
  31.4 0.1 copy.36
  31.5 0.7 convert_reduce_fusion
  32.2 0.2 fusion.3
  32.4 0.1 fusion.7
  32.5 5.9 select_reduce_fusion
  38.4 0.1 select_bitcast_fusion
  38.5 0.0 copy-start.1
  38.5 3.4 copy-done.1
  41.9 40.1 %lookup.1.refs_0_ = bf16[32,512,896]{2,1,0:T(8,128)(2,1)} custom-call(s32[32]{0:T(128)S(1)} %get-tuple-element.74.counts, s32[16384]{0:T(1024)S(1)} %bitcast.69, bf16[4752,896]{1,0:T(8,128)(2,1)S(1)} %copy-done.1), custom_call_target="tpu_custom_call" | custom-call | flops 50000000 | bytes 41943040 | tf_op jit(solution)/shard_map/lookup/pallas_call | solution.py:459
  82.0 0.0 copy-start.13
  82.0 0.0 copy-start.16
  82.0 0.0 copy-start.17
  82.0 0.0 copy-start.14
  82.0 159.4 %scatter_sum.2.x_ref = bf16[512,896]{1,0:T(8,128)(2,1)S(1)} custom-call(bf16[32,512,896]{2,1,0:T(8,128)(2,1)} %lookup.1.refs_0_), custom_call_target="tpu_custom_call" | custom-call | flops 200000000 | bytes 136937472 | tf_op jit(solution)/shard_map/scatter_sum/pallas_call | solution.py:408
  241.6 41.2 %gather_all.2 = bf16[32,28,2176]{2,1,0:T(8,128)(2,1)S(1)} custom-call(bf16[28,2176]{1,0:T(8,128)(2,1)S(1)} %constant_dynamic-update-slice_fusion.refs_0_), custom_call_target="tpu_custom_call" | custom-call | flops 200000000 | bytes 7798784 | tf_op jit(solution)/shard_map/gather_all/pallas_call | solution.py:273
  282.8 2.1 copy-done
  284.9 6.1 reshape.197.w_ref
  291.0 1.0 convert_bitcast_fusion
  292.0 0.2 copy.37
  292.2 1.0 multiply_sine_fusion
  293.2 2.1 copy-done.2
  295.3 19.8 %attn_forward.1 = (bf16[512,896]{1,0:T(8,128)(2,1)S(1)}, bf16[512,1152]{1,0:T(8,128)(2,1)S(1)}, bf16[512,896]{1,0:T(8,128)(2,1)S(1)}, bf16[512,128]{1,0:T(8,128)...) custom-call(bf16[512,896]{1,0:T(8,128)(2,1)S(1)} %scatter_sum.2.x_ref, ...), custom_call_target="tpu_custom_call" | custom-call | flops 4000000000 | bytes 12582912 | tf_op jit(solution)/shard_map/attn_forward/pallas_call | solution.py:651
  315.2 0.9 copy-done.8
  316.1 1.0 copy-done.9
  317.1 0.6 collective-permute-start
  317.7 1.6 pad_maximum_fusion.1.dy_ref
  319.4 0.4 collective-permute-done
  319.8 1.4 pad_maximum_fusion.x_ref
  321.2 62.9 %mlp.1 = (f32[2,512,896]{2,1,0:T(8,128)}, f32[2,512,896]{2,1,0:T(8,128)}, f32[896,2432]{1,0:T(8,128)}, f32[896,2432]{1,0:T(8,128)}, f32[2432,896]{1,0:T(8,128)}) custom-call(bf16[1024,896]{1,0:T(8,128)(2,1)} %pad_maximum_fusion.x_ref, bf16[1024,896]{1,0:T(8,128)(2,1)} %pad_maximum_fusion.1.dy_ref, bf16[896,4864]{1,0:T(8,128)(2,1)} %all-gather.3.cloned.1.call-done.wgu_ref, ...), custom_call_target="tpu_custom_call" | custom-call | flops 35701915648 | bytes 52428800 | tf_op jit(solution)/shard_map/mlp/pallas_call | solution.py:863
  384.1 2.9 slice_bitcast_fusion
  387.0 0.4 collective-permute-start.2
  387.3 1.6 slice_bitcast_fusion.1
  389.0 0.2 collective-permute-start.1
  389.2 1.6 collective-permute-done.2.recv_ref
  390.8 50.9 %attn_backward.1 = (f32[520,896]{1,0:T(8,128)}, f32[896,1152]{1,0:T(8,128)}, f32[896,896]{1,0:T(8,128)}) custom-call(bf16[512,896]{1,0:T(8,128)(2,1)S(1)} %scatter_sum.2.x_ref, bf16[896,2176]{1,0:T(8,128)(2,1)} %reshape.197.w_ref, f32[24,896]{1,0:T(8,128)S(1)} %pad.14.gain_ref, f32[512,128]{1,0:T(8,128)S(1)} %get-tuple-element.91.cos_ref, ...), custom_call_target="tpu_custom_call" | custom-call | flops 8999999488 | bytes 31457280 | tf_op jit(solution)/shard_map/attn_backward/pallas_call | solution.py:770
  441.7 213.7 %scatter_sum.3 = (f32[152,896]{1,0:T(8,128)S(1)}, f32[56,2432]{1,0:T(8,128)S(1)}, f32[56,2432]{1,0:T(8,128)S(1)}, f32[32,1152]{1,0:T(8,128)S(1)}, f32[32,896]{1,0:T(8,128)S(1)}) custom-call(f32[16,152,896]{2,1,0:T(8,128)} %bitcast.74, f32[16,56,2432]{2,1,0:T(8,128)} %bitcast.72, f32[16,56,2432]{2,1,0:T(8,128)} %bitcast.73, f32[16,56,1152]{2,1,0:T(8,128)} %bitcast.75, ...), custom_call_target="tpu_custom_call" | custom-call | flops 200000000 | bytes 193380352 | tf_op jit(solution)/shard_map/scatter_sum/pallas_call | solution.py:408
  655.5 0.1 constant_dynamic-slice_fusion.2.refs_2_
  655.6 1.3 copy-done.3
  656.9 219.0 %gather_all.3 = (f32[32,3640,128]{2,1,0:T(8,128)}, f32[152,896]{1,0:T(8,128)S(1)}, f32[28,4864]{1,0:T(8,128)S(1)}) custom-call(f32[3640,128]{1,0:T(8,128)S(1)} %bitcast.68, f32[152,896]{1,0:T(8,128)S(1)} %get-tuple-element.63.refs_1_, f32[28,4864]{1,0:T(8,128)S(1)} %constant_dynamic-slice_fusion.2.refs_2_), custom_call_target="tpu_custom_call" | custom-call | flops 200000000 | bytes 119275520 | tf_op jit(solution)/shard_map/gather_all/pallas_call | solution.py:273
  875.9 1.3 slice_reduce_fusion
  877.2 35.6 %add_rows.1 = f32[33264,128]{1,0:T(8,128)} custom-call(s32[32]{0:T(128)S(1)} %get-tuple-element.74.counts, s32[16384]{0:T(1024)S(1)} %bitcast.70, f32[32,3640,128]{2,1,0:T(8,128)} %get-tuple-element.66.dx_ref), custom_call_target="tpu_custom_call" | custom-call | flops 50000000 | bytes 83886080 | tf_op jit(solution)/shard_map/add_rows/pallas_call | solution.py:531
  912.8 0.7 constant_dynamic-slice_fusion
  913.4 0.7 constant_dynamic-slice_fusion.1
  914.1 0.1 dynamic-slice_select_fusion.1
  914.3 0.6 dynamic_slice.38
  914.9 0.6 dynamic_slice.35
  915.5 0.6 fusion.34
  916.1 0.7 fusion.33
  916.8 0.9 pad_maximum_fusion.3
  917.7 0.9 pad_maximum_fusion.2
  918.6 1.3 fusion.4
  919.8 0.8 copy.54
  (58 shorter events, 0.4 us)
Async XLA Ops:
  7.2 314.0 %all-gather.5.cloned.1.call-start = ((), (), s32[]{:S(2)}) async-start(), calls=%async_computation.1 | async-start | bytes 4630528 | tf_op jit(solution)/shard_map/all_gather | solution.py:910
  10.4 20.7 %copy-start.19 = (bf16[64]{0:T(256)(128)(2,1)S(1)}, bf16[64]{0:T(256)(128)(2,1)}, u32[]{:S(2)}) copy-start(bf16[64]{0:T(256)(128)(2,1)} %param.22) | copy-start | bytes 388
  10.4 20.8 %copy-start.20 = (bf16[64]{0:T(256)(128)(2,1)S(1)}, bf16[64]{0:T(256)(128)(2,1)}, u32[]{:S(2)}) copy-start(bf16[64]{0:T(256)(128)(2,1)} %param.23) | copy-start | bytes 388
  10.4 20.9 %copy-start.18 = (s32[1,512]{1,0:T(1,128)S(1)}, s32[1,512]{1,0:T(1,128)}, u32[]{:S(2)}) copy-start(s32[1,512]{1,0:T(1,128)} %param.16) | copy-start | bytes 6148
  10.5 20.9 %copy-start.21 = (bf16[28]{0:T(256)(128)(2,1)S(1)}, bf16[28]{0:T(256)(128)(2,1)}, u32[]{:S(2)}) copy-start(bf16[28]{0:T(256)(128)(2,1)} %param.25) | copy-start | bytes 172
  10.5 20.9 %copy-start.22 = (bf16[28]{0:T(256)(128)(2,1)S(1)}, bf16[28]{0:T(256)(128)(2,1)}, u32[]{:S(2)}) copy-start(bf16[28]{0:T(256)(128)(2,1)} %param.18) | copy-start | bytes 172
  28.9 2.6 copy-start.15
  28.9 292.3 %all-gather.3.cloned.1.call-start = ((), (), s32[]{:S(2)}) async-start(), calls=%async_computation | async-start | bytes 9261056 | tf_op jit(solution)/shard_map/all_gather | solution.py:910
  38.5 3.4 copy-start.1
  82.0 159.5 %copy-start.13 = (bf16[28,896]{1,0:T(8,128)(2,1)S(1)}, bf16[28,896]{1,0:T(8,128)(2,1)}, u32[]{:S(2)}) copy-start(bf16[28,896]{1,0:T(8,128)(2,1)} %param.19) | copy-start | bytes 150532
  82.0 159.5 %copy-start.16 = (bf16[28,128]{1,0:T(8,128)(2,1)S(1)}, bf16[28,128]{1,0:T(8,128)(2,1)}, u32[]{:S(2)}) copy-start(bf16[28,128]{1,0:T(8,128)(2,1)} %param.20) | copy-start | bytes 21508
  82.0 159.5 %copy-start.17 = (bf16[28,128]{1,0:T(8,128)(2,1)S(1)}, bf16[28,128]{1,0:T(8,128)(2,1)}, u32[]{:S(2)}) copy-start(bf16[28,128]{1,0:T(8,128)(2,1)} %param.21) | copy-start | bytes 21508
  82.0 159.5 %copy-start.14 = (bf16[28,896]{1,0:T(8,128)(2,1)S(1)}, bf16[28,896]{1,0:T(8,128)(2,1)}, u32[]{:S(2)}) copy-start(bf16[28,896]{1,0:T(8,128)(2,1)} %param.24) | copy-start | bytes 150532
  282.8 2.1 copy-start
  293.2 2.1 copy-start.2
  295.3 22.4 %copy-start.10 = (bf16[1,512,896]{2,1,0:T(8,128)(2,1)S(1)}, bf16[1,512,896]{2,1,0:T(8,128)(2,1)}, u32[]{:S(2)}) copy-start(bf16[1,512,896]{2,1,0:T(8,128)(2,1)} %param.29) | copy-start | bytes 2752516
  295.3 22.4 %copy-start.12 = (bf16[512,896]{1,0:T(8,128)(2,1)S(1)}, bf16[512,896]{1,0:T(8,128)(2,1)}, u32[]{:S(2)}) copy-start(bf16[512,896]{1,0:T(8,128)(2,1)} %get-tuple-element.47) | copy-start | bytes 2752516
  315.2 1.0 copy-start.8
  316.1 1.0 copy-start.9
  317.1 2.3 copy-start.4
  317.1 2.3 copy-start.6
  317.1 2.3 copy-start.7
  317.1 2.7 collective-permute-start
  387.0 3.8 collective-permute-start.2
  389.0 529.6 %collective-permute-start.1 = (f32[512,896]{1,0:T(8,128)S(1)}, f32[512,896]{1,0:T(8,128)S(1)}, u32[]{:S(2)}, u32[]{:S(2)}) collective-permute-start(f32[512,896]{1,0:T(8,128)S(1)} %slice_bitcast_fusion.1), channel_id=1, source_target_pairs={{0,1},{1,0},{2,3},{3,2},{4,5},{5,4},{6,7},{7,6},{8,9},{9,8},{10,11... | collective-permute-start | bytes 5505032 | tf_op jit(solution)/shard_map/ppermute | solution.py:907
  655.4 1.5 copy-start.3
  914.1 4.5 copy-start.11
  916.8 1.8 copy-start.5
Sparse Core Ops, SparseCore 0:
  29.0 87.2 all-gather.4
  119.6 167.6 all-gather.2

commit v7 on v6

--- a/solution.py
+++ b/solution.py
@@ -209,9 +209,12 @@
     at = _Place(me)
     ends = list(_passes(moves, me))
 
+    def slot_of(kc, core, kind):
+        return {'device': PAIR * kc + core, 'core': CHIPS * core + kc, 'chip': kc}[kind]
+
     def part(kc, core, piece):
-        arr, r0, rows, shared = pieces[piece]
-        slot = PAIR * kc + core if shared else kc
+        arr, r0, rows, kind = pieces[piece]
+        slot = slot_of(kc, core, kind)
         return outs[arr].at[slot] if rows == outs[arr].shape[1] else outs[arr].at[slot, pl.ds(r0, rows)]
 
     def run(u):
@@ -228,7 +231,7 @@
         count, handed = 0, [0] * m
         for key in [(0, 0, u, i) for i in range(m)] + [_unpack(c) for c in seq[u]]:
             piece = key[3]
-            arr, r0, rows, shared = pieces[piece]
+            arr, r0, rows, kind = pieces[piece]
             kc = at.chip(key)
             place = part(kc, at.core, piece)
             if _via(u, key, orders) is None:
@@ -239,17 +242,17 @@
             for side in _onward(u, key, orders):
                 send(ref, place, send_sem.at[count], recv_sem.at[piece, kc], at.side(side))
                 count += 1
-            if shared:
+            if kind != 'chip':
                 send(ref, place, p_send.at[piece, handed[piece]], p_recv.at[piece, kc], at.partner)
                 handed[piece] += 1
             if key == (0, 0, u, m - 1):
                 for i, (to, _) in enumerate(ends):
                     moving.append(_start_move(moves[i], src[i], dst[i], m_send.at[i], m_recv.at[i], to, me))
-                own = [pltpu.make_async_copy(ins[i], outs[i].at[me if pieces_shared[i] else me // PAIR], own_sem.at[i]) for i in range(n_arr)]
+                own = [pltpu.make_async_copy(ins[i], outs[i].at[slot_of(me // PAIR, at.core, kinds[i])], own_sem.at[i]) for i in range(n_arr)]
                 for copy in own:
                     copy.start()
         for piece in range(m):
-            if pieces[piece][3]:
+            if pieces[piece][3] != 'chip':
                 for kc in range(CHIPS):
                     _landed(part(kc, 1 - at.core, piece), p_recv.at[piece, kc])
         for i, (to, _) in enumerate(ends):
@@ -259,7 +262,7 @@
         for copy in started:
             copy.wait_send()
 
-    pieces_shared = {p[0]: p[3] for p in pieces}
+    kinds = {p[0]: p[3] for p in pieces}
     for u in (0, 1):
         pl.when(at.u == u)(functools.partial(run, u))
 
@@ -269,10 +272,10 @@
     dma = pltpu.SemaphoreType.DMA
     vmem, hbm = pl.BlockSpec(memory_space=pltpu.VMEM), pl.BlockSpec(memory_space=pl.ANY)
     nbytes = sum(v.size * v.dtype.itemsize for v in blocks)
-    shared = {p[0]: p[3] for p in pieces}
+    kinds = {p[0]: p[3] for p in pieces}
     res = pl.pallas_call(
         functools.partial(_gather_kernel, tuple(pieces), orders, seq, moves, n_arr),
-        out_shape=[jax.ShapeDtypeStruct((n_dev if shared[i] else n_dev // PAIR,) + v.shape, v.dtype) for i, v in enumerate(blocks)] + [
+        out_shape=[jax.ShapeDtypeStruct((n_dev // PAIR if kinds[i] == 'chip' else n_dev,) + v.shape, v.dtype) for i, v in enumerate(blocks)] + [
             jax.ShapeDtypeStruct(v.shape, v.dtype) for v in moved],
         in_specs=[vmem] * n_arr + [hbm] * n,
         out_specs=[hbm] * (n_arr + n),
@@ -504,20 +507,18 @@
             line = pl.ds(code & 65535, n_col, stride=SUB)
             out_ref[line, :] = out_ref[line, :] + buf[at, pl.ds(code >> CHIPS, n_col, stride=SUB), :]
 
-        def add_pair(i):
-            code0, code1 = codes[b * seq + i * PAIR], codes[b * seq + i * PAIR + 1]
-            line0, line1 = code0 & 65535, code1 & 65535
-            new0 = buf[at, pl.ds(code0 >> CHIPS, n_col, stride=SUB), :]
-            new1 = buf[at, pl.ds(code1 >> CHIPS, n_col, stride=SUB), :]
-            old0 = out_ref[pl.ds(line0, n_col, stride=SUB), :]
-            old1 = out_ref[pl.ds(line1, n_col, stride=SUB), :]
-            sum0 = old0 + new0
-            out_ref[pl.ds(line0, n_col, stride=SUB), :] = sum0
-            out_ref[pl.ds(line1, n_col, stride=SUB), :] = jnp.where(line0 == line1, sum0, old1) + new1
-
         def add_four(i):
-            add_pair(PAIR * i)
-            add_pair(PAIR * i + 1)
+            code = [codes[b * seq + i * 4 + t] for t in range(4)]
+            line = [c & 65535 for c in code]
+            news = [buf[at, pl.ds(c >> CHIPS, n_col, stride=SUB), :] for c in code]
+            sums = []
+            for t in range(4):
+                old = out_ref[pl.ds(line[t], n_col, stride=SUB), :]
+                for before in range(t):
+                    old = jnp.where(line[t] == line[before], sums[before], old)
+                sums.append(old + news[t])
+            for t in range(4):
+                out_ref[pl.ds(line[t], n_col, stride=SUB), :] = sums[t]
         n = counts[b]
         loop(n // 4, add_four)
 
@@ -604,7 +605,7 @@
         x = x_ref[at, :].astype(F32)
         m1 = (x * _rms(x) * gain_ref[0:1, :]).astype(BF16)
         in_ref[at, :] = m1
-        raw = mm(m1, w_ref[:, :n_in]).astype(BF16)
+        raw = mm(m1, w_ref[0]).astype(BF16)
         raw_ref[at, :] = raw
         cos_t, sin_t = cos_ref[at, :], sin_ref[at, :]
         for t in range(n_q + 1):
@@ -637,15 +638,16 @@
 
     def finish(r):
         at = pl.ds(pl.multiple_of(r * step, step), step)
-        h = (x_ref[at, :].astype(F32) + mm(flat_ref[at, :], w_ref[:, n_in:n_in + dim])).astype(BF16)
+        h = (x_ref[at, :].astype(F32) + mm(flat_ref[at, :], w_ref[1, :, :dim])).astype(BF16)
         hid_ref[at, :] = h
         h = h.astype(F32)
         mlp_ref[at, :] = (h * _rms(h) * gain_ref[SUB:9, :]).astype(BF16)
     loop(seq // step, finish)
 
 
-def attn_forward(x, w, gains, cos_t, sin_t, qk_gain, n_in):
+def attn_forward(x, w, gains, cos_t, sin_t, qk_gain):
     seq, dim = x.shape
+    n_in = w.shape[PAIR]
     vmem = pl.BlockSpec(memory_space=pltpu.VMEM)
     sds = lambda n: jax.ShapeDtypeStruct((seq, n), BF16)
     return pl.pallas_call(
@@ -674,7 +676,7 @@
 
     def hidden(r, total):
         at = pl.ds(pl.multiple_of(r * step, step), step)
-        grad = part_ref[0, at, :] + recv_ref[at, :]
+        grad = part_ref[at, :] + recv_ref[at, :]
         h = hid_ref[at, :].astype(F32)
         inv = _rms(h)
         normed = h * inv
@@ -682,7 +684,7 @@
         gh[at, :] = g
         g = g.astype(BF16)
         hb[at, :] = g
-        do[at, :] = mm_nt(g, w_ref[:, n_in:n_in + dim]).astype(BF16)
+        do[at, :] = mm_nt(g, w_ref[1, :, :dim]).astype(BF16)
         return total + jnp.sum(grad * normed, axis=0, keepdims=True)
     mlp_gain = lax.fori_loop(0, n_blk, hidden, jnp.zeros((1, dim), F32))
 
@@ -740,7 +742,7 @@
 
     def inputs(r, total):
         at = pl.ds(pl.multiple_of(r * step, step), step)
-        grad = mm_nt(dqkv[at, :], w_ref[:, :n_in])
+        grad = mm_nt(dqkv[at, :], w_ref[0])
         x = x_ref[at, :].astype(F32)
         inv = _rms(x)
         normed = x * inv
@@ -774,17 +776,17 @@
         out_specs=[vmem] * 3,
         scratch_shapes=[scr(4, seq, LANES, BF16), scr(4, seq, LANES, BF16), scr(4, seq, LANES, F32), scr(4, seq, LANES, F32), scr(seq, dim, F32),
                         scr(seq, dim, BF16), scr(seq, dim, BF16), scr(seq, n_in, BF16)],
-        compiler_params=pltpu.CompilerParams(vmem_limit_bytes=52 * MIB),
+        compiler_params=pltpu.CompilerParams(vmem_limit_bytes=44 * MIB),
         cost_estimate=cost(9_000_000_000, 30 * MIB, 4_000_000),
         name='attn_backward',
     )(x, w, gains, cos_t, sin_t, qk_gain, *saved[:6], dy, part, recv)
 
 
-def _mlp_kernel(x_ref, dy_ref, wgu_ref, wd_ref, y_ref, din_ref, dwg_ref, dwu_ref, dwd_ref, xt, wg, wu, wd, act, dg, du, og, ou, od, load_sem, store_sem):
+def _mlp_kernel(x_ref, dy_ref, wgu_ref, wd_ref, y_mine, y_other, din_mine, din_other, dwg_ref, dwu_ref, dwd_ref, xt, wg, wu, wd, act, dg, du, og, ou, od, load_sem, store_sem):
     half, tile = dwd_ref.shape[0], act.shape[1]
     n_tile = -(-half // tile)
     shared = n_tile * tile - half
-    seqs, seq, _ = y_ref.shape
+    seq = y_mine.shape[0]
     step = seq // PAIR
 
     def start_of(j):
@@ -805,8 +807,8 @@
 
     for copy in loads(jnp.int32(0)):
         copy.start()
-    y_ref[...] = jnp.zeros_like(y_ref)
-    din_ref[...] = jnp.zeros_like(din_ref)
+    for ref in (y_mine, y_other, din_mine, din_other):
+        ref[...] = jnp.zeros_like(ref)
     xt[...] = x_ref[...].T
 
     def columns(j):
@@ -819,9 +821,8 @@
         for copy in loads(j):
             copy.wait()
 
-        def rows(r):
-            at = pl.ds(pl.multiple_of(r * step, step), step)
-            s, inner = r // PAIR, pl.ds(pl.multiple_of(r % PAIR * step, step), step)
+        def rows(y_ref, din_ref, first, r):
+            at, inner = pl.ds(pl.multiple_of(first + r * step, step), step), pl.ds(pl.multiple_of(r * step, step), step)
             x = x_ref[at, :]
             gate, up, back = mm(x, wg[slot]), mm(x, wu[slot]), mm_nt(dy_ref[at, :], wd[slot])
             counts = lax.broadcasted_iota(jnp.int32, (step, tile), 1) >= (j == 0).astype(jnp.int32) * shared
@@ -832,9 +833,10 @@
             g = (back * up * sig * (1.0 + gate * (1.0 - sig))).astype(BF16)
             u = (back * silu).astype(BF16)
             act[at, :], dg[at, :], du[at, :] = a, g, u
-            y_ref[s, inner, :] = y_ref[s, inner, :] + mm(a, wd[slot])
-            din_ref[s, inner, :] = din_ref[s, inner, :] + mm_nt(g, wg[slot]) + mm_nt(u, wu[slot])
-        loop(PAIR * seqs, rows)
+            y_ref[inner, :] = y_ref[inner, :] + mm(a, wd[slot])
+            din_ref[inner, :] = din_ref[inner, :] + mm_nt(g, wg[slot]) + mm_nt(u, wu[slot])
+        loop(PAIR, functools.partial(rows, y_mine, din_mine, 0))
+        loop(PAIR, functools.partial(rows, y_other, din_other, seq))
 
         @pl.when(j >= PAIR)
         def _():
@@ -851,7 +853,7 @@
             copy.wait()
 
 
-def mlp(x, dy, wgu, wd, seqs):
+def mlp(x, dy, wgu, wd):
     rows, dim = x.shape
     half = wd.shape[0]
     tile = 512
@@ -862,12 +864,12 @@
     f = lambda *s: pltpu.VMEM(s, F32)
     return pl.pallas_call(
         _mlp_kernel,
-        out_shape=[sds(seqs, rows // seqs, dim), sds(seqs, rows // seqs, dim), sds(dim, half), sds(dim, half), sds(half, dim)],
+        out_shape=[sds(rows // PAIR, dim)] * 4 + [sds(dim, half), sds(dim, half), sds(half, dim)],
         in_specs=[vmem, vmem, hbm, hbm],
-        out_specs=[vmem, vmem, hbm, hbm, hbm],
+        out_specs=[vmem] * 4 + [hbm] * 3,
         scratch_shapes=[bf(dim, rows), bf(PAIR, dim, tile), bf(PAIR, dim, tile), bf(PAIR, tile, dim), bf(rows, tile), bf(rows, tile), bf(rows, tile),
                         f(PAIR, dim, tile), f(PAIR, dim, tile), f(PAIR, tile, dim), dma((3, PAIR)), dma((3, PAIR))],
-        compiler_params=pltpu.CompilerParams(vmem_limit_bytes=56 * MIB),
+        compiler_params=pltpu.CompilerParams(vmem_limit_bytes=44 * MIB),
         cost_estimate=cost(CHIPS * rows * dim * half, 50 * MIB, rows * half),
         name='mlp',
     )(x, dy, wgu, wd)
@@ -882,8 +884,8 @@
     _codes((166206088102504171520, 236385149464955200810, 603605329936848293224, 1039985241786269873361, 32734212313), 45),
 )
 ATTN_SEQ = (
-    _codes((741342462958222970888, 32448584808), 15),
-    _codes((965031540365288146944, 32448719928), 15),
+    _codes((370142165075936415752, 972012016723415295145, 1124725529257844811929), 30),
+    _codes((961577811093152729088, 751808515438843144256, 1124738970787495025897), 30),
 )
 GRAD_SEQ = (
     _codes((106232080133048504328, 890654452102748905891, 398002109975241450666, 965054631626560582091, 533961906380267493400, 829000359395158448539, 1143326429365316545848, 31381732460), 75),
@@ -919,15 +921,25 @@
         nq, nk = w_query.shape[1], w_key.shape[1]
         head_dim = q_norm.shape[0]
 
-        mine_gu = jnp.concatenate([lax.dynamic_slice(w_gate, (0, core * half), (rows_w, half)), lax.dynamic_slice(w_up, (0, core * half), (rows_w, half))], axis=1)
-        other_gu = jnp.concatenate([lax.dynamic_slice(w_gate, (0, (1 - core) * half), (rows_w, half)), lax.dynamic_slice(w_up, (0, (1 - core) * half), (rows_w, half))], axis=1)
-        token_rows = below(tokens.reshape(-1, LANES), 4)
+        n_in = nq + PAIR * nk
+
+        def gate_up(c):
+            return jnp.concatenate([lax.dynamic_slice(w, (0, c * half), (rows_w, half)) for w in (w_gate, w_up)], axis=1)
+
+        def both_cores(mine, other):
+            return jnp.where(core == 0, jnp.concatenate([mine, other], axis=0), jnp.concatenate([other, mine], axis=0))
+        attn_in = jnp.concatenate([w_query, w_key, w_value], axis=1)
+        attn_out = jnp.concatenate([w_out, below(jnp.stack([attn_norm, mlp_norm]), n_in - nq - PAIR).T], axis=1)
+        mine_attn, other_attn = jnp.where(core == 0, attn_in, attn_out), jnp.where(core == 0, attn_out, attn_in)
         dy = dy_out.reshape(seq_len, model_dim)
-        all_tokens, (down_block, recv_gu, dy_other) = all_rows(token_rows, n_dev, [w_down, other_gu, dy], ('use', 'pair', 'pair'), 0)
-        block_gu = jnp.where(core == 0, jnp.concatenate([mine_gu, recv_gu], axis=0), jnp.concatenate([recv_gu, mine_gu], axis=0))
-        wgu = gather_group(block_gu)
-
-        wd = gather_group(down_block)
+        all_tokens, (down_block, recv_gu, recv_attn, dy_other) = all_rows(
+            below(tokens.reshape(-1, LANES), 4), n_dev, [w_down, gate_up(1 - core), other_attn, dy], ('use', 'pair', 'pair', 'pair'), 0)
+        wgu = gather_group(both_cores(gate_up(core), recv_gu))
+
+        (attn_w, wd), _ = gather_all([both_cores(mine_attn, recv_attn), down_block], [(0, 0, PAIR * rows_w, 'core'), (1, 0, down_block.shape[0], 'chip')],
+                                     ('bza', 'zba'), ATTN_SEQ, [], (), n_dev, 1)
+        attn_w = attn_w.reshape(PAIR, model_dim, n_in)
+        wd = wd.reshape(-1, model_dim)
 
         all_ids = all_tokens[:, :seq_len // LANES].reshape(-1)
         local_ids = all_ids - me * rows_local
@@ -945,30 +957,23 @@
         picked = lookup(table_shard, counts, codes, seq_len)
         x_emb = scatter_sum([picked], [(0, 0, 192, 'device'), (0, 192, 208, 'device'), (0, 400, 112, 'device')], ('zba', 'zba', 'baz'), ROWS_SEQ, PAIR)[0]
 
-        gain_cols = below(jnp.stack([attn_norm, mlp_norm]), 126).T
-        attn_pack = jnp.concatenate([w_query, w_key, w_value, w_out, gain_cols], axis=1)
-        attn_pack, x_emb = lax.optimization_barrier((attn_pack, x_emb))
-        (attn_full,), _ = gather_all([attn_pack], [(0, 0, rows_w, True)], ('zba',), ATTN_SEQ, [], (), n_dev, 1)
-        attn_full = attn_full.reshape(-1, attn_pack.shape[1])
-
         dy2 = jnp.concatenate([dy, dy_other], axis=0)
 
-        n_in = nq + PAIR * nk
-        gains = below(jnp.repeat(attn_full[:, n_in + nq:n_in + nq + PAIR].astype(F32).T, SUB, axis=0), SUB)
+        gains = below(jnp.repeat(attn_w[1, :, nq:nq + PAIR].astype(F32).T, SUB, axis=0), SUB)
         qk_gain = jnp.repeat(jnp.stack([jnp.tile(q_norm, PAIR), jnp.tile(k_norm, PAIR)]).astype(F32), SUB, axis=0)
 
         inv_freq = jnp.exp((jnp.arange(LANES) % (head_dim // PAIR)).astype(F32) * (-2.0 * math.log(ROPE_THETA) / head_dim))
         angles = positions.reshape(seq_len, 1).astype(F32) * inv_freq
         cos_t, sin_t = jnp.cos(angles), jnp.sin(angles)
-        saved = attn_forward(x_emb, attn_full, gains, cos_t, sin_t, qk_gain, n_in)
+        saved = attn_forward(x_emb, attn_w, gains, cos_t, sin_t, qk_gain)
         hidden, mlp_in = saved[5:]
 
         mlp2 = jnp.concatenate([mlp_in, swap(mlp_in)], axis=0)
-        y, grad_in, grad_w_gate, grad_w_up, grad_w_down = mlp(mlp2, dy2, wgu, wd, PAIR)
-        grad_recv = swap(grad_in[1])
-        layer_out = (hidden.astype(F32) + (y[0] + swap(y[1]))).astype(BF16)
-
-        dx_block, grad_w_in, grad_w_out = attn_backward(x_emb, attn_full, gains, cos_t, sin_t, qk_gain, saved, dy, grad_in, grad_recv)
+        y_mine, y_other, grad_in, grad_other, grad_w_gate, grad_w_up, grad_w_down = mlp(mlp2, dy2, wgu, wd)
+        grad_recv = swap(grad_other)
+        layer_out = (hidden.astype(F32) + (y_mine + swap(y_other))).astype(BF16)
+
+        dx_block, grad_w_in, grad_w_out = attn_backward(x_emb, attn_w, gains, cos_t, sin_t, qk_gain, saved, dy, grad_in, grad_recv)
 
         by_chip = [u.reshape(n_chip, -1, u.shape[1]) for u in (grad_w_down, grad_w_gate, grad_w_up, grad_w_in, grad_w_out)]
         down_rows, gate_shard, up_shard, in_shard, out_shard = scatter_sum(
@@ -978,7 +983,7 @@
         mine = lax.dynamic_slice(chip_rows, (core * rows_w, 0), (rows_w, chip_rows.shape[1]))
         give = lax.dynamic_slice(chip_rows, ((1 - core) * rows_w, 0), (rows_w, chip_rows.shape[1]))
         (all_dx,), (down_shard, recv) = gather_all(
-            [to_lines(dx_block)], [(0, 0, 200 * lines, True), (0, 200 * lines, 200 * lines, True), (0, 400 * lines, 120 * lines, True)],
+            [to_lines(dx_block)], [(0, 0, 200 * lines, 'device'), (0, 200 * lines, 200 * lines, 'device'), (0, 400 * lines, 120 * lines, 'device')],
             ('zba', 'zba', 'baz'), ROWS_SEQ, [down_rows, give], ('store', 'pair'), n_dev, 4)
         d_table = from_lines(add_rows(all_dx, counts, codes, rows_local), model_dim)
         gains_grad = from_lines(jnp.sum(all_dx[:, seq_len * lines:], axis=0), model_dim)

time: 929 us -> 919 us (0.989)
  Pallas kernels: 861 us -> 844 us
    pallas_call x2, Pallas kernels: 373 us -> 321 us  [scatter_sum(): pl.pallas_call(functools.partial(_scatter_kernel, tuple(pieces), orders,...]
    pallas_call x2, Pallas kernels: 260 us -> 298 us  [gather_all(): pl.pallas_call(functools.partial(_gather_kernel, tuple(pieces), orders, s...]
    unnamed x53 -> x73, local copies, waits for them, and re-layouts: 11.8 us -> 28.5 us
  transfers between devices with their start and end apart: 5 -> 4, of which waited for: 2 -> 2; matrix products, arithmetic and copies ran while one was open for 3% -> 2% of each run, Pallas kernels for 84% -> 83%
where the time goes in v7:
time: 919 us; the launch traced here: 918 us
  Pallas kernels  844 us (92%)
  local copies, waits for them, and re-layouts  36.2 us (4%)
  other arithmetic  19.1 us (2%)
  between operations  14.5 us (2%)
    pallas_call x2, Pallas kernels, scatter_sum(): pl.pallas_call(functools.partial(_scatter_kernel, tuple(pieces), orders,...  321 us
    pallas_call x2, Pallas kernels, gather_all(): pl.pallas_call(functools.partial(_gather_kernel, tuple(pieces), orders, s...  298 us
    pallas_call x1, Pallas kernels, mlp(): pl.pallas_call(_mlp_kernel, out_shape=[sds(rows // PAIR, dim)] * 4 + [sds...  61.1 us
    pallas_call x1, Pallas kernels, attn_backward(): pl.pallas_call(_attn_bwd_kernel, out_shape=[jax.ShapeDtypeStruct((seq + S...  48.3 us
    pallas_call x1, Pallas kernels, lookup(): pl.pallas_call(_lookup_kernel, grid_spec=pltpu.PrefetchScalarGridSpec(num...  40 us
    pallas_call x1, Pallas kernels, add_rows(): pl.pallas_call(_add_rows_kernel, grid_spec=pltpu.PrefetchScalarGridSpec(n...  36.8 us
    unnamed x73, local copies, waits for them, and re-layouts  28.5 us
    pallas_call x1, Pallas kernels, attn_forward(): pl.pallas_call(_attn_fwd_kernel, out_shape=[sds(dim), sds(n_in), sds(dim)...  19.9 us
  transfers between devices with their start and end apart: 4, of which 2 were waited for; matrix products, arithmetic and copies ran while one was open for 2% of the time, Pallas kernels for 83%

profile of v7, /device:TPU:0, one launch (start us, length us, event | category | flops | bytes accessed | tf_op | source)
XLA Modules:
  0.0 917.9 jit_solution(15379415008409180832)
XLA Ops:
  7.3 1.3 pad.12.refs_0_
  8.5 0.7 pad_maximum_fusion.6
  9.2 0.1 copy.33
  9.3 0.8 constant_dynamic-update-slice_fusion.2
  10.2 0.7 constant_dynamic-update-slice_fusion.1
  10.9 0.7 constant_dynamic-update-slice_fusion
  11.6 1.2 constant_dynamic-slice_fusion.3
  12.8 0.7 pad_maximum_fusion.4.refs_2_
  13.5 0.7 broadcast_select_fusion
  14.2 18.4 %all_rows.1 = (s32[32,8,128]{2,1,0:T(8,128)}, bf16[152,896]{1,0:T(8,128)(2,1)}, bf16[28,4864]{1,0:T(8,128)(2,1)}, bf16[28,1152]{1,0:T(8,128)(2,1)}, bf16[512,896]{1,0:T(8,128)(2,1)}) custom-call(s32[8,128]{1,0:T(8,128)} %pad.12.refs_0_, bf16[152,896]{1,0:T(8,128)(2,1)} %refs_1_.1, bf16[28,4864]{1,0:T(8,128)(2,1)} %pad_maximum_fusion.4.refs_2_, ...), custom_call_target="tpu_custom_call" | custom-call | flops 10000000 | bytes 1048576 | tf_op jit(solution)/shard_map/all_rows/pallas_call | solution.py:191
  32.6 2.1 maximum_select_fusion
  35.0 1.6 convert_reduce_fusion
  36.5 0.2 fusion.1
  36.8 5.9 select_reduce_fusion
  42.9 80.0 %gather_all.2 = (bf16[32,56,1152]{2,1,0:T(8,128)(2,1)S(1)}, bf16[16,152,896]{2,1,0:T(8,128)(2,1)S(1)}) custom-call(bf16[56,1152]{1,0:T(8,128)(2,1)S(1)} %maximum_select_fusion.1.refs_0_, bf16[152,896]{1,0:T(8,128)(2,1)S(1)} %copy-done.13), custom_call_target="tpu_custom_call" | custom-call | flops 200000000 | bytes 25690112 | tf_op jit(solution)/shard_map/gather_all/pallas_call | solution.py:276
  122.9 2.0 copy-done.14
  125.0 2.0 copy-done.10
  127.0 0.2 copy.34
  127.2 3.4 copy-done
  130.6 40.0 %lookup.1.refs_0_ = bf16[32,512,896]{2,1,0:T(8,128)(2,1)} custom-call(s32[32]{0:T(128)S(1)} %get-tuple-element.80.counts, s32[16384]{0:T(1024)S(1)} %bitcast.67, bf16[4752,896]{1,0:T(8,128)(2,1)S(1)} %copy-done), custom_call_target="tpu_custom_call" | custom-call | flops 50000000 | bytes 41943040 | tf_op jit(solution)/shard_map/lookup/pallas_call | solution.py:462
  170.6 107.1 %scatter_sum.2.x_ref = bf16[512,896]{1,0:T(8,128)(2,1)S(1)} custom-call(bf16[32,512,896]{2,1,0:T(8,128)(2,1)} %lookup.1.refs_0_), custom_call_target="tpu_custom_call" | custom-call | flops 200000000 | bytes 136937472 | tf_op jit(solution)/shard_map/scatter_sum/pallas_call | solution.py:411
  277.7 1.0 multiply_sine_fusion
  278.7 19.9 %attn_forward.1 = (bf16[512,896]{1,0:T(8,128)(2,1)S(1)}, bf16[512,1152]{1,0:T(8,128)(2,1)S(1)}, bf16[512,896]{1,0:T(8,128)(2,1)S(1)}, bf16[512,128]{1,0:T(8,128)...) custom-call(bf16[512,896]{1,0:T(8,128)(2,1)S(1)} %scatter_sum.2.x_ref, ...), custom_call_target="tpu_custom_call" | custom-call | flops 4000000000 | bytes 12582912 | tf_op jit(solution)/shard_map/attn_forward/pallas_call | solution.py:653
  298.6 0.9 copy-done.19
  299.5 0.9 copy-done.21
  300.6 1.6 pad_maximum_fusion.1.dy_ref
  302.2 0.2 copy-done.15
  302.4 0.3 copy-done.17
  302.7 0.3 collective-permute-done
  303.0 0.1 pad_maximum_fusion.x_ref
  303.2 61.1 %mlp.1 = (f32[512,896]{1,0:T(8,128)S(1)}, f32[512,896]{1,0:T(8,128)S(1)}, f32[512,896]{1,0:T(8,128)S(1)}, f32[512,896]{1,0:T(8,128)}, f32[896,2432]{1,0:T(8,128)...) custom-call(bf16[1024,896]{1,0:T(8,128)(2,1)S(1)} %pad_maximum_fusion.x_ref, bf16[1024,896]{1,0:T(8,128)(2,1)} %pad_maximum_fusion.1.dy_ref, ...), custom_call_target="tpu_custom_call" | custom-call | flops 35701915648 | bytes 52428800 | tf_op jit(solution)/shard_map/mlp/pallas_call | solution.py:865
  364.3 1.2 copy-done.3
  365.5 1.3 copy-done.12
  366.8 1.3 copy-done.23
  368.1 0.1 collective-permute-start.2
  368.2 0.4 collective-permute-start.1
  368.6 3.3 collective-permute-done.2.recv_ref
  371.8 1.3 copy-done.31
  373.1 1.2 copy-done.6
  374.3 1.2 copy-done.9
  375.5 1.3 copy-done.16
  376.7 1.2 copy-done.18
  377.9 1.2 copy-done.20
  379.1 1.2 copy-done.22
  380.3 1.5 copy-done.24
  381.8 0.9 copy-done.26
  382.7 48.3 %attn_backward.1 = (f32[520,896]{1,0:T(8,128)}, f32[896,1152]{1,0:T(8,128)}, f32[896,896]{1,0:T(8,128)}) custom-call(bf16[512,896]{1,0:T(8,128)(2,1)S(1)} %copy-done.9, bf16[2,896,1152]{2,1,0:T(8,128)(2,1)} %bitcast.70, f32[24,896]{1,0:T(8,128)S(1)} %pad.14.gain_ref, f32[512,128]{1,0:T(8,128)S(1)} %get-tuple-element.99.cos_ref, ...), custom_call_target="tpu_custom_call" | custom-call | flops 8999999488 | bytes 31457280 | tf_op jit(solution)/shard_map/attn_backward/pallas_call | solution.py:772
  430.9 214.4 %scatter_sum.3 = (f32[152,896]{1,0:T(8,128)S(1)}, f32[56,2432]{1,0:T(8,128)S(1)}, f32[56,2432]{1,0:T(8,128)S(1)}, f32[32,1152]{1,0:T(8,128)S(1)}, f32[32,896]{1,0:T(8,128)S(1)}) custom-call(f32[16,152,896]{2,1,0:T(8,128)} %bitcast.76, f32[16,56,2432]{2,1,0:T(8,128)} %bitcast.74, f32[16,56,2432]{2,1,0:T(8,128)} %bitcast.75, f32[16,56,1152]{2,1,0:T(8,128)} %bitcast.77, ...), custom_call_target="tpu_custom_call" | custom-call | flops 200000000 | bytes 193380352 | tf_op jit(solution)/shard_map/scatter_sum/pallas_call | solution.py:411
  645.5 1.3 copy-done.2
  646.9 218.0 %gather_all.3 = (f32[32,3640,128]{2,1,0:T(8,128)}, f32[152,896]{1,0:T(8,128)S(1)}, f32[28,4864]{1,0:T(8,128)S(1)}) custom-call(f32[3640,128]{1,0:T(8,128)S(1)} %bitcast.66, f32[152,896]{1,0:T(8,128)S(1)} %get-tuple-element.69.refs_1_, f32[28,4864]{1,0:T(8,128)S(1)} %constant_dynamic-slice_fusion.2.refs_2_), custom_call_target="tpu_custom_call" | custom-call | flops 200000000 | bytes 119275520 | tf_op jit(solution)/shard_map/gather_all/pallas_call | solution.py:276
  864.9 1.3 slice_reduce_fusion
  866.1 36.8 %add_rows.1 = f32[33264,128]{1,0:T(8,128)} custom-call(s32[32]{0:T(128)S(1)} %get-tuple-element.80.counts, s32[16384]{0:T(1024)S(1)} %bitcast.68, f32[32,3640,128]{2,1,0:T(8,128)} %get-tuple-element.72.dx_ref), custom_call_target="tpu_custom_call" | custom-call | flops 50000000 | bytes 83886080 | tf_op jit(solution)/shard_map/add_rows/pallas_call | solution.py:532
  902.9 0.7 constant_dynamic-slice_fusion
  903.6 0.7 constant_dynamic-slice_fusion.1
  904.2 0.1 dynamic-slice_select_fusion.1
  904.4 0.6 dynamic_slice.38
  905.0 0.6 dynamic_slice.35
  905.6 0.6 fusion.32
  906.2 0.7 fusion.31
  906.9 0.9 pad_maximum_fusion.3
  907.8 0.9 pad_maximum_fusion.2
  908.7 0.4 copy-done.7
  909.0 1.3 fusion.2
  910.3 0.8 copy.49
  (75 shorter events, 1.0 us)
Async XLA Ops:
  7.2 6.3 copy-start.29
  7.2 296.0 %all-gather.2.cloned.1.call-start = ((), (), s32[]{:S(2)}) async-start(), calls=%async_computation | async-start | bytes 9261056 | tf_op jit(solution)/shard_map/all_gather | solution.py:912
  13.5 21.3 %copy-start.32 = (bf16[64]{0:T(256)(128)(2,1)S(1)}, bf16[64]{0:T(256)(128)(2,1)}, u32[]{:S(2)}) copy-start(bf16[64]{0:T(256)(128)(2,1)} %param.22) | copy-start | bytes 388
  13.5 21.4 %copy-start.33 = (bf16[64]{0:T(256)(128)(2,1)S(1)}, bf16[64]{0:T(256)(128)(2,1)}, u32[]{:S(2)}) copy-start(bf16[64]{0:T(256)(128)(2,1)} %param.23) | copy-start | bytes 388
  13.5 21.4 %copy-start.30 = (s32[1,512]{1,0:T(1,128)S(1)}, s32[1,512]{1,0:T(1,128)}, u32[]{:S(2)}) copy-start(s32[1,512]{1,0:T(1,128)} %param.16) | copy-start | bytes 6148
  32.6 10.3 %copy-start.28 = (bf16[28,1152]{1,0:T(8,128)(2,1)S(1)}, bf16[28,1152]{1,0:T(8,128)(2,1)}, u32[]{:S(2)}) copy-start(bf16[28,1152]{1,0:T(8,128)(2,1)} %get-tuple-element.46) | copy-start | bytes 193540
  32.6 10.4 %copy-start.13 = (bf16[152,896]{1,0:T(8,128)(2,1)S(1)}, bf16[152,896]{1,0:T(8,128)(2,1)}, u32[]{:S(2)}) copy-start(bf16[152,896]{1,0:T(8,128)(2,1)} %get-tuple-element.47.refs_1_) | copy-start | bytes 817156
  122.9 2.0 copy-start.14
  125.0 2.0 copy-start.10
  127.2 3.4 copy-start
  170.6 108.1 %copy-start.11 = (bf16[32,56,1152]{2,1,0:T(8,128)(2,1)S(1)}, bf16[32,56,1152]{2,1,0:T(8,128)(2,1)}, u32[]{:S(2)}) copy-start(bf16[32,56,1152]{2,1,0:T(8,128)(2,1)} %copy-done.10) | copy-start | bytes 12386308
  277.7 20.9 %copy-start.8 = (bf16[512,896]{1,0:T(8,128)(2,1)}, bf16[512,896]{1,0:T(8,128)(2,1)S(1)}, u32[]{:S(2)}) copy-start(bf16[512,896]{1,0:T(8,128)(2,1)S(1)} %scatter_sum.2.x_ref) | copy-start | bytes 2752516
  278.7 21.8 %copy-start.1 = (bf16[1,512,896]{2,1,0:T(8,128)(2,1)S(1)}, bf16[1,512,896]{2,1,0:T(8,128)(2,1)}, u32[]{:S(2)}) copy-start(bf16[1,512,896]{2,1,0:T(8,128)(2,1)} %param.29) | copy-start | bytes 2752516
  278.7 21.8 %copy-start.27 = (bf16[512,896]{1,0:T(8,128)(2,1)S(1)}, bf16[512,896]{1,0:T(8,128)(2,1)}, u32[]{:S(2)}) copy-start(bf16[512,896]{1,0:T(8,128)(2,1)} %get-tuple-element.51) | copy-start | bytes 2752516
  298.6 0.9 copy-start.19
  299.5 0.9 copy-start.21
  300.4 1.8 copy-start.5
  300.5 1.9 copy-start.15
  300.5 2.3 copy-start.17
  300.5 2.3 copy-start.25
  300.5 2.5 collective-permute-start
  364.3 1.2 copy-start.3
  365.5 1.3 copy-start.12
  366.8 1.3 copy-start.23
  368.1 3.8 collective-permute-start.2
  368.2 540.5 %collective-permute-start.1 = (f32[512,896]{1,0:T(8,128)}, f32[512,896]{1,0:T(8,128)S(1)}, u32[]{:S(2)}, u32[]{:S(2)}) collective-permute-start(f32[512,896]{1,0:T(8,128)} %copy-done.12), channel_id=1, source_target_pairs={{0,1},{1,0},{2,3},{3,2},{4,5},{5,4},{6,7},{7,6},{8,9},{9,8},{10,11... | collective-permute-start | bytes 5505032 | tf_op jit(solution)/shard_map/ppermute | solution.py:909
  371.8 1.3 copy-start.31
  373.1 1.2 copy-start.6
  374.3 1.2 copy-start.9
  375.5 1.3 copy-start.16
  376.7 1.2 copy-start.18
  377.9 1.2 copy-start.20
  379.1 1.2 copy-start.22
  380.3 1.5 copy-start.24
  381.8 0.9 copy-start.26
  645.3 1.5 copy-start.2
  906.9 1.8 copy-start.4
  906.9 2.1 copy-start.7
Sparse Core Ops, SparseCore 0:
  34.9 136.6 all-gather.1

commit v8 on v7

--- a/solution.py
+++ b/solution.py
@@ -13,7 +13,7 @@
 F32 = jnp.float32
 BF16 = jnp.bfloat16
 MESH = pl.DeviceIdType.MESH
-LANES, SUB, CHIPS, PAIR, MIB = 128, 8, 16, 2, 1 << 20
+LANES, HEAD, CHIPS, SUB, QUAD, PAIR, MIB = 128, 64, 16, 8, 4, 2, 1 << 20
 
 
 def mm(a, b):
@@ -44,7 +44,7 @@
 
 
 def _unpack(code):
-    return code // 64, code // 32 % PAIR, code // SUB % 4, code % SUB
+    return code // HEAD, code // 32 % PAIR, code // SUB % QUAD, code % SUB
 
 
 def _via(u, key, orders):
@@ -88,11 +88,11 @@
     def __init__(self, me, swapped=False):
         self.me = me
         self.core = me % PAIR
-        x, y, self.z = (me // PAIR) % PAIR, (me // 4) % PAIR, me // SUB
+        x, y, self.z = (me // PAIR) % PAIR, (me // QUAD) % PAIR, me // SUB
         other = 1 - self.core if swapped else self.core
         self.a = y * (1 - other) + x * other
         self.b = x * (1 - other) + y * other
-        self.a_str, self.b_str = 4 - PAIR * other, PAIR + PAIR * other
+        self.a_str, self.b_str = QUAD - PAIR * other, PAIR + PAIR * other
         self.far = self.z // PAIR
         self.u = 3 * self.far + (1 - PAIR * self.far) * self.z
         self.partner = me + 1 - PAIR * self.core
@@ -281,7 +281,7 @@
         out_specs=[hbm] * (n_arr + n),
         scratch_shapes=[dma((n_arr,)), dma((24 * m,)), dma((m, CHIPS)), dma((m, CHIPS)), dma((m, CHIPS)), dma((max(n, 1),)), dma((max(n, 1),))],
         compiler_params=pltpu.CompilerParams(collective_id=collective_id, has_side_effects=True, vmem_limit_bytes=nbytes + (SUB * MIB)),
-        cost_estimate=cost(200_000_000, nbytes * 64),
+        cost_estimate=cost(200_000_000, nbytes * HEAD),
         name='gather_all',
     )(*blocks, *moved)
     return res[:n_arr], res[n_arr:]
@@ -299,17 +299,45 @@
     return table, most
 
 
-def _scatter_kernel(pieces, orders, seq, n_arr, *refs):
+def _order(u, seq, orders, n, n_late, lead, after):
+    keys = [_unpack(c) for c in reversed(seq[u])]
+    roots = [(0, 0, u, i) for i in range(n)]
+    if not n_late:
+        return keys + roots, [], []
+    late = [key for key in keys if key[3] >= n - n_late]
+    rest = [key for key in keys if key not in late]
+    first = [key for key in rest if not _onward(u, key, orders)][:lead]
+    rest = [key for key in rest if key not in first]
+    sums = [key for key in rest if _onward(u, key, orders)]
+    parts = [[sums.pop(0)] if some else [] for some in after]
+    rest = [key for key in rest if [key] not in parts]
+    out, share = [], 0
+    rate = len(late) / (len(rest) * 0.85)
+    for key in rest:
+        out.append(key)
+        share += rate
+        while share >= 1 and late:
+            out.append(late.pop(0))
+            share -= 1
+    return first, parts, out + late + roots
+
+
+def _scatter_kernel(pieces, orders, seq, n_arr, work, *refs):
     table, _ = _slots(pieces, orders, seq)
     n = len(pieces)
-    n_pair = sum(1 for p in pieces if p[3] != 'chip')
-    ins, outs = refs[:n_arr], refs[n_arr:PAIR * n_arr]
-    k = PAIR * n_arr
-    land, stage, pair = refs[k:k + n], refs[k + n:k + PAIR * n], list(refs[k + PAIR * n:k + PAIR * n + n_pair])
-    load_sem, send_sem, recv_sem, d_send, d_recv = refs[k + PAIR * n + n_pair:]
-    got = [pair.pop(0) if p[3] != 'chip' else None for p in pieces]
+    paired = [p[3] != 'chip' for p in pieces]
+    n_late, n_in, n_out, n_scr = (work.arrays, work.inputs, work.outputs, work.scratches) if work else (0, 0, 0, 0)
+    cut = lambda count: [refs_left.pop(0) for _ in range(count)]
+    refs_left = list(refs)
+    ins, work_in, outs, made, work_out = cut(n_arr - n_late), cut(n_in), cut(n_arr), cut(n_late), cut(n_out)
+    ins += made
+    land, stage, pair = cut(n), cut(n), cut(sum(paired))
+    load_sem, send_sem, recv_sem, d_send, d_recv, out_sem = cut(6)
+    got = [pair.pop(0) if p else None for p in paired]
     me = lax.axis_index(AXIS_NAME)
     at, partner_at = _Place(me), _Place(me, swapped=True)
+    early = [i for i in range(n) if pieces[i][0] < n_arr - n_late]
+    late = [i for i in range(n) if i not in early]
 
     def rows_of(ref, piece):
         _, r0, rows, _ = pieces[piece]
@@ -318,106 +346,145 @@
     def term(piece, kc, core):
         arr, _, rows, kind = pieces[piece]
         if kind == 'rows':
-            return ins[arr].at[kc, pl.ds(pl.multiple_of(24 * core, SUB), rows)]
+            return ins[arr].at[pl.ds(pl.multiple_of(ins[arr].shape[0] // CHIPS * kc + 24 * core, SUB), rows)]
         return rows_of(ins[arr].at[PAIR * kc + core if kind == 'device' else kc], piece)
 
-    def run(u):
-        sides = ['a', 'b', 'z+'] + (['z-'] if u else [])
-        _meet([at.side(s) for s in sides] + [at.partner])
-        keys = [_unpack(c) for c in reversed(seq[u])] + [(0, 0, u, i) for i in range(n)]
-        started = []
-        given = [0] * n
-        for key in keys:
-            piece = key[3]
-            if pieces[piece][3] != 'chip':
-                kc = partner_at.chip(key)
-                copy = _remote(term(piece, kc, 1 - at.core), got[piece].at[kc], d_send.at[piece, given[piece]], d_recv.at[piece, kc], at.partner)
-                given[piece] += 1
-                copy.start()
-                started.append(copy)
-        adds = [[key for key in keys if key[3] == i and (pieces[i][3] != 'chip' or _onward(u, key, orders))] for i in range(n)]
-
-        def load(piece, j):
-            return pltpu.make_async_copy(term(piece, at.chip(adds[piece][j]), at.core), stage[piece].at[j % PAIR], load_sem.at[piece, j % PAIR])
-
-        for i in range(n):
-            for j in range(PAIR):
-                load(i, j).start()
-        done = [0] * n
-        count = 0
-        for key in keys:
-            piece = key[3]
-            arr, r0, rows, kind = pieces[piece]
-            paired = kind != 'chip'
+    class Node:
+        def __init__(self, u):
+            self.u = u
+            self.first, self.parts, self.rest = _order(u, seq, orders, n, len(late), 15, work.after if work else ())
+            self.keys = self.first + sum(self.parts, []) + self.rest
+            self.adds = [[key for key in self.keys if key[3] == i and (paired[i] or _onward(u, key, orders))] for i in range(n)]
+            self.sent, self.given, self.done = [], [0] * n, [0] * n
+
+        def meet(self):
+            _meet([at.side(s) for s in ['a', 'b', 'z+'] + (['z-'] if self.u else [])] + [at.partner])
+
+        def load(self, piece, j):
+            return pltpu.make_async_copy(term(piece, at.chip(self.adds[piece][j]), at.core), stage[piece].at[j % PAIR], load_sem.at[piece, j % PAIR])
+
+        def ready(self, some):
+            for key in self.keys:
+                piece = key[3]
+                if paired[piece] and piece in some:
+                    kc = partner_at.chip(key)
+                    copy = _remote(term(piece, kc, 1 - at.core), got[piece].at[kc], d_send.at[piece, self.given[piece]], d_recv.at[piece, kc], at.partner)
+                    self.given[piece] += 1
+                    copy.start()
+            for piece in some:
+                for j in range(PAIR):
+                    self.load(piece, j).start()
+
+        def step(self, key):
+            u, piece = self.u, key[3]
+            arr, _, rows, _ = pieces[piece]
             kc = at.chip(key)
+            root = key[:3] == (0, 0, u)
             children = _onward(u, key, orders)
-            if not children and not paired:
+            if not children and not paired[piece]:
                 src = term(piece, kc, at.core)
             else:
-                j = done[piece]
-                done[piece] += 1
+                j = self.done[piece]
+                self.done[piece] += 1
                 parts = []
-                if paired:
+                if paired[piece]:
                     _landed(got[piece].at[kc], d_recv.at[piece, kc])
                     parts.append(got[piece].at[kc])
                 for side in children:
                     slot = table[u, key, side]
                     _landed(land[piece].at[slot], recv_sem.at[piece, slot])
                     parts.append(land[piece].at[slot])
-                load(piece, j).wait()
+                self.load(piece, j).wait()
                 parts.append(stage[piece].at[j % PAIR])
-                root = key[:3] == (0, 0, u)
-                src = rows_of(outs[arr], piece) if root else parts[0]
+                src = parts[0]
                 dtype = ins[arr].dtype
-                step = SUB if dtype == F32 else CHIPS
-
-                def body(r, parts=parts, dst=src, step=step, dtype=dtype):
-                    some = pl.ds(pl.multiple_of(r * step, step), step)
+                size = SUB if dtype == F32 else CHIPS
+
+                def add(r):
+                    some = pl.ds(pl.multiple_of(r * size, size), size)
                     total = parts[0][some, :].astype(F32)
                     for ref in parts[1:]:
                         total = total + ref[some, :].astype(F32)
-                    dst[some, :] = total.astype(dtype)
-
-                loop(rows // step, body)
-                if j + PAIR < len(adds[piece]):
-                    load(piece, j + PAIR).start()
-                if root:
-                    continue
-            side = _via(u, key, orders)
-            slot = table[_seen_by_parent(u, key, orders)]
-            copy = _remote(src, land[piece].at[slot], send_sem.at[count], recv_sem.at[piece, slot], at.side(side))
+                    src[some, :] = total.astype(dtype)
+                loop(rows // size, add)
+                if j + PAIR < len(self.adds[piece]):
+                    self.load(piece, j + PAIR).start()
+            if root:
+                copy = pltpu.make_async_copy(src, rows_of(outs[arr], piece), out_sem.at[piece])
+            else:
+                slot = table[_seen_by_parent(u, key, orders)]
+                copy = _remote(src, land[piece].at[slot], send_sem.at[len(self.sent)], recv_sem.at[piece, slot], at.side(_via(u, key, orders)))
+                self.sent.append(piece)
             copy.start()
-            started.append(copy)
-            count += 1
-        for copy in started:
-            copy.wait_send()
-
-    for u in (0, 1):
-        pl.when(at.u == u)(functools.partial(run, u))
-
-
-def scatter_sum(arrays, pieces, orders, seq, collective_id):
-    n_arr, n = len(arrays), len(pieces)
+
+        def finish(self):
+            def sent(ref, sem):
+                _remote(ref, ref, sem, sem, at.partner).wait_send()
+            for i, piece in enumerate(self.sent):
+                sent(land[piece].at[0], send_sem.at[i])
+            for piece in range(n):
+                for i in range(self.given[piece]):
+                    sent(got[piece].at[0], d_send.at[piece, i])
+                out = rows_of(outs[pieces[piece][0]], piece)
+                _landed(out, out_sem.at[piece])
+
+    nodes = [Node(u) for u in (0, 1)]
+
+    def each(do):
+        for node in nodes:
+            pl.when(at.u == node.u)(functools.partial(do, node))
+
+    def begin(node):
+        node.meet()
+        node.ready(early)
+        for key in node.first:
+            node.step(key)
+
+    def end(node):
+        node.ready(late)
+        for key in node.rest:
+            node.step(key)
+        node.finish()
+    each(begin)
+    if work:
+        def between(part, when=None):
+            def steps(node):
+                for key in node.parts[part]:
+                    node.step(key)
+            if when is None:
+                each(steps)
+            else:
+                pl.when(when)(lambda: each(steps))
+        work.run(work_in, made, work_out, refs_left, between)
+    each(end)
+
+
+def scatter_sum(arrays, pieces, orders, seq, collective_id, work=None):
+    late = list(work.makes) if work else []
+    n_arr, n = len(arrays) + len(late), len(pieces)
     dma, hbm, vmem = pltpu.SemaphoreType.DMA, pl.BlockSpec(memory_space=pl.ANY), pl.BlockSpec(memory_space=pltpu.VMEM)
     _, most = _slots(pieces, orders, seq)
-    shapes = [(rows, arrays[arr].shape[PAIR], arrays[arr].dtype) for arr, _, rows, _ in pieces]
+    every = list(arrays) + late
+    shapes = [(rows, every[arr].shape[-1], every[arr].dtype) for arr, _, rows, _ in pieces]
     scratch = [pltpu.VMEM((m, r, c), d) for m, (r, c, d) in zip(most, shapes)]
     scratch += [pltpu.VMEM((PAIR, r, c), d) for r, c, d in shapes]
     scratch += [pltpu.VMEM((CHIPS, r, c), d) for (r, c, d), p in zip(shapes, pieces) if p[3] != 'chip']
-    outs = [jax.ShapeDtypeStruct((sum(p[PAIR] for p in pieces if p[0] == i), v.shape[PAIR]), v.dtype) for i, v in enumerate(arrays)]
-    nbytes = sum(v.size * v.dtype.itemsize for v in outs) + sum(
-        (m + PAIR + CHIPS * int(p[3] != 'chip')) * (-(-r // CHIPS) * CHIPS) * c * d.itemsize for m, (r, c, d), p in zip(most, shapes, pieces))
-    scratch += [dma((n, PAIR)), dma((CHIPS * n,)), dma((n, max(most))), dma((n, CHIPS)), dma((n, CHIPS))]
+    outs = [jax.ShapeDtypeStruct((sum(p[PAIR] for p in pieces if p[0] == i), v.shape[-1]), v.dtype) for i, v in enumerate(every)]
+    nbytes = sum((m + PAIR + CHIPS * int(p[3] != 'chip')) * (-(-r // CHIPS) * CHIPS) * c * d.itemsize for m, (r, c, d), p in zip(most, shapes, pieces))
+    scratch += [dma((n, PAIR)), dma((CHIPS * n,)), dma((n, max(most))), dma((n, CHIPS)), dma((n, CHIPS)), dma((n,))]
+    work_in = work.operands if work else []
+    work_out = work.results if work else []
+    limit = min(nbytes + (6 * MIB) + (work.nbytes if work else 0), 67043328)
     return pl.pallas_call(
-        functools.partial(_scatter_kernel, tuple(pieces), orders, seq, n_arr),
-        out_shape=outs,
-        in_specs=[hbm] * n_arr,
-        out_specs=[vmem] * n_arr,
-        scratch_shapes=scratch,
-        compiler_params=pltpu.CompilerParams(collective_id=collective_id, has_side_effects=True, vmem_limit_bytes=nbytes + (6 * MIB)),
-        cost_estimate=cost(200_000_000, nbytes * 4),
+        functools.partial(_scatter_kernel, tuple(pieces), orders, seq, n_arr, work),
+        out_shape=outs + late + work_out,
+        in_specs=[hbm] * len(arrays) + [vmem if near else hbm for _, near in work_in],
+        out_specs=[hbm] * (n_arr + len(late)) + [vmem] * len(work_out),
+        scratch_shapes=scratch + (work.scratch if work else []),
+        compiler_params=pltpu.CompilerParams(collective_id=collective_id, has_side_effects=True, vmem_limit_bytes=limit),
+        cost_estimate=cost(200_000_000, nbytes * QUAD),
         name='scatter_sum',
-    )(*arrays)
+    )(*arrays, *[v for v, _ in work_in])
 
 
 def _lookup_kernel(counts, codes, table_ref, out_ref, rows, block, sem):
@@ -508,21 +575,21 @@
             out_ref[line, :] = out_ref[line, :] + buf[at, pl.ds(code >> CHIPS, n_col, stride=SUB), :]
 
         def add_four(i):
-            code = [codes[b * seq + i * 4 + t] for t in range(4)]
+            code = [codes[b * seq + i * QUAD + t] for t in range(QUAD)]
             line = [c & 65535 for c in code]
             news = [buf[at, pl.ds(c >> CHIPS, n_col, stride=SUB), :] for c in code]
             sums = []
-            for t in range(4):
+            for t in range(QUAD):
                 old = out_ref[pl.ds(line[t], n_col, stride=SUB), :]
                 for before in range(t):
                     old = jnp.where(line[t] == line[before], sums[before], old)
                 sums.append(old + news[t])
-            for t in range(4):
+            for t in range(QUAD):
                 out_ref[pl.ds(line[t], n_col, stride=SUB), :] = sums[t]
         n = counts[b]
-        loop(n // 4, add_four)
-
-        rest = n // 4 * 4
+        loop(n // QUAD, add_four)
+
+        rest = n // QUAD * QUAD
         loop(n - rest, functools.partial(add, rest))
     loop(n_src, source)
 
@@ -536,7 +603,7 @@
             grid=(),
             in_specs=[pl.BlockSpec(memory_space=pl.ANY)],
             out_specs=pl.BlockSpec(memory_space=pltpu.VMEM),
-            scratch_shapes=[pltpu.VMEM((4, lines, LANES), F32), pltpu.SemaphoreType.DMA((4,))],
+            scratch_shapes=[pltpu.VMEM((QUAD, lines, LANES), F32), pltpu.SemaphoreType.DMA((QUAD,))],
         ),
         out_shape=jax.ShapeDtypeStruct((n_rows * 7, LANES), F32),
         compiler_params=pltpu.CompilerParams(vmem_limit_bytes=48 * MIB),
@@ -573,8 +640,8 @@
     first = jnp.where(low, tile, 0.0)
     second = jnp.where(low, 0.0, tile)
     ref[0] = first.astype(BF16)
-    ref[1] = pltpu.roll(first, 64, 1).astype(BF16)
-    ref[PAIR] = pltpu.roll(second, 64, 1).astype(BF16)
+    ref[1] = pltpu.roll(first, HEAD, 1).astype(BF16)
+    ref[PAIR] = pltpu.roll(second, HEAD, 1).astype(BF16)
     ref[3] = second.astype(BF16)
 
 
@@ -590,7 +657,7 @@
 
 def _lanes(rows):
     lane = lax.broadcasted_iota(jnp.int32, (rows, LANES), 1)
-    return lane < 64, lane % 64 < 32
+    return lane < HEAD, lane % HEAD < 32
 
 
 def _attn_fwd_kernel(x_ref, w_ref, gain_ref, cos_ref, sin_ref, qk_gain_ref, in_ref, raw_ref, q_ref, k_ref, flat_ref, hid_ref, mlp_ref, kk, vv):
@@ -655,131 +722,166 @@
         out_shape=[sds(dim), sds(n_in), sds(dim), sds(LANES), sds(dim), sds(dim), sds(dim)],
         in_specs=[vmem] * 6,
         out_specs=[vmem] * 7,
-        scratch_shapes=[pltpu.VMEM((4, seq, LANES), BF16), pltpu.VMEM((4, seq, LANES), BF16)],
+        scratch_shapes=[pltpu.VMEM((QUAD, seq, LANES), BF16), pltpu.VMEM((QUAD, seq, LANES), BF16)],
         compiler_params=pltpu.CompilerParams(vmem_limit_bytes=40 * MIB),
         cost_estimate=cost(4_000_000_000, 12 * MIB, 4_000_000),
         name='attn_forward',
     )(x, w, gains, cos_t, sin_t, qk_gain)
 
 
-def _attn_bwd_kernel(x_ref, w_ref, gain_ref, cos_ref, sin_ref, qk_gain_ref, in_ref, raw_ref, q_ref, k_ref, flat_ref, hid_ref, dy_ref, part_ref, recv_ref,
-                     dx_ref, dw_in_ref, dw_out_ref, kk, vv, dk, dv, gh, hb, do, dqkv):
-    seq, dim = x_ref.shape
-    n_q = dim // LANES
+def _norm_back(grad, normed, inv, gain):
+    grad = grad * gain
+    return inv * (grad - normed * jnp.mean(grad * normed, axis=-1, keepdims=True))
+
+
+def _hidden_bwd_kernel(w_ref, gain_ref, hid_ref, dy_ref, part_ref, recv_ref, gh_ref, hb_ref, do_ref, mlp_gain_ref):
     step = LANES
-    n_blk = seq // step
-    n_in = raw_ref.shape[1]
-
-    def norm_back(grad, normed, inv, gain):
-        grad = grad * gain
-        return inv * (grad - normed * jnp.mean(grad * normed, axis=-1, keepdims=True))
-
-    def hidden(r, total):
+    mlp_gain_ref[...] = jnp.zeros_like(mlp_gain_ref)
+
+    def hidden(r):
         at = pl.ds(pl.multiple_of(r * step, step), step)
         grad = part_ref[at, :] + recv_ref[at, :]
         h = hid_ref[at, :].astype(F32)
         inv = _rms(h)
         normed = h * inv
-        g = dy_ref[at, :].astype(F32) + norm_back(grad, normed, inv, gain_ref[SUB:9, :])
-        gh[at, :] = g
+        g = dy_ref[at, :].astype(F32) + _norm_back(grad, normed, inv, gain_ref[SUB:9, :])
+        gh_ref[at, :] = g
         g = g.astype(BF16)
-        hb[at, :] = g
-        do[at, :] = mm_nt(g, w_ref[1, :, :dim]).astype(BF16)
-        return total + jnp.sum(grad * normed, axis=0, keepdims=True)
-    mlp_gain = lax.fori_loop(0, n_blk, hidden, jnp.zeros((1, dim), F32))
-
-    low_all, _ = _lanes(seq)
-    _spread(k_ref[...].astype(F32), low_all, kk)
-    _spread(raw_ref[:, n_in - LANES:].astype(F32), low_all, vv)
-    dk[...] = jnp.zeros_like(dk)
-    dv[...] = jnp.zeros_like(dv)
-
-    def raw_back(grad, tile, at, which, low, lead):
-        v = raw_ref[at, tile].astype(F32)
-        inv = lax.rsqrt(_head_mean(v * v, low) + NORM_EPS)
-        normed = v * inv
-        grad = _turn(grad, cos_ref[at, :], -sin_ref[at, :], lead)
-        terms = jnp.sum(grad * normed, axis=0, keepdims=True)
-        grad = grad * qk_gain_ref[SUB * which:SUB * which + 1, :]
-        return inv * (grad - normed * _head_mean(grad * normed, low)), terms
-
-    def heads(t, total):
-        tile = pl.ds(pl.multiple_of(t * LANES, LANES), LANES)
-        low, lead = _lanes(step)
-        for b in range(n_blk):
-            n = (b + 1) * step
-            at = pl.ds(b * step, step)
-            q = q_ref[at, tile]
-            g = do[at, tile]
-            grad_q = None
-            for side in range(PAIR):
-                i = PAIR * ((PAIR * t + side) // 7) + side
-                k = kk[i, :n, :]
-                p = _probs(q, k, b * step)
-                dp = mm_nt(g, vv[i, :n, :])
-                ds = (p * (dp - jnp.sum(dp * p, axis=-1, keepdims=True)) * 0.125).astype(BF16)
-                dv[i, :n, :] = dv[i, :n, :] + mm_tn(p.astype(BF16), g)
-                dk[i, :n, :] = dk[i, :n, :] + mm_tn(ds, q)
-                part = mm(ds, k)
-                grad_q = part if grad_q is None else grad_q + part
-            back, terms = raw_back(grad_q, tile, at, 0, low, lead)
-            dqkv[at, tile] = back.astype(BF16)
-            total = total + terms
-        return total
-    q_gain = lax.fori_loop(0, n_q, heads, jnp.zeros((1, LANES), F32))
-
-    def keys(r, total):
-        at = pl.ds(pl.multiple_of(r * step, step), step)
-        low, lead = _lanes(step)
-
-        def join(ref):
-            return jnp.where(low, ref[0, at, :] + pltpu.roll(ref[1, at, :], 64, 1), ref[3, at, :] + pltpu.roll(ref[PAIR, at, :], 64, 1))
-        back, terms = raw_back(join(dk), pl.ds(dim, LANES), at, 1, low, lead)
-        dqkv[at, dim:dim + LANES] = back.astype(BF16)
-        dqkv[at, dim + LANES:] = join(dv).astype(BF16)
-        return total + terms
-    k_gain = lax.fori_loop(0, n_blk, keys, jnp.zeros((1, LANES), F32))
-
-    def inputs(r, total):
-        at = pl.ds(pl.multiple_of(r * step, step), step)
-        grad = mm_nt(dqkv[at, :], w_ref[0])
-        x = x_ref[at, :].astype(F32)
-        inv = _rms(x)
-        normed = x * inv
-        dx_ref[at, :] = gh[at, :] + norm_back(grad, normed, inv, gain_ref[0:1, :])
-        return total + jnp.sum(grad * normed, axis=0, keepdims=True)
-    attn_gain = lax.fori_loop(0, n_blk, inputs, jnp.zeros((1, dim), F32))
-
-    low, _ = _lanes(SUB)
-    row = lax.broadcasted_iota(jnp.int32, (SUB, dim), 0)
-    both = jnp.where(low, jnp.broadcast_to(q_gain, (SUB, LANES)) + pltpu.roll(jnp.broadcast_to(q_gain, (SUB, LANES)), 64, 1),
-                     jnp.broadcast_to(k_gain, (SUB, LANES)) + pltpu.roll(jnp.broadcast_to(k_gain, (SUB, LANES)), 64, 1))
-    dx_ref[seq:, :] = jnp.where(row == 1, jnp.broadcast_to(attn_gain, (SUB, dim)), jnp.where(row == PAIR, jnp.broadcast_to(mlp_gain, (SUB, dim)), 0.0))
-    dx_ref[seq:, :LANES] = jnp.where(row[:, :LANES] == 0, both, dx_ref[seq:, :LANES])
-
-    def weights(t):
-        tile = pl.ds(pl.multiple_of(t * LANES, LANES), LANES)
-        dw_in_ref[tile, :] = mm_tn(in_ref[:, tile], dqkv[...])
-        dw_out_ref[tile, :] = mm_tn(flat_ref[:, tile], hb[...])
-    loop(n_q, weights)
-
-
-def attn_backward(x, w, gains, cos_t, sin_t, qk_gain, saved, dy, part, recv):
-    seq, dim = x.shape
-    n_in = saved[1].shape[1]
+        hb_ref[at, :] = g
+        do_ref[at, :] = mm_nt(g, w_ref[1, :, :g.shape[1]]).astype(BF16)
+        mlp_gain_ref[...] = mlp_gain_ref[...] + jnp.sum(grad * normed, axis=0, keepdims=True)
+    loop(hid_ref.shape[0] // step, hidden)
+
+
+def hidden_backward(w, gains, hidden, dy, part, recv):
     vmem = pl.BlockSpec(memory_space=pltpu.VMEM)
-    scr = lambda *s: pltpu.VMEM(s[:-1], s[-1])
+    sds = jax.ShapeDtypeStruct
     return pl.pallas_call(
-        _attn_bwd_kernel,
-        out_shape=[jax.ShapeDtypeStruct((seq + SUB, dim), F32), jax.ShapeDtypeStruct((dim, n_in), F32), jax.ShapeDtypeStruct((dim, dim), F32)],
-        in_specs=[vmem] * 15,
-        out_specs=[vmem] * 3,
-        scratch_shapes=[scr(4, seq, LANES, BF16), scr(4, seq, LANES, BF16), scr(4, seq, LANES, F32), scr(4, seq, LANES, F32), scr(seq, dim, F32),
-                        scr(seq, dim, BF16), scr(seq, dim, BF16), scr(seq, n_in, BF16)],
-        compiler_params=pltpu.CompilerParams(vmem_limit_bytes=44 * MIB),
-        cost_estimate=cost(9_000_000_000, 30 * MIB, 4_000_000),
-        name='attn_backward',
-    )(x, w, gains, cos_t, sin_t, qk_gain, *saved[:6], dy, part, recv)
+        _hidden_bwd_kernel,
+        out_shape=[sds(part.shape, F32), sds(part.shape, BF16), sds(part.shape, BF16), sds((SUB, part.shape[1]), F32)],
+        in_specs=[vmem] * 6,
+        out_specs=[vmem] * QUAD,
+        compiler_params=pltpu.CompilerParams(vmem_limit_bytes=24 * MIB),
+        cost_estimate=cost(1_000_000_000, CHIPS * MIB),
+        name='hidden_backward',
+    )(w, gains, hidden, dy, part, recv)
+
+
+class AttnBackward:
+    arrays, inputs, outputs, scratches = PAIR, 15, 1, 11
+    after = (False, False, False, True, True, True, True, True)
+    nbytes = 22 * MIB
+
+    def __init__(self, x, w, gains, mlp_gain, cos_t, sin_t, qk_gain, saved, gh, hb, do):
+        seq, dim = x.shape
+        n_in = w.shape[PAIR]
+        far = (w, gh)
+        self.operands = [(v, all(v is not f for f in far)) for v in (gains, mlp_gain, cos_t, sin_t, qk_gain, x, *far, *saved[:5], hb, do)]
+        self.makes = [jax.ShapeDtypeStruct((dim, n), F32) for n in (n_in, dim)]
+        self.results = [jax.ShapeDtypeStruct((seq + SUB, dim), F32)]
+        scr = lambda *s: pltpu.VMEM(s[:-1], s[-1])
+        self.scratch = [scr(dim, n_in, BF16), scr(QUAD, seq, LANES, BF16), scr(QUAD, seq, LANES, BF16), scr(QUAD, seq, LANES, F32), scr(QUAD, seq, LANES, F32),
+                        scr(seq, n_in, BF16), scr(PAIR, SUB, LANES, F32), scr(PAIR, LANES, n_in, F32), scr(PAIR, LANES, dim, F32),
+                        pltpu.SemaphoreType.DMA((PAIR,)), pltpu.SemaphoreType.DMA((PAIR, PAIR))]
+
+    def run(self, operands, made, results, scratch, between):
+        (gain_ref, mlp_gain_ref, cos_ref, sin_ref, qk_gain_ref, x_ref, w_hbm, gh_hbm, in_ref, raw_ref, q_ref, k_ref, flat_ref, hb, do) = operands
+        w_ref, kk, vv, dk, dv, dqkv, qk_sum, in_out, out_out, in_sem, store_sem = scratch
+        dx_ref, = results
+        seq, dim = x_ref.shape
+        n_q = dim // LANES
+        step = LANES
+        n_blk = seq // step
+        n_in = raw_ref.shape[1]
+        fetch = [pltpu.make_async_copy(gh_hbm, dx_ref.at[pl.ds(0, seq)], in_sem.at[0]), pltpu.make_async_copy(w_hbm.at[0], w_ref, in_sem.at[1])]
+        for copy in fetch:
+            copy.start()
+        low_all, _ = _lanes(seq)
+        _spread(k_ref[...].astype(F32), low_all, kk)
+        _spread(raw_ref[:, n_in - LANES:].astype(F32), low_all, vv)
+        for ref in (dk, dv, qk_sum):
+            ref[...] = jnp.zeros_like(ref)
+
+        def raw_back(grad, tile, at, which, low, lead):
+            v = raw_ref[at, tile].astype(F32)
+            inv = lax.rsqrt(_head_mean(v * v, low) + NORM_EPS)
+            normed = v * inv
+            grad = _turn(grad, cos_ref[at, :], -sin_ref[at, :], lead)
+            qk_sum[which] = qk_sum[which] + jnp.sum(grad * normed, axis=0, keepdims=True)
+            grad = grad * qk_gain_ref[SUB * which:SUB * which + 1, :]
+            return inv * (grad - normed * _head_mean(grad * normed, low))
+
+        def heads(t):
+            tile = pl.ds(pl.multiple_of(t * LANES, LANES), LANES)
+            low, lead = _lanes(step)
+            for b in range(n_blk):
+                n = (b + 1) * step
+                at = pl.ds(b * step, step)
+                q = q_ref[at, tile]
+                g = do[at, tile]
+                grad_q = None
+                for side in range(PAIR):
+                    i = PAIR * ((PAIR * t + side) // 7) + side
+                    k = kk[i, :n, :]
+                    p = _probs(q, k, b * step)
+                    dp = mm_nt(g, vv[i, :n, :])
+                    ds = (p * (dp - jnp.sum(dp * p, axis=-1, keepdims=True)) * 0.125).astype(BF16)
+                    dv[i, :n, :] = dv[i, :n, :] + mm_tn(p.astype(BF16), g)
+                    dk[i, :n, :] = dk[i, :n, :] + mm_tn(ds, q)
+                    part = mm(ds, k)
+                    grad_q = part if grad_q is None else grad_q + part
+                dqkv[at, tile] = raw_back(grad_q, tile, at, 0, low, lead).astype(BF16)
+            for part in range(n_q):
+                between(part, t == part)
+        loop(n_q, heads)
+
+        def keys(r):
+            at = pl.ds(pl.multiple_of(r * step, step), step)
+            low, lead = _lanes(step)
+
+            def join(ref):
+                return jnp.where(low, ref[0, at, :] + pltpu.roll(ref[1, at, :], HEAD, 1), ref[3, at, :] + pltpu.roll(ref[PAIR, at, :], HEAD, 1))
+            dqkv[at, dim:dim + LANES] = raw_back(join(dk), pl.ds(dim, LANES), at, 1, low, lead).astype(BF16)
+            dqkv[at, dim + LANES:] = join(dv).astype(BF16)
+        loop(n_blk, keys)
+        for copy in fetch:
+            copy.wait()
+
+        def inputs(r, total):
+            at = pl.ds(pl.multiple_of(r * step, step), step)
+            grad = mm_nt(dqkv[at, :], w_ref[...])
+            x = x_ref[at, :].astype(F32)
+            inv = _rms(x)
+            normed = x * inv
+            dx_ref[at, :] = dx_ref[at, :] + _norm_back(grad, normed, inv, gain_ref[0:1, :])
+            return total + jnp.sum(grad * normed, axis=0, keepdims=True)
+        attn_gain = lax.fori_loop(0, n_blk, inputs, jnp.zeros((1, dim), F32))
+        between(n_q)
+
+        low, _ = _lanes(SUB)
+        row = lax.broadcasted_iota(jnp.int32, (SUB, dim), 0)
+        fold = lambda v: v + pltpu.roll(v, HEAD, 1)
+        dx_ref[seq:, :] = jnp.where(row == 1, jnp.broadcast_to(attn_gain, (SUB, dim)), jnp.where(row == PAIR, mlp_gain_ref[...], 0.0))
+        dx_ref[seq:, :LANES] = jnp.where(row[:, :LANES] == 0, jnp.where(low, fold(qk_sum[0]), fold(qk_sum[1])), dx_ref[seq:, :LANES])
+
+        def stores(t):
+            return [pltpu.make_async_copy(buf.at[t % PAIR], ref.at[pl.ds(pl.multiple_of(t * LANES, LANES), LANES)], store_sem.at[i, t % PAIR])
+                    for i, (buf, ref) in enumerate(((in_out, made[0]), (out_out, made[1])))]
+
+        def weights(t):
+            @pl.when(t >= PAIR)
+            def _():
+                for copy in stores(t - PAIR):
+                    copy.wait()
+            tile = pl.ds(pl.multiple_of(t * LANES, LANES), LANES)
+            in_out[t % PAIR] = mm_tn(in_ref[:, tile], dqkv[...])
+            out_out[t % PAIR] = mm_tn(flat_ref[:, tile], hb[...])
+            for copy in stores(t):
+                copy.start()
+        loop(n_q, weights)
+        for t in (n_q - PAIR, n_q - 1):
+            for copy in stores(t):
+                copy.wait()
 
 
 def _mlp_kernel(x_ref, dy_ref, wgu_ref, wd_ref, y_mine, y_other, din_mine, din_other, dwg_ref, dwu_ref, dwd_ref, xt, wg, wu, wd, act, dg, du, og, ou, od, load_sem, store_sem):
@@ -864,9 +966,9 @@
     f = lambda *s: pltpu.VMEM(s, F32)
     return pl.pallas_call(
         _mlp_kernel,
-        out_shape=[sds(rows // PAIR, dim)] * 4 + [sds(dim, half), sds(dim, half), sds(half, dim)],
+        out_shape=[sds(rows // PAIR, dim)] * QUAD + [sds(dim, half), sds(dim, half), sds(half, dim)],
         in_specs=[vmem, vmem, hbm, hbm],
-        out_specs=[vmem] * 4 + [hbm] * 3,
+        out_specs=[vmem] * QUAD + [hbm] * 3,
         scratch_shapes=[bf(dim, rows), bf(PAIR, dim, tile), bf(PAIR, dim, tile), bf(PAIR, tile, dim), bf(rows, tile), bf(rows, tile), bf(rows, tile),
                         f(PAIR, dim, tile), f(PAIR, dim, tile), f(PAIR, tile, dim), dma((3, PAIR)), dma((3, PAIR))],
         compiler_params=pltpu.CompilerParams(vmem_limit_bytes=44 * MIB),
@@ -888,8 +990,8 @@
     _codes((961577811093152729088, 751808515438843144256, 1124738970787495025897), 30),
 )
 GRAD_SEQ = (
-    _codes((106232080133048504328, 890654452102748905891, 398002109975241450666, 965054631626560582091, 533961906380267493400, 829000359395158448539, 1143326429365316545848, 31381732460), 75),
-    _codes((166206088102504171520, 704158088118449268010, 595216210114064208288, 531741816507597222992, 520744907820250718441, 1005047906396012195259, 910358688114310724092, 32470101362), 75),
+    _codes((106232080133048504328, 412786621588976116131, 918546169305131799568, 485409126374496736530, 238786845178607580779, 257151255934452689491, 843574817237186309276, 33002831324), 75),
+    _codes((166206088102504171520, 704158088118449268010, 330331505424276671520, 463101567523338654259, 770399732085151419931, 1050366487184744456811, 848110399440616747490, 33002831324), 75),
 )
 
 
@@ -933,7 +1035,7 @@
         mine_attn, other_attn = jnp.where(core == 0, attn_in, attn_out), jnp.where(core == 0, attn_out, attn_in)
         dy = dy_out.reshape(seq_len, model_dim)
         all_tokens, (down_block, recv_gu, recv_attn, dy_other) = all_rows(
-            below(tokens.reshape(-1, LANES), 4), n_dev, [w_down, gate_up(1 - core), other_attn, dy], ('use', 'pair', 'pair', 'pair'), 0)
+            below(tokens.reshape(-1, LANES), QUAD), n_dev, [w_down, gate_up(1 - core), other_attn, dy], ('use', 'pair', 'pair', 'pair'), 0)
         wgu = gather_group(both_cores(gate_up(core), recv_gu))
 
         (attn_w, wd), _ = gather_all([both_cores(mine_attn, recv_attn), down_block], [(0, 0, PAIR * rows_w, 'core'), (1, 0, down_block.shape[0], 'chip')],
@@ -973,18 +1075,18 @@
         grad_recv = swap(grad_other)
         layer_out = (hidden.astype(F32) + (y_mine + swap(y_other))).astype(BF16)
 
-        dx_block, grad_w_in, grad_w_out = attn_backward(x_emb, attn_w, gains, cos_t, sin_t, qk_gain, saved, dy, grad_in, grad_recv)
-
-        by_chip = [u.reshape(n_chip, -1, u.shape[1]) for u in (grad_w_down, grad_w_gate, grad_w_up, grad_w_in, grad_w_out)]
-        down_rows, gate_shard, up_shard, in_shard, out_shard = scatter_sum(
-            by_chip, [(i, 0, u.shape[1], 'chip') for i, u in enumerate(by_chip[:3])] + [(i, 0, 32, 'rows') for i in (3, 4)], ('bza', 'zba', 'zba', 'baz', 'baz'), GRAD_SEQ, 3)
+        gh, hb, grad_heads, mlp_gain = hidden_backward(attn_w, gains, hidden, dy, grad_in, grad_recv)
+        by_chip = [u.reshape(n_chip, -1, u.shape[1]) for u in (grad_w_down, grad_w_gate, grad_w_up)]
+        down_rows, gate_shard, up_shard, in_shard, out_shard, _, _, dx_block = scatter_sum(
+            by_chip, [(i, 0, u.shape[1], 'chip') for i, u in enumerate(by_chip)] + [(i, 0, 32, 'rows') for i in (3, QUAD)], ('bza', 'zba', 'bza', 'zba', 'zba'), GRAD_SEQ, 3,
+            AttnBackward(x_emb, attn_w, gains, mlp_gain, cos_t, sin_t, qk_gain, saved, gh, hb, grad_heads))
 
         chip_rows = jnp.concatenate([gate_shard, up_shard], axis=1)
         mine = lax.dynamic_slice(chip_rows, (core * rows_w, 0), (rows_w, chip_rows.shape[1]))
         give = lax.dynamic_slice(chip_rows, ((1 - core) * rows_w, 0), (rows_w, chip_rows.shape[1]))
         (all_dx,), (down_shard, recv) = gather_all(
             [to_lines(dx_block)], [(0, 0, 200 * lines, 'device'), (0, 200 * lines, 200 * lines, 'device'), (0, 400 * lines, 120 * lines, 'device')],
-            ('zba', 'zba', 'baz'), ROWS_SEQ, [down_rows, give], ('store', 'pair'), n_dev, 4)
+            ('zba', 'zba', 'baz'), ROWS_SEQ, [down_rows, give], ('store', 'pair'), n_dev, QUAD)
         d_table = from_lines(add_rows(all_dx, counts, codes, rows_local), model_dim)
         gains_grad = from_lines(jnp.sum(all_dx[:, seq_len * lines:], axis=0), model_dim)
         qk = gains_grad[0]

time: 919 us -> 884 us (0.962)
  Pallas kernels: 844 us -> 807 us
    pallas_call x2, Pallas kernels: 109 us -> 65.7 us  [the longest x1 61 us: mlp(): pl.pallas_call(_mlp_kernel, out_shape=[sds(rows // PAIR, dim)] * QUAD + [...]
    unnamed x73 -> x91, local copies, waits for them, and re-layouts: 28.5 us -> 26.4 us
  transfers between devices with their start and end apart: 4 -> 4, of which waited for: 2 -> 2; matrix products, arithmetic and copies ran while one was open for 2% -> 2% of each run, Pallas kernels for 83% -> 82%
where the time goes in v8:
time: 884 us; the launch traced here: 883 us
  Pallas kernels  807 us (91%)
  local copies, waits for them, and re-layouts  35.1 us (4%)
  other arithmetic  21.8 us (2%)
  between operations  14.6 us (2%)
    pallas_call x2, Pallas kernels, scatter_sum(): pl.pallas_call(functools.partial(_scatter_kernel, tuple(pieces), orders,...  329 us
    pallas_call x2, Pallas kernels, gather_all(): pl.pallas_call(functools.partial(_gather_kernel, tuple(pieces), orders, s...  297 us
    pallas_call x1, Pallas kernels, mlp(): pl.pallas_call(_mlp_kernel, out_shape=[sds(rows // PAIR, dim)] * QUAD + [...  61 us
    pallas_call x1, Pallas kernels, lookup(): pl.pallas_call(_lookup_kernel, grid_spec=pltpu.PrefetchScalarGridSpec(num...  39.8 us
    pallas_call x1, Pallas kernels, add_rows(): pl.pallas_call(_add_rows_kernel, grid_spec=pltpu.PrefetchScalarGridSpec(n...  36.4 us
    unnamed x91, local copies, waits for them, and re-layouts  26.4 us
    pallas_call x1, Pallas kernels, attn_forward(): pl.pallas_call(_attn_fwd_kernel, out_shape=[sds(dim), sds(n_in), sds(dim)...  19.9 us
    pallas_call x1, Pallas kernels, all_rows(): pl.pallas_call(functools.partial(_all_rows_kernel, n_dev, moves), out_sha...  18.4 us
  transfers between devices with their start and end apart: 4, of which 2 were waited for; matrix products, arithmetic and copies ran while one was open for 2% of the time, Pallas kernels for 82%

profile of v8, /device:TPU:0, one launch (start us, length us, event | category | flops | bytes accessed | tf_op | source)
XLA Modules:
  0.0 882.7 jit_solution(6534678582835250041)
XLA Ops:
  7.2 1.3 pad.12.refs_0_
  8.5 0.7 pad_maximum_fusion.6
  9.2 0.1 copy.33
  9.3 0.8 constant_dynamic-update-slice_fusion.2
  10.2 0.7 constant_dynamic-update-slice_fusion.1
  10.9 0.7 constant_dynamic-update-slice_fusion
  11.6 1.2 constant_dynamic-slice_fusion.3
  12.8 0.7 pad_maximum_fusion.4.refs_2_
  13.5 0.7 broadcast_select_fusion
  14.2 18.4 %all_rows.1 = (s32[32,8,128]{2,1,0:T(8,128)}, bf16[152,896]{1,0:T(8,128)(2,1)}, bf16[28,4864]{1,0:T(8,128)(2,1)}, bf16[28,1152]{1,0:T(8,128)(2,1)}, bf16[512,896]{1,0:T(8,128)(2,1)}) custom-call(s32[8,128]{1,0:T(8,128)} %pad.12.refs_0_, bf16[152,896]{1,0:T(8,128)(2,1)} %refs_1_.1, bf16[28,4864]{1,0:T(8,128)(2,1)} %pad_maximum_fusion.4.refs_2_, ...), custom_call_target="tpu_custom_call" | custom-call | flops 10000000 | bytes 1048576 | tf_op jit(solution)/shard_map/all_rows/pallas_call | solution.py:191
  32.6 2.1 maximum_select_fusion
  34.8 0.1 stack_tile.6
  34.9 0.1 stack_tile.7
  35.0 1.6 convert_reduce_fusion
  36.5 0.2 fusion.1
  36.8 5.9 select_reduce_fusion
  42.9 79.9 %gather_all.2 = (bf16[32,56,1152]{2,1,0:T(8,128)(2,1)S(1)}, bf16[16,152,896]{2,1,0:T(8,128)(2,1)S(1)}) custom-call(bf16[56,1152]{1,0:T(8,128)(2,1)S(1)} %maximum_select_fusion.1.refs_0_, bf16[152,896]{1,0:T(8,128)(2,1)S(1)} %copy-done.33), custom_call_target="tpu_custom_call" | custom-call | flops 200000000 | bytes 25690112 | tf_op jit(solution)/shard_map/gather_all/pallas_call | solution.py:276
  122.9 2.0 copy-done.34
  125.0 2.0 copy-done
  127.0 0.2 copy.34
  127.2 3.4 copy-done.3
  130.7 39.8 %lookup.1.refs_0_ = bf16[32,512,896]{2,1,0:T(8,128)(2,1)} custom-call(s32[32]{0:T(128)S(1)} %get-tuple-element.84.counts, s32[16384]{0:T(1024)S(1)} %bitcast.69, bf16[4752,896]{1,0:T(8,128)(2,1)S(1)} %copy-done.3), custom_call_target="tpu_custom_call" | custom-call | flops 50000000 | bytes 41943040 | tf_op jit(solution)/shard_map/lookup/pallas_call | solution.py:529
  170.5 107.9 %scatter_sum.2.x_ref.refs_8_ = bf16[512,896]{1,0:T(8,128)(2,1)S(1)} custom-call(bf16[32,512,896]{2,1,0:T(8,128)(2,1)} %lookup.1.refs_0_), custom_call_target="tpu_custom_call" | custom-call | flops 200000000 | bytes 133267456 | tf_op jit(solution)/shard_map/scatter_sum/pallas_call | solution.py:478
  278.4 1.0 multiply_sine_fusion
  279.4 19.9 %attn_forward.1 = (bf16[512,896]{1,0:T(8,128)(2,1)S(1)}, bf16[512,1152]{1,0:T(8,128)(2,1)S(1)}, bf16[512,896]{1,0:T(8,128)(2,1)S(1)}, bf16[512,128]{1,0:T(8,128)...) custom-call(bf16[512,896]{1,0:T(8,128)(2,1)S(1)} %scatter_sum.2.x_ref.refs_8_, ...), custom_call_target="tpu_custom_call" | custom-call | flops 4000000000 | bytes 12582912 | tf_op jit(solution)/shard_map/attn_forward/pallas_call | solution.py:720
  299.4 0.9 copy-done.19
  300.3 0.9 copy-done.20
  301.4 1.6 pad_maximum_fusion.1.dy_ref
  302.9 0.3 copy-done.18
  303.2 0.6 collective-permute-done
  303.8 1.4 pad_maximum_fusion.x_ref
  305.2 1.5 copy-done.9
  306.7 61.0 %mlp.1 = (f32[512,896]{1,0:T(8,128)S(1)}, f32[512,896]{1,0:T(8,128)S(1)}, f32[512,896]{1,0:T(8,128)S(1)}, f32[512,896]{1,0:T(8,128)}, f32[896,2432]{1,0:T(8,128)...) custom-call(bf16[1024,896]{1,0:T(8,128)(2,1)S(1)} %copy-done.9, bf16[1024,896]{1,0:T(8,128)(2,1)} %pad_maximum_fusion.1.dy_ref, ...), custom_call_target="tpu_custom_call" | custom-call | flops 35701915648 | bytes 52428800 | tf_op jit(solution)/shard_map/mlp/pallas_call | solution.py:967
  367.7 1.2 copy-done.10
  368.9 1.2 copy-done.12
  370.2 1.3 copy-done.32
  371.4 0.1 collective-permute-start.2
  371.6 0.4 collective-permute-start.1
  371.9 3.2 collective-permute-done.2.recv_ref
  375.2 2.2 copy-done.2
  377.3 1.5 copy-done.13
  378.8 4.7 hidden_backward.1
  383.6 1.2 copy-done.14
  384.8 1.0 copy-done.21
  385.8 0.9 copy-done.22
  386.7 0.6 copy-done.29
  387.3 221.5 %scatter_sum.3 = (f32[152,896]{1,0:T(8,128)}, f32[56,2432]{1,0:T(8,128)}, f32[56,2432]{1,0:T(8,128)}, f32[32,1152]{1,0:T(8,128)}, f32[32,896]{1,0:T(8,128)}, /*i...) custom-call(f32[16,152,896]{2,1,0:T(8,128)} %bitcast.75, f32[16,56,2432]{2,1,0:T(8,128)} %bitcast.73, ...), custom_call_target="tpu_custom_call" | custom-call | flops 200000000 | bytes 184483840 | tf_op jit(solution)/shard_map/scatter_sum/pallas_call | solution.py:478
  608.8 1.2 constant_dynamic-update-slice_fusion.4
  610.1 1.1 constant_dynamic-update-slice_fusion.3
  611.3 217.1 %gather_all.3 = (f32[32,3640,128]{2,1,0:T(8,128)}, f32[152,896]{1,0:T(8,128)S(1)}, f32[28,4864]{1,0:T(8,128)S(1)}) custom-call(f32[3640,128]{1,0:T(8,128)S(1)} %bitcast.68, f32[152,896]{1,0:T(8,128)S(1)} %copy-done.26, f32[28,4864]{1,0:T(8,128)S(1)} %constant_dynamic-slice_fusion.2.refs_2_), custom_call_target="tpu_custom_call" | custom-call | flops 200000000 | bytes 119275520 | tf_op jit(solution)/shard_map/gather_all/pallas_call | solution.py:276
  828.3 1.3 slice_reduce_fusion
  829.6 36.4 %add_rows.1 = f32[33264,128]{1,0:T(8,128)} custom-call(s32[32]{0:T(128)S(1)} %copy-done.31, s32[16384]{0:T(1024)S(1)} %bitcast.70, f32[32,3640,128]{2,1,0:T(8,128)} %get-tuple-element.76.dx_ref), custom_call_target="tpu_custom_call" | custom-call | flops 50000000 | bytes 83886080 | tf_op jit(solution)/shard_map/add_rows/pallas_call | solution.py:599
  866.1 0.7 constant_dynamic-slice_fusion
  866.7 0.7 constant_dynamic-slice_fusion.1
  867.4 0.1 dynamic-slice_select_fusion.1
  867.6 0.6 dynamic_slice.38
  868.2 0.6 dynamic_slice.35
  868.8 0.6 fusion.32
  869.4 0.7 fusion.31
  870.1 0.9 pad_maximum_fusion.3
  871.0 0.9 pad_maximum_fusion.2
  871.8 0.4 copy-done.11
  872.3 2.8 fusion.2
  875.0 0.8 copy.49
  (93 shorter events, 0.9 us)
Async XLA Ops:
  7.2 6.3 copy-start.39
  7.2 298.0 %all-gather.2.cloned.1.call-start = ((), (), s32[]{:S(2)}) async-start(), calls=%async_computation | async-start | bytes 9261056 | tf_op jit(solution)/shard_map/all_gather | solution.py:1014
  13.5 21.2 %copy-start.41 = (bf16[64]{0:T(256)(128)(2,1)S(1)}, bf16[64]{0:T(256)(128)(2,1)}, u32[]{:S(2)}) copy-start(bf16[64]{0:T(256)(128)(2,1)} %param.22) | copy-start | bytes 388
  13.5 21.3 %copy-start.42 = (bf16[64]{0:T(256)(128)(2,1)S(1)}, bf16[64]{0:T(256)(128)(2,1)}, u32[]{:S(2)}) copy-start(bf16[64]{0:T(256)(128)(2,1)} %param.23) | copy-start | bytes 388
  13.5 21.4 %copy-start.40 = (s32[1,512]{1,0:T(1,128)S(1)}, s32[1,512]{1,0:T(1,128)}, u32[]{:S(2)}) copy-start(s32[1,512]{1,0:T(1,128)} %param.16) | copy-start | bytes 6148
  32.6 10.3 %copy-start.38 = (bf16[28,1152]{1,0:T(8,128)(2,1)S(1)}, bf16[28,1152]{1,0:T(8,128)(2,1)}, u32[]{:S(2)}) copy-start(bf16[28,1152]{1,0:T(8,128)(2,1)} %get-tuple-element.48) | copy-start | bytes 193540
  32.6 10.4 %copy-start.33 = (bf16[152,896]{1,0:T(8,128)(2,1)S(1)}, bf16[152,896]{1,0:T(8,128)(2,1)}, u32[]{:S(2)}) copy-start(bf16[152,896]{1,0:T(8,128)(2,1)} %get-tuple-element.49.refs_1_) | copy-start | bytes 817156
  36.5 133.9 %copy-start.30 = (s32[32]{0:T(128)}, s32[32]{0:T(128)S(1)}, u32[]{:S(2)}) copy-start(s32[32]{0:T(128)S(1)} %get-tuple-element.84.counts) | copy-start | bytes 388
  42.9 127.6 %copy-start.24 = (s32[4,4,8,128]{3,1,2,0:T(4,128)}, s32[4,4,8,128]{3,1,2,0:T(4,128)S(1)}, u32[]{:S(2)}) copy-start(s32[4,4,8,128]{3,1,2,0:T(4,128)S(1)} %copy.36) | copy-start | bytes 196612
  122.9 2.0 copy-start.34
  125.0 2.0 copy-start
  127.2 248.0 %copy-start.23 = (f32[24,896]{1,0:T(8,128)}, f32[24,896]{1,0:T(8,128)S(1)}, u32[]{:S(2)}) copy-start(f32[24,896]{1,0:T(8,128)S(1)} %pad.14.gain_ref.refs_3_) | copy-start | bytes 258052
  127.2 3.5 copy-start.3
  170.4 108.9 %copy-start.1 = (bf16[32,56,1152]{2,1,0:T(8,128)(2,1)S(1)}, bf16[32,56,1152]{2,1,0:T(8,128)(2,1)}, u32[]{:S(2)}) copy-start(bf16[32,56,1152]{2,1,0:T(8,128)(2,1)} %copy-done) | copy-start | bytes 12386308
  278.3 21.0 %copy-start.7 = (bf16[512,896]{1,0:T(8,128)(2,1)}, bf16[512,896]{1,0:T(8,128)(2,1)S(1)}, u32[]{:S(2)}) copy-start(bf16[512,896]{1,0:T(8,128)(2,1)S(1)} %scatter_sum.2.x_ref.refs_8_) | copy-start | bytes 2752516
  278.4 21.0 %copy-start.28 = (f32[16,128]{1,0:T(8,128)}, f32[16,128]{1,0:T(8,128)S(1)}, u32[]{:S(2)}) copy-start(f32[16,128]{1,0:T(8,128)S(1)} %broadcast_bitcast_fusion.1.qk_gain_ref.refs_7_) | copy-start | bytes 24580
  279.4 20.0 %copy-start.16 = (f32[512,128]{1,0:T(8,128)}, f32[512,128]{1,0:T(8,128)S(1)}, u32[]{:S(2)}) copy-start(f32[512,128]{1,0:T(8,128)S(1)} %get-tuple-element.102.sin_ref.refs_6_) | copy-start | bytes 786436
  279.4 20.0 %copy-start.17 = (f32[512,128]{1,0:T(8,128)}, f32[512,128]{1,0:T(8,128)S(1)}, u32[]{:S(2)}) copy-start(f32[512,128]{1,0:T(8,128)S(1)} %get-tuple-element.103.cos_ref.refs_5_) | copy-start | bytes 786436
  279.4 21.9 %copy-start.4 = (bf16[1,512,896]{2,1,0:T(8,128)(2,1)S(1)}, bf16[1,512,896]{2,1,0:T(8,128)(2,1)}, u32[]{:S(2)}) copy-start(bf16[1,512,896]{2,1,0:T(8,128)(2,1)} %param.29) | copy-start | bytes 2752516
  279.4 21.9 %copy-start.35 = (bf16[512,896]{1,0:T(8,128)(2,1)S(1)}, bf16[512,896]{1,0:T(8,128)(2,1)}, u32[]{:S(2)}) copy-start(bf16[512,896]{1,0:T(8,128)(2,1)} %get-tuple-element.53) | copy-start | bytes 2752516
  299.4 0.9 copy-start.19
  300.3 0.9 copy-start.20
  301.3 1.7 copy-start.15
  301.3 1.9 copy-start.18
  301.3 2.0 copy-start.27
  301.3 73.9 %copy-start.5 = (bf16[512,896]{1,0:T(8,128)(2,1)}, bf16[512,896]{1,0:T(8,128)(2,1)S(1)}, u32[]{:S(2)}) copy-start(bf16[512,896]{1,0:T(8,128)(2,1)S(1)} %get-tuple-element.51.hid_ref) | copy-start | bytes 2752516
  301.3 2.5 collective-permute-start
  305.2 1.5 copy-start.9
  367.7 1.2 copy-start.10
  368.9 1.2 copy-start.12
  370.2 1.3 copy-start.32
  371.4 3.7 collective-permute-start.2
  371.6 500.3 %collective-permute-start.1 = (f32[512,896]{1,0:T(8,128)}, f32[512,896]{1,0:T(8,128)}, u32[]{:S(2)}, u32[]{:S(2)}) collective-permute-start(f32[512,896]{1,0:T(8,128)} %copy-done.32), channel_id=1, source_target_pairs={{0,1},{1,0},{2,3},{3,2},{4,5},{5,4},{6,7},{7,6},{8,9},{9,8},{10,11... | collective-permute-start | bytes 5505032 | tf_op jit(solution)/shard_map/ppermute | solution.py:1011
  375.2 2.2 copy-start.2
  377.3 1.5 copy-start.13
  383.5 1.2 copy-start.14
  384.8 1.0 copy-start.21
  385.8 0.9 copy-start.22
  386.7 0.6 copy-start.29
  608.8 2.4 copy-start.8
  608.8 2.4 copy-start.26
  611.3 218.3 %copy-start.25 = (s32[4,4,8,128]{3,1,2,0:T(4,128)S(1)}, s32[4,4,8,128]{3,1,2,0:T(4,128)}, u32[]{:S(2)}) copy-start(s32[4,4,8,128]{3,1,2,0:T(4,128)} %copy-done.24) | copy-start | bytes 196612
  611.3 218.3 %copy-start.31 = (s32[32]{0:T(128)S(1)}, s32[32]{0:T(128)}, u32[]{:S(2)}) copy-start(s32[32]{0:T(128)} %copy-done.30) | copy-start | bytes 388
  829.6 36.5 %copy-start.36 = (f32[32,1152]{1,0:T(8,128)S(1)}, f32[32,1152]{1,0:T(8,128)}, u32[]{:S(2)}) copy-start(f32[32,1152]{1,0:T(8,128)} %get-tuple-element.77) | copy-start | bytes 442372
  829.6 37.1 %copy-start.37 = (f32[32,896]{1,0:T(8,128)S(1)}, f32[32,896]{1,0:T(8,128)}, u32[]{:S(2)}) copy-start(f32[32,896]{1,0:T(8,128)} %get-tuple-element.78) | copy-start | bytes 344068
  870.1 1.8 copy-start.6
  870.1 2.2 copy-start.11
Sparse Core Ops, SparseCore 0:
  34.9 136.6 all-gather.1

commit v9 on v8

--- a/solution.py
+++ b/solution.py
@@ -14,6 +14,7 @@
 BF16 = jnp.bfloat16
 MESH = pl.DeviceIdType.MESH
 LANES, HEAD, CHIPS, SUB, QUAD, PAIR, MIB = 128, 64, 16, 8, 4, 2, 1 << 20
+KIND = PIECE = 3
 
 
 def mm(a, b):
@@ -59,7 +60,7 @@
 
 
 def _onward(u, key, orders):
-    order = orders[key[3]]
+    order = orders[key[PIECE]]
     via = _via(u, key, orders)
     left = order if via is None else order[order.index(via[0]) + 1:]
     out = []
@@ -201,13 +202,17 @@
     return res[0], res[1:]
 
 
-def _gather_kernel(pieces, orders, seq, moves, n_arr, *refs):
+def _gather_kernel(pieces, orders, seq, moves, n_arr, work, *refs):
     n, m = len(moves), len(pieces)
-    ins, src, outs, dst = refs[:n_arr], refs[n_arr:n_arr + n], refs[n_arr + n:PAIR * n_arr + n], refs[PAIR * n_arr + n:PAIR * n_arr + PAIR * n]
-    own_sem, send_sem, recv_sem, p_send, p_recv, m_send, m_recv = refs[PAIR * n_arr + PAIR * n:]
+    refs_left = list(refs)
+    cut = lambda count: [refs_left.pop(0) for _ in range(count)]
+    ins, src, work_in = cut(n_arr), cut(n), cut(PAIR if work else 0)
+    outs, dst, work_out = cut(n_arr), cut(n), cut(1 if work else 0)
+    own_sem, send_sem, recv_sem, p_send, p_recv, m_send, m_recv = cut(7)
     me = lax.axis_index(AXIS_NAME)
     at = _Place(me)
     ends = list(_passes(moves, me))
+    kinds = {p[0]: p[KIND] for p in pieces}
 
     def slot_of(kc, core, kind):
         return {'device': PAIR * kc + core, 'core': CHIPS * core + kc, 'chip': kc}[kind]
@@ -217,74 +222,170 @@
         slot = slot_of(kc, core, kind)
         return outs[arr].at[slot] if rows == outs[arr].shape[1] else outs[arr].at[slot, pl.ds(r0, rows)]
 
-    def run(u):
-        sides = ['a', 'b', 'z+'] + (['z-'] if u else [])
-        far = [end for kind, end in zip(moves, ends) if kind != 'pair']
-        _meet([at.side(s) for s in sides] + [at.partner], me, far[0] if far else ())
-        started, moving = [], []
-
-        def send(src_ref, dst_ref, s_sem, r_sem, dev):
-            copy = _remote(src_ref, dst_ref, s_sem, r_sem, dev)
-            copy.start()
-            started.append(copy)
-
-        count, handed = 0, [0] * m
-        for key in [(0, 0, u, i) for i in range(m)] + [_unpack(c) for c in seq[u]]:
-            piece = key[3]
+    def own(i):
+        return pltpu.make_async_copy(ins[i], outs[i].at[slot_of(me // PAIR, at.core, kinds[i])], own_sem.at[i])
+
+    class Node:
+        def __init__(self, u):
+            self.u, self.sent, self.handed = u, [], [0] * m
+            self.keys = [_unpack(c) for c in seq[u]]
+
+        def step(self, key):
+            piece = key[PIECE]
             arr, r0, rows, kind = pieces[piece]
             kc = at.chip(key)
             place = part(kc, at.core, piece)
-            if _via(u, key, orders) is None:
+            if _via(self.u, key, orders) is None:
                 ref = ins[arr] if rows == ins[arr].shape[0] else ins[arr].at[pl.ds(r0, rows)]
             else:
                 ref = place
                 _landed(ref, recv_sem.at[piece, kc])
-            for side in _onward(u, key, orders):
-                send(ref, place, send_sem.at[count], recv_sem.at[piece, kc], at.side(side))
-                count += 1
+            for side in _onward(self.u, key, orders):
+                _remote(ref, place, send_sem.at[len(self.sent)], recv_sem.at[piece, kc], at.side(side)).start()
+                self.sent.append(piece)
             if kind != 'chip':
-                send(ref, place, p_send.at[piece, handed[piece]], p_recv.at[piece, kc], at.partner)
-                handed[piece] += 1
-            if key == (0, 0, u, m - 1):
-                for i, (to, _) in enumerate(ends):
-                    moving.append(_start_move(moves[i], src[i], dst[i], m_send.at[i], m_recv.at[i], to, me))
-                own = [pltpu.make_async_copy(ins[i], outs[i].at[slot_of(me // PAIR, at.core, kinds[i])], own_sem.at[i]) for i in range(n_arr)]
-                for copy in own:
-                    copy.start()
+                _remote(ref, place, p_send.at[piece, self.handed[piece]], p_recv.at[piece, kc], at.partner).start()
+                self.handed[piece] += 1
+
+    nodes = [Node(u) for u in (0, 1)]
+
+    def each(do):
+        for node in nodes:
+            pl.when(at.u == node.u)(functools.partial(do, node))
+
+    def begin(node):
+        far = [end for kind, end in zip(moves, ends) if kind != 'pair']
+        _meet([at.side(s) for s in ['a', 'b', 'z+'] + (['z-'] if node.u else [])] + [at.partner], me, far[0] if far else ())
         for piece in range(m):
-            if pieces[piece][3] != 'chip':
+            node.step((0, 0, node.u, piece))
+
+    def between(part, parts, when=None):
+        def steps(node):
+            count = len(node.keys)
+            for key in node.keys[part * count // parts:(part + 1) * count // parts]:
+                node.step(key)
+        if when is None:
+            each(steps)
+        else:
+            pl.when(when)(lambda: each(steps))
+
+    def end(node):
+        def sent(piece, sem):
+            ref = part(0, 0, piece)
+            _remote(ref, ref, sem, sem, at.partner).wait_send()
+        for piece in range(m):
+            if pieces[piece][KIND] != 'chip':
                 for kc in range(CHIPS):
                     _landed(part(kc, 1 - at.core, piece), p_recv.at[piece, kc])
-        for i, (to, _) in enumerate(ends):
-            _end_move(moves[i], moving[i], dst[i], m_recv.at[i], to, me)
-        for copy in own:
-            copy.wait()
-        for copy in started:
-            copy.wait_send()
-
-    kinds = {p[0]: p[3] for p in pieces}
-    for u in (0, 1):
-        pl.when(at.u == u)(functools.partial(run, u))
-
-
-def gather_all(blocks, pieces, orders, seq, moved, moves, n_dev, collective_id):
+            for i in range(node.handed[piece]):
+                sent(piece, p_send.at[piece, i])
+        for i, piece in enumerate(node.sent):
+            sent(piece, send_sem.at[i])
+    each(begin)
+    for i, (to, _) in enumerate(ends):
+        _start_move(moves[i], src[i], dst[i], m_send.at[i], m_recv.at[i], to, me)
+    for i in range(n_arr):
+        own(i).start()
+    if work:
+        work(work_in, work_out, refs_left, between)
+    else:
+        between(0, 1)
+    each(end)
+    for i, (to, _) in enumerate(ends):
+        _end_move(moves[i], _remote(src[i], dst[i], m_send.at[i], m_recv.at[i], to), dst[i], m_recv.at[i], to, me)
+    for i in range(n_arr):
+        own(i).wait()
+
+
+def gather_all(blocks, pieces, orders, seq, moved, moves, n_dev, collective_id, found=None):
     n, m, n_arr = len(moves), len(pieces), len(blocks)
     dma = pltpu.SemaphoreType.DMA
     vmem, hbm = pl.BlockSpec(memory_space=pltpu.VMEM), pl.BlockSpec(memory_space=pl.ANY)
     nbytes = sum(v.size * v.dtype.itemsize for v in blocks)
-    kinds = {p[0]: p[3] for p in pieces}
+    kinds = {p[0]: p[KIND] for p in pieces}
+    scratch = [dma((n_arr,)), dma((24 * m,)), dma((m, CHIPS)), dma((m, CHIPS)), dma((m, CHIPS)), dma((max(n, 1),)), dma((max(n, 1),))]
+    outs = [jax.ShapeDtypeStruct((n_dev // PAIR if kinds[i] == 'chip' else n_dev,) + v.shape, v.dtype) for i, v in enumerate(blocks)]
+    outs += [jax.ShapeDtypeStruct(v.shape, v.dtype) for v in moved]
+    extra, near = [], []
+    if found is not None:
+        codes, table, seq_len = found
+        n_rows, dim = table.shape
+        extra, near = [codes, table], [pl.BlockSpec(memory_space=pltpu.SMEM), hbm]
+        outs.append(jax.ShapeDtypeStruct((codes.size // seq_len, seq_len, dim), table.dtype))
+        scratch += [pltpu.VMEM((PAIR, _chunk(n_rows), dim), BF16), pltpu.VMEM(((n_rows + SUB) * dim // LANES, LANES), F32), pltpu.VMEM((seq_len * dim // LANES, LANES), F32),
+                    pltpu.VMEM((PAIR, seq_len, dim), BF16), dma((PAIR,)), dma((PAIR,))]
+        nbytes += 26 * MIB
     res = pl.pallas_call(
-        functools.partial(_gather_kernel, tuple(pieces), orders, seq, moves, n_arr),
-        out_shape=[jax.ShapeDtypeStruct((n_dev // PAIR if kinds[i] == 'chip' else n_dev,) + v.shape, v.dtype) for i, v in enumerate(blocks)] + [
-            jax.ShapeDtypeStruct(v.shape, v.dtype) for v in moved],
-        in_specs=[vmem] * n_arr + [hbm] * n,
-        out_specs=[hbm] * (n_arr + n),
-        scratch_shapes=[dma((n_arr,)), dma((24 * m,)), dma((m, CHIPS)), dma((m, CHIPS)), dma((m, CHIPS)), dma((max(n, 1),)), dma((max(n, 1),))],
+        functools.partial(_gather_kernel, tuple(pieces), orders, seq, moves, n_arr, _pick if found is not None else None),
+        out_shape=outs,
+        in_specs=[vmem] * n_arr + [hbm] * n + near,
+        out_specs=[hbm] * len(outs),
+        scratch_shapes=scratch,
         compiler_params=pltpu.CompilerParams(collective_id=collective_id, has_side_effects=True, vmem_limit_bytes=nbytes + (SUB * MIB)),
         cost_estimate=cost(200_000_000, nbytes * HEAD),
         name='gather_all',
-    )(*blocks, *moved)
+    )(*blocks, *moved, *extra)
     return res[:n_arr], res[n_arr:]
+
+
+def _chunk(n_rows):
+    return n_rows // 9 if n_rows % 144 == 0 else n_rows
+
+
+def _pick(operands, results, scratch, between):
+    codes, table = operands
+    picked, = results
+    chunk, rows, block, out, load_sem, store_sem = scratch
+    n_src, seq, dim = picked.shape
+    n_col = dim // LANES
+    size = chunk.shape[1]
+    n_chunk = table.shape[0] // size
+
+    def load(i):
+        return pltpu.make_async_copy(table.at[pl.ds(pl.multiple_of(i * size, SUB), size)], chunk.at[i % PAIR], load_sem.at[i % PAIR])
+    load(jnp.int32(0)).start()
+
+    def widen(c):
+        pl.when(c + 1 < n_chunk)(lambda: load(c + 1).start())
+        load(c).wait()
+
+        def part(i):
+            line = (c * size + i * CHIPS) * n_col
+            for j in range(n_col):
+                v = chunk[c % PAIR, pl.ds(pl.multiple_of(i * CHIPS, CHIPS), CHIPS), j * LANES:(j + 1) * LANES].astype(F32)
+                rows[pl.ds(pl.multiple_of(line + j * SUB, SUB), SUB), :] = v[:SUB]
+                rows[pl.ds(pl.multiple_of(line + (n_col + j) * SUB, SUB), SUB), :] = v[SUB:]
+        loop(size // CHIPS, part)
+    loop(n_chunk, widen)
+    rows[table.shape[0] * n_col:, :] = jnp.zeros((SUB * n_col, LANES), F32)
+
+    def store(b):
+        return pltpu.make_async_copy(out.at[b % PAIR], picked.at[b], store_sem.at[b % PAIR])
+
+    def source(b):
+        def eight(i):
+            for t in range(SUB):
+                block[pl.ds(i * (SUB * n_col) + t, n_col, stride=SUB), :] = rows[pl.ds(codes[b * seq + i * SUB + t], n_col, stride=SUB), :]
+        loop(seq // SUB, eight)
+        pl.when(b >= PAIR)(lambda: store(b - PAIR).wait())
+
+        def narrow(i):
+            line = pl.multiple_of(i * (CHIPS * n_col), SUB)
+            for j in range(n_col):
+                v = jnp.concatenate([block[pl.ds(line + j * SUB, SUB), :], block[pl.ds(line + (n_col + j) * SUB, SUB), :]], axis=0)
+                out[b % PAIR, pl.ds(pl.multiple_of(i * CHIPS, CHIPS), CHIPS), j * LANES:(j + 1) * LANES] = v.astype(BF16)
+        loop(seq // CHIPS, narrow)
+        store(b).start()
+
+    parts = n_src // PAIR
+
+    def some(t):
+        loop(PAIR, lambda i: source(PAIR * t + i))
+        for part in range(parts):
+            between(part, parts, t == part)
+    loop(parts, some)
+    for b in (n_src - PAIR, n_src - 1):
+        store(jnp.int32(b)).wait()
 
 
 def _slots(pieces, orders, seq):
@@ -293,8 +394,8 @@
         used = [0] * len(pieces)
         for key in [_unpack(c) for c in reversed(seq[u])] + [(0, 0, u, i) for i in range(len(pieces))]:
             for side in _onward(u, key, orders):
-                table[u, key, side] = used[key[3]]
-                used[key[3]] += 1
+                table[u, key, side] = used[key[PIECE]]
+                used[key[PIECE]] += 1
         most = [max(a, b) for a, b in zip(most, used)]
     return table, most
 
@@ -304,7 +405,7 @@
     roots = [(0, 0, u, i) for i in range(n)]
     if not n_late:
         return keys + roots, [], []
-    late = [key for key in keys if key[3] >= n - n_late]
+    late = [key for key in keys if key[PIECE] >= n - n_late]
     rest = [key for key in keys if key not in late]
     first = [key for key in rest if not _onward(u, key, orders)][:lead]
     rest = [key for key in rest if key not in first]
@@ -325,7 +426,7 @@
 def _scatter_kernel(pieces, orders, seq, n_arr, work, *refs):
     table, _ = _slots(pieces, orders, seq)
     n = len(pieces)
-    paired = [p[3] != 'chip' for p in pieces]
+    paired = [p[KIND] != 'chip' for p in pieces]
     n_late, n_in, n_out, n_scr = (work.arrays, work.inputs, work.outputs, work.scratches) if work else (0, 0, 0, 0)
     cut = lambda count: [refs_left.pop(0) for _ in range(count)]
     refs_left = list(refs)
@@ -354,7 +455,7 @@
             self.u = u
             self.first, self.parts, self.rest = _order(u, seq, orders, n, len(late), 15, work.after if work else ())
             self.keys = self.first + sum(self.parts, []) + self.rest
-            self.adds = [[key for key in self.keys if key[3] == i and (paired[i] or _onward(u, key, orders))] for i in range(n)]
+            self.adds = [[key for key in self.keys if key[PIECE] == i and (paired[i] or _onward(u, key, orders))] for i in range(n)]
             self.sent, self.given, self.done = [], [0] * n, [0] * n
 
         def meet(self):
@@ -365,7 +466,7 @@
 
         def ready(self, some):
             for key in self.keys:
-                piece = key[3]
+                piece = key[PIECE]
                 if paired[piece] and piece in some:
                     kc = partner_at.chip(key)
                     copy = _remote(term(piece, kc, 1 - at.core), got[piece].at[kc], d_send.at[piece, self.given[piece]], d_recv.at[piece, kc], at.partner)
@@ -376,7 +477,7 @@
                     self.load(piece, j).start()
 
         def step(self, key):
-            u, piece = self.u, key[3]
+            u, piece = self.u, key[PIECE]
             arr, _, rows, _ = pieces[piece]
             kc = at.chip(key)
             root = key[:3] == (0, 0, u)
@@ -468,9 +569,9 @@
     shapes = [(rows, every[arr].shape[-1], every[arr].dtype) for arr, _, rows, _ in pieces]
     scratch = [pltpu.VMEM((m, r, c), d) for m, (r, c, d) in zip(most, shapes)]
     scratch += [pltpu.VMEM((PAIR, r, c), d) for r, c, d in shapes]
-    scratch += [pltpu.VMEM((CHIPS, r, c), d) for (r, c, d), p in zip(shapes, pieces) if p[3] != 'chip']
+    scratch += [pltpu.VMEM((CHIPS, r, c), d) for (r, c, d), p in zip(shapes, pieces) if p[KIND] != 'chip']
     outs = [jax.ShapeDtypeStruct((sum(p[PAIR] for p in pieces if p[0] == i), v.shape[-1]), v.dtype) for i, v in enumerate(every)]
-    nbytes = sum((m + PAIR + CHIPS * int(p[3] != 'chip')) * (-(-r // CHIPS) * CHIPS) * c * d.itemsize for m, (r, c, d), p in zip(most, shapes, pieces))
+    nbytes = sum((m + PAIR + CHIPS * int(p[KIND] != 'chip')) * (-(-r // CHIPS) * CHIPS) * c * d.itemsize for m, (r, c, d), p in zip(most, shapes, pieces))
     scratch += [dma((n, PAIR)), dma((CHIPS * n,)), dma((n, max(most))), dma((n, CHIPS)), dma((n, CHIPS)), dma((n,))]
     work_in = work.operands if work else []
     work_out = work.results if work else []
@@ -485,61 +586,6 @@
         cost_estimate=cost(200_000_000, nbytes * QUAD),
         name='scatter_sum',
     )(*arrays, *[v for v, _ in work_in])
-
-
-def _lookup_kernel(counts, codes, table_ref, out_ref, rows, block, sem):
-    b = pl.program_id(0)
-    n_col = out_ref.shape[PAIR] // LANES
-    n_rows = rows.shape[0] // n_col
-
-    @pl.when(b == 0)
-    def _():
-        def widen(i):
-            for j in range(n_col):
-                part = table_ref[pl.ds(pl.multiple_of(i * CHIPS, CHIPS), CHIPS), j * LANES:(j + 1) * LANES].astype(F32)
-                line = pl.multiple_of(i * CHIPS * n_col, SUB)
-                rows[pl.ds(line + j * SUB, SUB), :] = part[:SUB]
-                rows[pl.ds(line + (n_col + j) * SUB, SUB), :] = part[SUB:]
-        loop(n_rows // CHIPS, widen)
-
-    seq = out_ref.shape[1]
-
-    def clear(i):
-        block[pl.ds(pl.multiple_of(i * SUB * n_col, SUB), SUB * n_col), :] = jnp.zeros((SUB * n_col, LANES), F32)
-    loop(seq // SUB, clear)
-
-    def pick(i):
-        for t in range(SUB):
-            code = codes[b * seq + i * SUB + t]
-            block[pl.ds(code >> CHIPS, n_col, stride=SUB), :] = rows[pl.ds(code & 65535, n_col, stride=SUB), :]
-    loop((counts[b] + 7) // SUB, pick)
-
-    def narrow(i):
-        line = pl.multiple_of(i * CHIPS * n_col, SUB)
-        for j in range(n_col):
-            part = jnp.concatenate([block[pl.ds(line + j * SUB, SUB), :], block[pl.ds(line + (n_col + j) * SUB, SUB), :]], axis=0)
-            out_ref[0, pl.ds(pl.multiple_of(i * CHIPS, CHIPS), CHIPS), j * LANES:(j + 1) * LANES] = part.astype(BF16)
-    loop(seq // CHIPS, narrow)
-
-
-def lookup(table, counts, codes, seq):
-    n_rows, dim = table.shape
-    n_src = counts.shape[0]
-    lines = dim // LANES
-    return pl.pallas_call(
-        _lookup_kernel,
-        grid_spec=pltpu.PrefetchScalarGridSpec(
-            num_scalar_prefetch=PAIR,
-            grid=(n_src,),
-            in_specs=[pl.BlockSpec(memory_space=pltpu.VMEM)],
-            out_specs=pl.BlockSpec((1, seq, dim), lambda b, *_: (b, 0, 0)),
-            scratch_shapes=[pltpu.VMEM((n_rows * lines, LANES), F32), pltpu.VMEM(((seq + SUB) * lines, LANES), F32), pltpu.SemaphoreType.DMA],
-        ),
-        out_shape=jax.ShapeDtypeStruct((n_src, seq, dim), table.dtype),
-        compiler_params=pltpu.CompilerParams(vmem_limit_bytes=40 * MIB, dimension_semantics=('arbitrary',)),
-        cost_estimate=cost(50_000_000, 40 * MIB),
-        name='lookup',
-    )(counts, codes, table)
 
 
 def _add_rows_kernel(counts, codes, dx_ref, out_ref, buf, sem):
@@ -1038,25 +1084,17 @@
             below(tokens.reshape(-1, LANES), QUAD), n_dev, [w_down, gate_up(1 - core), other_attn, dy], ('use', 'pair', 'pair', 'pair'), 0)
         wgu = gather_group(both_cores(gate_up(core), recv_gu))
 
-        (attn_w, wd), _ = gather_all([both_cores(mine_attn, recv_attn), down_block], [(0, 0, PAIR * rows_w, 'core'), (1, 0, down_block.shape[0], 'chip')],
-                                     ('bza', 'zba'), ATTN_SEQ, [], (), n_dev, 1)
-        attn_w = attn_w.reshape(PAIR, model_dim, n_in)
-        wd = wd.reshape(-1, model_dim)
-
         all_ids = all_tokens[:, :seq_len // LANES].reshape(-1)
         local_ids = all_ids - me * rows_local
         is_owner = (local_ids >= 0) & (local_ids < rows_local)
-        own = is_owner.reshape(n_dev, seq_len)
-        slot = jnp.arange(seq_len, dtype=jnp.int32)
-        upto = (slot[:, None] <= slot[None, :]).astype(BF16)
-        rank = jnp.where(own, mm(own.astype(BF16), upto).astype(jnp.int32) - 1, -1)
-        counts = jnp.sum(own.astype(jnp.int32), axis=1)
         lines = model_dim // LANES
         line = lambda row: row // SUB * (SUB * lines) + row % SUB
-        code = line(slot)[None] * 65536 + line(jnp.where(own, local_ids.reshape(n_dev, seq_len), 0))
-        codes = jnp.sum(jnp.where(rank[:, :, None] == slot, code[:, :, None], 0), axis=1)
-        codes = jnp.where(slot[None] < counts[:, None], codes, seq_len * lines * 65536).reshape(-1)
-        picked = lookup(table_shard, counts, codes, seq_len)
+        found = (jnp.where(is_owner, line(local_ids), rows_local * lines), table_shard, seq_len)
+        (attn_w, wd), (picked,) = gather_all([both_cores(mine_attn, recv_attn), down_block], [(0, 0, PAIR * rows_w, 'core'), (1, 0, down_block.shape[0], 'chip')],
+                                     ('bza', 'zba'), ATTN_SEQ, [], (), n_dev, 1, found)
+        attn_w = attn_w.reshape(PAIR, model_dim, n_in)
+        wd = wd.reshape(-1, model_dim)
+
         x_emb = scatter_sum([picked], [(0, 0, 192, 'device'), (0, 192, 208, 'device'), (0, 400, 112, 'device')], ('zba', 'zba', 'baz'), ROWS_SEQ, PAIR)[0]
 
         dy2 = jnp.concatenate([dy, dy_other], axis=0)
@@ -1087,6 +1125,14 @@
         (all_dx,), (down_shard, recv) = gather_all(
             [to_lines(dx_block)], [(0, 0, 200 * lines, 'device'), (0, 200 * lines, 200 * lines, 'device'), (0, 400 * lines, 120 * lines, 'device')],
             ('zba', 'zba', 'baz'), ROWS_SEQ, [down_rows, give], ('store', 'pair'), n_dev, QUAD)
+        own = is_owner.reshape(n_dev, seq_len)
+        slot = jnp.arange(seq_len, dtype=jnp.int32)
+        upto = (slot[:, None] <= slot[None, :]).astype(BF16)
+        rank = jnp.where(own, mm(own.astype(BF16), upto).astype(jnp.int32) - 1, -1)
+        counts = jnp.sum(own.astype(jnp.int32), axis=1)
+        code = line(slot)[None] * 65536 + line(jnp.where(own, local_ids.reshape(n_dev, seq_len), 0))
+        codes = jnp.sum(jnp.where(rank[:, :, None] == slot, code[:, :, None], 0), axis=1)
+        codes = jnp.where(slot[None] < counts[:, None], codes, seq_len * lines * 65536).reshape(-1)
         d_table = from_lines(add_rows(all_dx, counts, codes, rows_local), model_dim)
         gains_grad = from_lines(jnp.sum(all_dx[:, seq_len * lines:], axis=0), model_dim)
         qk = gains_grad[0]

time: 884 us -> 883 us (level)
    pallas_call x1 -> x0, Pallas kernels: 39.8 us -> none  [lookup(): pl.pallas_call(_lookup_kernel, grid_spec=pltpu.PrefetchScalarGridSpec(num...]
    pallas_call x2, Pallas kernels: 329 us -> 360 us  [scatter_sum(): pl.pallas_call(functools.partial(_scatter_kernel, tuple(pieces), orders,...]
    unnamed x91 -> x87, local copies, waits for them, and re-layouts: 26.4 us -> 26.8 us
  transfers between devices with their start and end apart: 4 -> 4, of which waited for: 2 -> 1; matrix products, arithmetic and copies ran while one was open for 2% -> 3% of each run, Pallas kernels for 82% -> 82%
where the time goes in v9:
time: 883 us; the launch traced here: 881 us
  Pallas kernels  806 us (91%)
  local copies, waits for them, and re-layouts  37.1 us (4%)
  other arithmetic  21.9 us (2%)
  between operations  14.6 us (2%)
    pallas_call x2, Pallas kernels, scatter_sum(): pl.pallas_call(functools.partial(_scatter_kernel, tuple(pieces), orders,...  360 us
    pallas_call x2, Pallas kernels, gather_all(): pl.pallas_call(functools.partial(_gather_kernel, tuple(pieces), orders, s...  306 us
    pallas_call x1, Pallas kernels, mlp(): pl.pallas_call(_mlp_kernel, out_shape=[sds(rows // PAIR, dim)] * QUAD + [...  61.1 us
    pallas_call x1, Pallas kernels, add_rows(): pl.pallas_call(_add_rows_kernel, grid_spec=pltpu.PrefetchScalarGridSpec(n...  36.8 us
    unnamed x87, local copies, waits for them, and re-layouts  26.8 us
    pallas_call x1, Pallas kernels, attn_forward(): pl.pallas_call(_attn_fwd_kernel, out_shape=[sds(dim), sds(n_in), sds(dim)...  20.1 us
    pallas_call x1, Pallas kernels, all_rows(): pl.pallas_call(functools.partial(_all_rows_kernel, n_dev, moves), out_sha...  18.4 us
  transfers between devices with their start and end apart: 4, of which 1 were waited for; matrix products, arithmetic and copies ran while one was open for 3% of the time, Pallas kernels for 82%

profile of v9, /device:TPU:0, one launch (start us, length us, event | category | flops | bytes accessed | tf_op | source)
XLA Modules:
  0.0 881.5 jit_solution(9653711495405539696)
XLA Ops:
  7.3 1.3 pad.13.refs_0_
  8.5 0.7 pad_maximum_fusion.6
  9.2 0.1 copy.33
  9.3 0.8 constant_dynamic-update-slice_fusion.2
  10.2 0.7 constant_dynamic-update-slice_fusion.1
  10.9 0.7 constant_dynamic-update-slice_fusion
  11.6 1.2 constant_dynamic-slice_fusion.3
  12.8 0.7 pad_maximum_fusion.4.refs_2_
  13.5 0.7 broadcast_select_fusion.1
  14.2 18.4 %all_rows.1 = (s32[32,8,128]{2,1,0:T(8,128)}, bf16[152,896]{1,0:T(8,128)(2,1)}, bf16[28,4864]{1,0:T(8,128)(2,1)}, bf16[28,1152]{1,0:T(8,128)(2,1)}, bf16[512,896]{1,0:T(8,128)(2,1)}) custom-call(s32[8,128]{1,0:T(8,128)} %pad.13.refs_0_, bf16[152,896]{1,0:T(8,128)(2,1)} %refs_1_.1, bf16[28,4864]{1,0:T(8,128)(2,1)} %pad_maximum_fusion.4.refs_2_, ...), custom_call_target="tpu_custom_call" | custom-call | flops 10000000 | bytes 1048576 | tf_op jit(solution)/shard_map/all_rows/pallas_call | solution.py:192
  32.6 2.1 maximum_select_fusion
  34.8 0.1 stack_tile.6
  34.8 0.1 stack_tile.7
  34.9 1.6 convert_reduce_fusion
  36.7 3.4 copy-done.3
  40.1 87.0 %gather_all.2 = (bf16[32,56,1152]{2,1,0:T(8,128)(2,1)S(1)}, bf16[16,152,896]{2,1,0:T(8,128)(2,1)S(1)}, bf16[32,512,896]{2,1,0:T(8,128)(2,1)}) custom-call(bf16[56,1152]{1,0:T(8,128)(2,1)S(1)} %maximum_select_fusion.1.refs_0_, bf16[152,896]{1,0:T(8,128)(2,1)S(1)} %copy-done.25, s32[16384]{0:T(1024)S(1)} %fusion.5.refs_2_, bf16[4752,896]{1,0:T(8,128)(2,1)S(1)} %copy-done.3), custom_call_target="tpu_custom_call" | custom-call | flops 200000000 | bytes 1770520576 | tf_op jit(solution)/shard_map/gather_all/pallas_call | solution.py:318
  127.1 2.0 copy-done.32
  129.1 2.0 copy-done
  131.2 0.2 copy.34
  131.4 134.3 %scatter_sum.2.x_ref.refs_8_ = bf16[512,896]{1,0:T(8,128)(2,1)S(1)} custom-call(bf16[32,512,896]{2,1,0:T(8,128)(2,1)} %get-tuple-element.51.refs_0_), custom_call_target="tpu_custom_call" | custom-call | flops 200000000 | bytes 133267456 | tf_op jit(solution)/shard_map/scatter_sum/pallas_call | solution.py:579
  265.8 1.0 multiply_sine_fusion
  266.8 20.1 %attn_forward.1 = (bf16[512,896]{1,0:T(8,128)(2,1)S(1)}, bf16[512,1152]{1,0:T(8,128)(2,1)S(1)}, bf16[512,896]{1,0:T(8,128)(2,1)S(1)}, bf16[512,128]{1,0:T(8,128)...) custom-call(bf16[512,896]{1,0:T(8,128)(2,1)S(1)} %scatter_sum.2.x_ref.refs_8_, ...), custom_call_target="tpu_custom_call" | custom-call | flops 4000000000 | bytes 12582912 | tf_op jit(solution)/shard_map/attn_forward/pallas_call | solution.py:766
  287.0 0.9 copy-done.19
  287.9 0.9 copy-done.20
  288.9 1.6 pad_maximum_fusion.1.dy_ref
  290.5 0.2 copy-done.18
  290.8 0.6 collective-permute-done
  291.4 1.4 pad_maximum_fusion.x_ref
  292.8 1.5 copy-done.9
  294.2 61.1 %mlp.1 = (f32[512,896]{1,0:T(8,128)S(1)}, f32[512,896]{1,0:T(8,128)S(1)}, f32[512,896]{1,0:T(8,128)S(1)}, f32[512,896]{1,0:T(8,128)}, f32[896,2432]{1,0:T(8,128)...) custom-call(bf16[1024,896]{1,0:T(8,128)(2,1)S(1)} %copy-done.9, bf16[1024,896]{1,0:T(8,128)(2,1)} %pad_maximum_fusion.1.dy_ref, ...), custom_call_target="tpu_custom_call" | custom-call | flops 35701915648 | bytes 52428800 | tf_op jit(solution)/shard_map/mlp/pallas_call | solution.py:1013
  355.3 1.2 copy-done.10
  356.5 1.2 copy-done.12
  357.8 1.3 copy-done.33
  359.0 0.1 collective-permute-start.2
  359.2 0.2 fusion.1
  359.4 0.1 fusion.8
  359.5 5.9 select_reduce_fusion
  365.4 0.1 select_bitcast_fusion
  365.5 0.6 copy.36
  366.1 0.4 collective-permute-start.1
  366.5 2.2 copy-done.2
  368.7 1.5 copy-done.13
  370.2 4.7 hidden_backward.1
  374.9 1.2 copy-done.14
  376.1 1.0 copy-done.21
  377.1 0.9 copy-done.22
  378.1 0.6 copy-done.29
  378.7 225.4 %scatter_sum.3 = (f32[152,896]{1,0:T(8,128)}, f32[56,2432]{1,0:T(8,128)}, f32[56,2432]{1,0:T(8,128)}, f32[32,1152]{1,0:T(8,128)}, f32[32,896]{1,0:T(8,128)}, /*i...) custom-call(f32[16,152,896]{2,1,0:T(8,128)} %bitcast.75, f32[16,56,2432]{2,1,0:T(8,128)} %bitcast.73, ...), custom_call_target="tpu_custom_call" | custom-call | flops 200000000 | bytes 184483840 | tf_op jit(solution)/shard_map/scatter_sum/pallas_call | solution.py:579
  604.1 1.6 constant_dynamic-slice_fusion
  605.7 1.7 constant_dynamic-slice_fusion.1
  607.4 1.1 constant_dynamic-update-slice_fusion.4
  608.7 218.7 %gather_all.3 = (f32[32,3640,128]{2,1,0:T(8,128)}, f32[152,896]{1,0:T(8,128)S(1)}, f32[28,4864]{1,0:T(8,128)S(1)}) custom-call(f32[3640,128]{1,0:T(8,128)S(1)} %bitcast.69, f32[152,896]{1,0:T(8,128)S(1)} %copy-done.24, f32[28,4864]{1,0:T(8,128)S(1)} %constant_dynamic-slice_fusion.2.refs_2_), custom_call_target="tpu_custom_call" | custom-call | flops 200000000 | bytes 119275520 | tf_op jit(solution)/shard_map/gather_all/pallas_call | solution.py:318
  827.4 0.1 dynamic-slice_select_fusion.1
  827.6 1.3 slice_reduce_fusion
  828.9 36.8 %add_rows.1 = f32[33264,128]{1,0:T(8,128)} custom-call(s32[32]{0:T(128)S(1)} %copy-done.31, s32[16384]{0:T(1024)S(1)} %bitcast.70, f32[32,3640,128]{2,1,0:T(8,128)} %get-tuple-element.78.dx_ref), custom_call_target="tpu_custom_call" | custom-call | flops 50000000 | bytes 83886080 | tf_op jit(solution)/shard_map/add_rows/pallas_call | solution.py:645
  865.7 0.6 dynamic_slice.38
  866.3 0.6 dynamic_slice.35
  866.9 0.6 fusion.39
  867.5 1.4 fusion.38
  868.9 0.9 pad_maximum_fusion.3
  869.8 0.9 pad_maximum_fusion.2
  870.7 0.4 copy-done.11
  871.1 2.8 fusion.2
  873.9 0.8 copy.49
  (89 shorter events, 0.8 us)
Async XLA Ops:
  7.2 6.3 copy-start.37
  7.2 285.6 %all-gather.2.cloned.1.call-start = ((), (), s32[]{:S(2)}) async-start(), calls=%async_computation | async-start | bytes 9261056 | tf_op jit(solution)/shard_map/all_gather | solution.py:1060
  13.5 21.2 %copy-start.39 = (bf16[64]{0:T(256)(128)(2,1)S(1)}, bf16[64]{0:T(256)(128)(2,1)}, u32[]{:S(2)}) copy-start(bf16[64]{0:T(256)(128)(2,1)} %param.22) | copy-start | bytes 388
  13.5 21.3 %copy-start.40 = (bf16[64]{0:T(256)(128)(2,1)S(1)}, bf16[64]{0:T(256)(128)(2,1)}, u32[]{:S(2)}) copy-start(bf16[64]{0:T(256)(128)(2,1)} %param.23) | copy-start | bytes 388
  13.5 21.4 %copy-start.38 = (s32[1,512]{1,0:T(1,128)S(1)}, s32[1,512]{1,0:T(1,128)}, u32[]{:S(2)}) copy-start(s32[1,512]{1,0:T(1,128)} %param.16) | copy-start | bytes 6148
  32.6 4.0 copy-start.36
  32.6 4.1 copy-start.25
  36.5 328.9 %copy-start.30 = (s32[32]{0:T(128)}, s32[32]{0:T(128)S(1)}, u32[]{:S(2)}) copy-start(s32[32]{0:T(128)S(1)} %get-tuple-element.86.counts) | copy-start | bytes 388
  36.7 3.4 copy-start.3
  127.1 2.0 copy-start.32
  129.1 2.0 copy-start
  131.4 235.2 %copy-start.23 = (f32[24,896]{1,0:T(8,128)}, f32[24,896]{1,0:T(8,128)S(1)}, u32[]{:S(2)}) copy-start(f32[24,896]{1,0:T(8,128)S(1)} %pad.14.gain_ref.refs_3_) | copy-start | bytes 258052
  131.4 135.4 %copy-start.1 = (bf16[32,56,1152]{2,1,0:T(8,128)(2,1)S(1)}, bf16[32,56,1152]{2,1,0:T(8,128)(2,1)}, u32[]{:S(2)}) copy-start(bf16[32,56,1152]{2,1,0:T(8,128)(2,1)} %copy-done) | copy-start | bytes 12386308
  265.7 21.2 %copy-start.7 = (bf16[512,896]{1,0:T(8,128)(2,1)}, bf16[512,896]{1,0:T(8,128)(2,1)S(1)}, u32[]{:S(2)}) copy-start(bf16[512,896]{1,0:T(8,128)(2,1)S(1)} %scatter_sum.2.x_ref.refs_8_) | copy-start | bytes 2752516
  265.8 21.2 %copy-start.28 = (f32[16,128]{1,0:T(8,128)}, f32[16,128]{1,0:T(8,128)S(1)}, u32[]{:S(2)}) copy-start(f32[16,128]{1,0:T(8,128)S(1)} %broadcast_bitcast_fusion.1.qk_gain_ref.refs_7_) | copy-start | bytes 24580
  266.8 20.2 %copy-start.16 = (f32[512,128]{1,0:T(8,128)}, f32[512,128]{1,0:T(8,128)S(1)}, u32[]{:S(2)}) copy-start(f32[512,128]{1,0:T(8,128)S(1)} %get-tuple-element.104.sin_ref.refs_6_) | copy-start | bytes 786436
  266.8 20.2 %copy-start.17 = (f32[512,128]{1,0:T(8,128)}, f32[512,128]{1,0:T(8,128)S(1)}, u32[]{:S(2)}) copy-start(f32[512,128]{1,0:T(8,128)S(1)} %get-tuple-element.105.cos_ref.refs_5_) | copy-start | bytes 786436
  266.8 22.1 %copy-start.4 = (bf16[1,512,896]{2,1,0:T(8,128)(2,1)S(1)}, bf16[1,512,896]{2,1,0:T(8,128)(2,1)}, u32[]{:S(2)}) copy-start(bf16[1,512,896]{2,1,0:T(8,128)(2,1)} %param.29) | copy-start | bytes 2752516
  266.8 22.1 %copy-start.34 = (bf16[512,896]{1,0:T(8,128)(2,1)S(1)}, bf16[512,896]{1,0:T(8,128)(2,1)}, u32[]{:S(2)}) copy-start(bf16[512,896]{1,0:T(8,128)(2,1)} %get-tuple-element.55) | copy-start | bytes 2752516
  287.0 0.9 copy-start.19
  287.9 0.9 copy-start.20
  288.8 1.7 copy-start.15
  288.8 1.9 copy-start.18
  288.8 1.9 copy-start.27
  288.8 77.7 %copy-start.5 = (bf16[512,896]{1,0:T(8,128)(2,1)}, bf16[512,896]{1,0:T(8,128)(2,1)S(1)}, u32[]{:S(2)}) copy-start(bf16[512,896]{1,0:T(8,128)(2,1)S(1)} %get-tuple-element.53.hid_ref) | copy-start | bytes 2752516
  288.8 2.5 collective-permute-start
  292.7 1.5 copy-start.9
  355.3 1.2 copy-start.10
  356.5 1.2 copy-start.12
  357.8 1.3 copy-start.33
  359.0 7.5 collective-permute-start.2
  366.1 504.5 %collective-permute-start.1 = (f32[512,896]{1,0:T(8,128)}, f32[512,896]{1,0:T(8,128)}, u32[]{:S(2)}, u32[]{:S(2)}) collective-permute-start(f32[512,896]{1,0:T(8,128)} %copy-done.33), channel_id=1, source_target_pairs={{0,1},{1,0},{2,3},{3,2},{4,5},{5,4},{6,7},{7,6},{8,9},{9,8},{10,11... | collective-permute-start | bytes 5505032 | tf_op jit(solution)/shard_map/ppermute | solution.py:1057
  366.5 2.2 copy-start.2
  368.7 1.5 copy-start.13
  374.9 1.2 copy-start.14
  376.1 1.0 copy-start.21
  377.1 0.9 copy-start.22
  378.1 0.6 copy-start.29
  604.1 4.4 copy-start.35
  605.7 2.9 copy-start.8
  605.7 2.9 copy-start.24
  827.4 1.5 copy-start.26
  827.4 1.5 copy-start.31
  868.9 1.8 copy-start.6
  868.9 2.2 copy-start.11
Sparse Core Ops, SparseCore 0:
  34.9 164.1 all-gather.1
